TPU v7x, 256 devices: a whole 4x4x8 slice. The times are simulated.
256 devices in a mesh: blk: 128 (over x, y, z), grp: 2 (over core).
Axes of the slice: x: 4, y: 4, z: 8, core: 2. Of those that a mesh axis runs over, the one named last changes fastest.
Arguments:
- item_start: bfloat16 [32768, 128], P(('blk', 'grp')), may hold values from -0.5 to 0.5
- ratings: bfloat16 [4, 8192, 256], P(None, 'blk', 'grp'), may hold values from -6 to 6
- rating_bits: int32 [4, 8192], P(None, 'blk'), may hold values from -2147483648 to 2147483647, as said below
- plan: int32 [4], replicated, may hold values from 1 to 127, as said below
Outputs:
- user_factors: bfloat16 [8192, 128], P(('blk', 'grp'))
- item_factors: bfloat16 [32768, 128], P(('blk', 'grp'))
Inputs may be any that keep to these rules, and one draw needn't show every extreme that they name: `plan`: the 4 offsets are distinct, and among them are 127 and 64. `rating_bits`: every word has a set bit among bits 0 to 15 and one among bits 16 to 31.
All inputs are finite; a program needn't handle non-finite values. Where the computation divides by a largest or mean magnitude, that divisor is 1e-20 or more.
Results may differ from a plain program's by a relative error of at most 0.015.
Values may be sent and summed in bfloat16 or wider, within the bound.
No kernel may reach another device: no remote copies, remote signals or barrier semaphores. Data moves between devices by JAX's collectives and lax.ppermute only.
A program may use at most 64 MiB of HBM per device.

v0:
```python
import functools

import jax
import jax.numpy as jnp
from jax import lax
from jax.experimental import pallas as pl
from jax.experimental.pallas import tpu as pltpu
from jax.sharding import Mesh, PartitionSpec as P

SWEEPS = 4
RIDGE = 0.005
UNRATED = 64.0
RATED_BELOW = 32.0
AXES = ("x", "y", "z")
VMEM = pltpu.MemorySpace.VMEM
SMEM = pltpu.MemorySpace.SMEM


def split_parts(value):
    high = value.astype(jnp.bfloat16)
    low = (value - high.astype(jnp.float32)).astype(jnp.bfloat16)
    return jnp.concatenate([high, low], axis=0)


def dot_f32(a, b, dims=((1,), (0,))):
    return lax.dot_general(a, b, (dims, ((), ())), preferred_element_type=jnp.float32)


def relax(right, ridge, bound, rated, factors):
    rows = right.shape[0]
    inverse = 1.0 / bound
    answer = right * inverse
    for _ in range(SWEEPS - 1):
        inner = dot_f32(split_parts(answer), factors, ((1,), (1,)))
        inner = jnp.where(rated, inner[:rows] + inner[rows:], 0.0)
        outer = dot_f32(split_parts(inner), factors)
        applied = outer[:rows] + outer[rows:] + ridge * answer
        answer = answer + (right - applied) * inverse
    return answer.astype(jnp.bfloat16)


def users_kernel(own_ref, other_ref, own_marks_ref, other_marks_ref, out_ref, factor_t_ref, mask_ref, sums_ref):
    tiles = own_ref.shape[0]
    half = own_ref.shape[1]
    rank = own_ref.shape[2]
    rows = out_ref.shape[0]
    parts = []
    marks = []
    for k in range(tiles):
        parts += [own_ref[k], other_ref[k]]
        marks += [own_marks_ref[k], other_marks_ref[k]]
    factors = jnp.concatenate(parts, axis=0)
    marked = jnp.concatenate(marks, axis=1).astype(jnp.float32)
    rated = jnp.abs(marked) < RATED_BELOW
    factor_t_ref[...] = factors.T
    mask = jnp.where(rated, 1.0, 0.0)
    mask_ref[...] = mask
    count = jnp.sum(mask, axis=1, keepdims=True)
    right = dot_f32(jnp.where(rated, marked, 0.0).astype(jnp.bfloat16), factors)

    def one(step, carry):
        for j in range(4):
            u = step * 4 + j
            row = mask_ref[pl.ds(u, 1), :].astype(jnp.bfloat16)
            gram = dot_f32(factor_t_ref[...] * row, factors)
            sums_ref[pl.ds(u, 1), :] = jnp.sum(jnp.abs(gram), axis=0, keepdims=True)
        return carry

    lax.fori_loop(0, rows // 4, one, 0)
    ridge = RIDGE * (count + 1.0)
    bound = jnp.max(sums_ref[...], axis=1, keepdims=True) + ridge
    out_ref[...] = relax(right, ridge, bound, rated, factors)


def items_kernel(own_ref, other_ref, marks_ref, out_ref, sums_ref):
    tiles = own_ref.shape[0]
    rank = own_ref.shape[2]
    items = out_ref.shape[0]
    parts = []
    for k in range(tiles):
        parts += [own_ref[k], other_ref[k]]
    factors = jnp.concatenate(parts, axis=0)
    factor_t = factors.T
    marked = jnp.concatenate([marks_ref[k].astype(jnp.float32) for k in range(tiles)], axis=0).T
    rated = jnp.abs(marked) < RATED_BELOW
    mask = jnp.where(rated, 1.0, 0.0)
    count = jnp.sum(mask, axis=1, keepdims=True)
    right = dot_f32(jnp.where(rated, marked, 0.0).astype(jnp.bfloat16), factors)
    group = 8
    for j in range(items // group):
        row = mask[j * group : j * group + 1].astype(jnp.bfloat16)
        gram = dot_f32(factor_t * row, factors)
        total = jnp.sum(jnp.abs(gram), axis=0, keepdims=True)
        sums_ref[j * group : (j + 1) * group, :] = jnp.broadcast_to(total, (group, rank))
    ridge = RIDGE * (count + 1.0)
    bound = jnp.max(sums_ref[...], axis=1, keepdims=True) + ridge
    out_ref[...] = relax(right, ridge, bound, rated, factors)


def vmem_specs(count):
    return [pl.BlockSpec(memory_space=VMEM)] * count


def solve_users(own, other, own_marks, other_marks):
    tiles, half, rank = own.shape
    rows = own_marks.shape[1]
    width = tiles * 2 * half
    return pl.pallas_call(
        users_kernel,
        out_shape=jax.ShapeDtypeStruct((rows, rank), jnp.bfloat16),
        in_specs=vmem_specs(4),
        out_specs=pl.BlockSpec(memory_space=VMEM),
        scratch_shapes=[
            pltpu.VMEM((rank, width), jnp.bfloat16),
            pltpu.VMEM((rows, width), jnp.float32),
            pltpu.VMEM((rows, rank), jnp.float32),
        ],
        name="users",
    )(own, other, own_marks, other_marks)


def solve_items(own, other, marks):
    tiles, half, rank = own.shape
    items = marks.shape[2]
    return pl.pallas_call(
        items_kernel,
        out_shape=jax.ShapeDtypeStruct((items, rank), jnp.bfloat16),
        in_specs=vmem_specs(3),
        out_specs=pl.BlockSpec(memory_space=VMEM),
        scratch_shapes=[pltpu.VMEM((items, rank), jnp.float32)],
        name="items",
    )(own, other, marks)


def pick_kernel(index_ref, source_ref, out_ref, *, units):
    for j, unit in enumerate(units):
        out_ref[j] = source_ref[index_ref[j], unit]


def pick(index, source, units):
    return pl.pallas_call(
        functools.partial(pick_kernel, units=units),
        out_shape=jax.ShapeDtypeStruct((len(units), *source.shape[2:]), source.dtype),
        in_specs=[pl.BlockSpec(memory_space=SMEM), pl.BlockSpec(memory_space=VMEM)],
        out_specs=pl.BlockSpec(memory_space=VMEM),
        name="pick",
    )(index, source)


def sent_to_all(value, axes):
    count = lax.axis_size(axes)
    copies = jnp.broadcast_to(value, (count, *value.shape))
    return lax.all_to_all(copies, axes, split_axis=0, concat_axis=0, tiled=True)


def fetched_from(value, axis, steps):
    count = lax.axis_size(axis)
    return lax.ppermute(value, axis, [((target + steps) % count, target) for target in range(count)])


def shift_digits(shift):
    nz, ny, nx = lax.axis_size("z"), lax.axis_size("y"), lax.axis_size("x")
    z = lax.axis_index("z") + shift % nz
    y_step = (shift // nz) % ny + z // nz
    y = lax.axis_index("y") + y_step
    x_step = shift // (nz * ny) + y // ny
    return z % nz, y_step % ny, x_step % nx


def fetch(value, source_units, digits):
    z_at, y_step, x_step = digits
    held = pick(z_at, sent_to_all(value, "z"), source_units)
    for axis, steps in (("y", y_step), ("x", x_step)):
        chosen = held
        for step in range(1, lax.axis_size(axis)):
            arrived = fetched_from(held, axis, step)
            chosen = jnp.where((steps == step)[:, None, None], arrived, chosen)
        held = chosen
    return held


def body(item_start, ratings, rating_bits, plan):
    tiles, users, items = ratings.shape
    rank = item_start.shape[1]
    own_half = lax.axis_index("grp")
    blocks = lax.axis_size(AXES)
    rows = users // 2
    partner = lambda value: fetched_from(value, "grp", 1)

    bit_count = 32 // lax.axis_size("grp")
    item_bits = own_half * bit_count + lax.broadcasted_iota(jnp.int32, (1, 1, items), 2) // (items // bit_count)
    rated = (jnp.right_shift(rating_bits[:, :, None], item_bits) & 1) == 1
    marks = jnp.where(rated, ratings, jnp.asarray(UNRATED, ratings.dtype))
    swapped = jnp.concatenate([marks[:, rows:], marks[:, :rows]], axis=1)
    marks = jnp.where(own_half == 0, marks, swapped)
    own_marks = marks[:, :rows]
    other_marks = partner(marks[:, rows:])

    forward = shift_digits(plan)
    backward = shift_digits((blocks - plan) % blocks)
    twice = lambda digits: tuple(jnp.repeat(d, 2) for d in digits)
    item_units = item_start.shape[0] // users

    value = jnp.concatenate([item_start.reshape(item_units, users, rank), marks], axis=0)
    units = [u for k in range(tiles) for u in range(item_units)] + [item_units + k for k in range(tiles)]
    both = tuple(jnp.concatenate([jnp.repeat(f, item_units), b]) for f, b in zip(forward, backward))
    arrived = fetch(value, units, both)
    own_items = arrived[: tiles * item_units].reshape(tiles, -1, rank)
    moved_marks = arrived[tiles * item_units :]
    first_users = solve_users(own_items, partner(own_items), own_marks, other_marks)

    own_users = fetch(first_users[None], [0] * tiles, backward)
    item_factors = solve_items(own_users, partner(own_users), moved_marks)

    own_items = fetch(item_factors[None], [0] * tiles, forward)
    user_factors = solve_users(own_items, partner(own_items), own_marks, other_marks)
    return (user_factors, item_factors)


def solution(mesh):
    torus = Mesh(mesh.devices.reshape(4, 4, 8, 2), (*AXES, "grp"))
    everywhere = (*AXES, "grp")
    in_specs = (P(everywhere, None), P(None, AXES, "grp"), P(None, AXES), P())
    out_specs = (P(everywhere, None), P(everywhere, None))
    return jax.shard_map(body, mesh=torus, in_specs=in_specs, out_specs=out_specs, check_vma=False)
```

profile of v0, /device:TPU:1, one launch (start us, length us, event | category | flops | bytes accessed | tf_op | source)
XLA Modules:
  0.0 161.0 jit_solution(9334592909566961820)
XLA Ops:
  1.3 0.9 fusion
  2.3 0.8 copy-done.3
  3.9 1.1 broadcast_in_dim.152
  5.0 9.0 %all-to-all-start = ((bf16[8,6,64,128]{3,2,1,0:T(8,128)(2,1)}), bf16[8,6,64,128]{3,2,1,0:T(8,128)(2,1)S(1)}, u32[]{:S(2)}, u32[]{:S(2)}) async-start(bf16[8,6,64,128]{3,2,1,0:T(8,128)(2,1)} %broadcast_in_dim.152), calls=%async_computation | async-start | bytes 1572864 | tf_op jit(solution)/shard_map/all_to_all | solution.py:153
  16.4 21.2 %all-to-all-done.source_ref = bf16[8,6,64,128]{3,2,1,0:T(8,128)(2,1)S(1)} async-done(((bf16[8,6,64,128]{3,2,1,0:T(8,128)(2,1)}), bf16[8,6,64,128]{3,2,1,0:T(8,128)(2,1)S(1)}, u32[]{:S(2)}, u32[]{:S(2)}) %all-to-all-start) | async-done | bytes 786464 | tf_op jit(solution)/shard_map/all_to_all | solution.py:153
  37.5 0.9 copy-done
  38.4 1.8 %pick.3 = bf16[12,64,128]{2,1,0:T(8,128)(2,1)} custom-call(s32[12]{0:T(128)} %pad_add_fusion.2.index_ref, bf16[8,6,64,128]{3,2,1,0:T(8,128)(2,1)} %copy-done), custom_call_target="tpu_custom_call" | custom-call | tf_op jit(solution)/shard_map/pick/pallas_call | solution.py:141
  40.3 1.3 collective-permute-start
  41.6 2.6 %collective-permute-start.1 = (bf16[12,64,128]{2,1,0:T(8,128)(2,1)}, bf16[12,64,128]{2,1,0:T(8,128)(2,1)S(1)}, u32[]{:S(2)}, u32[]{:S(2)}) collective-permute-start(bf16[12,64,128]{2,1,0:T(8,128)(2,1)} %pick.3), channel_id=1, source_target_pairs={{32,0},{48,16},{0,32},{16,48},{33,1},{49,17},{1,33},{17,49},{34,2}... | collective-permute-start | bytes 589832 | tf_op jit(solution)/shard_map/ppermute | solution.py:158
  44.2 1.1 collective-permute-start.2
  45.3 2.5 %collective-permute-done = bf16[12,64,128]{2,1,0:T(8,128)(2,1)S(1)} collective-permute-done((bf16[12,64,128]{2,1,0:T(8,128)(2,1)}, bf16[12,64,128]{2,1,0:T(8,128)(2,1)S(1)}, u32[]{:S(2)}, u32[]{:S(2)}) %collective-permute-start) | collective-permute-done | bytes 196640 | tf_op jit(solution)/shard_map/ppermute | solution.py:158
  47.8 5.3 %collective-permute-done.1 = bf16[12,64,128]{2,1,0:T(8,128)(2,1)S(1)} collective-permute-done((bf16[12,64,128]{2,1,0:T(8,128)(2,1)}, bf16[12,64,128]{2,1,0:T(8,128)(2,1)S(1)}, u32[]{:S(2)}, u32[]{:S(2)}) %collective-permute-start.1) | collective-permute-done | bytes 196640 | tf_op jit(solution)/shard_map/ppermute | solution.py:158
  53.1 1.0 select_select_fusion.1
  54.2 1.3 collective-permute-start.3
  55.5 2.5 %collective-permute-start.4 = (bf16[12,64,128]{2,1,0:T(8,128)(2,1)S(1)}, bf16[12,64,128]{2,1,0:T(8,128)(2,1)S(1)}, u32[]{:S(2)}, u32[]{:S(2)}) collective-permute-start(bf16[12,64,128]{2,1,0:T(8,128)(2,1)S(1)} %select_select_fusion.1), channel_id=1, source_target_pairs={{128,0},{192,64},{0,128},{64,192},{129,1},{193,65},{1,129},{65,193... | collective-permute-start | bytes 589832 | tf_op jit(solution)/shard_map/ppermute | solution.py:158
  57.9 1.2 collective-permute-start.5
  59.1 1.5 collective-permute-done.3
  60.6 5.2 %collective-permute-done.4 = bf16[12,64,128]{2,1,0:T(8,128)(2,1)S(1)} collective-permute-done((bf16[12,64,128]{2,1,0:T(8,128)(2,1)S(1)}, bf16[12,64,128]{2,1,0:T(8,128)(2,1)S(1)}, u32[]{:S(2)}, u32[]{:S(2)}) %collective-permute-start.4) | collective-permute-done | bytes 196640 | tf_op jit(solution)/shard_map/ppermute | solution.py:158
  65.9 2.3 %collective-permute-start.6 = (bf16[4,128,128]{2,1,0:T(8,128)(2,1)S(1)}, bf16[4,128,128]{2,1,0:T(8,128)(2,1)S(1)}, u32[]{:S(2)}, u32[]{:S(2)}) collective-permute-start(bf16[4,128,128]{2,1,0:T(8,128)(2,1)S(1)} %bitcast.2), channel_id=1, source_target_pairs={{1,0},{0,1},{3,2},{2,3},{5,4},{4,5},{7,6},{6,7},{9,8},{8,9},{11,10... | collective-permute-start | bytes 393224 | tf_op jit(solution)/shard_map/ppermute | solution.py:158
  68.9 1.2 collective-permute-done.7.other_marks_ref
  70.7 6.2 %users.2 = bf16[32,128]{1,0:T(8,128)(2,1)} custom-call(bf16[4,128,128]{2,1,0:T(8,128)(2,1)} %bitcast.3, bf16[4,128,128]{2,1,0:T(8,128)(2,1)} %copy-done.5, bf16[4,32,128]{2,1,0:T(8,128)(2,1)} %get-tuple-element.19.own_marks_ref, bf16[4,32,128]{2,1,0:T(8,128)(2,1)} %copy-done.7), custom_call_target="tpu_custom_call" | custom-call | tf_op jit(solution)/shard_map/users/pallas_call | solution.py:108
  77.0 0.7 broadcast_in_dim.157
  77.7 10.2 %all_to_all.15.source_ref = bf16[8,1,32,128]{3,2,1,0:T(8,128)(2,1)} all-to-all(bf16[8,1,32,128]{3,2,1,0:T(8,128)(2,1)S(1)} %broadcast_in_dim.157), channel_id=1, replica_groups=mesh['x'=4,'y'=4,'z'=8,'grp'=2] {'z'}, dimensions={0} | all-to-all | bytes 131072 | tf_op jit(solution)/shard_map/all_to_all | solution.py:153
  87.9 1.5 pick.4
  89.4 2.5 %collective-permute-start.10 = (bf16[4,32,128]{2,1,0:T(8,128)(2,1)}, bf16[4,32,128]{2,1,0:T(8,128)(2,1)S(1)}, u32[]{:S(2)}, u32[]{:S(2)}) collective-permute-start(bf16[4,32,128]{2,1,0:T(8,128)(2,1)} %pick.4), channel_id=1, source_target_pairs={{16,0},{32,16},{48,32},{0,48},{17,1},{33,17},{49,33},{1,49},{18,2}... | collective-permute-start | bytes 98312 | tf_op jit(solution)/shard_map/ppermute | solution.py:158
  91.9 1.2 collective-permute-start.9
  93.2 2.9 %collective-permute-done.8 = bf16[4,32,128]{2,1,0:T(8,128)(2,1)S(1)} collective-permute-done((bf16[4,32,128]{2,1,0:T(8,128)(2,1)}, bf16[4,32,128]{2,1,0:T(8,128)(2,1)S(1)}, u32[]{:S(2)}, u32[]{:S(2)}) %collective-permute-start.8) | collective-permute-done | bytes 32800 | tf_op jit(solution)/shard_map/ppermute | solution.py:158
  96.4 0.8 select_select_fusion.5
  97.3 1.3 collective-permute-start.11
  98.6 2.0 %collective-permute-start.12 = (bf16[4,32,128]{2,1,0:T(8,128)(2,1)S(1)}, bf16[4,32,128]{2,1,0:T(8,128)(2,1)S(1)}, u32[]{:S(2)}, u32[]{:S(2)}) collective-permute-start(bf16[4,32,128]{2,1,0:T(8,128)(2,1)S(1)} %select_select_fusion.5), channel_id=1, source_target_pairs={{128,0},{192,64},{0,128},{64,192},{129,1},{193,65},{1,129},{65,193... | collective-permute-start | bytes 98312 | tf_op jit(solution)/shard_map/ppermute | solution.py:158
  100.5 1.3 collective-permute-start.13
  101.9 0.9 collective-permute-done.12
  103.4 4.9 %collective-permute-start.14 = (bf16[4,32,128]{2,1,0:T(8,128)(2,1)S(1)}, bf16[4,32,128]{2,1,0:T(8,128)(2,1)S(1)}, u32[]{:S(2)}, u32[]{:S(2)}) collective-permute-start(bf16[4,32,128]{2,1,0:T(8,128)(2,1)S(1)} %select_select_fusion.4.own_ref), channel_id=1, source_target_pairs={{1,0},{0,1},{3,2},{2,3},{5,4},{4,5},{7,6},{6,7},{9,8},{8,9},{11,10... | collective-permute-start | bytes 98312 | tf_op jit(solution)/shard_map/ppermute | solution.py:158
  109.8 3.0 %items.1 = bf16[128,128]{1,0:T(8,128)(2,1)} custom-call(bf16[4,32,128]{2,1,0:T(8,128)(2,1)} %copy-done.4, bf16[4,32,128]{2,1,0:T(8,128)(2,1)} %copy-done.8, bf16[4,64,128]{2,1,0:T(8,128)(2,1)} %slice.29.marks_ref), custom_call_target="tpu_custom_call" | custom-call | tf_op jit(solution)/shard_map/items/pallas_call | solution.py:125
  112.8 0.8 broadcast_in_dim.162
  113.6 15.4 %all_to_all.16.source_ref = bf16[8,1,128,128]{3,2,1,0:T(8,128)(2,1)} all-to-all(bf16[8,1,128,128]{3,2,1,0:T(8,128)(2,1)S(1)} %broadcast_in_dim.162), channel_id=1, replica_groups=mesh['x'=4,'y'=4,'z'=8,'grp'=2] {'z'}, dimensions={0} | all-to-all | bytes 524288 | tf_op jit(solution)/shard_map/all_to_all | solution.py:153
  129.0 1.6 %pick.5 = bf16[4,128,128]{2,1,0:T(8,128)(2,1)} custom-call(s32[4]{0:T(128)} %copy-done.11, bf16[8,1,128,128]{3,2,1,0:T(8,128)(2,1)} %all_to_all.16.source_ref), custom_call_target="tpu_custom_call" | custom-call | tf_op jit(solution)/shard_map/pick/pallas_call | solution.py:141
  130.9 3.8 %collective-permute-start.16 = (bf16[4,128,128]{2,1,0:T(8,128)(2,1)}, bf16[4,128,128]{2,1,0:T(8,128)(2,1)S(1)}, u32[]{:S(2)}, u32[]{:S(2)}) collective-permute-start(bf16[4,128,128]{2,1,0:T(8,128)(2,1)} %pick.5), channel_id=1, source_target_pairs={{32,0},{48,16},{0,32},{16,48},{33,1},{49,17},{1,33},{17,49},{34,2}... | collective-permute-start | bytes 393224 | tf_op jit(solution)/shard_map/ppermute | solution.py:158
  134.7 2.4 %collective-permute-done.15 = bf16[4,128,128]{2,1,0:T(8,128)(2,1)S(1)} collective-permute-done((bf16[4,128,128]{2,1,0:T(8,128)(2,1)}, bf16[4,128,128]{2,1,0:T(8,128)(2,1)S(1)}, u32[]{:S(2)}, u32[]{:S(2)}) %collective-permute-start.15) | collective-permute-done | bytes 131104 | tf_op jit(solution)/shard_map/ppermute | solution.py:158
  137.1 3.8 %collective-permute-done.16 = bf16[4,128,128]{2,1,0:T(8,128)(2,1)S(1)} collective-permute-done((bf16[4,128,128]{2,1,0:T(8,128)(2,1)}, bf16[4,128,128]{2,1,0:T(8,128)(2,1)S(1)}, u32[]{:S(2)}, u32[]{:S(2)}) %collective-permute-start.16) | collective-permute-done | bytes 131104 | tf_op jit(solution)/shard_map/ppermute | solution.py:158
  140.9 1.0 select_select_fusion.3
  142.4 3.2 %collective-permute-start.19 = (bf16[4,128,128]{2,1,0:T(8,128)(2,1)S(1)}, bf16[4,128,128]{2,1,0:T(8,128)(2,1)S(1)}, u32[]{:S(2)}, u32[]{:S(2)}) collective-permute-start(bf16[4,128,128]{2,1,0:T(8,128)(2,1)S(1)} %select_select_fusion.3), channel_id=1, source_target_pairs={{128,0},{192,64},{0,128},{64,192},{129,1},{193,65},{1,129},{65,193... | collective-permute-start | bytes 393224 | tf_op jit(solution)/shard_map/ppermute | solution.py:158
  145.6 1.4 collective-permute-done.18
  147.0 3.4 %collective-permute-done.19 = bf16[4,128,128]{2,1,0:T(8,128)(2,1)S(1)} collective-permute-done((bf16[4,128,128]{2,1,0:T(8,128)(2,1)S(1)}, bf16[4,128,128]{2,1,0:T(8,128)(2,1)S(1)}, u32[]{:S(2)}, u32[]{:S(2)}) %collective-permute-start.19) | collective-permute-done | bytes 131104 | tf_op jit(solution)/shard_map/ppermute | solution.py:158
  150.7 2.4 %collective-permute-start.21 = (bf16[4,128,128]{2,1,0:T(8,128)(2,1)S(1)}, bf16[4,128,128]{2,1,0:T(8,128)(2,1)S(1)}, u32[]{:S(2)}, u32[]{:S(2)}) collective-permute-start(bf16[4,128,128]{2,1,0:T(8,128)(2,1)S(1)} %select_select_fusion.2.own_ref), channel_id=1, source_target_pairs={{1,0},{0,1},{3,2},{2,3},{5,4},{4,5},{7,6},{6,7},{9,8},{8,9},{11,10... | collective-permute-start | bytes 393224 | tf_op jit(solution)/shard_map/ppermute | solution.py:158
  153.1 1.0 collective-permute-done.21.other_ref
  154.1 0.7 copy-done.6
  154.8 6.3 %users.3 = bf16[32,128]{1,0:T(8,128)(2,1)} custom-call(bf16[4,128,128]{2,1,0:T(8,128)(2,1)} %copy-done.2, bf16[4,128,128]{2,1,0:T(8,128)(2,1)} %copy-done.6, bf16[4,32,128]{2,1,0:T(8,128)(2,1)} %get-tuple-element.19.own_marks_ref, bf16[4,32,128]{2,1,0:T(8,128)(2,1)} %copy-done.7), custom_call_target="tpu_custom_call" | custom-call | tf_op jit(solution)/shard_map/users/pallas_call | solution.py:108
  (71 shorter events, 9.0 us)
Async XLA Ops:
  0.6 0.7 copy-start.10
  2.3 0.8 copy-start.3
  3.1 0.8 copy-start.9
  5.0 32.6 %all-to-all-start = ((bf16[8,6,64,128]{3,2,1,0:T(8,128)(2,1)}), bf16[8,6,64,128]{3,2,1,0:T(8,128)(2,1)S(1)}, u32[]{:S(2)}, u32[]{:S(2)}) async-start(bf16[8,6,64,128]{3,2,1,0:T(8,128)(2,1)} %broadcast_in_dim.152), calls=%async_computation | async-start | bytes 1572864 | tf_op jit(solution)/shard_map/all_to_all | solution.py:153
  14.0 0.7 copy-start.13
  14.7 0.5 copy-start.11
  15.6 0.6 copy-start.12
  37.5 0.9 copy-start
  40.3 7.5 %collective-permute-start = (bf16[12,64,128]{2,1,0:T(8,128)(2,1)}, bf16[12,64,128]{2,1,0:T(8,128)(2,1)S(1)}, u32[]{:S(2)}, u32[]{:S(2)}) collective-permute-start(bf16[12,64,128]{2,1,0:T(8,128)(2,1)} %pick.3), channel_id=1, source_target_pairs={{48,0},{0,16},{16,32},{32,48},{49,1},{1,17},{17,33},{33,49},{50,2}... | collective-permute-start | bytes 589832 | tf_op jit(solution)/shard_map/ppermute | solution.py:158
  41.6 11.5 %collective-permute-start.1 = (bf16[12,64,128]{2,1,0:T(8,128)(2,1)}, bf16[12,64,128]{2,1,0:T(8,128)(2,1)S(1)}, u32[]{:S(2)}, u32[]{:S(2)}) collective-permute-start(bf16[12,64,128]{2,1,0:T(8,128)(2,1)} %pick.3), channel_id=1, source_target_pairs={{32,0},{48,16},{0,32},{16,48},{33,1},{49,17},{1,33},{17,49},{34,2}... | collective-permute-start | bytes 589832 | tf_op jit(solution)/shard_map/ppermute | solution.py:158
  44.2 8.9 %collective-permute-start.2 = (bf16[12,64,128]{2,1,0:T(8,128)(2,1)}, bf16[12,64,128]{2,1,0:T(8,128)(2,1)S(1)}, u32[]{:S(2)}, u32[]{:S(2)}) collective-permute-start(bf16[12,64,128]{2,1,0:T(8,128)(2,1)} %pick.3), channel_id=1, source_target_pairs={{16,0},{32,16},{48,32},{0,48},{17,1},{33,17},{49,33},{1,49},{18,2}... | collective-permute-start | bytes 589832 | tf_op jit(solution)/shard_map/ppermute | solution.py:158
  54.2 6.4 %collective-permute-start.3 = (bf16[12,64,128]{2,1,0:T(8,128)(2,1)S(1)}, bf16[12,64,128]{2,1,0:T(8,128)(2,1)S(1)}, u32[]{:S(2)}, u32[]{:S(2)}) collective-permute-start(bf16[12,64,128]{2,1,0:T(8,128)(2,1)S(1)} %select_select_fusion.1), channel_id=1, source_target_pairs={{192,0},{0,64},{64,128},{128,192},{193,1},{1,65},{65,129},{129,193... | collective-permute-start | bytes 589832 | tf_op jit(solution)/shard_map/ppermute | solution.py:158
  55.5 10.3 %collective-permute-start.4 = (bf16[12,64,128]{2,1,0:T(8,128)(2,1)S(1)}, bf16[12,64,128]{2,1,0:T(8,128)(2,1)S(1)}, u32[]{:S(2)}, u32[]{:S(2)}) collective-permute-start(bf16[12,64,128]{2,1,0:T(8,128)(2,1)S(1)} %select_select_fusion.1), channel_id=1, source_target_pairs={{128,0},{192,64},{0,128},{64,192},{129,1},{193,65},{1,129},{65,193... | collective-permute-start | bytes 589832 | tf_op jit(solution)/shard_map/ppermute | solution.py:158
  57.9 7.9 %collective-permute-start.5 = (bf16[12,64,128]{2,1,0:T(8,128)(2,1)S(1)}, bf16[12,64,128]{2,1,0:T(8,128)(2,1)S(1)}, u32[]{:S(2)}, u32[]{:S(2)}) collective-permute-start(bf16[12,64,128]{2,1,0:T(8,128)(2,1)S(1)} %select_select_fusion.1), channel_id=1, source_target_pairs={{64,0},{128,64},{192,128},{0,192},{65,1},{129,65},{193,129},{1,193... | collective-permute-start | bytes 589832 | tf_op jit(solution)/shard_map/ppermute | solution.py:158
  65.9 4.1 %copy-start.1 = (bf16[8,64,128]{2,1,0:T(8,128)(2,1)}, bf16[8,64,128]{2,1,0:T(8,128)(2,1)S(1)}, u32[]{:S(2)}) copy-start(bf16[8,64,128]{2,1,0:T(8,128)(2,1)S(1)} %slice.26) | copy-start | bytes 393220
  65.9 4.1 %collective-permute-start.6 = (bf16[4,128,128]{2,1,0:T(8,128)(2,1)S(1)}, bf16[4,128,128]{2,1,0:T(8,128)(2,1)S(1)}, u32[]{:S(2)}, u32[]{:S(2)}) collective-permute-start(bf16[4,128,128]{2,1,0:T(8,128)(2,1)S(1)} %bitcast.2), channel_id=1, source_target_pairs={{1,0},{0,1},{3,2},{2,3},{5,4},{4,5},{7,6},{6,7},{9,8},{8,9},{11,10... | collective-permute-start | bytes 393224 | tf_op jit(solution)/shard_map/ppermute | solution.py:158
  68.8 1.2 collective-permute-start.7
  70.1 0.6 copy-start.7
  70.1 0.7 copy-start.5
  89.4 3.9 %collective-permute-start.10 = (bf16[4,32,128]{2,1,0:T(8,128)(2,1)}, bf16[4,32,128]{2,1,0:T(8,128)(2,1)S(1)}, u32[]{:S(2)}, u32[]{:S(2)}) collective-permute-start(bf16[4,32,128]{2,1,0:T(8,128)(2,1)} %pick.4), channel_id=1, source_target_pairs={{16,0},{32,16},{48,32},{0,48},{17,1},{33,17},{49,33},{1,49},{18,2}... | collective-permute-start | bytes 98312 | tf_op jit(solution)/shard_map/ppermute | solution.py:158
  91.9 4.2 %collective-permute-start.8 = (bf16[4,32,128]{2,1,0:T(8,128)(2,1)}, bf16[4,32,128]{2,1,0:T(8,128)(2,1)S(1)}, u32[]{:S(2)}, u32[]{:S(2)}) collective-permute-start(bf16[4,32,128]{2,1,0:T(8,128)(2,1)} %pick.4), channel_id=1, source_target_pairs={{48,0},{0,16},{16,32},{32,48},{49,1},{1,17},{17,33},{33,49},{50,2}... | collective-permute-start | bytes 98312 | tf_op jit(solution)/shard_map/ppermute | solution.py:158
  91.9 4.5 %collective-permute-start.9 = (bf16[4,32,128]{2,1,0:T(8,128)(2,1)}, bf16[4,32,128]{2,1,0:T(8,128)(2,1)S(1)}, u32[]{:S(2)}, u32[]{:S(2)}) collective-permute-start(bf16[4,32,128]{2,1,0:T(8,128)(2,1)} %pick.4), channel_id=1, source_target_pairs={{32,0},{48,16},{0,32},{16,48},{33,1},{49,17},{1,33},{17,49},{34,2}... | collective-permute-start | bytes 98312 | tf_op jit(solution)/shard_map/ppermute | solution.py:158
  97.3 4.6 %collective-permute-start.11 = (bf16[4,32,128]{2,1,0:T(8,128)(2,1)S(1)}, bf16[4,32,128]{2,1,0:T(8,128)(2,1)S(1)}, u32[]{:S(2)}, u32[]{:S(2)}) collective-permute-start(bf16[4,32,128]{2,1,0:T(8,128)(2,1)S(1)} %select_select_fusion.5), channel_id=1, source_target_pairs={{192,0},{0,64},{64,128},{128,192},{193,1},{1,65},{65,129},{129,193... | collective-permute-start | bytes 98312 | tf_op jit(solution)/shard_map/ppermute | solution.py:158
  98.6 4.3 %collective-permute-start.12 = (bf16[4,32,128]{2,1,0:T(8,128)(2,1)S(1)}, bf16[4,32,128]{2,1,0:T(8,128)(2,1)S(1)}, u32[]{:S(2)}, u32[]{:S(2)}) collective-permute-start(bf16[4,32,128]{2,1,0:T(8,128)(2,1)S(1)} %select_select_fusion.5), channel_id=1, source_target_pairs={{128,0},{192,64},{0,128},{64,192},{129,1},{193,65},{1,129},{65,193... | collective-permute-start | bytes 98312 | tf_op jit(solution)/shard_map/ppermute | solution.py:158
  100.5 2.8 %collective-permute-start.13 = (bf16[4,32,128]{2,1,0:T(8,128)(2,1)S(1)}, bf16[4,32,128]{2,1,0:T(8,128)(2,1)S(1)}, u32[]{:S(2)}, u32[]{:S(2)}) collective-permute-start(bf16[4,32,128]{2,1,0:T(8,128)(2,1)S(1)} %select_select_fusion.5), channel_id=1, source_target_pairs={{64,0},{128,64},{192,128},{0,192},{65,1},{129,65},{193,129},{1,193... | collective-permute-start | bytes 98312 | tf_op jit(solution)/shard_map/ppermute | solution.py:158
  103.4 5.5 %copy-start.4 = (bf16[4,32,128]{2,1,0:T(8,128)(2,1)}, bf16[4,32,128]{2,1,0:T(8,128)(2,1)S(1)}, u32[]{:S(2)}) copy-start(bf16[4,32,128]{2,1,0:T(8,128)(2,1)S(1)} %select_select_fusion.4.own_ref) | copy-start | bytes 98308
  103.4 5.8 %collective-permute-start.14 = (bf16[4,32,128]{2,1,0:T(8,128)(2,1)S(1)}, bf16[4,32,128]{2,1,0:T(8,128)(2,1)S(1)}, u32[]{:S(2)}, u32[]{:S(2)}) collective-permute-start(bf16[4,32,128]{2,1,0:T(8,128)(2,1)S(1)} %select_select_fusion.4.own_ref), channel_id=1, source_target_pairs={{1,0},{0,1},{3,2},{2,3},{5,4},{4,5},{7,6},{6,7},{9,8},{8,9},{11,10... | collective-permute-start | bytes 98312 | tf_op jit(solution)/shard_map/ppermute | solution.py:158
  109.2 0.6 copy-start.8
  130.6 6.4 %collective-permute-start.15 = (bf16[4,128,128]{2,1,0:T(8,128)(2,1)}, bf16[4,128,128]{2,1,0:T(8,128)(2,1)S(1)}, u32[]{:S(2)}, u32[]{:S(2)}) collective-permute-start(bf16[4,128,128]{2,1,0:T(8,128)(2,1)} %pick.5), channel_id=1, source_target_pairs={{48,0},{0,16},{16,32},{32,48},{49,1},{1,17},{17,33},{33,49},{50,2}... | collective-permute-start | bytes 393224 | tf_op jit(solution)/shard_map/ppermute | solution.py:158
  130.9 10.0 %collective-permute-start.16 = (bf16[4,128,128]{2,1,0:T(8,128)(2,1)}, bf16[4,128,128]{2,1,0:T(8,128)(2,1)S(1)}, u32[]{:S(2)}, u32[]{:S(2)}) collective-permute-start(bf16[4,128,128]{2,1,0:T(8,128)(2,1)} %pick.5), channel_id=1, source_target_pairs={{32,0},{48,16},{0,32},{16,48},{33,1},{49,17},{1,33},{17,49},{34,2}... | collective-permute-start | bytes 393224 | tf_op jit(solution)/shard_map/ppermute | solution.py:158
  134.7 6.1 %collective-permute-start.17 = (bf16[4,128,128]{2,1,0:T(8,128)(2,1)}, bf16[4,128,128]{2,1,0:T(8,128)(2,1)S(1)}, u32[]{:S(2)}, u32[]{:S(2)}) collective-permute-start(bf16[4,128,128]{2,1,0:T(8,128)(2,1)} %pick.5), channel_id=1, source_target_pairs={{16,0},{32,16},{48,32},{0,48},{17,1},{33,17},{49,33},{1,49},{18,2}... | collective-permute-start | bytes 393224 | tf_op jit(solution)/shard_map/ppermute | solution.py:158
  141.9 5.1 %collective-permute-start.18 = (bf16[4,128,128]{2,1,0:T(8,128)(2,1)S(1)}, bf16[4,128,128]{2,1,0:T(8,128)(2,1)S(1)}, u32[]{:S(2)}, u32[]{:S(2)}) collective-permute-start(bf16[4,128,128]{2,1,0:T(8,128)(2,1)S(1)} %select_select_fusion.3), channel_id=1, source_target_pairs={{192,0},{0,64},{64,128},{128,192},{193,1},{1,65},{65,129},{129,193... | collective-permute-start | bytes 393224 | tf_op jit(solution)/shard_map/ppermute | solution.py:158
  142.4 8.0 %collective-permute-start.19 = (bf16[4,128,128]{2,1,0:T(8,128)(2,1)S(1)}, bf16[4,128,128]{2,1,0:T(8,128)(2,1)S(1)}, u32[]{:S(2)}, u32[]{:S(2)}) collective-permute-start(bf16[4,128,128]{2,1,0:T(8,128)(2,1)S(1)} %select_select_fusion.3), channel_id=1, source_target_pairs={{128,0},{192,64},{0,128},{64,192},{129,1},{193,65},{1,129},{65,193... | collective-permute-start | bytes 393224 | tf_op jit(solution)/shard_map/ppermute | solution.py:158
  145.6 5.0 %collective-permute-start.20 = (bf16[4,128,128]{2,1,0:T(8,128)(2,1)S(1)}, bf16[4,128,128]{2,1,0:T(8,128)(2,1)S(1)}, u32[]{:S(2)}, u32[]{:S(2)}) collective-permute-start(bf16[4,128,128]{2,1,0:T(8,128)(2,1)S(1)} %select_select_fusion.3), channel_id=1, source_target_pairs={{64,0},{128,64},{192,128},{0,192},{65,1},{129,65},{193,129},{1,193... | collective-permute-start | bytes 393224 | tf_op jit(solution)/shard_map/ppermute | solution.py:158
  150.7 3.4 %copy-start.2 = (bf16[4,128,128]{2,1,0:T(8,128)(2,1)}, bf16[4,128,128]{2,1,0:T(8,128)(2,1)S(1)}, u32[]{:S(2)}) copy-start(bf16[4,128,128]{2,1,0:T(8,128)(2,1)S(1)} %select_select_fusion.2.own_ref) | copy-start | bytes 393220
  150.7 3.4 %collective-permute-start.21 = (bf16[4,128,128]{2,1,0:T(8,128)(2,1)S(1)}, bf16[4,128,128]{2,1,0:T(8,128)(2,1)S(1)}, u32[]{:S(2)}, u32[]{:S(2)}) collective-permute-start(bf16[4,128,128]{2,1,0:T(8,128)(2,1)S(1)} %select_select_fusion.2.own_ref), channel_id=1, source_target_pairs={{1,0},{0,1},{3,2},{2,3},{5,4},{4,5},{7,6},{6,7},{9,8},{8,9},{11,10... | collective-permute-start | bytes 393224 | tf_op jit(solution)/shard_map/ppermute | solution.py:158
  154.1 0.7 copy-start.6
where the time goes:
time: 162 us; the launch traced here: 161 us
  waiting for transfers between devices  54 us (33%)
  starting transfers between devices  44.6 us (28%)
  blocking collectives  25.6 us (16%)
  Pallas kernels  20.5 us (13%)
  local copies, waits for them, and re-layouts  10.4 us (6%)
  other arithmetic  5.08 us (3%)
    ppermute x22, starting transfers between devices, fetched_from(): lax.ppermute(value, axis, [((target + steps) % count, target) for target...  35.6 us
    ppermute x22, waiting for transfers between devices, fetched_from(): lax.ppermute(value, axis, [((target + steps) % count, target) for target...  32.9 us
    all_to_all x2, blocking collectives, sent_to_all(): return lax.all_to_all(copies, axes, split_axis=0, concat_axis=0, tiled=True)  25.6 us
    all_to_all x1, waiting for transfers between devices, sent_to_all(): return lax.all_to_all(copies, axes, split_axis=0, concat_axis=0, tiled=True)  21.2 us
    pallas_call x2, Pallas kernels, solve_users(): pl.pallas_call(users_kernel, out_shape=jax.ShapeDtypeStruct((rows, rank),...  12.5 us
    all_to_all x1, starting transfers between devices, sent_to_all(): return lax.all_to_all(copies, axes, split_axis=0, concat_axis=0, tiled=True)  9 us
    unnamed x28, local copies, waits for them, and re-layouts  6.08 us
    pallas_call x3, Pallas kernels, pick(): pl.pallas_call(functools.partial(pick_kernel, units=units), out_shape=jax...  4.94 us
  transfers between devices with their start and end apart: 23, of which 18 were waited for; matrix products, arithmetic and copies ran while one was open for 2% of the time, Pallas kernels for 0%

commit v1 on v0

v1 whole, which is shorter than its diff:
```python
import functools

import jax
import jax.numpy as jnp
from jax import lax
from jax.experimental import pallas as pl
from jax.experimental.pallas import tpu as pltpu
from jax.sharding import Mesh, PartitionSpec as P

SWEEPS = 4
RIDGE = 0.005
UNRATED = 64.0
RATED_BELOW = 32.0
AXES = ("x", "y", "z")
VMEM = pltpu.MemorySpace.VMEM
SMEM = pltpu.MemorySpace.SMEM


def split_parts(value):
    high = value.astype(jnp.bfloat16)
    low = (value - high.astype(jnp.float32)).astype(jnp.bfloat16)
    return jnp.concatenate([high, low], axis=0)


def dot_f32(a, b, dims=((1,), (0,))):
    return lax.dot_general(a, b, (dims, ((), ())), preferred_element_type=jnp.float32)


def relax(right, ridge, bound, rated, factors):
    rows = right.shape[0]
    inverse = 1.0 / bound
    answer = right * inverse
    for _ in range(SWEEPS - 1):
        inner = dot_f32(split_parts(answer), factors, ((1,), (1,)))
        inner = jnp.where(rated, inner[:rows] + inner[rows:], 0.0)
        outer = dot_f32(split_parts(inner), factors)
        applied = outer[:rows] + outer[rows:] + ridge * answer
        answer = answer + (right - applied) * inverse
    return answer.astype(jnp.bfloat16)


def users_kernel(*refs, static, copies, extra):
    refs = list(refs)
    own = [refs.pop(0) for _ in range(static + 1)]
    other = [refs.pop(0) for _ in range(static + 1)]
    own_marks_ref, other_marks_ref = refs.pop(0), refs.pop(0)
    extra_ref = refs.pop(0) if extra else None
    out_ref, factor_t_ref, mask_ref, sums_ref = refs
    rank = own[0].shape[1]
    rows = own_marks_ref.shape[1]
    parts = []
    for k in range(static):
        parts += [own[k][...], other[k][...]]
    for k in range(own[static].shape[0]):
        parts += [own[static][k], other[static][k]]
    marks = []
    for k in range(own_marks_ref.shape[0]):
        marks += [own_marks_ref[k], other_marks_ref[k]]
    factors = jnp.concatenate(parts, axis=0)
    marked = jnp.concatenate(marks, axis=1).astype(jnp.float32)
    rated = jnp.abs(marked) < RATED_BELOW
    factor_t_ref[...] = factors.T
    mask = jnp.where(rated, 1.0, 0.0)
    mask_ref[...] = mask
    count = jnp.sum(mask, axis=1, keepdims=True)
    right = dot_f32(jnp.where(rated, marked, 0.0).astype(jnp.bfloat16), factors)
    together = 16

    def some(step, carry):
        chosen = mask_ref[pl.ds(step * together, together), :].astype(jnp.bfloat16)
        weighted = (factor_t_ref[...][None] * chosen[:, None, :]).reshape(together * rank, -1)
        gram = dot_f32(weighted, factors)
        total = jnp.sum(jnp.abs(gram).reshape(together, rank, rank), axis=1)
        sums_ref[pl.ds(step * together, together), :] = total
        return carry

    lax.fori_loop(0, rows // together, some, 0)
    ridge = RIDGE * (count + 1.0)
    bound = jnp.max(sums_ref[...], axis=1, keepdims=True) + ridge
    answer = relax(right, ridge, bound, rated, factors)
    if not copies:
        out_ref[...] = answer
    for c in range(copies):
        out_ref[c, :rows, :] = answer
        for k in range(extra_ref.shape[0] if extra else 0):
            start = rows + k * extra_ref.shape[1]
            out_ref[c, start : start + extra_ref.shape[1], :] = extra_ref[k]


def items_kernel(own_ref, other_ref, *refs, static, copies):
    marks_refs, (out_ref, copies_ref, sums_ref) = refs[: static + 1], refs[static + 1 :]
    tiles = own_ref.shape[0]
    rank = own_ref.shape[2]
    items = out_ref.shape[0]
    parts = []
    for k in range(tiles):
        parts += [own_ref[k], other_ref[k]]
    factors = jnp.concatenate(parts, axis=0)
    factor_t = factors.T
    marks = [ref[...] for ref in marks_refs[:static]]
    marks += [marks_refs[static][k] for k in range(marks_refs[static].shape[0])]
    marked = jnp.concatenate([m.astype(jnp.float32) for m in marks], axis=0).T
    rated = jnp.abs(marked) < RATED_BELOW
    mask = jnp.where(rated, 1.0, 0.0)
    count = jnp.sum(mask, axis=1, keepdims=True)
    right = dot_f32(jnp.where(rated, marked, 0.0).astype(jnp.bfloat16), factors)
    group = 8
    for j in range(items // group):
        row = mask[j * group : j * group + 1].astype(jnp.bfloat16)
        gram = dot_f32(factor_t * row, factors)
        total = jnp.sum(jnp.abs(gram), axis=0, keepdims=True)
        sums_ref[j * group : (j + 1) * group, :] = jnp.broadcast_to(total, (group, rank))
    ridge = RIDGE * (count + 1.0)
    bound = jnp.max(sums_ref[...], axis=1, keepdims=True) + ridge
    answer = relax(right, ridge, bound, rated, factors)
    out_ref[...] = answer
    for c in range(copies):
        copies_ref[c] = answer


def vmem_specs(count):
    return [pl.BlockSpec(memory_space=VMEM)] * count


def solve_users(own, other, own_marks, other_marks, copies=0, extra=None):
    static = len(own) - 1
    tiles, rows, half = own_marks.shape
    rank = own[0].shape[1]
    width = tiles * 2 * half
    args = [*own, *other, own_marks, other_marks]
    shape = (rows, rank)
    if copies:
        args.append(extra)
        shape = (copies, rows + extra.shape[0] * extra.shape[1], rank)
    return pl.pallas_call(
        functools.partial(users_kernel, static=static, copies=copies, extra=copies > 0),
        out_shape=jax.ShapeDtypeStruct(shape, jnp.bfloat16),
        in_specs=vmem_specs(len(args)),
        out_specs=pl.BlockSpec(memory_space=VMEM),
        scratch_shapes=[
            pltpu.VMEM((rank, width), jnp.bfloat16),
            pltpu.VMEM((rows, width), jnp.float32),
            pltpu.VMEM((rows, rank), jnp.float32),
        ],
        name="users",
    )(*args)


def solve_items(own, other, marks, copies):
    tiles, half, rank = own.shape
    items = marks[0].shape[1]
    return pl.pallas_call(
        functools.partial(items_kernel, static=len(marks) - 1, copies=copies),
        out_shape=(
            jax.ShapeDtypeStruct((items, rank), jnp.bfloat16),
            jax.ShapeDtypeStruct((copies, items, rank), jnp.bfloat16),
        ),
        in_specs=vmem_specs(2 + len(marks)),
        out_specs=tuple(vmem_specs(2)),
        scratch_shapes=[pltpu.VMEM((items, rank), jnp.float32)],
        name="items",
    )(own, other, *marks)


def small_call(kernel, name, index, arrays, out_shapes):
    return pl.pallas_call(
        kernel,
        out_shape=tuple(jax.ShapeDtypeStruct(shape, jnp.bfloat16) for shape in out_shapes),
        in_specs=[pl.BlockSpec(memory_space=SMEM)] + vmem_specs(len(arrays)),
        out_specs=tuple(vmem_specs(len(out_shapes))),
        name=name,
    )(index, *arrays)


def arrange_kernel(index_ref, marks_ref, out_ref):
    tiles, users, _ = marks_ref.shape
    rows = users // 2
    half = index_ref[tiles]
    for k in range(tiles):
        for part, at in ((0, half), (1, 1 - half)):
            start = pl.multiple_of(at * rows, rows)
            out_ref[k, part * rows : (part + 1) * rows, :] = marks_ref[index_ref[k], pl.ds(start, rows), :]


def pick_kernel(index_ref, source_ref, out_ref):
    for k in range(out_ref.shape[0]):
        out_ref[k] = source_ref[index_ref[k]]


def pick_items_kernel(index_ref, source_ref, marks_ref, out_ref):
    tiles, users, _ = marks_ref.shape
    for k in range(tiles):
        for unit in range(source_ref.shape[1] // users):
            out_ref[k * (source_ref.shape[1] // users) + unit] = source_ref[
                index_ref[k], unit * users : (unit + 1) * users, :
            ]
        out_ref[out_ref.shape[0] - tiles + k] = marks_ref[k]


def pick_users_kernel(index_ref, source_ref, copies_ref, marks_ref):
    copies, tiles, rows, _ = copies_ref.shape
    for k in range(tiles):
        piece = source_ref[index_ref[k], :rows, :]
        for c in range(copies):
            copies_ref[c, k] = piece
    first = tiles - marks_ref.shape[0]
    users = marks_ref.shape[1]
    for k in range(marks_ref.shape[0]):
        marks_ref[k] = source_ref[index_ref[first + k], rows + k * users : rows + (k + 1) * users, :]


def pick_own_kernel(index_ref, source_ref, out_ref):
    for k in range(out_ref.shape[0]):
        out_ref[k] = source_ref[index_ref[k], k]


def swapped_with_all(copies, axes):
    return lax.all_to_all(copies, axes, split_axis=0, concat_axis=0, tiled=True)


def fetched_from(value, axis, steps):
    count = 1
    for name in (axis if isinstance(axis, tuple) else (axis,)):
        count *= lax.axis_size(name)
    return lax.ppermute(value, axis, [((target + steps) % count, target) for target in range(count)])


def shift_digits(shift, z_first):
    nz, ny, nx = lax.axis_size("z"), lax.axis_size("y"), lax.axis_size("x")
    z, z_shift = lax.axis_index("z"), shift % nz
    carry = (z + z_shift) // nz if z_first else (z < z_shift).astype(jnp.int32)
    y_step = (shift // nz) % ny + carry
    x_step = shift // (nz * ny) + (lax.axis_index("y") + y_step) // ny
    return (z + z_shift) % nz, y_step % ny, x_step % nx


def stepped(held, axis, steps):
    chosen = held
    for step in range(1, lax.axis_size(axis)):
        arrived = fetched_from(held, axis, step)
        chosen = jnp.where((steps == step)[:, None, None], arrived, chosen)
    return chosen


def body(item_start, ratings, rating_bits, plan):
    tiles, users, items = ratings.shape
    rank = item_start.shape[1]
    own_half = lax.axis_index("grp")
    blocks = lax.axis_size(AXES)
    nz, ny, nx = lax.axis_size("z"), lax.axis_size("y"), lax.axis_size("x")
    rows = users // 2
    partner = lambda value: fetched_from(value, "grp", 1)

    fixed = (blocks - 1, blocks // 2)
    rank_of = jnp.where(plan == fixed[0], 0, jnp.where(plan == fixed[1], 1, 2))
    before = (rank_of[None, :] < rank_of[:, None]) | (
        (rank_of[None, :] == rank_of[:, None]) & (jnp.arange(tiles)[None, :] < jnp.arange(tiles)[:, None])
    )
    place = jnp.sum(before.astype(jnp.int32), axis=1)
    at_place = (place[None, :] == jnp.arange(tiles)[:, None]).astype(jnp.int32)
    order = jnp.sum(at_place * jnp.arange(tiles)[None, :], axis=1)
    shifts = jnp.sum(at_place * plan[None, :], axis=1)
    moving = shifts[len(fixed) :]
    moves = tiles - len(fixed)
    z_items, y_items, x_items = shift_digits(moving, True)
    _, y_marks, x_marks = shift_digits((blocks - moving) % blocks, False)
    z_users, y_users, x_users = shift_digits((blocks - shifts) % blocks, True)
    x_users = (lax.axis_index("x") + x_users) % nx
    y_users = (lax.axis_index("y") + y_users) % ny

    bit_count = 32 // lax.axis_size("grp")
    item_bits = own_half * bit_count + lax.broadcasted_iota(jnp.int32, (1, 1, items), 2) // (items // bit_count)
    rated = (jnp.right_shift(rating_bits[:, :, None], item_bits) & 1) == 1
    marks = jnp.where(rated, ratings, jnp.asarray(UNRATED, ratings.dtype))
    index = jnp.concatenate([order, own_half[None]])
    (marks,) = small_call(arrange_kernel, "arrange", index, [marks], [marks.shape])
    own_marks = marks[:, :rows]
    other_marks = partner(marks[:, rows:])
    fixed_marks = [fetched_from(marks[k], AXES, -fixed[k]) for k in range(len(fixed))]

    def gather_items(factors, copies, extra):
        fixed_own = [fetched_from(factors, AXES, shift) for shift in fixed]
        fixed_other = [partner(value) for value in fixed_own]
        held = swapped_with_all(copies, "z")
        if extra is None:
            (held,) = small_call(pick_kernel, "pick", z_items, [held], [(moves, items, rank)])
            y_steps, x_steps = y_items, x_items
        else:
            units = moves * (items // users)
            shape = (units + moves, users, rank)
            (held,) = small_call(pick_items_kernel, "pick_items", z_items, [held, extra], [shape])
            y_steps = jnp.concatenate([jnp.repeat(y_items, items // users), y_marks])
            x_steps = jnp.concatenate([jnp.repeat(x_items, items // users), x_marks])
        held = stepped(stepped(held, "y", y_steps), "x", x_steps)
        if extra is not None:
            extra = held[units:]
            held = held[:units].reshape(moves, items, rank)
        return [*fixed_own, held], [*fixed_other, partner(held)], extra

    copies = jnp.broadcast_to(item_start, (nz, items, rank))
    own, other, moved = gather_items(item_start, copies, marks[len(fixed) :])
    held = solve_users(own, other, own_marks, other_marks, nz, moved)

    held = swapped_with_all(held, "z")
    copies, moved = small_call(
        pick_users_kernel, "pick_users", z_users, [held], [(nx * ny, tiles, rows, rank), (moves, users, items)]
    )
    held = swapped_with_all(copies, ("x", "y"))
    (own_users,) = small_call(pick_own_kernel, "pick_own", x_users * ny + y_users, [held], [(tiles, rows, rank)])
    item_factors, copies = solve_items(own_users, partner(own_users), [*fixed_marks, moved], nz)

    own, other, _ = gather_items(item_factors, copies, None)
    user_factors = solve_users(own, other, own_marks, other_marks)
    return (user_factors, item_factors)


def solution(mesh):
    torus = Mesh(mesh.devices.reshape(4, 4, 8, 2), (*AXES, "grp"))
    everywhere = (*AXES, "grp")
    in_specs = (P(everywhere, None), P(None, AXES, "grp"), P(None, AXES), P())
    out_specs = (P(everywhere, None), P(everywhere, None))
    return jax.shard_map(body, mesh=torus, in_specs=in_specs, out_specs=out_specs, check_vma=False)
```

time: 162 us -> 157 us (0.969)
  blocking collectives: 25.6 us -> 14.3 us
  starting transfers between devices: 44.6 us -> 55.4 us
  waiting for transfers between devices: 54 us -> 47.4 us
    ppermute x22 -> x26, waiting for transfers between devices: 32.9 us -> 20.7 us  [fetched_from(): lax.ppermute(value, axis, [((target + steps) % count, target) for target...]
    all_to_all x2 -> x1, blocking collectives: 25.6 us -> 14.3 us  [swapped_with_all(): return lax.all_to_all(copies, axes, split_axis=0, concat_axis=0, tiled=True)]
    all_to_all x1 -> x3, waiting for transfers between devices: 21.2 us -> 26.7 us  [swapped_with_all(): return lax.all_to_all(copies, axes, split_axis=0, concat_axis=0, tiled=True)]
    all_to_all x1 -> x3, starting transfers between devices: 9 us -> 14.4 us  [swapped_with_all(): return lax.all_to_all(copies, axes, split_axis=0, concat_axis=0, tiled=True)]
    ppermute x22 -> x26, starting transfers between devices: 35.6 us -> 41 us  [fetched_from(): lax.ppermute(value, axis, [((target + steps) % count, target) for target...]
    pallas_call x6 -> x8, Pallas kernels: 20.5 us -> 22.1 us  [the longest x2 10.7 us: solve_users(): pl.pallas_call(functools.partial(users_kernel, static=static, copies=copi...]
    unnamed x28 -> x48, local copies, waits for them, and re-layouts: 6.08 us -> 5.44 us
  transfers between devices with their start and end apart: 23 -> 29, of which waited for: 18 -> 19; matrix products, arithmetic and copies ran while one was open for 2% -> 6% of each run, Pallas kernels for 0% -> 2%
where the time goes in v1:
time: 157 us; the launch traced here: 156 us
  starting transfers between devices  55.4 us (35%)
  waiting for transfers between devices  47.4 us (30%)
  Pallas kernels  22.1 us (14%)
  blocking collectives  14.3 us (9%)
  local copies, waits for them, and re-layouts  9.89 us (6%)
  other arithmetic  5.8 us (4%)
    ppermute x26, starting transfers between devices, fetched_from(): lax.ppermute(value, axis, [((target + steps) % count, target) for target...  41 us
    all_to_all x3, waiting for transfers between devices, swapped_with_all(): return lax.all_to_all(copies, axes, split_axis=0, concat_axis=0, tiled=True)  26.7 us
    ppermute x26, waiting for transfers between devices, fetched_from(): lax.ppermute(value, axis, [((target + steps) % count, target) for target...  20.7 us
    all_to_all x3, starting transfers between devices, swapped_with_all(): return lax.all_to_all(copies, axes, split_axis=0, concat_axis=0, tiled=True)  14.4 us
    all_to_all x1, blocking collectives, swapped_with_all(): return lax.all_to_all(copies, axes, split_axis=0, concat_axis=0, tiled=True)  14.3 us
    pallas_call x2, Pallas kernels, solve_users(): pl.pallas_call(functools.partial(users_kernel, static=static, copies=copi...  10.7 us
    pallas_call x5, Pallas kernels, small_call(): pl.pallas_call(kernel, out_shape=tuple((jax.ShapeDtypeStruct(shape, jnp.b...  8.24 us
    unnamed x48, local copies, waits for them, and re-layouts  5.44 us
  transfers between devices with their start and end apart: 29, of which 19 were waited for; matrix products, arithmetic and copies ran while one was open for 6% of the time, Pallas kernels for 2%

profile of v1, /device:TPU:1, one launch (start us, length us, event | category | flops | bytes accessed | tf_op | source)
XLA Modules:
  0.0 155.7 jit_solution(2318900438331364732)
XLA Ops:
  0.6 2.5 %collective-permute-start = (bf16[128,128]{1,0:T(8,128)(2,1)}, bf16[128,128]{1,0:T(8,128)(2,1)S(1)}, u32[]{:S(2)}, u32[]{:S(2)}) collective-permute-start(bf16[128,128]{1,0:T(8,128)(2,1)} %param.4), channel_id=1, source_target_pairs={{254,0},{0,2},{2,4},{4,6},{6,8},{8,10},{10,12},{12,14},{14,16},{16... | collective-permute-start | bytes 98312 | tf_op jit(solution)/shard_map/ppermute | solution.py:225
  3.2 2.7 %collective-permute-start.1 = (bf16[128,128]{1,0:T(8,128)(2,1)}, bf16[128,128]{1,0:T(8,128)(2,1)S(1)}, u32[]{:S(2)}, u32[]{:S(2)}) collective-permute-start(bf16[128,128]{1,0:T(8,128)(2,1)} %param.4), channel_id=1, source_target_pairs={{128,0},{130,2},{132,4},{134,6},{136,8},{138,10},{140,12},{142,14}... | collective-permute-start | bytes 98312 | tf_op jit(solution)/shard_map/ppermute | solution.py:225
  5.9 1.5 broadcast_in_dim.124
  7.5 7.4 %all-to-all-start = ((bf16[8,128,128]{2,1,0:T(8,128)(2,1)}), bf16[8,128,128]{2,1,0:T(8,128)(2,1)S(1)}, u32[]{:S(2)}, u32[]{:S(2)}) async-start(bf16[8,128,128]{2,1,0:T(8,128)(2,1)} %broadcast_in_dim.124), calls=%async_computation | async-start | bytes 524288 | tf_op jit(solution)/shard_map/all_to_all | solution.py:218
  18.4 1.5 arrange.1
  19.8 1.4 slice.32.marks_ref
  21.3 3.7 %all-to-all-done.source_ref = bf16[8,128,128]{2,1,0:T(8,128)(2,1)S(1)} async-done(((bf16[8,128,128]{2,1,0:T(8,128)(2,1)}), bf16[8,128,128]{2,1,0:T(8,128)(2,1)S(1)}, u32[]{:S(2)}, u32[]{:S(2)}) %all-to-all-start) | async-done | bytes 262176 | tf_op jit(solution)/shard_map/all_to_all | solution.py:218
  25.1 0.7 copy-done.2
  25.8 1.6 %pick_items.1 = bf16[6,64,128]{2,1,0:T(8,128)(2,1)} custom-call(s32[2]{0:T(128)} %get-tuple-element.39.index_ref, bf16[8,128,128]{2,1,0:T(8,128)(2,1)} %copy-done.2, bf16[2,64,128]{2,1,0:T(8,128)(2,1)} %slice.32.marks_ref), custom_call_target="tpu_custom_call" | custom-call | tf_op jit(solution)/shard_map/pick_items/pallas_call | solution.py:166
  27.4 2.7 %collective-permute-start.4 = (bf16[6,64,128]{2,1,0:T(8,128)(2,1)}, bf16[6,64,128]{2,1,0:T(8,128)(2,1)S(1)}, u32[]{:S(2)}, u32[]{:S(2)}) collective-permute-start(bf16[6,64,128]{2,1,0:T(8,128)(2,1)} %pick_items.1), channel_id=1, source_target_pairs={{16,0},{32,16},{48,32},{0,48},{17,1},{33,17},{49,33},{1,49},{18,2}... | collective-permute-start | bytes 294920 | tf_op jit(solution)/shard_map/ppermute | solution.py:225
  31.2 1.7 %collective-permute-done.4 = bf16[6,64,128]{2,1,0:T(8,128)(2,1)S(1)} collective-permute-done((bf16[6,64,128]{2,1,0:T(8,128)(2,1)}, bf16[6,64,128]{2,1,0:T(8,128)(2,1)S(1)}, u32[]{:S(2)}, u32[]{:S(2)}) %collective-permute-start.4) | collective-permute-done | bytes 98336 | tf_op jit(solution)/shard_map/ppermute | solution.py:225
  32.9 2.5 %collective-permute-done.3 = bf16[6,64,128]{2,1,0:T(8,128)(2,1)S(1)} collective-permute-done((bf16[6,64,128]{2,1,0:T(8,128)(2,1)}, bf16[6,64,128]{2,1,0:T(8,128)(2,1)S(1)}, u32[]{:S(2)}, u32[]{:S(2)}) %collective-permute-start.3) | collective-permute-done | bytes 98336 | tf_op jit(solution)/shard_map/ppermute | solution.py:225
  35.4 1.0 collective-permute-done.2
  36.3 1.0 select_select_fusion.1
  37.3 0.9 collective-permute-start.7
  38.3 1.2 collective-permute-start.6
  39.5 1.4 collective-permute-done.7
  40.9 2.4 %collective-permute-done.6 = bf16[6,64,128]{2,1,0:T(8,128)(2,1)S(1)} collective-permute-done((bf16[6,64,128]{2,1,0:T(8,128)(2,1)S(1)}, bf16[6,64,128]{2,1,0:T(8,128)(2,1)S(1)}, u32[]{:S(2)}, u32[]{:S(2)}) %collective-permute-start.6) | collective-permute-done | bytes 98336 | tf_op jit(solution)/shard_map/ppermute | solution.py:225
  43.2 1.0 collective-permute-done.5
  44.4 5.8 %collective-permute-start.10 = (bf16[2,128,128]{2,1,0:T(8,128)(2,1)S(1)}, bf16[2,128,128]{2,1,0:T(8,128)(2,1)S(1)}, u32[]{:S(2)}, u32[]{:S(2)}) collective-permute-start(bf16[2,128,128]{2,1,0:T(8,128)(2,1)S(1)} %bitcast.6), channel_id=1, source_target_pairs={{1,0},{0,1},{3,2},{2,3},{5,4},{4,5},{7,6},{6,7},{9,8},{8,9},{11,10... | collective-permute-start | bytes 196616 | tf_op jit(solution)/shard_map/ppermute | solution.py:225
  53.5 5.5 %users.2 = bf16[8,160,128]{2,1,0:T(8,128)(2,1)} custom-call(bf16[128,128]{1,0:T(8,128)(2,1)} %copy-done.15, bf16[128,128]{1,0:T(8,128)(2,1)} %copy-done.16, bf16[2,128,128]{2,1,0:T(8,128)(2,1)} %bitcast.7, bf16[128,128]{1,0:T(8,128)(2,1)} %copy-done.17, bf16[128,128]{1,0:T(8,128)(2,1)} %copy-done.18, bf16[2,128,128]{2,1,0:T(8,128)(2,1)} %copy-done.9, ...), custom_call_target="tpu_custom_call" | custom-call | tf_op jit(solution)/shard_map/users/pallas_call | solution.py:135
  59.0 3.4 %all-to-all-start.1 = ((bf16[8,160,128]{2,1,0:T(8,128)(2,1)}), bf16[8,160,128]{2,1,0:T(8,128)(2,1)S(1)}, u32[]{:S(2)}, u32[]{:S(2)}) async-start(bf16[8,160,128]{2,1,0:T(8,128)(2,1)} %users.2), calls=%async_computation.1 | async-start | bytes 655360 | tf_op jit(solution)/shard_map/all_to_all | solution.py:218
  63.0 13.1 %all-to-all-done.1.source_ref = bf16[8,160,128]{2,1,0:T(8,128)(2,1)S(1)} async-done(((bf16[8,160,128]{2,1,0:T(8,128)(2,1)}), bf16[8,160,128]{2,1,0:T(8,128)(2,1)S(1)}, u32[]{:S(2)}, u32[]{:S(2)}) %all-to-all-start.1) | async-done | bytes 327712 | tf_op jit(solution)/shard_map/all_to_all | solution.py:218
  76.1 0.7 copy-done.1
  76.8 1.9 %pick_users.1 = (bf16[16,4,32,128]{3,2,1,0:T(8,128)(2,1)}, bf16[2,64,128]{2,1,0:T(8,128)(2,1)}) custom-call(s32[4]{0:T(128)} %get-tuple-element.23.index_ref, bf16[8,160,128]{2,1,0:T(8,128)(2,1)} %copy-done.1), custom_call_target="tpu_custom_call" | custom-call | tf_op jit(solution)/shard_map/pick_users/pallas_call | solution.py:166
  78.8 3.6 %all-to-all-start.2 = ((bf16[16,4,32,128]{3,2,1,0:T(8,128)(2,1)}), bf16[16,4,32,128]{3,2,1,0:T(8,128)(2,1)S(1)}, u32[]{:S(2)}, u32[]{:S(2)}) async-start(bf16[16,4,32,128]{3,2,1,0:T(8,128)(2,1)} %get-tuple-element.6), calls=%async_computation.2 | async-start | bytes 1048576 | tf_op jit(solution)/shard_map/all_to_all | solution.py:218
  82.9 9.8 %all-to-all-done.2.source_ref = bf16[16,4,32,128]{3,2,1,0:T(8,128)(2,1)S(1)} async-done(((bf16[16,4,32,128]{3,2,1,0:T(8,128)(2,1)}), bf16[16,4,32,128]{3,2,1,0:T(8,128)(2,1)S(1)}, u32[]{:S(2)}, u32[]{:S(2)}) %all-to-all-start.2) | async-done | bytes 524320 | tf_op jit(solution)/shard_map/all_to_all | solution.py:218
  92.7 0.8 copy-done
  93.5 1.7 %pick_own.1.own_ref = bf16[4,32,128]{2,1,0:T(8,128)(2,1)} custom-call(s32[4]{0:T(128)} %fusion.4.index_ref, bf16[16,4,32,128]{3,2,1,0:T(8,128)(2,1)} %copy-done), custom_call_target="tpu_custom_call" | custom-call | tf_op jit(solution)/shard_map/pick_own/pallas_call | solution.py:166
  95.2 2.1 %collective-permute-start.12 = (bf16[4,32,128]{2,1,0:T(8,128)(2,1)}, bf16[4,32,128]{2,1,0:T(8,128)(2,1)S(1)}, u32[]{:S(2)}, u32[]{:S(2)}) collective-permute-start(bf16[4,32,128]{2,1,0:T(8,128)(2,1)} %pick_own.1.own_ref), channel_id=1, source_target_pairs={{1,0},{0,1},{3,2},{2,3},{5,4},{4,5},{7,6},{6,7},{9,8},{8,9},{11,10... | collective-permute-start | bytes 98312 | tf_op jit(solution)/shard_map/ppermute | solution.py:225
  97.2 0.8 collective-permute-start.14
  98.1 3.3 %collective-permute-done.14.refs_1_ = bf16[64,128]{1,0:T(8,128)(2,1)S(1)} collective-permute-done((bf16[64,128]{1,0:T(8,128)(2,1)S(1)}, bf16[64,128]{1,0:T(8,128)(2,1)S(1)}, u32[]{:S(2)}, u32[]{:S(2)}) %collective-permute-start.14) | collective-permute-done | bytes 16416 | tf_op jit(solution)/shard_map/ppermute | solution.py:225
  101.9 3.1 %items.1 = (bf16[128,128]{1,0:T(8,128)(2,1)}, bf16[8,128,128]{2,1,0:T(8,128)(2,1)}) custom-call(bf16[4,32,128]{2,1,0:T(8,128)(2,1)} %pick_own.1.own_ref, bf16[4,32,128]{2,1,0:T(8,128)(2,1)} %copy-done.10, bf16[64,128]{1,0:T(8,128)(2,1)} %copy-done.20, bf16[64,128]{1,0:T(8,128)(2,1)} %copy-done.19, bf16[2,64,128]{2,1,0:T(8,128)(2,1)} %get-tuple-element.7.refs_2_), custom_call_target="tpu_custom_call" | custom-call | tf_op jit(solution)/shard_map/items/pallas_call | solution.py:152
  105.0 14.3 %all_to_all.20.source_ref = bf16[8,128,128]{2,1,0:T(8,128)(2,1)} all-to-all(bf16[8,128,128]{2,1,0:T(8,128)(2,1)} %get-tuple-element.9), channel_id=1, replica_groups=mesh['x'=4,'y'=4,'z'=8,'grp'=2] {'z'}, dimensions={0} | all-to-all | bytes 524288 | tf_op jit(solution)/shard_map/all_to_all | solution.py:218
  119.3 1.6 %pick.1 = bf16[2,128,128]{2,1,0:T(8,128)(2,1)} custom-call(s32[2]{0:T(128)} %get-tuple-element.39.index_ref, bf16[8,128,128]{2,1,0:T(8,128)(2,1)} %all_to_all.20.source_ref), custom_call_target="tpu_custom_call" | custom-call | tf_op jit(solution)/shard_map/pick/pallas_call | solution.py:166
  121.4 1.6 %collective-permute-start.18 = (bf16[2,128,128]{2,1,0:T(8,128)(2,1)}, bf16[2,128,128]{2,1,0:T(8,128)(2,1)S(1)}, u32[]{:S(2)}, u32[]{:S(2)}) collective-permute-start(bf16[2,128,128]{2,1,0:T(8,128)(2,1)} %pick.1), channel_id=1, source_target_pairs={{32,0},{48,16},{0,32},{16,48},{33,1},{49,17},{1,33},{17,49},{34,2}... | collective-permute-start | bytes 196616 | tf_op jit(solution)/shard_map/ppermute | solution.py:225
  123.0 1.2 collective-permute-done.19
  124.2 2.0 %collective-permute-done.18 = bf16[2,128,128]{2,1,0:T(8,128)(2,1)S(1)} collective-permute-done((bf16[2,128,128]{2,1,0:T(8,128)(2,1)}, bf16[2,128,128]{2,1,0:T(8,128)(2,1)S(1)}, u32[]{:S(2)}, u32[]{:S(2)}) %collective-permute-start.18) | collective-permute-done | bytes 65568 | tf_op jit(solution)/shard_map/ppermute | solution.py:225
  126.2 1.3 collective-permute-done.17
  127.5 0.9 select_select_fusion.3
  128.4 1.6 %collective-permute-start.22 = (bf16[2,128,128]{2,1,0:T(8,128)(2,1)S(1)}, bf16[2,128,128]{2,1,0:T(8,128)(2,1)S(1)}, u32[]{:S(2)}, u32[]{:S(2)}) collective-permute-start(bf16[2,128,128]{2,1,0:T(8,128)(2,1)S(1)} %select_select_fusion.3), channel_id=1, source_target_pairs={{64,0},{128,64},{192,128},{0,192},{65,1},{129,65},{193,129},{1,193... | collective-permute-start | bytes 196616 | tf_op jit(solution)/shard_map/ppermute | solution.py:225
  130.0 0.9 collective-permute-start.21
  130.9 2.6 %collective-permute-start.16 = (bf16[128,128]{1,0:T(8,128)(2,1)S(1)}, bf16[128,128]{1,0:T(8,128)(2,1)S(1)}, u32[]{:S(2)}, u32[]{:S(2)}) collective-permute-start(bf16[128,128]{1,0:T(8,128)(2,1)S(1)} %copy-done.23), channel_id=1, source_target_pairs={{128,0},{130,2},{132,4},{134,6},{136,8},{138,10},{140,12},{142,14}... | collective-permute-start | bytes 98312 | tf_op jit(solution)/shard_map/ppermute | solution.py:225
  133.6 1.0 collective-permute-done.21
  135.4 5.9 %collective-permute-start.25 = (bf16[2,128,128]{2,1,0:T(8,128)(2,1)S(1)}, bf16[2,128,128]{2,1,0:T(8,128)(2,1)S(1)}, u32[]{:S(2)}, u32[]{:S(2)}) collective-permute-start(bf16[2,128,128]{2,1,0:T(8,128)(2,1)S(1)} %select_select_fusion.2.refs_2_), channel_id=1, source_target_pairs={{1,0},{0,1},{3,2},{2,3},{5,4},{4,5},{7,6},{6,7},{9,8},{8,9},{11,10... | collective-permute-start | bytes 196616 | tf_op jit(solution)/shard_map/ppermute | solution.py:225
  141.8 6.6 %collective-permute-start.23 = (bf16[128,128]{1,0:T(8,128)(2,1)S(1)}, bf16[128,128]{1,0:T(8,128)(2,1)S(1)}, u32[]{:S(2)}, u32[]{:S(2)}) collective-permute-start(bf16[128,128]{1,0:T(8,128)(2,1)S(1)} %collective-permute-done.15.refs_0_), channel_id=1, source_target_pairs={{1,0},{0,1},{3,2},{2,3},{5,4},{4,5},{7,6},{6,7},{9,8},{8,9},{11,10... | collective-permute-start | bytes 98312 | tf_op jit(solution)/shard_map/ppermute | solution.py:225
  148.3 0.9 collective-permute-done.23.refs_3_
  150.4 5.3 %users.3 = bf16[32,128]{1,0:T(8,128)(2,1)} custom-call(bf16[128,128]{1,0:T(8,128)(2,1)} %copy-done.12, bf16[128,128]{1,0:T(8,128)(2,1)} %copy-done.11, bf16[2,128,128]{2,1,0:T(8,128)(2,1)} %copy-done.4, bf16[128,128]{1,0:T(8,128)(2,1)} %copy-done.14, bf16[128,128]{1,0:T(8,128)(2,1)} %copy-done.13, bf16[2,128,128]{2,1,0:T(8,128)(2,1)} %copy-done.8, ...), custom_call_target="tpu_custom_call" | custom-call | tf_op jit(solution)/shard_map/users/pallas_call | solution.py:135
  (100 shorter events, 12.8 us)
Async XLA Ops:
  0.6 50.9 %collective-permute-start = (bf16[128,128]{1,0:T(8,128)(2,1)}, bf16[128,128]{1,0:T(8,128)(2,1)S(1)}, u32[]{:S(2)}, u32[]{:S(2)}) collective-permute-start(bf16[128,128]{1,0:T(8,128)(2,1)} %param.4), channel_id=1, source_target_pairs={{254,0},{0,2},{2,4},{4,6},{6,8},{8,10},{10,12},{12,14},{14,16},{16... | collective-permute-start | bytes 98312 | tf_op jit(solution)/shard_map/ppermute | solution.py:225
  3.2 48.5 %collective-permute-start.1 = (bf16[128,128]{1,0:T(8,128)(2,1)}, bf16[128,128]{1,0:T(8,128)(2,1)S(1)}, u32[]{:S(2)}, u32[]{:S(2)}) collective-permute-start(bf16[128,128]{1,0:T(8,128)(2,1)} %param.4), channel_id=1, source_target_pairs={{128,0},{130,2},{132,4},{134,6},{136,8},{138,10},{140,12},{142,14}... | collective-permute-start | bytes 98312 | tf_op jit(solution)/shard_map/ppermute | solution.py:225
  7.4 10.1 %copy-start.7 = (bf16[4,64,128]{2,1,0:T(8,128)(2,1)S(1)}, bf16[4,64,128]{2,1,0:T(8,128)(2,1)}, u32[]{:S(2)}) copy-start(bf16[4,64,128]{2,1,0:T(8,128)(2,1)} %param.5) | copy-start | bytes 196612
  7.5 17.6 %all-to-all-start = ((bf16[8,128,128]{2,1,0:T(8,128)(2,1)}), bf16[8,128,128]{2,1,0:T(8,128)(2,1)S(1)}, u32[]{:S(2)}, u32[]{:S(2)}) async-start(bf16[8,128,128]{2,1,0:T(8,128)(2,1)} %broadcast_in_dim.124), calls=%async_computation | async-start | bytes 524288 | tf_op jit(solution)/shard_map/all_to_all | solution.py:218
  14.9 0.7 copy-start.22
  17.0 0.7 copy-start.21
  25.1 0.7 copy-start.2
  27.4 5.6 %collective-permute-start.4 = (bf16[6,64,128]{2,1,0:T(8,128)(2,1)}, bf16[6,64,128]{2,1,0:T(8,128)(2,1)S(1)}, u32[]{:S(2)}, u32[]{:S(2)}) collective-permute-start(bf16[6,64,128]{2,1,0:T(8,128)(2,1)} %pick_items.1), channel_id=1, source_target_pairs={{16,0},{32,16},{48,32},{0,48},{17,1},{33,17},{49,33},{1,49},{18,2}... | collective-permute-start | bytes 294920 | tf_op jit(solution)/shard_map/ppermute | solution.py:225
  30.1 5.3 %collective-permute-start.3 = (bf16[6,64,128]{2,1,0:T(8,128)(2,1)}, bf16[6,64,128]{2,1,0:T(8,128)(2,1)S(1)}, u32[]{:S(2)}, u32[]{:S(2)}) collective-permute-start(bf16[6,64,128]{2,1,0:T(8,128)(2,1)} %pick_items.1), channel_id=1, source_target_pairs={{32,0},{48,16},{0,32},{16,48},{33,1},{49,17},{1,33},{17,49},{34,2}... | collective-permute-start | bytes 294920 | tf_op jit(solution)/shard_map/ppermute | solution.py:225
  30.5 5.9 %collective-permute-start.2 = (bf16[6,64,128]{2,1,0:T(8,128)(2,1)}, bf16[6,64,128]{2,1,0:T(8,128)(2,1)S(1)}, u32[]{:S(2)}, u32[]{:S(2)}) collective-permute-start(bf16[6,64,128]{2,1,0:T(8,128)(2,1)} %pick_items.1), channel_id=1, source_target_pairs={{48,0},{0,16},{16,32},{32,48},{49,1},{1,17},{17,33},{33,49},{50,2}... | collective-permute-start | bytes 294920 | tf_op jit(solution)/shard_map/ppermute | solution.py:225
  37.3 3.5 %collective-permute-start.7 = (bf16[6,64,128]{2,1,0:T(8,128)(2,1)S(1)}, bf16[6,64,128]{2,1,0:T(8,128)(2,1)S(1)}, u32[]{:S(2)}, u32[]{:S(2)}) collective-permute-start(bf16[6,64,128]{2,1,0:T(8,128)(2,1)S(1)} %select_select_fusion.1), channel_id=1, source_target_pairs={{64,0},{128,64},{192,128},{0,192},{65,1},{129,65},{193,129},{1,193... | collective-permute-start | bytes 294920 | tf_op jit(solution)/shard_map/ppermute | solution.py:225
  38.3 5.0 %collective-permute-start.6 = (bf16[6,64,128]{2,1,0:T(8,128)(2,1)S(1)}, bf16[6,64,128]{2,1,0:T(8,128)(2,1)S(1)}, u32[]{:S(2)}, u32[]{:S(2)}) collective-permute-start(bf16[6,64,128]{2,1,0:T(8,128)(2,1)S(1)} %select_select_fusion.1), channel_id=1, source_target_pairs={{128,0},{192,64},{0,128},{64,192},{129,1},{193,65},{1,129},{65,193... | collective-permute-start | bytes 294920 | tf_op jit(solution)/shard_map/ppermute | solution.py:225
  39.5 4.8 %collective-permute-start.5 = (bf16[6,64,128]{2,1,0:T(8,128)(2,1)S(1)}, bf16[6,64,128]{2,1,0:T(8,128)(2,1)S(1)}, u32[]{:S(2)}, u32[]{:S(2)}) collective-permute-start(bf16[6,64,128]{2,1,0:T(8,128)(2,1)S(1)} %select_select_fusion.1), channel_id=1, source_target_pairs={{192,0},{0,64},{64,128},{128,192},{193,1},{1,65},{65,129},{129,193... | collective-permute-start | bytes 294920 | tf_op jit(solution)/shard_map/ppermute | solution.py:225
  44.4 5.8 %copy-start.3 = (bf16[4,64,128]{2,1,0:T(8,128)(2,1)S(1)}, bf16[4,64,128]{2,1,0:T(8,128)(2,1)}, u32[]{:S(2)}) copy-start(bf16[4,64,128]{2,1,0:T(8,128)(2,1)} %arrange.1) | copy-start | bytes 196612
  44.4 6.4 %copy-start.5 = (bf16[4,64,128]{2,1,0:T(8,128)(2,1)}, bf16[4,64,128]{2,1,0:T(8,128)(2,1)S(1)}, u32[]{:S(2)}) copy-start(bf16[4,64,128]{2,1,0:T(8,128)(2,1)S(1)} %slice.33) | copy-start | bytes 196612
  44.4 8.5 %collective-permute-start.10 = (bf16[2,128,128]{2,1,0:T(8,128)(2,1)S(1)}, bf16[2,128,128]{2,1,0:T(8,128)(2,1)S(1)}, u32[]{:S(2)}, u32[]{:S(2)}) collective-permute-start(bf16[2,128,128]{2,1,0:T(8,128)(2,1)S(1)} %bitcast.6), channel_id=1, source_target_pairs={{1,0},{0,1},{3,2},{2,3},{5,4},{4,5},{7,6},{6,7},{9,8},{8,9},{11,10... | collective-permute-start | bytes 196616 | tf_op jit(solution)/shard_map/ppermute | solution.py:225
  50.8 1.9 %collective-permute-start.11 = (bf16[4,32,128]{2,1,0:T(8,128)(2,1)S(1)}, bf16[4,32,128]{2,1,0:T(8,128)(2,1)S(1)}, u32[]{:S(2)}, u32[]{:S(2)}) collective-permute-start(bf16[4,32,128]{2,1,0:T(8,128)(2,1)S(1)} %get-tuple-element.28), channel_id=1, source_target_pairs={{1,0},{0,1},{3,2},{2,3},{5,4},{4,5},{7,6},{6,7},{9,8},{8,9},{11,10... | collective-permute-start | bytes 98312 | tf_op jit(solution)/shard_map/ppermute | solution.py:225
  51.5 1.1 copy-start.15
  51.5 1.2 collective-permute-start.8
  51.6 1.0 copy-start.16
  51.6 1.3 collective-permute-start.9
  52.7 0.6 copy-start.6
  52.9 0.6 copy-start.9
  59.0 17.1 %all-to-all-start.1 = ((bf16[8,160,128]{2,1,0:T(8,128)(2,1)}), bf16[8,160,128]{2,1,0:T(8,128)(2,1)S(1)}, u32[]{:S(2)}, u32[]{:S(2)}) async-start(bf16[8,160,128]{2,1,0:T(8,128)(2,1)} %users.2), calls=%async_computation.1 | async-start | bytes 655360 | tf_op jit(solution)/shard_map/all_to_all | solution.py:218
  76.1 0.7 copy-start.1
  78.8 13.9 %all-to-all-start.2 = ((bf16[16,4,32,128]{3,2,1,0:T(8,128)(2,1)}), bf16[16,4,32,128]{3,2,1,0:T(8,128)(2,1)S(1)}, u32[]{:S(2)}, u32[]{:S(2)}) async-start(bf16[16,4,32,128]{3,2,1,0:T(8,128)(2,1)} %get-tuple-element.6), calls=%async_computation.2 | async-start | bytes 1048576 | tf_op jit(solution)/shard_map/all_to_all | solution.py:218
  92.7 0.8 copy-start
  95.2 6.2 %collective-permute-start.12 = (bf16[4,32,128]{2,1,0:T(8,128)(2,1)}, bf16[4,32,128]{2,1,0:T(8,128)(2,1)S(1)}, u32[]{:S(2)}, u32[]{:S(2)}) collective-permute-start(bf16[4,32,128]{2,1,0:T(8,128)(2,1)} %pick_own.1.own_ref), channel_id=1, source_target_pairs={{1,0},{0,1},{3,2},{2,3},{5,4},{4,5},{7,6},{6,7},{9,8},{8,9},{11,10... | collective-permute-start | bytes 98312 | tf_op jit(solution)/shard_map/ppermute | solution.py:225
  97.2 4.1 %collective-permute-start.14 = (bf16[64,128]{1,0:T(8,128)(2,1)S(1)}, bf16[64,128]{1,0:T(8,128)(2,1)S(1)}, u32[]{:S(2)}, u32[]{:S(2)}) collective-permute-start(bf16[64,128]{1,0:T(8,128)(2,1)S(1)} %get-tuple-element.26), channel_id=1, source_target_pairs={{128,0},{130,2},{132,4},{134,6},{136,8},{138,10},{140,12},{142,14}... | collective-permute-start | bytes 49160 | tf_op jit(solution)/shard_map/ppermute | solution.py:225
  98.1 3.3 %collective-permute-start.13 = (bf16[64,128]{1,0:T(8,128)(2,1)S(1)}, bf16[64,128]{1,0:T(8,128)(2,1)S(1)}, u32[]{:S(2)}, u32[]{:S(2)}) collective-permute-start(bf16[64,128]{1,0:T(8,128)(2,1)S(1)} %get-tuple-element.27), channel_id=1, source_target_pairs={{2,0},{4,2},{6,4},{8,6},{10,8},{12,10},{14,12},{16,14},{18,16},{20... | collective-permute-start | bytes 49160 | tf_op jit(solution)/shard_map/ppermute | solution.py:225
  101.3 0.6 copy-start.10
  120.9 3.3 %collective-permute-start.19 = (bf16[2,128,128]{2,1,0:T(8,128)(2,1)}, bf16[2,128,128]{2,1,0:T(8,128)(2,1)S(1)}, u32[]{:S(2)}, u32[]{:S(2)}) collective-permute-start(bf16[2,128,128]{2,1,0:T(8,128)(2,1)} %pick.1), channel_id=1, source_target_pairs={{16,0},{32,16},{48,32},{0,48},{17,1},{33,17},{49,33},{1,49},{18,2}... | collective-permute-start | bytes 196616 | tf_op jit(solution)/shard_map/ppermute | solution.py:225
  121.4 4.8 %collective-permute-start.18 = (bf16[2,128,128]{2,1,0:T(8,128)(2,1)}, bf16[2,128,128]{2,1,0:T(8,128)(2,1)S(1)}, u32[]{:S(2)}, u32[]{:S(2)}) collective-permute-start(bf16[2,128,128]{2,1,0:T(8,128)(2,1)} %pick.1), channel_id=1, source_target_pairs={{32,0},{48,16},{0,32},{16,48},{33,1},{49,17},{1,33},{17,49},{34,2}... | collective-permute-start | bytes 196616 | tf_op jit(solution)/shard_map/ppermute | solution.py:225
  123.0 4.5 %collective-permute-start.17 = (bf16[2,128,128]{2,1,0:T(8,128)(2,1)}, bf16[2,128,128]{2,1,0:T(8,128)(2,1)S(1)}, u32[]{:S(2)}, u32[]{:S(2)}) collective-permute-start(bf16[2,128,128]{2,1,0:T(8,128)(2,1)} %pick.1), channel_id=1, source_target_pairs={{48,0},{0,16},{16,32},{32,48},{49,1},{1,17},{17,33},{33,49},{50,2}... | collective-permute-start | bytes 196616 | tf_op jit(solution)/shard_map/ppermute | solution.py:225
  127.5 3.4 %copy-start.23 = (bf16[128,128]{1,0:T(8,128)(2,1)S(1)}, bf16[128,128]{1,0:T(8,128)(2,1)}, u32[]{:S(2)}) copy-start(bf16[128,128]{1,0:T(8,128)(2,1)} %get-tuple-element.5) | copy-start | bytes 98308
  128.4 5.1 %collective-permute-start.22 = (bf16[2,128,128]{2,1,0:T(8,128)(2,1)S(1)}, bf16[2,128,128]{2,1,0:T(8,128)(2,1)S(1)}, u32[]{:S(2)}, u32[]{:S(2)}) collective-permute-start(bf16[2,128,128]{2,1,0:T(8,128)(2,1)S(1)} %select_select_fusion.3), channel_id=1, source_target_pairs={{64,0},{128,64},{192,128},{0,192},{65,1},{129,65},{193,129},{1,193... | collective-permute-start | bytes 196616 | tf_op jit(solution)/shard_map/ppermute | solution.py:225
  130.0 4.6 %collective-permute-start.21 = (bf16[2,128,128]{2,1,0:T(8,128)(2,1)S(1)}, bf16[2,128,128]{2,1,0:T(8,128)(2,1)S(1)}, u32[]{:S(2)}, u32[]{:S(2)}) collective-permute-start(bf16[2,128,128]{2,1,0:T(8,128)(2,1)S(1)} %select_select_fusion.3), channel_id=1, source_target_pairs={{128,0},{192,64},{0,128},{64,192},{129,1},{193,65},{1,129},{65,193... | collective-permute-start | bytes 196616 | tf_op jit(solution)/shard_map/ppermute | solution.py:225
  130.9 4.4 %collective-permute-start.20 = (bf16[2,128,128]{2,1,0:T(8,128)(2,1)S(1)}, bf16[2,128,128]{2,1,0:T(8,128)(2,1)S(1)}, u32[]{:S(2)}, u32[]{:S(2)}) collective-permute-start(bf16[2,128,128]{2,1,0:T(8,128)(2,1)S(1)} %select_select_fusion.3), channel_id=1, source_target_pairs={{192,0},{0,64},{64,128},{128,192},{193,1},{1,65},{65,129},{129,193... | collective-permute-start | bytes 196616 | tf_op jit(solution)/shard_map/ppermute | solution.py:225
  130.9 10.3 %collective-permute-start.16 = (bf16[128,128]{1,0:T(8,128)(2,1)S(1)}, bf16[128,128]{1,0:T(8,128)(2,1)S(1)}, u32[]{:S(2)}, u32[]{:S(2)}) collective-permute-start(bf16[128,128]{1,0:T(8,128)(2,1)S(1)} %copy-done.23), channel_id=1, source_target_pairs={{128,0},{130,2},{132,4},{134,6},{136,8},{138,10},{140,12},{142,14}... | collective-permute-start | bytes 98312 | tf_op jit(solution)/shard_map/ppermute | solution.py:225
  133.6 8.2 %collective-permute-start.15 = (bf16[128,128]{1,0:T(8,128)(2,1)S(1)}, bf16[128,128]{1,0:T(8,128)(2,1)S(1)}, u32[]{:S(2)}, u32[]{:S(2)}) collective-permute-start(bf16[128,128]{1,0:T(8,128)(2,1)S(1)} %copy-done.23), channel_id=1, source_target_pairs={{254,0},{0,2},{2,4},{4,6},{6,8},{8,10},{10,12},{12,14},{14,16},{16... | collective-permute-start | bytes 98312 | tf_op jit(solution)/shard_map/ppermute | solution.py:225
  135.4 13.8 %copy-start.4 = (bf16[2,128,128]{2,1,0:T(8,128)(2,1)}, bf16[2,128,128]{2,1,0:T(8,128)(2,1)S(1)}, u32[]{:S(2)}) copy-start(bf16[2,128,128]{2,1,0:T(8,128)(2,1)S(1)} %select_select_fusion.2.refs_2_) | copy-start | bytes 196612
  135.4 13.8 %collective-permute-start.25 = (bf16[2,128,128]{2,1,0:T(8,128)(2,1)S(1)}, bf16[2,128,128]{2,1,0:T(8,128)(2,1)S(1)}, u32[]{:S(2)}, u32[]{:S(2)}) collective-permute-start(bf16[2,128,128]{2,1,0:T(8,128)(2,1)S(1)} %select_select_fusion.2.refs_2_), channel_id=1, source_target_pairs={{1,0},{0,1},{3,2},{2,3},{5,4},{4,5},{7,6},{6,7},{9,8},{8,9},{11,10... | collective-permute-start | bytes 196616 | tf_op jit(solution)/shard_map/ppermute | solution.py:225
  141.3 7.9 %copy-start.11 = (bf16[128,128]{1,0:T(8,128)(2,1)}, bf16[128,128]{1,0:T(8,128)(2,1)S(1)}, u32[]{:S(2)}) copy-start(bf16[128,128]{1,0:T(8,128)(2,1)S(1)} %collective-permute-done.16.refs_1_) | copy-start | bytes 98308
  141.3 7.0 %collective-permute-start.24 = (bf16[128,128]{1,0:T(8,128)(2,1)S(1)}, bf16[128,128]{1,0:T(8,128)(2,1)S(1)}, u32[]{:S(2)}, u32[]{:S(2)}) collective-permute-start(bf16[128,128]{1,0:T(8,128)(2,1)S(1)} %collective-permute-done.16.refs_1_), channel_id=1, source_target_pairs={{1,0},{0,1},{3,2},{2,3},{5,4},{4,5},{7,6},{6,7},{9,8},{8,9},{11,10... | collective-permute-start | bytes 98312 | tf_op jit(solution)/shard_map/ppermute | solution.py:225
  141.8 7.4 %copy-start.12 = (bf16[128,128]{1,0:T(8,128)(2,1)}, bf16[128,128]{1,0:T(8,128)(2,1)S(1)}, u32[]{:S(2)}) copy-start(bf16[128,128]{1,0:T(8,128)(2,1)S(1)} %collective-permute-done.15.refs_0_) | copy-start | bytes 98308
  141.8 7.4 %collective-permute-start.23 = (bf16[128,128]{1,0:T(8,128)(2,1)S(1)}, bf16[128,128]{1,0:T(8,128)(2,1)S(1)}, u32[]{:S(2)}, u32[]{:S(2)}) collective-permute-start(bf16[128,128]{1,0:T(8,128)(2,1)S(1)} %collective-permute-done.15.refs_0_), channel_id=1, source_target_pairs={{1,0},{0,1},{3,2},{2,3},{5,4},{4,5},{7,6},{6,7},{9,8},{8,9},{11,10... | collective-permute-start | bytes 98312 | tf_op jit(solution)/shard_map/ppermute | solution.py:225
  148.3 0.9 copy-start.13
  149.8 0.6 copy-start.8
  (5 other events, 3.0 us)

commit v2 on v0

v2 whole, which is shorter than its diff:
```python
import functools

import jax
import jax.numpy as jnp
from jax import lax
from jax.experimental import pallas as pl
from jax.experimental.pallas import tpu as pltpu
from jax.sharding import Mesh, PartitionSpec as P

SWEEPS = 4
RIDGE = 0.005
UNRATED = 64.0
RATED_BELOW = 32.0
AXES = ("x", "y", "z")
VMEM = pltpu.MemorySpace.VMEM
SMEM = pltpu.MemorySpace.SMEM


def split_parts(value):
    high = value.astype(jnp.bfloat16)
    low = (value - high.astype(jnp.float32)).astype(jnp.bfloat16)
    return jnp.concatenate([high, low], axis=0)


def dot_f32(a, b, dims=((1,), (0,))):
    return lax.dot_general(a, b, (dims, ((), ())), preferred_element_type=jnp.float32)


def relax(right, ridge, bound, rated, factors):
    rows = right.shape[0]
    inverse = 1.0 / bound
    answer = right * inverse
    for _ in range(SWEEPS - 1):
        inner = dot_f32(split_parts(answer), factors, ((1,), (1,)))
        inner = jnp.where(rated, inner[:rows] + inner[rows:], 0.0)
        outer = dot_f32(split_parts(inner), factors)
        applied = outer[:rows] + outer[rows:] + ridge * answer
        answer = answer + (right - applied) * inverse
    return answer.astype(jnp.bfloat16)


def users_kernel(*refs, tiles, copies):
    own, other = refs[:tiles], refs[tiles : 2 * tiles]
    own_marks_ref, other_marks_ref, *extra, out_ref, factor_t_ref, mask_ref, sums_ref = refs[2 * tiles :]
    rank = own[0].shape[1]
    rows = own_marks_ref.shape[1]
    parts = []
    for k in range(tiles):
        parts += [own[k][...], other[k][...]]
    marks = []
    for k in range(own_marks_ref.shape[0]):
        marks += [own_marks_ref[k], other_marks_ref[k]]
    factors = jnp.concatenate(parts, axis=0)
    marked = jnp.concatenate(marks, axis=1).astype(jnp.float32)
    rated = jnp.abs(marked) < RATED_BELOW
    factor_t_ref[...] = factors.T
    mask = jnp.where(rated, 1.0, 0.0)
    mask_ref[...] = mask
    count = jnp.sum(mask, axis=1, keepdims=True)
    right = dot_f32(jnp.where(rated, marked, 0.0).astype(jnp.bfloat16), factors)
    together = 16

    def some(step, carry):
        chosen = mask_ref[pl.ds(step * together, together), :].astype(jnp.bfloat16)
        weighted = (factor_t_ref[...][None] * chosen[:, None, :]).reshape(together * rank, -1)
        gram = dot_f32(weighted, factors)
        total = jnp.sum(jnp.abs(gram).reshape(together, rank, rank), axis=1)
        sums_ref[pl.ds(step * together, together), :] = total
        return carry

    lax.fori_loop(0, rows // together, some, 0)
    ridge = RIDGE * (count + 1.0)
    bound = jnp.max(sums_ref[...], axis=1, keepdims=True) + ridge
    answer = relax(right, ridge, bound, rated, factors)
    if not copies:
        out_ref[...] = answer
    for c in range(copies):
        out_ref[c, :rows, :] = answer
        for k, ref in enumerate(extra):
            users = ref.shape[0]
            out_ref[c, rows + k * users : rows + (k + 1) * users, :] = ref[...]


def items_kernel(*refs):
    *ins, out_ref, copies_ref, sums_ref = refs
    own, other, marks = (ins[i * len(ins) // 3 : (i + 1) * len(ins) // 3] for i in range(3))
    rank = own[0].shape[1]
    items = out_ref.shape[0]
    parts = []
    for k in range(len(own)):
        parts += [own[k][...], other[k][...]]
    factors = jnp.concatenate(parts, axis=0)
    factor_t = factors.T
    marked = jnp.concatenate([ref[...].astype(jnp.float32) for ref in marks], axis=0).T
    rated = jnp.abs(marked) < RATED_BELOW
    mask = jnp.where(rated, 1.0, 0.0)
    count = jnp.sum(mask, axis=1, keepdims=True)
    right = dot_f32(jnp.where(rated, marked, 0.0).astype(jnp.bfloat16), factors)
    group = 8
    for j in range(items // group):
        row = mask[j * group : j * group + 1].astype(jnp.bfloat16)
        gram = dot_f32(factor_t * row, factors)
        total = jnp.sum(jnp.abs(gram), axis=0, keepdims=True)
        sums_ref[j * group : (j + 1) * group, :] = jnp.broadcast_to(total, (group, rank))
    ridge = RIDGE * (count + 1.0)
    bound = jnp.max(sums_ref[...], axis=1, keepdims=True) + ridge
    answer = relax(right, ridge, bound, rated, factors)
    out_ref[...] = answer
    for c in range(copies_ref.shape[0]):
        copies_ref[c] = answer


def vmem_specs(count):
    return [pl.BlockSpec(memory_space=VMEM)] * count


def solve_users(own, other, own_marks, other_marks, copies=0, extra=()):
    tiles, rows, half = own_marks.shape
    rank = own[0].shape[1]
    width = tiles * 2 * half
    args = [*own, *other, own_marks, other_marks, *extra]
    shape = (rows, rank)
    if copies:
        shape = (copies, rows + sum(e.shape[0] for e in extra), rank)
    return pl.pallas_call(
        functools.partial(users_kernel, tiles=tiles, copies=copies),
        out_shape=jax.ShapeDtypeStruct(shape, jnp.bfloat16),
        in_specs=vmem_specs(len(args)),
        out_specs=pl.BlockSpec(memory_space=VMEM),
        scratch_shapes=[
            pltpu.VMEM((rank, width), jnp.bfloat16),
            pltpu.VMEM((rows, width), jnp.float32),
            pltpu.VMEM((rows, rank), jnp.float32),
        ],
        name="users",
    )(*args)


def solve_items(own, other, marks, copies):
    rank = own[0].shape[1]
    items = marks[0].shape[1]
    args = [*own, *other, *marks]
    return pl.pallas_call(
        items_kernel,
        out_shape=(
            jax.ShapeDtypeStruct((items, rank), jnp.bfloat16),
            jax.ShapeDtypeStruct((copies, items, rank), jnp.bfloat16),
        ),
        in_specs=vmem_specs(len(args)),
        out_specs=tuple(vmem_specs(2)),
        scratch_shapes=[pltpu.VMEM((items, rank), jnp.float32)],
        name="items",
    )(*args)


def swapped_with_all(copies, axes):
    return lax.all_to_all(copies, axes, split_axis=0, concat_axis=0, tiled=True)


def fetched_from(value, axis, steps):
    count = 1
    for name in (axis if isinstance(axis, tuple) else (axis,)):
        count *= lax.axis_size(name)
    return lax.ppermute(value, axis, [((target + steps) % count, target) for target in range(count)])


def shift_digits(shift, z_first):
    nz, ny, nx = lax.axis_size("z"), lax.axis_size("y"), lax.axis_size("x")
    z, z_shift = lax.axis_index("z"), shift % nz
    carry = (z + z_shift) // nz if z_first else jnp.where(z < z_shift, 1, 0)
    y = lax.axis_index("y") + (shift // nz) % ny + carry
    x = lax.axis_index("x") + shift // (nz * ny) + y // ny
    return (x % nx) * ny + y % ny, (z + z_shift) % nz


def taken(source, index, start, size):
    picked = lax.dynamic_slice(source, (index, jnp.int32(start), jnp.int32(0)), (1, size, source.shape[2]))
    return picked[0]


def body(item_start, ratings, rating_bits, plan):
    tiles, users, items = ratings.shape
    own_half = lax.axis_index("grp")
    blocks = lax.axis_size(AXES)
    plane = lax.axis_size(("x", "y"))
    ring = lax.axis_size("z")
    rows = users // 2
    partner = lambda value: fetched_from(value, "grp", 1)

    near, across = blocks - 1, blocks // 2
    place = lambda wanted: jnp.sum(jnp.where(plan == wanted, jnp.arange(tiles), 0))
    first, second = place(near), place(across)
    low, high = jnp.minimum(first, second), jnp.maximum(first, second)
    third = jnp.where(low > 0, 0, jnp.where(high > 1, 1, 2))
    fourth = tiles * (tiles - 1) // 2 - first - second - third
    order = (first, second, third, fourth)
    shifts = (near, across, plan[third], plan[fourth])
    forward = [shift_digits(shift, False) for shift in shifts]
    backward = [shift_digits((blocks - shift) % blocks, False) for shift in shifts]
    marks_at = [shift_digits(blocks - shift, True) for shift in shifts[2:]]

    bit_count = 32 // lax.axis_size("grp")
    item_bits = own_half * bit_count + lax.broadcasted_iota(jnp.int32, (1, 1, items), 2) // (items // bit_count)
    rated = (jnp.right_shift(rating_bits[:, :, None], item_bits) & 1) == 1
    marks = jnp.where(rated, ratings, jnp.asarray(UNRATED, ratings.dtype))
    cut = lambda k, at: lax.dynamic_slice(marks, (k, at * rows, 0), (1, rows, items))[0]
    own_marks = [cut(k, own_half) for k in order]
    away_marks = [cut(k, 1 - own_half) for k in order]
    marks = [jnp.concatenate(pair, axis=0) for pair in zip(own_marks, away_marks)]
    own_marks = jnp.stack(own_marks)
    other_marks = partner(jnp.stack(away_marks))

    def gather(copies, size, digits, z_step, extra=()):
        held = swapped_with_all(copies, ("x", "y"))
        pieces = [taken(held, at, 0, size) for at, _ in digits]
        pieces[0] = fetched_from(pieces[0], "z", z_step)
        moving = jnp.concatenate([*pieces[2:], *extra], axis=0)
        ring_held = swapped_with_all(jnp.broadcast_to(moving, (ring, *moving.shape)), "z")
        for k in (2, 3):
            pieces[k] = taken(ring_held, digits[k][1], (k - 2) * size, size)
        return held, ring_held, pieces, [partner(piece) for piece in pieces]

    copies = jnp.broadcast_to(item_start, (plane, *item_start.shape))
    _, held, own, other = gather(copies, items, forward, -1, marks[2:])
    moved = [taken(held, z_at, 2 * items + k * users, users) for k, (_, z_at) in enumerate(marks_at)]
    near_marks, across_marks = (fetched_from(m, AXES, -shift) for m, shift in zip(marks, (near, across)))
    near_marks, across_marks, *moved = lax.optimization_barrier((near_marks, across_marks, *moved))
    copies = solve_users(own, other, own_marks, other_marks, plane, moved)

    held, _, own, other = gather(copies, rows, backward, 1)
    moved = [taken(held, at, rows + k * users, users) for k, (at, _) in enumerate(marks_at)]
    item_factors, copies = solve_items(own, other, [near_marks, across_marks, *moved], plane)

    _, _, own, other = gather(copies, items, forward, -1)
    user_factors = solve_users(own, other, own_marks, other_marks)
    return (user_factors, item_factors)


def solution(mesh):
    torus = Mesh(mesh.devices.reshape(4, 4, 8, 2), (*AXES, "grp"))
    everywhere = (*AXES, "grp")
    in_specs = (P(everywhere, None), P(None, AXES, "grp"), P(None, AXES), P())
    out_specs = (P(everywhere, None), P(everywhere, None))
    return jax.shard_map(body, mesh=torus, in_specs=in_specs, out_specs=out_specs, check_vma=False)
```

time: 162 us -> 147 us (0.907)
  waiting for transfers between devices: 54 us -> 24 us
  starting transfers between devices: 44.6 us -> 67.3 us
  between operations: 0.85 us -> 15.2 us
  blocking collectives: 25.6 us -> 13.7 us
  Pallas kernels: 20.5 us -> 14 us
  other arithmetic: 5.08 us -> 1.38 us
    ppermute x22 -> x18, waiting for transfers between devices: 32.9 us -> 10.8 us  [fetched_from(): lax.ppermute(value, axis, [((target + steps) % count, target) for target...]
    all_to_all x1 -> x5, starting transfers between devices: 9 us -> 29.3 us  [swapped_with_all(): return lax.all_to_all(copies, axes, split_axis=0, concat_axis=0, tiled=True)]
    all_to_all x2 -> x1, blocking collectives: 25.6 us -> 13.7 us  [swapped_with_all(): return lax.all_to_all(copies, axes, split_axis=0, concat_axis=0, tiled=True)]
    all_to_all x1 -> x5, waiting for transfers between devices: 21.2 us -> 13.2 us  [swapped_with_all(): return lax.all_to_all(copies, axes, split_axis=0, concat_axis=0, tiled=True)]
    pallas_call x6 -> x3, Pallas kernels: 20.5 us -> 14 us  [the longest x2 10.8 us: solve_users(): pl.pallas_call(functools.partial(users_kernel, tiles=tiles, copies=copies...]
    select_n x9 -> x0, other arithmetic: 3.28 us -> none  [the longest x6 3.16 us: fetch(): chosen = jnp.where((steps == step)[:, None, None], arrived, chosen)]
    ppermute x22 -> x18, starting transfers between devices: 35.6 us -> 38 us  [fetched_from(): lax.ppermute(value, axis, [((target + steps) % count, target) for target...]
    unnamed x28 -> x65, local copies, waits for them, and re-layouts: 6.08 us -> 3.88 us
  transfers between devices with their start and end apart: 23 -> 23, of which waited for: 18 -> 11; matrix products, arithmetic and copies ran while one was open for 2% -> 2% of each run, Pallas kernels for 0% -> 0%
where the time goes in v2:
time: 147 us; the launch traced here: 146 us
  starting transfers between devices  67.3 us (46%)
  waiting for transfers between devices  24 us (16%)
  between operations  15.2 us (10%)
  Pallas kernels  14 us (10%)
  blocking collectives  13.7 us (9%)
  local copies, waits for them, and re-layouts  10 us (7%)
    ppermute x18, starting transfers between devices, fetched_from(): lax.ppermute(value, axis, [((target + steps) % count, target) for target...  38 us
    all_to_all x5, starting transfers between devices, swapped_with_all(): return lax.all_to_all(copies, axes, split_axis=0, concat_axis=0, tiled=True)  29.3 us
    all_to_all x1, blocking collectives, swapped_with_all(): return lax.all_to_all(copies, axes, split_axis=0, concat_axis=0, tiled=True)  13.7 us
    all_to_all x5, waiting for transfers between devices, swapped_with_all(): return lax.all_to_all(copies, axes, split_axis=0, concat_axis=0, tiled=True)  13.2 us
    ppermute x18, waiting for transfers between devices, fetched_from(): lax.ppermute(value, axis, [((target + steps) % count, target) for target...  10.8 us
    pallas_call x2, Pallas kernels, solve_users(): pl.pallas_call(functools.partial(users_kernel, tiles=tiles, copies=copies...  10.8 us
    unnamed x65, local copies, waits for them, and re-layouts  3.88 us
    pallas_call x1, Pallas kernels, solve_items(): pl.pallas_call(items_kernel, out_shape=(jax.ShapeDtypeStruct((items, rank...  3.26 us
  transfers between devices with their start and end apart: 23, of which 11 were waited for; matrix products, arithmetic and copies ran while one was open for 2% of the time, Pallas kernels for 0%

profile of v2, /device:TPU:1, one launch (start us, length us, event | category | flops | bytes accessed | tf_op | source)
XLA Modules:
  0.0 145.6 jit_solution(5293559030518876271)
XLA Ops:
  0.6 1.7 %broadcast_in_dim.22 = bf16[16,128,128]{2,1,0:T(8,128)(2,1)} broadcast(bf16[128,128]{1,0:T(8,128)(2,1)} %param.4), dimensions={1,2} | broadcast | bytes 557056 | tf_op jit(solution)/shard_map/broadcast_in_dim | solution.py:223
  2.3 7.6 %all-to-all-start = ((bf16[16,128,128]{2,1,0:T(8,128)(2,1)}), bf16[16,128,128]{2,1,0:T(8,128)(2,1)S(1)}, u32[]{:S(2)}, u32[]{:S(2)}) async-start(bf16[16,128,128]{2,1,0:T(8,128)(2,1)} %broadcast_in_dim.22), calls=%async_computation | async-start | bytes 1048576 | tf_op jit(solution)/shard_map/all_to_all | solution.py:157
  9.9 0.6 copy-done.29
  10.5 0.6 fusion.3
  15.1 0.6 fusion.4
  20.6 0.7 copy-done.7
  21.5 1.0 broadcast_in_dim.25
  22.6 8.2 %all-to-all-start.1 = ((bf16[8,384,128]{2,1,0:T(8,128)(2,1)}), bf16[8,384,128]{2,1,0:T(8,128)(2,1)S(1)}, u32[]{:S(2)}, u32[]{:S(2)}) async-start(bf16[8,384,128]{2,1,0:T(8,128)(2,1)} %broadcast_in_dim.25), calls=%async_computation.1 | async-start | bytes 1572864 | tf_op jit(solution)/shard_map/all_to_all | solution.py:157
  34.7 7.2 %collective-permute-start.6 = (bf16[64,128]{1,0:T(8,128)(2,1)S(1)}, bf16[64,128]{1,0:T(8,128)(2,1)S(1)}, u32[]{:S(2)}, u32[]{:S(2)}) collective-permute-start(bf16[64,128]{1,0:T(8,128)(2,1)S(1)} %pad_maximum_fusion.3), channel_id=1, source_target_pairs={{2,0},{4,2},{6,4},{8,6},{10,8},{12,10},{14,12},{16,14},{18,16},{20... | collective-permute-start | bytes 49160 | tf_op jit(solution)/shard_map/ppermute | solution.py:164
  41.8 0.6 collective-permute-start.7
  43.8 2.4 %collective-permute-start.2 = (bf16[128,128]{1,0:T(8,128)(2,1)S(1)}, bf16[128,128]{1,0:T(8,128)(2,1)S(1)}, u32[]{:S(2)}, u32[]{:S(2)}) collective-permute-start(bf16[128,128]{1,0:T(8,128)(2,1)S(1)} %get-tuple-element.40.refs_1_), channel_id=1, source_target_pairs={{1,0},{0,1},{3,2},{2,3},{5,4},{4,5},{7,6},{6,7},{9,8},{8,9},{11,10... | collective-permute-start | bytes 98312 | tf_op jit(solution)/shard_map/ppermute | solution.py:164
  46.2 0.4 collective-permute-start.5
  46.6 0.6 pad_maximum_fusion.1.refs_8_
  47.3 0.7 collective-permute-done.refs_0_
  48.0 5.5 %collective-permute-start.1 = (bf16[128,128]{1,0:T(8,128)(2,1)S(1)}, bf16[128,128]{1,0:T(8,128)(2,1)S(1)}, u32[]{:S(2)}, u32[]{:S(2)}) collective-permute-start(bf16[128,128]{1,0:T(8,128)(2,1)S(1)} %collective-permute-done.refs_0_), channel_id=1, source_target_pairs={{1,0},{0,1},{3,2},{2,3},{5,4},{4,5},{7,6},{6,7},{9,8},{8,9},{11,10... | collective-permute-start | bytes 98312 | tf_op jit(solution)/shard_map/ppermute | solution.py:164
  53.5 0.4 all-to-all-done.1
  54.0 1.1 collective-permute-start.3
  55.2 0.6 dynamic-slice_bitcast_fusion.12
  55.9 0.4 collective-permute-done.4.refs_7_
  56.5 0.6 copy-done.12
  57.1 5.6 %users.2 = bf16[16,160,128]{2,1,0:T(8,128)(2,1)} custom-call(bf16[128,128]{1,0:T(8,128)(2,1)} %copy-done.8, bf16[128,128]{1,0:T(8,128)(2,1)} %copy-done, bf16[128,128]{1,0:T(8,128)(2,1)} %copy-done.2, bf16[128,128]{1,0:T(8,128)(2,1)} %copy-done.1, bf16[128,128]{1,0:T(8,128)(2,1)} %copy-done.10, bf16[128,128]{1,0:T(8,128)(2,1)} %copy-done.9, ...), custom_call_target="tpu_custom_call" | custom-call | tf_op jit(solution)/shard_map/users/pallas_call | solution.py:125
  62.7 6.7 %all-to-all-start.2 = ((bf16[16,160,128]{2,1,0:T(8,128)(2,1)}), bf16[16,160,128]{2,1,0:T(8,128)(2,1)S(1)}, u32[]{:S(2)}, u32[]{:S(2)}) async-start(bf16[16,160,128]{2,1,0:T(8,128)(2,1)} %users.2), calls=%async_computation.2 | async-start | bytes 1310720 | tf_op jit(solution)/shard_map/all_to_all | solution.py:157
  69.7 11.1 %all-to-all-done.2 = bf16[16,160,128]{2,1,0:T(8,128)(2,1)S(1)} async-done(((bf16[16,160,128]{2,1,0:T(8,128)(2,1)}), bf16[16,160,128]{2,1,0:T(8,128)(2,1)S(1)}, u32[]{:S(2)}, u32[]{:S(2)}) %all-to-all-start.2) | async-done | bytes 655392 | tf_op jit(solution)/shard_map/all_to_all | solution.py:157
  80.8 0.7 broadcast_in_dim.26
  81.5 3.4 %all-to-all-start.3 = ((bf16[8,64,128]{2,1,0:T(8,128)(2,1)}), bf16[8,64,128]{2,1,0:T(8,128)(2,1)S(1)}, u32[]{:S(2)}, u32[]{:S(2)}) async-start(bf16[8,64,128]{2,1,0:T(8,128)(2,1)} %broadcast_in_dim.26), calls=%async_computation.3 | async-start | bytes 262144 | tf_op jit(solution)/shard_map/all_to_all | solution.py:157
  84.9 2.6 %collective-permute-start.8 = (bf16[32,128]{1,0:T(8,128)(2,1)S(1)}, bf16[32,128]{1,0:T(8,128)(2,1)S(1)}, u32[]{:S(2)}, u32[]{:S(2)}) collective-permute-start(bf16[32,128]{1,0:T(8,128)(2,1)S(1)} %get-tuple-element.33), channel_id=1, source_target_pairs={{2,0},{4,2},{6,4},{8,6},{10,8},{12,10},{14,12},{0,14},{3,1},{5,3},... | collective-permute-start | bytes 24584 | tf_op jit(solution)/shard_map/ppermute | solution.py:164
  87.5 3.0 %collective-permute-start.10 = (bf16[32,128]{1,0:T(8,128)(2,1)S(1)}, bf16[32,128]{1,0:T(8,128)(2,1)S(1)}, u32[]{:S(2)}, u32[]{:S(2)}) collective-permute-start(bf16[32,128]{1,0:T(8,128)(2,1)S(1)} %get-tuple-element.32.refs_1_), channel_id=1, source_target_pairs={{1,0},{0,1},{3,2},{2,3},{5,4},{4,5},{7,6},{6,7},{9,8},{8,9},{11,10... | collective-permute-start | bytes 24584 | tf_op jit(solution)/shard_map/ppermute | solution.py:164
  90.5 1.4 collective-permute-start.9
  91.8 1.0 all-to-all-done.3
  92.8 3.6 %collective-permute-start.11 = (bf16[32,128]{1,0:T(8,128)(2,1)S(1)}, bf16[32,128]{1,0:T(8,128)(2,1)S(1)}, u32[]{:S(2)}, u32[]{:S(2)}) collective-permute-start(bf16[32,128]{1,0:T(8,128)(2,1)S(1)} %get-tuple-element.43.refs_2_), channel_id=1, source_target_pairs={{1,0},{0,1},{3,2},{2,3},{5,4},{4,5},{7,6},{6,7},{9,8},{8,9},{11,10... | collective-permute-start | bytes 24584 | tf_op jit(solution)/shard_map/ppermute | solution.py:164
  96.4 0.3 collective-permute-start.12
  96.7 0.6 dynamic-slice_bitcast_fusion.10
  97.6 0.3 copy-done.24
  98.1 3.3 %items.1 = (bf16[128,128]{1,0:T(8,128)(2,1)}, bf16[16,128,128]{2,1,0:T(8,128)(2,1)}) custom-call(bf16[32,128]{1,0:T(8,128)(2,1)} %copy-done.23, bf16[32,128]{1,0:T(8,128)(2,1)} %copy-done.13, bf16[32,128]{1,0:T(8,128)(2,1)} %copy-done.15, bf16[32,128]{1,0:T(8,128)(2,1)} %copy-done.14, bf16[32,128]{1,0:T(8,128)(2,1)} %copy-done.25, ...), custom_call_target="tpu_custom_call" | custom-call | tf_op jit(solution)/shard_map/items/pallas_call | solution.py:143
  101.4 13.7 %all_to_all.30 = bf16[16,128,128]{2,1,0:T(8,128)(2,1)S(1)} all-to-all(bf16[16,128,128]{2,1,0:T(8,128)(2,1)} %get-tuple-element.12), channel_id=1, replica_groups=mesh['x'=4,'y'=4,'z'=8,'grp'=2] {'x','y'}, dimensions={0} | all-to-all | bytes 1048576 | tf_op jit(solution)/shard_map/all_to_all | solution.py:157
  115.1 0.9 broadcast_in_dim.27
  116.0 3.5 %all-to-all-start.5 = ((bf16[8,256,128]{2,1,0:T(8,128)(2,1)}), bf16[8,256,128]{2,1,0:T(8,128)(2,1)S(1)}, u32[]{:S(2)}, u32[]{:S(2)}) async-start(bf16[8,256,128]{2,1,0:T(8,128)(2,1)} %broadcast_in_dim.27), calls=%async_computation.5 | async-start | bytes 1048576 | tf_op jit(solution)/shard_map/all_to_all | solution.py:157
  119.5 1.4 collective-permute-start.13
  120.8 2.9 %collective-permute-start.15 = (bf16[128,128]{1,0:T(8,128)(2,1)S(1)}, bf16[128,128]{1,0:T(8,128)(2,1)S(1)}, u32[]{:S(2)}, u32[]{:S(2)}) collective-permute-start(bf16[128,128]{1,0:T(8,128)(2,1)S(1)} %get-tuple-element.38.refs_1_), channel_id=1, source_target_pairs={{1,0},{0,1},{3,2},{2,3},{5,4},{4,5},{7,6},{6,7},{9,8},{8,9},{11,10... | collective-permute-start | bytes 98312 | tf_op jit(solution)/shard_map/ppermute | solution.py:164
  123.7 8.4 %collective-permute-done.13.refs_0_ = bf16[128,128]{1,0:T(8,128)(2,1)S(1)} collective-permute-done((bf16[128,128]{1,0:T(8,128)(2,1)S(1)}, bf16[128,128]{1,0:T(8,128)(2,1)S(1)}, u32[]{:S(2)}, u32[]{:S(2)}) %collective-permute-start.13) | collective-permute-done | bytes 32800 | tf_op jit(solution)/shard_map/ppermute | solution.py:164
  132.1 2.1 %collective-permute-start.14 = (bf16[128,128]{1,0:T(8,128)(2,1)S(1)}, bf16[128,128]{1,0:T(8,128)(2,1)S(1)}, u32[]{:S(2)}, u32[]{:S(2)}) collective-permute-start(bf16[128,128]{1,0:T(8,128)(2,1)S(1)} %collective-permute-done.13.refs_0_), channel_id=1, source_target_pairs={{1,0},{0,1},{3,2},{2,3},{5,4},{4,5},{7,6},{6,7},{9,8},{8,9},{11,10... | collective-permute-start | bytes 98312 | tf_op jit(solution)/shard_map/ppermute | solution.py:164
  134.2 0.7 all-to-all-done.5
  134.8 3.5 %collective-permute-start.16 = (bf16[128,128]{1,0:T(8,128)(2,1)S(1)}, bf16[128,128]{1,0:T(8,128)(2,1)S(1)}, u32[]{:S(2)}, u32[]{:S(2)}) collective-permute-start(bf16[128,128]{1,0:T(8,128)(2,1)S(1)} %get-tuple-element.35.refs_2_), channel_id=1, source_target_pairs={{1,0},{0,1},{3,2},{2,3},{5,4},{4,5},{7,6},{6,7},{9,8},{8,9},{11,10... | collective-permute-start | bytes 98312 | tf_op jit(solution)/shard_map/ppermute | solution.py:164
  138.4 0.7 collective-permute-done.16.refs_6_
  139.2 0.3 collective-permute-done.17.refs_7_
  139.5 0.2 copy-done.19
  139.8 0.6 copy-done.20
  140.4 5.2 %users.3 = bf16[32,128]{1,0:T(8,128)(2,1)} custom-call(bf16[128,128]{1,0:T(8,128)(2,1)} %copy-done.16, bf16[128,128]{1,0:T(8,128)(2,1)} %copy-done.6, bf16[128,128]{1,0:T(8,128)(2,1)} %copy-done.5, bf16[128,128]{1,0:T(8,128)(2,1)} %copy-done.4, bf16[128,128]{1,0:T(8,128)(2,1)} %copy-done.18, bf16[128,128]{1,0:T(8,128)(2,1)} %copy-done.17, ...), custom_call_target="tpu_custom_call" | custom-call | tf_op jit(solution)/shard_map/users/pallas_call | solution.py:125
  (91 shorter events, 1.5 us)
Async XLA Ops:
  2.3 19.1 %all-to-all-start = ((bf16[16,128,128]{2,1,0:T(8,128)(2,1)}), bf16[16,128,128]{2,1,0:T(8,128)(2,1)S(1)}, u32[]{:S(2)}, u32[]{:S(2)}) async-start(bf16[16,128,128]{2,1,0:T(8,128)(2,1)} %broadcast_in_dim.22), calls=%async_computation | async-start | bytes 1048576 | tf_op jit(solution)/shard_map/all_to_all | solution.py:157
  9.9 0.7 copy-start.29
  20.4 0.8 copy-start.7
  20.5 0.8 copy-start.28
  22.6 31.3 %all-to-all-start.1 = ((bf16[8,384,128]{2,1,0:T(8,128)(2,1)}), bf16[8,384,128]{2,1,0:T(8,128)(2,1)S(1)}, u32[]{:S(2)}, u32[]{:S(2)}) async-start(bf16[8,384,128]{2,1,0:T(8,128)(2,1)} %broadcast_in_dim.25), calls=%async_computation.1 | async-start | bytes 1572864 | tf_op jit(solution)/shard_map/all_to_all | solution.py:157
  34.7 19.3 %collective-permute-start.6 = (bf16[64,128]{1,0:T(8,128)(2,1)S(1)}, bf16[64,128]{1,0:T(8,128)(2,1)S(1)}, u32[]{:S(2)}, u32[]{:S(2)}) collective-permute-start(bf16[64,128]{1,0:T(8,128)(2,1)S(1)} %pad_maximum_fusion.3), channel_id=1, source_target_pairs={{2,0},{4,2},{6,4},{8,6},{10,8},{12,10},{14,12},{16,14},{18,16},{20... | collective-permute-start | bytes 49160 | tf_op jit(solution)/shard_map/ppermute | solution.py:164
  41.8 13.2 %collective-permute-start.7 = (bf16[64,128]{1,0:T(8,128)(2,1)S(1)}, bf16[64,128]{1,0:T(8,128)(2,1)S(1)}, u32[]{:S(2)}, u32[]{:S(2)}) collective-permute-start(bf16[64,128]{1,0:T(8,128)(2,1)S(1)} %pad_maximum_fusion.4), channel_id=1, source_target_pairs={{128,0},{130,2},{132,4},{134,6},{136,8},{138,10},{140,12},{142,14}... | collective-permute-start | bytes 49160 | tf_op jit(solution)/shard_map/ppermute | solution.py:164
  43.7 2.6 %copy-start = (bf16[128,128]{1,0:T(8,128)(2,1)}, bf16[128,128]{1,0:T(8,128)(2,1)S(1)}, u32[]{:S(2)}) copy-start(bf16[128,128]{1,0:T(8,128)(2,1)S(1)} %get-tuple-element.40.refs_1_) | copy-start | bytes 98308
  43.7 4.3 %collective-permute-start = (bf16[128,128]{1,0:T(8,128)(2,1)S(1)}, bf16[128,128]{1,0:T(8,128)(2,1)S(1)}, u32[]{:S(2)}, u32[]{:S(2)}) collective-permute-start(bf16[128,128]{1,0:T(8,128)(2,1)S(1)} %get-tuple-element.41), channel_id=1, source_target_pairs={{14,0},{0,2},{2,4},{4,6},{6,8},{8,10},{10,12},{12,14},{15,1},{1,3}... | collective-permute-start | bytes 98312 | tf_op jit(solution)/shard_map/ppermute | solution.py:164
  43.8 12.0 %collective-permute-start.2 = (bf16[128,128]{1,0:T(8,128)(2,1)S(1)}, bf16[128,128]{1,0:T(8,128)(2,1)S(1)}, u32[]{:S(2)}, u32[]{:S(2)}) collective-permute-start(bf16[128,128]{1,0:T(8,128)(2,1)S(1)} %get-tuple-element.40.refs_1_), channel_id=1, source_target_pairs={{1,0},{0,1},{3,2},{2,3},{5,4},{4,5},{7,6},{6,7},{9,8},{8,9},{11,10... | collective-permute-start | bytes 98312 | tf_op jit(solution)/shard_map/ppermute | solution.py:164
  46.2 9.6 %collective-permute-start.5 = (bf16[4,32,128]{2,1,0:T(8,128)(2,1)S(1)}, bf16[4,32,128]{2,1,0:T(8,128)(2,1)S(1)}, u32[]{:S(2)}, u32[]{:S(2)}) collective-permute-start(bf16[4,32,128]{2,1,0:T(8,128)(2,1)S(1)} %pad_maximum_fusion.2), channel_id=1, source_target_pairs={{1,0},{0,1},{3,2},{2,3},{5,4},{4,5},{7,6},{6,7},{9,8},{8,9},{11,10... | collective-permute-start | bytes 98312 | tf_op jit(solution)/shard_map/ppermute | solution.py:164
  48.0 5.9 %copy-start.8 = (bf16[128,128]{1,0:T(8,128)(2,1)}, bf16[128,128]{1,0:T(8,128)(2,1)S(1)}, u32[]{:S(2)}) copy-start(bf16[128,128]{1,0:T(8,128)(2,1)S(1)} %collective-permute-done.refs_0_) | copy-start | bytes 98308
  48.0 7.9 %collective-permute-start.1 = (bf16[128,128]{1,0:T(8,128)(2,1)S(1)}, bf16[128,128]{1,0:T(8,128)(2,1)S(1)}, u32[]{:S(2)}, u32[]{:S(2)}) collective-permute-start(bf16[128,128]{1,0:T(8,128)(2,1)S(1)} %collective-permute-done.refs_0_), channel_id=1, source_target_pairs={{1,0},{0,1},{3,2},{2,3},{5,4},{4,5},{7,6},{6,7},{9,8},{8,9},{11,10... | collective-permute-start | bytes 98312 | tf_op jit(solution)/shard_map/ppermute | solution.py:164
  53.9 1.9 %copy-start.1 = (bf16[128,128]{1,0:T(8,128)(2,1)}, bf16[128,128]{1,0:T(8,128)(2,1)S(1)}, u32[]{:S(2)}) copy-start(bf16[128,128]{1,0:T(8,128)(2,1)S(1)} %get-tuple-element.26.refs_3_) | copy-start | bytes 98308
  53.9 1.9 %copy-start.2 = (bf16[128,128]{1,0:T(8,128)(2,1)}, bf16[128,128]{1,0:T(8,128)(2,1)S(1)}, u32[]{:S(2)}) copy-start(bf16[128,128]{1,0:T(8,128)(2,1)S(1)} %get-tuple-element.27.refs_2_) | copy-start | bytes 98308
  53.9 8.8 %copy-start.21 = (bf16[64,128]{1,0:T(8,128)(2,1)}, bf16[64,128]{1,0:T(8,128)(2,1)S(1)}, u32[]{:S(2)}) copy-start(bf16[64,128]{1,0:T(8,128)(2,1)S(1)} %collective-permute-done.6.refs_8_) | copy-start | bytes 49156
  54.0 2.0 %collective-permute-start.3 = (bf16[128,128]{1,0:T(8,128)(2,1)S(1)}, bf16[128,128]{1,0:T(8,128)(2,1)S(1)}, u32[]{:S(2)}, u32[]{:S(2)}) collective-permute-start(bf16[128,128]{1,0:T(8,128)(2,1)S(1)} %get-tuple-element.27.refs_2_), channel_id=1, source_target_pairs={{1,0},{0,1},{3,2},{2,3},{5,4},{4,5},{7,6},{6,7},{9,8},{8,9},{11,10... | collective-permute-start | bytes 98312 | tf_op jit(solution)/shard_map/ppermute | solution.py:164
  55.0 7.7 %copy-start.22 = (bf16[64,128]{1,0:T(8,128)(2,1)}, bf16[64,128]{1,0:T(8,128)(2,1)S(1)}, u32[]{:S(2)}) copy-start(bf16[64,128]{1,0:T(8,128)(2,1)S(1)} %collective-permute-done.7.refs_9_) | copy-start | bytes 49156
  55.0 1.2 collective-permute-start.4
  55.8 0.6 copy-start.3
  55.8 0.6 copy-start.10
  55.9 0.6 copy-start.11
  56.5 0.6 copy-start.12
  62.7 18.1 %all-to-all-start.2 = ((bf16[16,160,128]{2,1,0:T(8,128)(2,1)}), bf16[16,160,128]{2,1,0:T(8,128)(2,1)S(1)}, u32[]{:S(2)}, u32[]{:S(2)}) async-start(bf16[16,160,128]{2,1,0:T(8,128)(2,1)} %users.2), calls=%async_computation.2 | async-start | bytes 1310720 | tf_op jit(solution)/shard_map/all_to_all | solution.py:157
  80.8 6.7 %copy-start.13 = (bf16[32,128]{1,0:T(8,128)(2,1)}, bf16[32,128]{1,0:T(8,128)(2,1)S(1)}, u32[]{:S(2)}) copy-start(bf16[32,128]{1,0:T(8,128)(2,1)S(1)} %get-tuple-element.32.refs_1_) | copy-start | bytes 24580
  81.5 11.3 %all-to-all-start.3 = ((bf16[8,64,128]{2,1,0:T(8,128)(2,1)}), bf16[8,64,128]{2,1,0:T(8,128)(2,1)S(1)}, u32[]{:S(2)}, u32[]{:S(2)}) async-start(bf16[8,64,128]{2,1,0:T(8,128)(2,1)} %broadcast_in_dim.26), calls=%async_computation.3 | async-start | bytes 262144 | tf_op jit(solution)/shard_map/all_to_all | solution.py:157
  84.9 5.6 %collective-permute-start.8 = (bf16[32,128]{1,0:T(8,128)(2,1)S(1)}, bf16[32,128]{1,0:T(8,128)(2,1)S(1)}, u32[]{:S(2)}, u32[]{:S(2)}) collective-permute-start(bf16[32,128]{1,0:T(8,128)(2,1)S(1)} %get-tuple-element.33), channel_id=1, source_target_pairs={{2,0},{4,2},{6,4},{8,6},{10,8},{12,10},{14,12},{0,14},{3,1},{5,3},... | collective-permute-start | bytes 24584 | tf_op jit(solution)/shard_map/ppermute | solution.py:164
  87.5 9.8 %collective-permute-start.10 = (bf16[32,128]{1,0:T(8,128)(2,1)S(1)}, bf16[32,128]{1,0:T(8,128)(2,1)S(1)}, u32[]{:S(2)}, u32[]{:S(2)}) collective-permute-start(bf16[32,128]{1,0:T(8,128)(2,1)S(1)} %get-tuple-element.32.refs_1_), channel_id=1, source_target_pairs={{1,0},{0,1},{3,2},{2,3},{5,4},{4,5},{7,6},{6,7},{9,8},{8,9},{11,10... | collective-permute-start | bytes 24584 | tf_op jit(solution)/shard_map/ppermute | solution.py:164
  90.5 2.3 %copy-start.23 = (bf16[32,128]{1,0:T(8,128)(2,1)}, bf16[32,128]{1,0:T(8,128)(2,1)S(1)}, u32[]{:S(2)}) copy-start(bf16[32,128]{1,0:T(8,128)(2,1)S(1)} %collective-permute-done.8.refs_0_) | copy-start | bytes 24580
  90.5 6.8 %collective-permute-start.9 = (bf16[32,128]{1,0:T(8,128)(2,1)S(1)}, bf16[32,128]{1,0:T(8,128)(2,1)S(1)}, u32[]{:S(2)}, u32[]{:S(2)}) collective-permute-start(bf16[32,128]{1,0:T(8,128)(2,1)S(1)} %collective-permute-done.8.refs_0_), channel_id=1, source_target_pairs={{1,0},{0,1},{3,2},{2,3},{5,4},{4,5},{7,6},{6,7},{9,8},{8,9},{11,10... | collective-permute-start | bytes 24584 | tf_op jit(solution)/shard_map/ppermute | solution.py:164
  92.8 4.5 %copy-start.14 = (bf16[32,128]{1,0:T(8,128)(2,1)}, bf16[32,128]{1,0:T(8,128)(2,1)S(1)}, u32[]{:S(2)}) copy-start(bf16[32,128]{1,0:T(8,128)(2,1)S(1)} %get-tuple-element.42.refs_3_) | copy-start | bytes 24580
  92.8 4.5 %copy-start.15 = (bf16[32,128]{1,0:T(8,128)(2,1)}, bf16[32,128]{1,0:T(8,128)(2,1)S(1)}, u32[]{:S(2)}) copy-start(bf16[32,128]{1,0:T(8,128)(2,1)S(1)} %get-tuple-element.43.refs_2_) | copy-start | bytes 24580
  92.8 4.5 %collective-permute-start.11 = (bf16[32,128]{1,0:T(8,128)(2,1)S(1)}, bf16[32,128]{1,0:T(8,128)(2,1)S(1)}, u32[]{:S(2)}, u32[]{:S(2)}) collective-permute-start(bf16[32,128]{1,0:T(8,128)(2,1)S(1)} %get-tuple-element.43.refs_2_), channel_id=1, source_target_pairs={{1,0},{0,1},{3,2},{2,3},{5,4},{4,5},{7,6},{6,7},{9,8},{8,9},{11,10... | collective-permute-start | bytes 24584 | tf_op jit(solution)/shard_map/ppermute | solution.py:164
  96.4 1.2 collective-permute-start.12
  115.1 5.8 %copy-start.6 = (bf16[128,128]{1,0:T(8,128)(2,1)}, bf16[128,128]{1,0:T(8,128)(2,1)S(1)}, u32[]{:S(2)}) copy-start(bf16[128,128]{1,0:T(8,128)(2,1)S(1)} %get-tuple-element.38.refs_1_) | copy-start | bytes 98308
  116.0 18.8 %all-to-all-start.5 = ((bf16[8,256,128]{2,1,0:T(8,128)(2,1)}), bf16[8,256,128]{2,1,0:T(8,128)(2,1)S(1)}, u32[]{:S(2)}, u32[]{:S(2)}) async-start(bf16[8,256,128]{2,1,0:T(8,128)(2,1)} %broadcast_in_dim.27), calls=%async_computation.5 | async-start | bytes 1048576 | tf_op jit(solution)/shard_map/all_to_all | solution.py:157
  119.5 12.6 %collective-permute-start.13 = (bf16[128,128]{1,0:T(8,128)(2,1)S(1)}, bf16[128,128]{1,0:T(8,128)(2,1)S(1)}, u32[]{:S(2)}, u32[]{:S(2)}) collective-permute-start(bf16[128,128]{1,0:T(8,128)(2,1)S(1)} %get-tuple-element.39), channel_id=1, source_target_pairs={{14,0},{0,2},{2,4},{4,6},{6,8},{8,10},{10,12},{12,14},{15,1},{1,3}... | collective-permute-start | bytes 98312 | tf_op jit(solution)/shard_map/ppermute | solution.py:164
  120.8 17.6 %collective-permute-start.15 = (bf16[128,128]{1,0:T(8,128)(2,1)S(1)}, bf16[128,128]{1,0:T(8,128)(2,1)S(1)}, u32[]{:S(2)}, u32[]{:S(2)}) collective-permute-start(bf16[128,128]{1,0:T(8,128)(2,1)S(1)} %get-tuple-element.38.refs_1_), channel_id=1, source_target_pairs={{1,0},{0,1},{3,2},{2,3},{5,4},{4,5},{7,6},{6,7},{9,8},{8,9},{11,10... | collective-permute-start | bytes 98312 | tf_op jit(solution)/shard_map/ppermute | solution.py:164
  132.1 2.7 %copy-start.16 = (bf16[128,128]{1,0:T(8,128)(2,1)}, bf16[128,128]{1,0:T(8,128)(2,1)S(1)}, u32[]{:S(2)}) copy-start(bf16[128,128]{1,0:T(8,128)(2,1)S(1)} %collective-permute-done.13.refs_0_) | copy-start | bytes 98308
  132.1 6.3 %collective-permute-start.14 = (bf16[128,128]{1,0:T(8,128)(2,1)S(1)}, bf16[128,128]{1,0:T(8,128)(2,1)S(1)}, u32[]{:S(2)}, u32[]{:S(2)}) collective-permute-start(bf16[128,128]{1,0:T(8,128)(2,1)S(1)} %collective-permute-done.13.refs_0_), channel_id=1, source_target_pairs={{1,0},{0,1},{3,2},{2,3},{5,4},{4,5},{7,6},{6,7},{9,8},{8,9},{11,10... | collective-permute-start | bytes 98312 | tf_op jit(solution)/shard_map/ppermute | solution.py:164
  134.8 4.7 %copy-start.4 = (bf16[128,128]{1,0:T(8,128)(2,1)}, bf16[128,128]{1,0:T(8,128)(2,1)S(1)}, u32[]{:S(2)}) copy-start(bf16[128,128]{1,0:T(8,128)(2,1)S(1)} %get-tuple-element.34.refs_3_) | copy-start | bytes 98308
  134.8 4.7 %copy-start.5 = (bf16[128,128]{1,0:T(8,128)(2,1)}, bf16[128,128]{1,0:T(8,128)(2,1)S(1)}, u32[]{:S(2)}) copy-start(bf16[128,128]{1,0:T(8,128)(2,1)S(1)} %get-tuple-element.35.refs_2_) | copy-start | bytes 98308
  134.8 4.3 %collective-permute-start.16 = (bf16[128,128]{1,0:T(8,128)(2,1)S(1)}, bf16[128,128]{1,0:T(8,128)(2,1)S(1)}, u32[]{:S(2)}, u32[]{:S(2)}) collective-permute-start(bf16[128,128]{1,0:T(8,128)(2,1)S(1)} %get-tuple-element.35.refs_2_), channel_id=1, source_target_pairs={{1,0},{0,1},{3,2},{2,3},{5,4},{4,5},{7,6},{6,7},{9,8},{8,9},{11,10... | collective-permute-start | bytes 98312 | tf_op jit(solution)/shard_map/ppermute | solution.py:164
  138.3 1.2 collective-permute-start.17
  138.4 1.1 copy-start.17
  138.4 1.1 copy-start.18
  139.2 0.6 copy-start.19
  139.8 0.6 copy-start.20
  (5 other events, 3.0 us)

commit v3 on v2

--- a/solution.py
+++ b/solution.py
@@ -41,7 +41,9 @@
 
 def users_kernel(*refs, tiles, copies):
     own, other = refs[:tiles], refs[tiles : 2 * tiles]
-    own_marks_ref, other_marks_ref, *extra, out_ref, factor_t_ref, mask_ref, sums_ref = refs[2 * tiles :]
+    own_marks_ref, other_marks_ref, *rest, factor_t_ref, mask_ref, sums_ref = refs[2 * tiles :]
+    copies_ref = rest.pop() if copies else None
+    *extra, out_ref = rest
     rank = own[0].shape[1]
     rows = own_marks_ref.shape[1]
     parts = []
@@ -72,13 +74,12 @@
     ridge = RIDGE * (count + 1.0)
     bound = jnp.max(sums_ref[...], axis=1, keepdims=True) + ridge
     answer = relax(right, ridge, bound, rated, factors)
-    if not copies:
-        out_ref[...] = answer
+    out_ref[...] = answer
     for c in range(copies):
-        out_ref[c, :rows, :] = answer
+        copies_ref[c, :rows, :] = answer
         for k, ref in enumerate(extra):
             users = ref.shape[0]
-            out_ref[c, rows + k * users : rows + (k + 1) * users, :] = ref[...]
+            copies_ref[c, rows + k * users : rows + (k + 1) * users, :] = ref[...]
 
 
 def items_kernel(*refs):
@@ -97,11 +98,13 @@
     count = jnp.sum(mask, axis=1, keepdims=True)
     right = dot_f32(jnp.where(rated, marked, 0.0).astype(jnp.bfloat16), factors)
     group = 8
-    for j in range(items // group):
-        row = mask[j * group : j * group + 1].astype(jnp.bfloat16)
-        gram = dot_f32(factor_t * row, factors)
-        total = jnp.sum(jnp.abs(gram), axis=0, keepdims=True)
-        sums_ref[j * group : (j + 1) * group, :] = jnp.broadcast_to(total, (group, rank))
+    kinds = items // group
+    chosen = jnp.concatenate([mask[j * group : j * group + 1] for j in range(kinds)], axis=0).astype(jnp.bfloat16)
+    weighted = (factor_t[None] * chosen[:, None, :]).reshape(kinds * rank, -1)
+    gram = dot_f32(weighted, factors)
+    total = jnp.sum(jnp.abs(gram).reshape(kinds, rank, rank), axis=1)
+    for j in range(kinds):
+        sums_ref[j * group : (j + 1) * group, :] = jnp.broadcast_to(total[j : j + 1], (group, rank))
     ridge = RIDGE * (count + 1.0)
     bound = jnp.max(sums_ref[...], axis=1, keepdims=True) + ridge
     answer = relax(right, ridge, bound, rated, factors)
@@ -119,14 +122,14 @@
     rank = own[0].shape[1]
     width = tiles * 2 * half
     args = [*own, *other, own_marks, other_marks, *extra]
-    shape = (rows, rank)
+    shapes = [(rows, rank)]
     if copies:
-        shape = (copies, rows + sum(e.shape[0] for e in extra), rank)
+        shapes.append((copies, rows + sum(e.shape[0] for e in extra), rank))
     return pl.pallas_call(
         functools.partial(users_kernel, tiles=tiles, copies=copies),
-        out_shape=jax.ShapeDtypeStruct(shape, jnp.bfloat16),
+        out_shape=tuple(jax.ShapeDtypeStruct(shape, jnp.bfloat16) for shape in shapes),
         in_specs=vmem_specs(len(args)),
-        out_specs=pl.BlockSpec(memory_space=VMEM),
+        out_specs=tuple(vmem_specs(len(shapes))),
         scratch_shapes=[
             pltpu.VMEM((rank, width), jnp.bfloat16),
             pltpu.VMEM((rows, width), jnp.float32),
@@ -164,18 +167,21 @@
     return lax.ppermute(value, axis, [((target + steps) % count, target) for target in range(count)])
 
 
+def place_on(axis):
+    return lax.axis_index(axis).astype(jnp.uint32)
+
+
 def shift_digits(shift, z_first):
-    nz, ny, nx = lax.axis_size("z"), lax.axis_size("y"), lax.axis_size("x")
-    z, z_shift = lax.axis_index("z"), shift % nz
-    carry = (z + z_shift) // nz if z_first else jnp.where(z < z_shift, 1, 0)
-    y = lax.axis_index("y") + (shift // nz) % ny + carry
-    x = lax.axis_index("x") + shift // (nz * ny) + y // ny
-    return (x % nx) * ny + y % ny, (z + z_shift) % nz
+    ring, plane = lax.axis_size("z"), lax.axis_size(("x", "y"))
+    z_bits = ring.bit_length() - 1
+    z, z_shift = place_on("z"), shift & (ring - 1)
+    carry = (z + z_shift) >> z_bits if z_first else (z < z_shift).astype(jnp.uint32)
+    return (place_on(("x", "y")) + (shift >> z_bits) + carry) & (plane - 1), (z + z_shift) & (ring - 1)
 
 
 def taken(source, index, start, size):
-    picked = lax.dynamic_slice(source, (index, jnp.int32(start), jnp.int32(0)), (1, size, source.shape[2]))
-    return picked[0]
+    zero = jnp.uint32(0)
+    return lax.dynamic_slice(source, (index, zero + start, zero), (1, size, source.shape[2]))[0]
 
 
 def body(item_start, ratings, rating_bits, plan):
@@ -188,32 +194,49 @@
     partner = lambda value: fetched_from(value, "grp", 1)
 
     near, across = blocks - 1, blocks // 2
-    place = lambda wanted: jnp.sum(jnp.where(plan == wanted, jnp.arange(tiles), 0))
+    offsets = [plan[k].astype(jnp.uint32) for k in range(tiles)]
+    zero = jnp.uint32(0)
+
+    def place(wanted):
+        at = zero
+        for k in range(1, tiles):
+            at = jnp.where(offsets[k] == wanted, jnp.uint32(k), at)
+        return at
+
     first, second = place(near), place(across)
     low, high = jnp.minimum(first, second), jnp.maximum(first, second)
-    third = jnp.where(low > 0, 0, jnp.where(high > 1, 1, 2))
-    fourth = tiles * (tiles - 1) // 2 - first - second - third
+    third = jnp.where(low > 0, zero, jnp.where(high > 1, jnp.uint32(1), jnp.uint32(2)))
+    fourth = jnp.uint32(tiles * (tiles - 1) // 2) - first - second - third
     order = (first, second, third, fourth)
-    shifts = (near, across, plan[third], plan[fourth])
+
+    def offset_at(k):
+        value = offsets[0]
+        for j in range(1, tiles):
+            value = jnp.where(k == j, offsets[j], value)
+        return value
+
+    shifts = (jnp.uint32(near), jnp.uint32(across), offset_at(third), offset_at(fourth))
     forward = [shift_digits(shift, False) for shift in shifts]
-    backward = [shift_digits((blocks - shift) % blocks, False) for shift in shifts]
+    backward = [shift_digits(blocks - shift, False) for shift in shifts]
     marks_at = [shift_digits(blocks - shift, True) for shift in shifts[2:]]
 
     bit_count = 32 // lax.axis_size("grp")
     item_bits = own_half * bit_count + lax.broadcasted_iota(jnp.int32, (1, 1, items), 2) // (items // bit_count)
     rated = (jnp.right_shift(rating_bits[:, :, None], item_bits) & 1) == 1
     marks = jnp.where(rated, ratings, jnp.asarray(UNRATED, ratings.dtype))
-    cut = lambda k, at: lax.dynamic_slice(marks, (k, at * rows, 0), (1, rows, items))[0]
-    own_marks = [cut(k, own_half) for k in order]
-    away_marks = [cut(k, 1 - own_half) for k in order]
+    own_row = place_on("grp") * rows
+    cut = lambda k, at: lax.dynamic_slice(marks, (k, at, zero), (1, rows, items))[0]
+    own_marks = [cut(k, own_row) for k in order]
+    away_marks = [cut(k, rows - own_row) for k in order]
     marks = [jnp.concatenate(pair, axis=0) for pair in zip(own_marks, away_marks)]
     own_marks = jnp.stack(own_marks)
     other_marks = partner(jnp.stack(away_marks))
 
-    def gather(copies, size, digits, z_step, extra=()):
+    def gather(shard, copies, digits, near_shift, extra=()):
+        size = shard.shape[0]
+        neighbour = fetched_from(shard, AXES, near_shift)
         held = swapped_with_all(copies, ("x", "y"))
-        pieces = [taken(held, at, 0, size) for at, _ in digits]
-        pieces[0] = fetched_from(pieces[0], "z", z_step)
+        pieces = [neighbour] + [taken(held, at, 0, size) for at, _ in digits[1:]]
         moving = jnp.concatenate([*pieces[2:], *extra], axis=0)
         ring_held = swapped_with_all(jnp.broadcast_to(moving, (ring, *moving.shape)), "z")
         for k in (2, 3):
@@ -221,18 +244,18 @@
         return held, ring_held, pieces, [partner(piece) for piece in pieces]
 
     copies = jnp.broadcast_to(item_start, (plane, *item_start.shape))
-    _, held, own, other = gather(copies, items, forward, -1, marks[2:])
+    _, held, own, other = gather(item_start, copies, forward, near, marks[2:])
     moved = [taken(held, z_at, 2 * items + k * users, users) for k, (_, z_at) in enumerate(marks_at)]
     near_marks, across_marks = (fetched_from(m, AXES, -shift) for m, shift in zip(marks, (near, across)))
     near_marks, across_marks, *moved = lax.optimization_barrier((near_marks, across_marks, *moved))
-    copies = solve_users(own, other, own_marks, other_marks, plane, moved)
-
-    held, _, own, other = gather(copies, rows, backward, 1)
+    first_users, copies = solve_users(own, other, own_marks, other_marks, plane, moved)
+
+    held, _, own, other = gather(first_users, copies, backward, -near)
     moved = [taken(held, at, rows + k * users, users) for k, (at, _) in enumerate(marks_at)]
     item_factors, copies = solve_items(own, other, [near_marks, across_marks, *moved], plane)
 
-    _, _, own, other = gather(copies, items, forward, -1)
-    user_factors = solve_users(own, other, own_marks, other_marks)
+    _, _, own, other = gather(item_factors, copies, forward, near)
+    (user_factors,) = solve_users(own, other, own_marks, other_marks)
     return (user_factors, item_factors)
 
 

time: 147 us -> 145 us (0.986)
  waiting for transfers between devices: 24 us -> 42.5 us
  between operations: 15.2 us -> 3.7 us
  starting transfers between devices: 67.3 us -> 58.7 us
    ppermute x18, waiting for transfers between devices: 10.8 us -> 25.2 us  [fetched_from(): lax.ppermute(value, axis, [((target + steps) % count, target) for target...]
    ppermute x18, starting transfers between devices: 38 us -> 31.3 us  [fetched_from(): lax.ppermute(value, axis, [((target + steps) % count, target) for target...]
    all_to_all x5, waiting for transfers between devices: 13.2 us -> 17.3 us  [swapped_with_all(): return lax.all_to_all(copies, axes, split_axis=0, concat_axis=0, tiled=True)]
    all_to_all x5, starting transfers between devices: 29.3 us -> 27.4 us  [swapped_with_all(): return lax.all_to_all(copies, axes, split_axis=0, concat_axis=0, tiled=True)]
    unnamed x65 -> x71, local copies, waits for them, and re-layouts: 3.88 us -> 3.76 us
where the time goes in v3:
time: 145 us; the launch traced here: 144 us
  starting transfers between devices  58.7 us (40%)
  waiting for transfers between devices  42.5 us (29%)
  Pallas kernels  14.3 us (10%)
  blocking collectives  13.7 us (9%)
  local copies, waits for them, and re-layouts  9.95 us (7%)
  between operations  3.7 us (3%)
    ppermute x18, starting transfers between devices, fetched_from(): lax.ppermute(value, axis, [((target + steps) % count, target) for target...  31.3 us
    all_to_all x5, starting transfers between devices, swapped_with_all(): return lax.all_to_all(copies, axes, split_axis=0, concat_axis=0, tiled=True)  27.4 us
    ppermute x18, waiting for transfers between devices, fetched_from(): lax.ppermute(value, axis, [((target + steps) % count, target) for target...  25.2 us
    all_to_all x5, waiting for transfers between devices, swapped_with_all(): return lax.all_to_all(copies, axes, split_axis=0, concat_axis=0, tiled=True)  17.3 us
    all_to_all x1, blocking collectives, swapped_with_all(): return lax.all_to_all(copies, axes, split_axis=0, concat_axis=0, tiled=True)  13.7 us
    pallas_call x2, Pallas kernels, solve_users(): pl.pallas_call(functools.partial(users_kernel, tiles=tiles, copies=copies...  10.8 us
    unnamed x71, local copies, waits for them, and re-layouts  3.76 us
    pallas_call x1, Pallas kernels, solve_items(): pl.pallas_call(items_kernel, out_shape=(jax.ShapeDtypeStruct((items, rank...  3.48 us
  transfers between devices with their start and end apart: 23, of which 11 were waited for; matrix products, arithmetic and copies ran while one was open for 2% of the time, Pallas kernels for 0%

profile of v3, /device:TPU:1, one launch (start us, length us, event | category | flops | bytes accessed | tf_op | source)
XLA Modules:
  0.0 143.6 jit_solution(10502794142140150259)
XLA Ops:
  0.6 1.7 %broadcast_in_dim.17 = bf16[16,128,128]{2,1,0:T(8,128)(2,1)} broadcast(bf16[128,128]{1,0:T(8,128)(2,1)} %param.4), dimensions={1,2} | broadcast | bytes 557056 | tf_op jit(solution)/shard_map/broadcast_in_dim | solution.py:246
  2.3 7.6 %all-to-all-start = ((bf16[16,128,128]{2,1,0:T(8,128)(2,1)}), bf16[16,128,128]{2,1,0:T(8,128)(2,1)S(1)}, u32[]{:S(2)}, u32[]{:S(2)}) async-start(bf16[16,128,128]{2,1,0:T(8,128)(2,1)} %broadcast_in_dim.17), calls=%async_computation | async-start | bytes 1048576 | tf_op jit(solution)/shard_map/all_to_all | solution.py:160
  9.9 0.6 copy-done.29
  10.5 0.7 fusion.2
  14.0 0.6 copy-done.30
  14.7 5.5 %all-to-all-done = bf16[16,128,128]{2,1,0:T(8,128)(2,1)S(1)} async-done(((bf16[16,128,128]{2,1,0:T(8,128)(2,1)}), bf16[16,128,128]{2,1,0:T(8,128)(2,1)S(1)}, u32[]{:S(2)}, u32[]{:S(2)}) %all-to-all-start) | async-done | bytes 524320 | tf_op jit(solution)/shard_map/all_to_all | solution.py:160
  20.4 1.0 broadcast_in_dim.19
  21.4 8.3 %all-to-all-start.1 = ((bf16[8,384,128]{2,1,0:T(8,128)(2,1)}), bf16[8,384,128]{2,1,0:T(8,128)(2,1)S(1)}, u32[]{:S(2)}, u32[]{:S(2)}) async-start(bf16[8,384,128]{2,1,0:T(8,128)(2,1)} %broadcast_in_dim.19), calls=%async_computation.1 | async-start | bytes 1572864 | tf_op jit(solution)/shard_map/all_to_all | solution.py:160
  29.7 1.5 %collective-permute-start = (bf16[128,128]{1,0:T(8,128)(2,1)S(1)}, bf16[128,128]{1,0:T(8,128)(2,1)S(1)}, u32[]{:S(2)}, u32[]{:S(2)}) collective-permute-start(bf16[128,128]{1,0:T(8,128)(2,1)S(1)} %copy-done.8), channel_id=1, source_target_pairs={{254,0},{0,2},{2,4},{4,6},{6,8},{8,10},{10,12},{12,14},{14,16},{16... | collective-permute-start | bytes 98312 | tf_op jit(solution)/shard_map/ppermute | solution.py:167
  31.2 5.5 %collective-permute-start.6 = (bf16[64,128]{1,0:T(8,128)(2,1)S(1)}, bf16[64,128]{1,0:T(8,128)(2,1)S(1)}, u32[]{:S(2)}, u32[]{:S(2)}) collective-permute-start(bf16[64,128]{1,0:T(8,128)(2,1)S(1)} %pad_maximum_fusion.3), channel_id=1, source_target_pairs={{2,0},{4,2},{6,4},{8,6},{10,8},{12,10},{14,12},{16,14},{18,16},{20... | collective-permute-start | bytes 49160 | tf_op jit(solution)/shard_map/ppermute | solution.py:167
  36.7 10.3 %collective-permute-done.refs_0_ = bf16[128,128]{1,0:T(8,128)(2,1)S(1)} collective-permute-done((bf16[128,128]{1,0:T(8,128)(2,1)S(1)}, bf16[128,128]{1,0:T(8,128)(2,1)S(1)}, u32[]{:S(2)}, u32[]{:S(2)}) %collective-permute-start) | collective-permute-done | bytes 32800 | tf_op jit(solution)/shard_map/ppermute | solution.py:167
  47.0 2.1 %collective-permute-start.1 = (bf16[128,128]{1,0:T(8,128)(2,1)S(1)}, bf16[128,128]{1,0:T(8,128)(2,1)S(1)}, u32[]{:S(2)}, u32[]{:S(2)}) collective-permute-start(bf16[128,128]{1,0:T(8,128)(2,1)S(1)} %collective-permute-done.refs_0_), channel_id=1, source_target_pairs={{1,0},{0,1},{3,2},{2,3},{5,4},{4,5},{7,6},{6,7},{9,8},{8,9},{11,10... | collective-permute-start | bytes 98312 | tf_op jit(solution)/shard_map/ppermute | solution.py:167
  49.1 0.6 collective-permute-start.2
  49.7 0.6 collective-permute-start.5
  50.3 0.6 pad_maximum_fusion.1.refs_8_
  50.9 0.4 all-to-all-done.1
  51.4 2.9 %collective-permute-start.3 = (bf16[128,128]{1,0:T(8,128)(2,1)S(1)}, bf16[128,128]{1,0:T(8,128)(2,1)S(1)}, u32[]{:S(2)}, u32[]{:S(2)}) collective-permute-start(bf16[128,128]{1,0:T(8,128)(2,1)S(1)} %get-tuple-element.29.refs_2_), channel_id=1, source_target_pairs={{1,0},{0,1},{3,2},{2,3},{5,4},{4,5},{7,6},{6,7},{9,8},{8,9},{11,10... | collective-permute-start | bytes 98312 | tf_op jit(solution)/shard_map/ppermute | solution.py:167
  54.4 0.6 dynamic-slice_bitcast_fusion.10
  55.1 0.4 collective-permute-done.4.refs_7_
  55.5 0.1 copy-done.13
  55.7 0.6 copy-done.19
  56.3 5.6 %users.2 = (bf16[32,128]{1,0:T(8,128)(2,1)}, bf16[16,160,128]{2,1,0:T(8,128)(2,1)}) custom-call(bf16[128,128]{1,0:T(8,128)(2,1)} %copy-done.12, bf16[128,128]{1,0:T(8,128)(2,1)} %copy-done, bf16[128,128]{1,0:T(8,128)(2,1)} %copy-done.3, bf16[128,128]{1,0:T(8,128)(2,1)} %copy-done.2, bf16[128,128]{1,0:T(8,128)(2,1)} %copy-done.13, ...), custom_call_target="tpu_custom_call" | custom-call | tf_op jit(solution)/shard_map/users/pallas_call | solution.py:128
  61.9 3.6 %all-to-all-start.2 = ((bf16[16,160,128]{2,1,0:T(8,128)(2,1)}), bf16[16,160,128]{2,1,0:T(8,128)(2,1)S(1)}, u32[]{:S(2)}, u32[]{:S(2)}) async-start(bf16[16,160,128]{2,1,0:T(8,128)(2,1)} %get-tuple-element.13), calls=%async_computation.2 | async-start | bytes 1310720 | tf_op jit(solution)/shard_map/all_to_all | solution.py:160
  65.5 11.4 %all-to-all-done.2 = bf16[16,160,128]{2,1,0:T(8,128)(2,1)S(1)} async-done(((bf16[16,160,128]{2,1,0:T(8,128)(2,1)}), bf16[16,160,128]{2,1,0:T(8,128)(2,1)S(1)}, u32[]{:S(2)}, u32[]{:S(2)}) %all-to-all-start.2) | async-done | bytes 655392 | tf_op jit(solution)/shard_map/all_to_all | solution.py:160
  76.9 0.7 broadcast_in_dim.20
  77.6 4.2 %all-to-all-start.3 = ((bf16[8,64,128]{2,1,0:T(8,128)(2,1)}), bf16[8,64,128]{2,1,0:T(8,128)(2,1)S(1)}, u32[]{:S(2)}, u32[]{:S(2)}) async-start(bf16[8,64,128]{2,1,0:T(8,128)(2,1)} %broadcast_in_dim.20), calls=%async_computation.3 | async-start | bytes 262144 | tf_op jit(solution)/shard_map/all_to_all | solution.py:160
  81.7 4.7 %collective-permute-start.8 = (bf16[32,128]{1,0:T(8,128)(2,1)S(1)}, bf16[32,128]{1,0:T(8,128)(2,1)S(1)}, u32[]{:S(2)}, u32[]{:S(2)}) collective-permute-start(bf16[32,128]{1,0:T(8,128)(2,1)S(1)} %copy-done.32), channel_id=1, source_target_pairs={{2,0},{4,2},{6,4},{8,6},{10,8},{12,10},{14,12},{16,14},{18,16},{20... | collective-permute-start | bytes 24584 | tf_op jit(solution)/shard_map/ppermute | solution.py:167
  86.4 0.8 collective-permute-done.8.refs_0_
  87.2 2.5 %collective-permute-start.9 = (bf16[32,128]{1,0:T(8,128)(2,1)S(1)}, bf16[32,128]{1,0:T(8,128)(2,1)S(1)}, u32[]{:S(2)}, u32[]{:S(2)}) collective-permute-start(bf16[32,128]{1,0:T(8,128)(2,1)S(1)} %collective-permute-done.8.refs_0_), channel_id=1, source_target_pairs={{1,0},{0,1},{3,2},{2,3},{5,4},{4,5},{7,6},{6,7},{9,8},{8,9},{11,10... | collective-permute-start | bytes 24584 | tf_op jit(solution)/shard_map/ppermute | solution.py:167
  89.8 4.0 %collective-permute-start.11 = (bf16[32,128]{1,0:T(8,128)(2,1)S(1)}, bf16[32,128]{1,0:T(8,128)(2,1)S(1)}, u32[]{:S(2)}, u32[]{:S(2)}) collective-permute-start(bf16[32,128]{1,0:T(8,128)(2,1)S(1)} %get-tuple-element.41.refs_2_), channel_id=1, source_target_pairs={{1,0},{0,1},{3,2},{2,3},{5,4},{4,5},{7,6},{6,7},{9,8},{8,9},{11,10... | collective-permute-start | bytes 24584 | tf_op jit(solution)/shard_map/ppermute | solution.py:167
  93.8 0.3 collective-permute-start.12
  94.0 0.6 dynamic-slice_bitcast_fusion.8
  94.7 0.2 collective-permute-done.12.refs_7_
  94.9 0.3 copy-done.25
  95.3 0.2 copy-done.28
  95.5 3.5 %items.1 = (bf16[128,128]{1,0:T(8,128)(2,1)}, bf16[16,128,128]{2,1,0:T(8,128)(2,1)}) custom-call(bf16[32,128]{1,0:T(8,128)(2,1)} %copy-done.24, bf16[32,128]{1,0:T(8,128)(2,1)} %copy-done.9, bf16[32,128]{1,0:T(8,128)(2,1)} %copy-done.11, bf16[32,128]{1,0:T(8,128)(2,1)} %copy-done.10, bf16[32,128]{1,0:T(8,128)(2,1)} %copy-done.25, ...), custom_call_target="tpu_custom_call" | custom-call | tf_op jit(solution)/shard_map/items/pallas_call | solution.py:146
  99.0 13.7 %all_to_all.30 = bf16[16,128,128]{2,1,0:T(8,128)(2,1)S(1)} all-to-all(bf16[16,128,128]{2,1,0:T(8,128)(2,1)} %get-tuple-element.17), channel_id=1, replica_groups=mesh['x'=4,'y'=4,'z'=8,'grp'=2] {'x','y'}, dimensions={0} | all-to-all | bytes 1048576 | tf_op jit(solution)/shard_map/all_to_all | solution.py:160
  112.7 0.9 broadcast_in_dim.21
  113.6 3.7 %all-to-all-start.5 = ((bf16[8,256,128]{2,1,0:T(8,128)(2,1)}), bf16[8,256,128]{2,1,0:T(8,128)(2,1)S(1)}, u32[]{:S(2)}, u32[]{:S(2)}) async-start(bf16[8,256,128]{2,1,0:T(8,128)(2,1)} %broadcast_in_dim.21), calls=%async_computation.5 | async-start | bytes 1048576 | tf_op jit(solution)/shard_map/all_to_all | solution.py:160
  117.4 1.5 %collective-permute-start.13 = (bf16[128,128]{1,0:T(8,128)(2,1)S(1)}, bf16[128,128]{1,0:T(8,128)(2,1)S(1)}, u32[]{:S(2)}, u32[]{:S(2)}) collective-permute-start(bf16[128,128]{1,0:T(8,128)(2,1)S(1)} %copy-done.31), channel_id=1, source_target_pairs={{254,0},{0,2},{2,4},{4,6},{6,8},{8,10},{10,12},{12,14},{14,16},{16... | collective-permute-start | bytes 98312 | tf_op jit(solution)/shard_map/ppermute | solution.py:167
  118.8 12.4 %collective-permute-done.13.refs_0_ = bf16[128,128]{1,0:T(8,128)(2,1)S(1)} collective-permute-done((bf16[128,128]{1,0:T(8,128)(2,1)S(1)}, bf16[128,128]{1,0:T(8,128)(2,1)S(1)}, u32[]{:S(2)}, u32[]{:S(2)}) %collective-permute-start.13) | collective-permute-done | bytes 32800 | tf_op jit(solution)/shard_map/ppermute | solution.py:167
  131.2 2.4 %collective-permute-start.14 = (bf16[128,128]{1,0:T(8,128)(2,1)S(1)}, bf16[128,128]{1,0:T(8,128)(2,1)S(1)}, u32[]{:S(2)}, u32[]{:S(2)}) collective-permute-start(bf16[128,128]{1,0:T(8,128)(2,1)S(1)} %collective-permute-done.13.refs_0_), channel_id=1, source_target_pairs={{1,0},{0,1},{3,2},{2,3},{5,4},{4,5},{7,6},{6,7},{9,8},{8,9},{11,10... | collective-permute-start | bytes 98312 | tf_op jit(solution)/shard_map/ppermute | solution.py:167
  133.7 2.6 %collective-permute-start.16 = (bf16[128,128]{1,0:T(8,128)(2,1)S(1)}, bf16[128,128]{1,0:T(8,128)(2,1)S(1)}, u32[]{:S(2)}, u32[]{:S(2)}) collective-permute-start(bf16[128,128]{1,0:T(8,128)(2,1)S(1)} %get-tuple-element.36.refs_2_), channel_id=1, source_target_pairs={{1,0},{0,1},{3,2},{2,3},{5,4},{4,5},{7,6},{6,7},{9,8},{8,9},{11,10... | collective-permute-start | bytes 98312 | tf_op jit(solution)/shard_map/ppermute | solution.py:167
  136.4 0.7 collective-permute-done.16.refs_6_
  137.1 0.3 collective-permute-done.17.refs_7_
  137.5 0.2 copy-done.20
  137.7 0.6 copy-done.21
  138.3 5.3 %users.3 = bf16[32,128]{1,0:T(8,128)(2,1)} custom-call(bf16[128,128]{1,0:T(8,128)(2,1)} %copy-done.15, bf16[128,128]{1,0:T(8,128)(2,1)} %copy-done.1, bf16[128,128]{1,0:T(8,128)(2,1)} %copy-done.5, bf16[128,128]{1,0:T(8,128)(2,1)} %copy-done.4, bf16[128,128]{1,0:T(8,128)(2,1)} %copy-done.16, bf16[128,128]{1,0:T(8,128)(2,1)} %copy-done.18, ...), custom_call_target="tpu_custom_call" | custom-call | tf_op jit(solution)/shard_map/users/pallas_call | solution.py:128
  (96 shorter events, 1.0 us)
Async XLA Ops:
  2.3 17.9 %all-to-all-start = ((bf16[16,128,128]{2,1,0:T(8,128)(2,1)}), bf16[16,128,128]{2,1,0:T(8,128)(2,1)S(1)}, u32[]{:S(2)}, u32[]{:S(2)}) async-start(bf16[16,128,128]{2,1,0:T(8,128)(2,1)} %broadcast_in_dim.17), calls=%async_computation | async-start | bytes 1048576 | tf_op jit(solution)/shard_map/all_to_all | solution.py:160
  9.9 0.7 copy-start.29
  13.2 0.8 copy-start.7
  13.9 0.7 copy-start.30
  21.4 8.3 %copy-start.8 = (bf16[128,128]{1,0:T(8,128)(2,1)S(1)}, bf16[128,128]{1,0:T(8,128)(2,1)}, u32[]{:S(2)}) copy-start(bf16[128,128]{1,0:T(8,128)(2,1)} %param.4) | copy-start | bytes 98308
  21.4 29.9 %all-to-all-start.1 = ((bf16[8,384,128]{2,1,0:T(8,128)(2,1)}), bf16[8,384,128]{2,1,0:T(8,128)(2,1)S(1)}, u32[]{:S(2)}, u32[]{:S(2)}) async-start(bf16[8,384,128]{2,1,0:T(8,128)(2,1)} %broadcast_in_dim.19), calls=%async_computation.1 | async-start | bytes 1572864 | tf_op jit(solution)/shard_map/all_to_all | solution.py:160
  29.7 17.2 %collective-permute-start = (bf16[128,128]{1,0:T(8,128)(2,1)S(1)}, bf16[128,128]{1,0:T(8,128)(2,1)S(1)}, u32[]{:S(2)}, u32[]{:S(2)}) collective-permute-start(bf16[128,128]{1,0:T(8,128)(2,1)S(1)} %copy-done.8), channel_id=1, source_target_pairs={{254,0},{0,2},{2,4},{4,6},{6,8},{8,10},{10,12},{12,14},{14,16},{16... | collective-permute-start | bytes 98312 | tf_op jit(solution)/shard_map/ppermute | solution.py:167
  31.2 20.2 %collective-permute-start.6 = (bf16[64,128]{1,0:T(8,128)(2,1)S(1)}, bf16[64,128]{1,0:T(8,128)(2,1)S(1)}, u32[]{:S(2)}, u32[]{:S(2)}) collective-permute-start(bf16[64,128]{1,0:T(8,128)(2,1)S(1)} %pad_maximum_fusion.3), channel_id=1, source_target_pairs={{2,0},{4,2},{6,4},{8,6},{10,8},{12,10},{14,12},{16,14},{18,16},{20... | collective-permute-start | bytes 49160 | tf_op jit(solution)/shard_map/ppermute | solution.py:167
  36.7 17.6 %collective-permute-start.7 = (bf16[64,128]{1,0:T(8,128)(2,1)S(1)}, bf16[64,128]{1,0:T(8,128)(2,1)S(1)}, u32[]{:S(2)}, u32[]{:S(2)}) collective-permute-start(bf16[64,128]{1,0:T(8,128)(2,1)S(1)} %pad_maximum_fusion.4), channel_id=1, source_target_pairs={{128,0},{130,2},{132,4},{134,6},{136,8},{138,10},{140,12},{142,14}... | collective-permute-start | bytes 49160 | tf_op jit(solution)/shard_map/ppermute | solution.py:167
  47.0 2.1 %copy-start.12 = (bf16[128,128]{1,0:T(8,128)(2,1)}, bf16[128,128]{1,0:T(8,128)(2,1)S(1)}, u32[]{:S(2)}) copy-start(bf16[128,128]{1,0:T(8,128)(2,1)S(1)} %collective-permute-done.refs_0_) | copy-start | bytes 98308
  47.0 8.0 %collective-permute-start.1 = (bf16[128,128]{1,0:T(8,128)(2,1)S(1)}, bf16[128,128]{1,0:T(8,128)(2,1)S(1)}, u32[]{:S(2)}, u32[]{:S(2)}) collective-permute-start(bf16[128,128]{1,0:T(8,128)(2,1)S(1)} %collective-permute-done.refs_0_), channel_id=1, source_target_pairs={{1,0},{0,1},{3,2},{2,3},{5,4},{4,5},{7,6},{6,7},{9,8},{8,9},{11,10... | collective-permute-start | bytes 98312 | tf_op jit(solution)/shard_map/ppermute | solution.py:167
  49.1 0.6 copy-start
  49.1 5.9 %collective-permute-start.2 = (bf16[128,128]{1,0:T(8,128)(2,1)S(1)}, bf16[128,128]{1,0:T(8,128)(2,1)S(1)}, u32[]{:S(2)}, u32[]{:S(2)}) collective-permute-start(bf16[128,128]{1,0:T(8,128)(2,1)S(1)} %dynamic-slice_bitcast_fusion.7.refs_1_), channel_id=1, source_target_pairs={{1,0},{0,1},{3,2},{2,3},{5,4},{4,5},{7,6},{6,7},{9,8},{8,9},{11,10... | collective-permute-start | bytes 98312 | tf_op jit(solution)/shard_map/ppermute | solution.py:167
  49.7 5.3 %collective-permute-start.5 = (bf16[4,32,128]{2,1,0:T(8,128)(2,1)S(1)}, bf16[4,32,128]{2,1,0:T(8,128)(2,1)S(1)}, u32[]{:S(2)}, u32[]{:S(2)}) collective-permute-start(bf16[4,32,128]{2,1,0:T(8,128)(2,1)S(1)} %pad_maximum_fusion.2), channel_id=1, source_target_pairs={{1,0},{0,1},{3,2},{2,3},{5,4},{4,5},{7,6},{6,7},{9,8},{8,9},{11,10... | collective-permute-start | bytes 98312 | tf_op jit(solution)/shard_map/ppermute | solution.py:167
  51.3 3.6 %copy-start.2 = (bf16[128,128]{1,0:T(8,128)(2,1)}, bf16[128,128]{1,0:T(8,128)(2,1)S(1)}, u32[]{:S(2)}) copy-start(bf16[128,128]{1,0:T(8,128)(2,1)S(1)} %get-tuple-element.28.refs_3_) | copy-start | bytes 98308
  51.3 3.6 %copy-start.3 = (bf16[128,128]{1,0:T(8,128)(2,1)}, bf16[128,128]{1,0:T(8,128)(2,1)S(1)}, u32[]{:S(2)}) copy-start(bf16[128,128]{1,0:T(8,128)(2,1)S(1)} %get-tuple-element.29.refs_2_) | copy-start | bytes 98308
  51.4 10.5 %copy-start.22 = (bf16[64,128]{1,0:T(8,128)(2,1)}, bf16[64,128]{1,0:T(8,128)(2,1)S(1)}, u32[]{:S(2)}) copy-start(bf16[64,128]{1,0:T(8,128)(2,1)S(1)} %collective-permute-done.6.refs_8_) | copy-start | bytes 49156
  51.4 3.7 %collective-permute-start.3 = (bf16[128,128]{1,0:T(8,128)(2,1)S(1)}, bf16[128,128]{1,0:T(8,128)(2,1)S(1)}, u32[]{:S(2)}, u32[]{:S(2)}) collective-permute-start(bf16[128,128]{1,0:T(8,128)(2,1)S(1)} %get-tuple-element.29.refs_2_), channel_id=1, source_target_pairs={{1,0},{0,1},{3,2},{2,3},{5,4},{4,5},{7,6},{6,7},{9,8},{8,9},{11,10... | collective-permute-start | bytes 98312 | tf_op jit(solution)/shard_map/ppermute | solution.py:167
  54.3 7.6 %copy-start.23 = (bf16[64,128]{1,0:T(8,128)(2,1)}, bf16[64,128]{1,0:T(8,128)(2,1)S(1)}, u32[]{:S(2)}) copy-start(bf16[64,128]{1,0:T(8,128)(2,1)S(1)} %collective-permute-done.7.refs_9_) | copy-start | bytes 49156
  54.3 1.2 collective-permute-start.4
  55.1 0.6 copy-start.17
  61.9 15.0 %all-to-all-start.2 = ((bf16[16,160,128]{2,1,0:T(8,128)(2,1)}), bf16[16,160,128]{2,1,0:T(8,128)(2,1)S(1)}, u32[]{:S(2)}, u32[]{:S(2)}) async-start(bf16[16,160,128]{2,1,0:T(8,128)(2,1)} %get-tuple-element.13), calls=%async_computation.2 | async-start | bytes 1310720 | tf_op jit(solution)/shard_map/all_to_all | solution.py:160
  76.9 12.8 %copy-start.9 = (bf16[32,128]{1,0:T(8,128)(2,1)}, bf16[32,128]{1,0:T(8,128)(2,1)S(1)}, u32[]{:S(2)}) copy-start(bf16[32,128]{1,0:T(8,128)(2,1)S(1)} %get-tuple-element.34.refs_1_) | copy-start | bytes 24580
  77.6 4.2 %copy-start.32 = (bf16[32,128]{1,0:T(8,128)(2,1)S(1)}, bf16[32,128]{1,0:T(8,128)(2,1)}, u32[]{:S(2)}) copy-start(bf16[32,128]{1,0:T(8,128)(2,1)} %get-tuple-element.12) | copy-start | bytes 24580
  77.6 12.1 %all-to-all-start.3 = ((bf16[8,64,128]{2,1,0:T(8,128)(2,1)}), bf16[8,64,128]{2,1,0:T(8,128)(2,1)S(1)}, u32[]{:S(2)}, u32[]{:S(2)}) async-start(bf16[8,64,128]{2,1,0:T(8,128)(2,1)} %broadcast_in_dim.20), calls=%async_computation.3 | async-start | bytes 262144 | tf_op jit(solution)/shard_map/all_to_all | solution.py:160
  81.7 5.5 %collective-permute-start.8 = (bf16[32,128]{1,0:T(8,128)(2,1)S(1)}, bf16[32,128]{1,0:T(8,128)(2,1)S(1)}, u32[]{:S(2)}, u32[]{:S(2)}) collective-permute-start(bf16[32,128]{1,0:T(8,128)(2,1)S(1)} %copy-done.32), channel_id=1, source_target_pairs={{2,0},{4,2},{6,4},{8,6},{10,8},{12,10},{14,12},{16,14},{18,16},{20... | collective-permute-start | bytes 24584 | tf_op jit(solution)/shard_map/ppermute | solution.py:167
  87.2 2.5 %copy-start.24 = (bf16[32,128]{1,0:T(8,128)(2,1)}, bf16[32,128]{1,0:T(8,128)(2,1)S(1)}, u32[]{:S(2)}) copy-start(bf16[32,128]{1,0:T(8,128)(2,1)S(1)} %collective-permute-done.8.refs_0_) | copy-start | bytes 24580
  87.2 7.5 %collective-permute-start.9 = (bf16[32,128]{1,0:T(8,128)(2,1)S(1)}, bf16[32,128]{1,0:T(8,128)(2,1)S(1)}, u32[]{:S(2)}, u32[]{:S(2)}) collective-permute-start(bf16[32,128]{1,0:T(8,128)(2,1)S(1)} %collective-permute-done.8.refs_0_), channel_id=1, source_target_pairs={{1,0},{0,1},{3,2},{2,3},{5,4},{4,5},{7,6},{6,7},{9,8},{8,9},{11,10... | collective-permute-start | bytes 24584 | tf_op jit(solution)/shard_map/ppermute | solution.py:167
  89.7 5.0 %collective-permute-start.10 = (bf16[32,128]{1,0:T(8,128)(2,1)S(1)}, bf16[32,128]{1,0:T(8,128)(2,1)S(1)}, u32[]{:S(2)}, u32[]{:S(2)}) collective-permute-start(bf16[32,128]{1,0:T(8,128)(2,1)S(1)} %get-tuple-element.34.refs_1_), channel_id=1, source_target_pairs={{1,0},{0,1},{3,2},{2,3},{5,4},{4,5},{7,6},{6,7},{9,8},{8,9},{11,10... | collective-permute-start | bytes 24584 | tf_op jit(solution)/shard_map/ppermute | solution.py:167
  89.7 4.9 %copy-start.10 = (bf16[32,128]{1,0:T(8,128)(2,1)}, bf16[32,128]{1,0:T(8,128)(2,1)S(1)}, u32[]{:S(2)}) copy-start(bf16[32,128]{1,0:T(8,128)(2,1)S(1)} %get-tuple-element.40.refs_3_) | copy-start | bytes 24580
  89.7 4.9 %copy-start.11 = (bf16[32,128]{1,0:T(8,128)(2,1)}, bf16[32,128]{1,0:T(8,128)(2,1)S(1)}, u32[]{:S(2)}) copy-start(bf16[32,128]{1,0:T(8,128)(2,1)S(1)} %get-tuple-element.41.refs_2_) | copy-start | bytes 24580
  89.8 4.9 %collective-permute-start.11 = (bf16[32,128]{1,0:T(8,128)(2,1)S(1)}, bf16[32,128]{1,0:T(8,128)(2,1)S(1)}, u32[]{:S(2)}, u32[]{:S(2)}) collective-permute-start(bf16[32,128]{1,0:T(8,128)(2,1)S(1)} %get-tuple-element.41.refs_2_), channel_id=1, source_target_pairs={{1,0},{0,1},{3,2},{2,3},{5,4},{4,5},{7,6},{6,7},{9,8},{8,9},{11,10... | collective-permute-start | bytes 24584 | tf_op jit(solution)/shard_map/ppermute | solution.py:167
  93.8 1.2 collective-permute-start.12
  94.9 0.6 copy-start.28
  112.7 20.9 %copy-start.1 = (bf16[128,128]{1,0:T(8,128)(2,1)}, bf16[128,128]{1,0:T(8,128)(2,1)S(1)}, u32[]{:S(2)}) copy-start(bf16[128,128]{1,0:T(8,128)(2,1)S(1)} %get-tuple-element.39.refs_1_) | copy-start | bytes 98308
  113.6 3.7 %copy-start.31 = (bf16[128,128]{1,0:T(8,128)(2,1)S(1)}, bf16[128,128]{1,0:T(8,128)(2,1)}, u32[]{:S(2)}) copy-start(bf16[128,128]{1,0:T(8,128)(2,1)} %get-tuple-element.9) | copy-start | bytes 98308
  113.6 20.1 %all-to-all-start.5 = ((bf16[8,256,128]{2,1,0:T(8,128)(2,1)}), bf16[8,256,128]{2,1,0:T(8,128)(2,1)S(1)}, u32[]{:S(2)}, u32[]{:S(2)}) async-start(bf16[8,256,128]{2,1,0:T(8,128)(2,1)} %broadcast_in_dim.21), calls=%async_computation.5 | async-start | bytes 1048576 | tf_op jit(solution)/shard_map/all_to_all | solution.py:160
  117.4 13.9 %collective-permute-start.13 = (bf16[128,128]{1,0:T(8,128)(2,1)S(1)}, bf16[128,128]{1,0:T(8,128)(2,1)S(1)}, u32[]{:S(2)}, u32[]{:S(2)}) collective-permute-start(bf16[128,128]{1,0:T(8,128)(2,1)S(1)} %copy-done.31), channel_id=1, source_target_pairs={{254,0},{0,2},{2,4},{4,6},{6,8},{8,10},{10,12},{12,14},{14,16},{16... | collective-permute-start | bytes 98312 | tf_op jit(solution)/shard_map/ppermute | solution.py:167
  131.2 2.5 %copy-start.15 = (bf16[128,128]{1,0:T(8,128)(2,1)}, bf16[128,128]{1,0:T(8,128)(2,1)S(1)}, u32[]{:S(2)}) copy-start(bf16[128,128]{1,0:T(8,128)(2,1)S(1)} %collective-permute-done.13.refs_0_) | copy-start | bytes 98308
  131.2 5.2 %collective-permute-start.14 = (bf16[128,128]{1,0:T(8,128)(2,1)S(1)}, bf16[128,128]{1,0:T(8,128)(2,1)S(1)}, u32[]{:S(2)}, u32[]{:S(2)}) collective-permute-start(bf16[128,128]{1,0:T(8,128)(2,1)S(1)} %collective-permute-done.13.refs_0_), channel_id=1, source_target_pairs={{1,0},{0,1},{3,2},{2,3},{5,4},{4,5},{7,6},{6,7},{9,8},{8,9},{11,10... | collective-permute-start | bytes 98312 | tf_op jit(solution)/shard_map/ppermute | solution.py:167
  133.6 2.8 %collective-permute-start.15 = (bf16[128,128]{1,0:T(8,128)(2,1)S(1)}, bf16[128,128]{1,0:T(8,128)(2,1)S(1)}, u32[]{:S(2)}, u32[]{:S(2)}) collective-permute-start(bf16[128,128]{1,0:T(8,128)(2,1)S(1)} %get-tuple-element.39.refs_1_), channel_id=1, source_target_pairs={{1,0},{0,1},{3,2},{2,3},{5,4},{4,5},{7,6},{6,7},{9,8},{8,9},{11,10... | collective-permute-start | bytes 98312 | tf_op jit(solution)/shard_map/ppermute | solution.py:167
  133.7 3.8 %copy-start.4 = (bf16[128,128]{1,0:T(8,128)(2,1)}, bf16[128,128]{1,0:T(8,128)(2,1)S(1)}, u32[]{:S(2)}) copy-start(bf16[128,128]{1,0:T(8,128)(2,1)S(1)} %get-tuple-element.35.refs_3_) | copy-start | bytes 98308
  133.7 3.8 %copy-start.5 = (bf16[128,128]{1,0:T(8,128)(2,1)}, bf16[128,128]{1,0:T(8,128)(2,1)S(1)}, u32[]{:S(2)}) copy-start(bf16[128,128]{1,0:T(8,128)(2,1)S(1)} %get-tuple-element.36.refs_2_) | copy-start | bytes 98308
  133.7 3.4 %collective-permute-start.16 = (bf16[128,128]{1,0:T(8,128)(2,1)S(1)}, bf16[128,128]{1,0:T(8,128)(2,1)S(1)}, u32[]{:S(2)}, u32[]{:S(2)}) collective-permute-start(bf16[128,128]{1,0:T(8,128)(2,1)S(1)} %get-tuple-element.36.refs_2_), channel_id=1, source_target_pairs={{1,0},{0,1},{3,2},{2,3},{5,4},{4,5},{7,6},{6,7},{9,8},{8,9},{11,10... | collective-permute-start | bytes 98312 | tf_op jit(solution)/shard_map/ppermute | solution.py:167
  136.3 1.2 collective-permute-start.17
  136.4 1.1 copy-start.16
  136.4 1.1 copy-start.18
  137.1 0.6 copy-start.20
  (8 other events, 4.8 us)

commit v4 on v3

--- a/solution.py
+++ b/solution.py
@@ -98,13 +98,11 @@
     count = jnp.sum(mask, axis=1, keepdims=True)
     right = dot_f32(jnp.where(rated, marked, 0.0).astype(jnp.bfloat16), factors)
     group = 8
-    kinds = items // group
-    chosen = jnp.concatenate([mask[j * group : j * group + 1] for j in range(kinds)], axis=0).astype(jnp.bfloat16)
-    weighted = (factor_t[None] * chosen[:, None, :]).reshape(kinds * rank, -1)
-    gram = dot_f32(weighted, factors)
-    total = jnp.sum(jnp.abs(gram).reshape(kinds, rank, rank), axis=1)
-    for j in range(kinds):
-        sums_ref[j * group : (j + 1) * group, :] = jnp.broadcast_to(total[j : j + 1], (group, rank))
+    for j in range(items // group):
+        row = mask[j * group : j * group + 1].astype(jnp.bfloat16)
+        gram = dot_f32(factor_t * row, factors)
+        total = jnp.sum(jnp.abs(gram), axis=0, keepdims=True)
+        sums_ref[j * group : (j + 1) * group, :] = jnp.broadcast_to(total, (group, rank))
     ridge = RIDGE * (count + 1.0)
     bound = jnp.max(sums_ref[...], axis=1, keepdims=True) + ridge
     answer = relax(right, ridge, bound, rated, factors)
@@ -232,29 +230,29 @@
     own_marks = jnp.stack(own_marks)
     other_marks = partner(jnp.stack(away_marks))
 
-    def gather(shard, copies, digits, near_shift, extra=()):
+    def gather(shard, copies, digits, near_shift, extra=(), direct=()):
         size = shard.shape[0]
         neighbour = fetched_from(shard, AXES, near_shift)
         held = swapped_with_all(copies, ("x", "y"))
         pieces = [neighbour] + [taken(held, at, 0, size) for at, _ in digits[1:]]
         moving = jnp.concatenate([*pieces[2:], *extra], axis=0)
+        moving, pieces[0], *direct = lax.optimization_barrier((moving, neighbour, *direct))
         ring_held = swapped_with_all(jnp.broadcast_to(moving, (ring, *moving.shape)), "z")
         for k in (2, 3):
             pieces[k] = taken(ring_held, digits[k][1], (k - 2) * size, size)
-        return held, ring_held, pieces, [partner(piece) for piece in pieces]
+        return held, ring_held, pieces, [partner(piece) for piece in pieces], direct
 
     copies = jnp.broadcast_to(item_start, (plane, *item_start.shape))
-    _, held, own, other = gather(item_start, copies, forward, near, marks[2:])
+    sent = [fetched_from(m, AXES, -shift) for m, shift in zip(marks, (near, across))]
+    _, held, own, other, direct_marks = gather(item_start, copies, forward, near, marks[2:], sent)
     moved = [taken(held, z_at, 2 * items + k * users, users) for k, (_, z_at) in enumerate(marks_at)]
-    near_marks, across_marks = (fetched_from(m, AXES, -shift) for m, shift in zip(marks, (near, across)))
-    near_marks, across_marks, *moved = lax.optimization_barrier((near_marks, across_marks, *moved))
     first_users, copies = solve_users(own, other, own_marks, other_marks, plane, moved)
 
-    held, _, own, other = gather(first_users, copies, backward, -near)
+    held, _, own, other, _ = gather(first_users, copies, backward, -near)
     moved = [taken(held, at, rows + k * users, users) for k, (at, _) in enumerate(marks_at)]
-    item_factors, copies = solve_items(own, other, [near_marks, across_marks, *moved], plane)
-
-    _, _, own, other = gather(item_factors, copies, forward, near)
+    item_factors, copies = solve_items(own, other, [*direct_marks, *moved], plane)
+
+    _, _, own, other, _ = gather(item_factors, copies, forward, near)
     (user_factors,) = solve_users(own, other, own_marks, other_marks)
     return (user_factors, item_factors)
 

time: 145 us -> 146 us (level)
  waiting for transfers between devices: 42.5 us -> 58.2 us
  blocking collectives: 13.7 us -> 0 us
    all_to_all x5 -> x6, waiting for transfers between devices: 17.3 us -> 53.7 us  [swapped_with_all(): return lax.all_to_all(copies, axes, split_axis=0, concat_axis=0, tiled=True)]
    ppermute x18, waiting for transfers between devices: 25.2 us -> 4.45 us  [fetched_from(): lax.ppermute(value, axis, [((target + steps) % count, target) for target...]
    all_to_all x1 -> x0, blocking collectives: 13.7 us -> none  [swapped_with_all(): return lax.all_to_all(copies, axes, split_axis=0, concat_axis=0, tiled=True)]
    all_to_all x5 -> x6, starting transfers between devices: 27.4 us -> 25.1 us  [swapped_with_all(): return lax.all_to_all(copies, axes, split_axis=0, concat_axis=0, tiled=True)]
    unnamed x71 -> x69, local copies, waits for them, and re-layouts: 3.76 us -> 4.68 us
  transfers between devices with their start and end apart: 23 -> 24, of which waited for: 11 -> 11; matrix products, arithmetic and copies ran while one was open for 2% -> 3% of each run, Pallas kernels for 0% -> 0%
where the time goes in v4:
time: 146 us; the launch traced here: 145 us
  waiting for transfers between devices  58.2 us (40%)
  starting transfers between devices  57.5 us (39%)
  Pallas kernels  14 us (10%)
  local copies, waits for them, and re-layouts  10.9 us (7%)
  between operations  3.76 us (3%)
    all_to_all x6, waiting for transfers between devices, swapped_with_all(): return lax.all_to_all(copies, axes, split_axis=0, concat_axis=0, tiled=True)  53.7 us
    ppermute x18, starting transfers between devices, fetched_from(): lax.ppermute(value, axis, [((target + steps) % count, target) for target...  32.4 us
    all_to_all x6, starting transfers between devices, swapped_with_all(): return lax.all_to_all(copies, axes, split_axis=0, concat_axis=0, tiled=True)  25.1 us
    pallas_call x2, Pallas kernels, solve_users(): pl.pallas_call(functools.partial(users_kernel, tiles=tiles, copies=copies...  10.8 us
    unnamed x69, local copies, waits for them, and re-layouts  4.68 us
    ppermute x18, waiting for transfers between devices, fetched_from(): lax.ppermute(value, axis, [((target + steps) % count, target) for target...  4.45 us
    pallas_call x1, Pallas kernels, solve_items(): pl.pallas_call(items_kernel, out_shape=(jax.ShapeDtypeStruct((items, rank...  3.26 us
  transfers between devices with their start and end apart: 24, of which 11 were waited for; matrix products, arithmetic and copies ran while one was open for 3% of the time, Pallas kernels for 0%

profile of v4, /device:TPU:1, one launch (start us, length us, event | category | flops | bytes accessed | tf_op | source)
XLA Modules:
  0.0 145.1 jit_solution(1698531790795686160)
XLA Ops:
  0.6 2.5 %collective-permute-start = (bf16[128,128]{1,0:T(8,128)(2,1)}, bf16[128,128]{1,0:T(8,128)(2,1)S(1)}, u32[]{:S(2)}, u32[]{:S(2)}) collective-permute-start(bf16[128,128]{1,0:T(8,128)(2,1)} %param.4), channel_id=1, source_target_pairs={{254,0},{0,2},{2,4},{4,6},{6,8},{8,10},{10,12},{12,14},{14,16},{16... | collective-permute-start | bytes 98312 | tf_op jit(solution)/shard_map/ppermute | solution.py:165
  3.2 1.7 %broadcast_in_dim.17 = bf16[16,128,128]{2,1,0:T(8,128)(2,1)} broadcast(bf16[128,128]{1,0:T(8,128)(2,1)} %param.4), dimensions={1,2} | broadcast | bytes 557056 | tf_op jit(solution)/shard_map/broadcast_in_dim | solution.py:245
  4.9 6.9 %all-to-all-start = ((bf16[16,128,128]{2,1,0:T(8,128)(2,1)}), bf16[16,128,128]{2,1,0:T(8,128)(2,1)S(1)}, u32[]{:S(2)}, u32[]{:S(2)}) async-start(bf16[16,128,128]{2,1,0:T(8,128)(2,1)} %broadcast_in_dim.17), calls=%async_computation | async-start | bytes 1048576 | tf_op jit(solution)/shard_map/all_to_all | solution.py:158
  11.8 0.6 copy-done.28
  12.4 0.7 fusion.2
  15.1 0.7 copy-done.29
  15.9 8.4 %collective-permute-start.1 = (bf16[64,128]{1,0:T(8,128)(2,1)S(1)}, bf16[64,128]{1,0:T(8,128)(2,1)S(1)}, u32[]{:S(2)}, u32[]{:S(2)}) collective-permute-start(bf16[64,128]{1,0:T(8,128)(2,1)S(1)} %pad_maximum_fusion.3), channel_id=1, source_target_pairs={{2,0},{4,2},{6,4},{8,6},{10,8},{12,10},{14,12},{16,14},{18,16},{20... | collective-permute-start | bytes 49160 | tf_op jit(solution)/shard_map/ppermute | solution.py:165
  24.3 0.6 collective-permute-start.2
  25.7 2.7 %collective-permute-done.2.refs_9_ = bf16[64,128]{1,0:T(8,128)(2,1)S(1)} collective-permute-done((bf16[64,128]{1,0:T(8,128)(2,1)S(1)}, bf16[64,128]{1,0:T(8,128)(2,1)S(1)}, u32[]{:S(2)}, u32[]{:S(2)}) %collective-permute-start.2) | collective-permute-done | bytes 16416 | tf_op jit(solution)/shard_map/ppermute | solution.py:165
  28.4 1.0 broadcast_in_dim.19
  29.4 3.5 %all-to-all-start.1 = ((bf16[8,384,128]{2,1,0:T(8,128)(2,1)}), bf16[8,384,128]{2,1,0:T(8,128)(2,1)S(1)}, u32[]{:S(2)}, u32[]{:S(2)}) async-start(bf16[8,384,128]{2,1,0:T(8,128)(2,1)} %broadcast_in_dim.19), calls=%async_computation.1 | async-start | bytes 1572864 | tf_op jit(solution)/shard_map/all_to_all | solution.py:158
  33.0 2.8 %collective-permute-start.3 = (bf16[128,128]{1,0:T(8,128)(2,1)S(1)}, bf16[128,128]{1,0:T(8,128)(2,1)S(1)}, u32[]{:S(2)}, u32[]{:S(2)}) collective-permute-start(bf16[128,128]{1,0:T(8,128)(2,1)S(1)} %collective-permute-done.refs_0_), channel_id=1, source_target_pairs={{1,0},{0,1},{3,2},{2,3},{5,4},{4,5},{7,6},{6,7},{9,8},{8,9},{11,10... | collective-permute-start | bytes 98312 | tf_op jit(solution)/shard_map/ppermute | solution.py:165
  35.9 0.5 copy-done
  36.4 0.6 pad_maximum_fusion.1.refs_8_
  37.0 17.0 %all-to-all-done.1 = bf16[8,384,128]{2,1,0:T(8,128)(2,1)S(1)} async-done(((bf16[8,384,128]{2,1,0:T(8,128)(2,1)}), bf16[8,384,128]{2,1,0:T(8,128)(2,1)S(1)}, u32[]{:S(2)}, u32[]{:S(2)}) %all-to-all-start.1) | async-done | bytes 786464 | tf_op jit(solution)/shard_map/all_to_all | solution.py:158
  54.1 3.0 %collective-permute-start.5 = (bf16[128,128]{1,0:T(8,128)(2,1)S(1)}, bf16[128,128]{1,0:T(8,128)(2,1)S(1)}, u32[]{:S(2)}, u32[]{:S(2)}) collective-permute-start(bf16[128,128]{1,0:T(8,128)(2,1)S(1)} %get-tuple-element.37.refs_2_), channel_id=1, source_target_pairs={{1,0},{0,1},{3,2},{2,3},{5,4},{4,5},{7,6},{6,7},{9,8},{8,9},{11,10... | collective-permute-start | bytes 98312 | tf_op jit(solution)/shard_map/ppermute | solution.py:165
  57.2 0.6 dynamic-slice_bitcast_fusion.10
  58.0 0.3 collective-permute-done.6.refs_7_
  58.6 0.3 copy-done.18
  59.0 5.6 %users.2 = (bf16[32,128]{1,0:T(8,128)(2,1)}, bf16[16,160,128]{2,1,0:T(8,128)(2,1)}) custom-call(bf16[128,128]{1,0:T(8,128)(2,1)} %copy-done.11, bf16[128,128]{1,0:T(8,128)(2,1)} %copy-done, bf16[128,128]{1,0:T(8,128)(2,1)} %copy-done.3, bf16[128,128]{1,0:T(8,128)(2,1)} %copy-done.2, bf16[128,128]{1,0:T(8,128)(2,1)} %copy-done.13, ...), custom_call_target="tpu_custom_call" | custom-call | tf_op jit(solution)/shard_map/users/pallas_call | solution.py:126
  64.5 4.1 %all-to-all-start.2 = ((bf16[16,160,128]{2,1,0:T(8,128)(2,1)}), bf16[16,160,128]{2,1,0:T(8,128)(2,1)S(1)}, u32[]{:S(2)}, u32[]{:S(2)}) async-start(bf16[16,160,128]{2,1,0:T(8,128)(2,1)} %get-tuple-element.16), calls=%async_computation.2 | async-start | bytes 1310720 | tf_op jit(solution)/shard_map/all_to_all | solution.py:158
  68.6 0.7 copy-done.31
  69.3 2.9 %collective-permute-start.8 = (bf16[32,128]{1,0:T(8,128)(2,1)S(1)}, bf16[32,128]{1,0:T(8,128)(2,1)S(1)}, u32[]{:S(2)}, u32[]{:S(2)}) collective-permute-start(bf16[32,128]{1,0:T(8,128)(2,1)S(1)} %copy-done.31), channel_id=1, source_target_pairs={{2,0},{4,2},{6,4},{8,6},{10,8},{12,10},{14,12},{16,14},{18,16},{20... | collective-permute-start | bytes 24584 | tf_op jit(solution)/shard_map/ppermute | solution.py:165
  72.2 7.7 %all-to-all-done.2 = bf16[16,160,128]{2,1,0:T(8,128)(2,1)S(1)} async-done(((bf16[16,160,128]{2,1,0:T(8,128)(2,1)}), bf16[16,160,128]{2,1,0:T(8,128)(2,1)S(1)}, u32[]{:S(2)}, u32[]{:S(2)}) %all-to-all-start.2) | async-done | bytes 655392 | tf_op jit(solution)/shard_map/all_to_all | solution.py:158
  79.9 0.7 broadcast_in_dim.20
  80.6 3.4 %all-to-all-start.3 = ((bf16[8,64,128]{2,1,0:T(8,128)(2,1)}), bf16[8,64,128]{2,1,0:T(8,128)(2,1)S(1)}, u32[]{:S(2)}, u32[]{:S(2)}) async-start(bf16[8,64,128]{2,1,0:T(8,128)(2,1)} %broadcast_in_dim.20), calls=%async_computation.3 | async-start | bytes 262144 | tf_op jit(solution)/shard_map/all_to_all | solution.py:158
  84.0 2.7 %collective-permute-start.9 = (bf16[32,128]{1,0:T(8,128)(2,1)S(1)}, bf16[32,128]{1,0:T(8,128)(2,1)S(1)}, u32[]{:S(2)}, u32[]{:S(2)}) collective-permute-start(bf16[32,128]{1,0:T(8,128)(2,1)S(1)} %collective-permute-done.8.refs_0_), channel_id=1, source_target_pairs={{1,0},{0,1},{3,2},{2,3},{5,4},{4,5},{7,6},{6,7},{9,8},{8,9},{11,10... | collective-permute-start | bytes 24584 | tf_op jit(solution)/shard_map/ppermute | solution.py:165
  86.8 5.0 %all-to-all-done.3 = bf16[8,64,128]{2,1,0:T(8,128)(2,1)S(1)} async-done(((bf16[8,64,128]{2,1,0:T(8,128)(2,1)}), bf16[8,64,128]{2,1,0:T(8,128)(2,1)S(1)}, u32[]{:S(2)}, u32[]{:S(2)}) %all-to-all-start.3) | async-done | bytes 131104 | tf_op jit(solution)/shard_map/all_to_all | solution.py:158
  91.8 3.7 %collective-permute-start.11 = (bf16[32,128]{1,0:T(8,128)(2,1)S(1)}, bf16[32,128]{1,0:T(8,128)(2,1)S(1)}, u32[]{:S(2)}, u32[]{:S(2)}) collective-permute-start(bf16[32,128]{1,0:T(8,128)(2,1)S(1)} %get-tuple-element.49.refs_2_), channel_id=1, source_target_pairs={{1,0},{0,1},{3,2},{2,3},{5,4},{4,5},{7,6},{6,7},{9,8},{8,9},{11,10... | collective-permute-start | bytes 24584 | tf_op jit(solution)/shard_map/ppermute | solution.py:165
  95.6 0.3 collective-permute-start.12
  95.9 0.6 dynamic-slice_bitcast_fusion.8
  96.5 0.2 collective-permute-done.12.refs_7_
  96.8 0.3 copy-done.24
  97.1 0.2 copy-done.27
  97.3 3.3 %items.1 = (bf16[128,128]{1,0:T(8,128)(2,1)}, bf16[16,128,128]{2,1,0:T(8,128)(2,1)}) custom-call(bf16[32,128]{1,0:T(8,128)(2,1)} %copy-done.23, bf16[32,128]{1,0:T(8,128)(2,1)} %copy-done.8, bf16[32,128]{1,0:T(8,128)(2,1)} %copy-done.10, bf16[32,128]{1,0:T(8,128)(2,1)} %copy-done.9, bf16[32,128]{1,0:T(8,128)(2,1)} %copy-done.24, bf16[32,128]{1,0:T(8,128)(2,1)} %copy-done.25, ...), custom_call_target="tpu_custom_call" | custom-call | tf_op jit(solution)/shard_map/items/pallas_call | solution.py:144
  100.6 3.7 %all-to-all-start.4 = ((bf16[16,128,128]{2,1,0:T(8,128)(2,1)}), bf16[16,128,128]{2,1,0:T(8,128)(2,1)S(1)}, u32[]{:S(2)}, u32[]{:S(2)}) async-start(bf16[16,128,128]{2,1,0:T(8,128)(2,1)} %get-tuple-element.22), calls=%async_computation.4 | async-start | bytes 1048576 | tf_op jit(solution)/shard_map/all_to_all | solution.py:158
  104.3 0.4 collective-permute-start.13
  104.7 10.2 %all-to-all-done.4 = bf16[16,128,128]{2,1,0:T(8,128)(2,1)S(1)} async-done(((bf16[16,128,128]{2,1,0:T(8,128)(2,1)}), bf16[16,128,128]{2,1,0:T(8,128)(2,1)S(1)}, u32[]{:S(2)}, u32[]{:S(2)}) %all-to-all-start.4) | async-done | bytes 524320 | tf_op jit(solution)/shard_map/all_to_all | solution.py:158
  114.9 0.9 broadcast_in_dim.21
  115.8 3.5 %all-to-all-start.5 = ((bf16[8,256,128]{2,1,0:T(8,128)(2,1)}), bf16[8,256,128]{2,1,0:T(8,128)(2,1)S(1)}, u32[]{:S(2)}, u32[]{:S(2)}) async-start(bf16[8,256,128]{2,1,0:T(8,128)(2,1)} %broadcast_in_dim.21), calls=%async_computation.5 | async-start | bytes 1048576 | tf_op jit(solution)/shard_map/all_to_all | solution.py:158
  119.3 2.0 %collective-permute-start.14 = (bf16[128,128]{1,0:T(8,128)(2,1)S(1)}, bf16[128,128]{1,0:T(8,128)(2,1)S(1)}, u32[]{:S(2)}, u32[]{:S(2)}) collective-permute-start(bf16[128,128]{1,0:T(8,128)(2,1)S(1)} %collective-permute-done.13.refs_0_), channel_id=1, source_target_pairs={{1,0},{0,1},{3,2},{2,3},{5,4},{4,5},{7,6},{6,7},{9,8},{8,9},{11,10... | collective-permute-start | bytes 98312 | tf_op jit(solution)/shard_map/ppermute | solution.py:165
  121.4 13.8 %all-to-all-done.5 = bf16[8,256,128]{2,1,0:T(8,128)(2,1)S(1)} async-done(((bf16[8,256,128]{2,1,0:T(8,128)(2,1)}), bf16[8,256,128]{2,1,0:T(8,128)(2,1)S(1)}, u32[]{:S(2)}, u32[]{:S(2)}) %all-to-all-start.5) | async-done | bytes 524320 | tf_op jit(solution)/shard_map/all_to_all | solution.py:158
  135.2 2.6 %collective-permute-start.16 = (bf16[128,128]{1,0:T(8,128)(2,1)S(1)}, bf16[128,128]{1,0:T(8,128)(2,1)S(1)}, u32[]{:S(2)}, u32[]{:S(2)}) collective-permute-start(bf16[128,128]{1,0:T(8,128)(2,1)S(1)} %get-tuple-element.44.refs_2_), channel_id=1, source_target_pairs={{1,0},{0,1},{3,2},{2,3},{5,4},{4,5},{7,6},{6,7},{9,8},{8,9},{11,10... | collective-permute-start | bytes 98312 | tf_op jit(solution)/shard_map/ppermute | solution.py:165
  137.9 0.7 collective-permute-done.16.refs_6_
  138.7 0.3 collective-permute-done.17.refs_7_
  139.0 0.2 copy-done.19
  139.3 0.6 copy-done.20
  139.9 5.2 %users.3 = bf16[32,128]{1,0:T(8,128)(2,1)} custom-call(bf16[128,128]{1,0:T(8,128)(2,1)} %copy-done.12, bf16[128,128]{1,0:T(8,128)(2,1)} %copy-done.1, bf16[128,128]{1,0:T(8,128)(2,1)} %copy-done.5, bf16[128,128]{1,0:T(8,128)(2,1)} %copy-done.4, bf16[128,128]{1,0:T(8,128)(2,1)} %copy-done.15, bf16[128,128]{1,0:T(8,128)(2,1)} %copy-done.16, ...), custom_call_target="tpu_custom_call" | custom-call | tf_op jit(solution)/shard_map/users/pallas_call | solution.py:126
  (95 shorter events, 1.4 us)
Async XLA Ops:
  0.6 27.8 %collective-permute-start = (bf16[128,128]{1,0:T(8,128)(2,1)}, bf16[128,128]{1,0:T(8,128)(2,1)S(1)}, u32[]{:S(2)}, u32[]{:S(2)}) collective-permute-start(bf16[128,128]{1,0:T(8,128)(2,1)} %param.4), channel_id=1, source_target_pairs={{254,0},{0,2},{2,4},{4,6},{6,8},{8,10},{10,12},{12,14},{14,16},{16... | collective-permute-start | bytes 98312 | tf_op jit(solution)/shard_map/ppermute | solution.py:165
  4.9 10.2 %copy-start.7 = (bf16[4,64,128]{2,1,0:T(8,128)(2,1)S(1)}, bf16[4,64,128]{2,1,0:T(8,128)(2,1)}, u32[]{:S(2)}) copy-start(bf16[4,64,128]{2,1,0:T(8,128)(2,1)} %param.5) | copy-start | bytes 196612
  4.9 20.7 %all-to-all-start = ((bf16[16,128,128]{2,1,0:T(8,128)(2,1)}), bf16[16,128,128]{2,1,0:T(8,128)(2,1)S(1)}, u32[]{:S(2)}, u32[]{:S(2)}) async-start(bf16[16,128,128]{2,1,0:T(8,128)(2,1)} %broadcast_in_dim.17), calls=%async_computation | async-start | bytes 1048576 | tf_op jit(solution)/shard_map/all_to_all | solution.py:158
  11.8 0.7 copy-start.28
  15.1 0.7 copy-start.29
  15.9 9.8 %collective-permute-start.1 = (bf16[64,128]{1,0:T(8,128)(2,1)S(1)}, bf16[64,128]{1,0:T(8,128)(2,1)S(1)}, u32[]{:S(2)}, u32[]{:S(2)}) collective-permute-start(bf16[64,128]{1,0:T(8,128)(2,1)S(1)} %pad_maximum_fusion.3), channel_id=1, source_target_pairs={{2,0},{4,2},{6,4},{8,6},{10,8},{12,10},{14,12},{16,14},{18,16},{20... | collective-permute-start | bytes 49160 | tf_op jit(solution)/shard_map/ppermute | solution.py:165
  24.3 4.1 %collective-permute-start.2 = (bf16[64,128]{1,0:T(8,128)(2,1)S(1)}, bf16[64,128]{1,0:T(8,128)(2,1)S(1)}, u32[]{:S(2)}, u32[]{:S(2)}) collective-permute-start(bf16[64,128]{1,0:T(8,128)(2,1)S(1)} %pad_maximum_fusion.4), channel_id=1, source_target_pairs={{128,0},{130,2},{132,4},{134,6},{136,8},{138,10},{140,12},{142,14}... | collective-permute-start | bytes 49160 | tf_op jit(solution)/shard_map/ppermute | solution.py:165
  25.7 3.7 %copy-start.21 = (bf16[64,128]{1,0:T(8,128)(2,1)}, bf16[64,128]{1,0:T(8,128)(2,1)S(1)}, u32[]{:S(2)}) copy-start(bf16[64,128]{1,0:T(8,128)(2,1)S(1)} %collective-permute-done.1.refs_8_) | copy-start | bytes 49156
  28.4 1.0 copy-start.22
  28.4 4.6 %copy-start.11 = (bf16[128,128]{1,0:T(8,128)(2,1)}, bf16[128,128]{1,0:T(8,128)(2,1)S(1)}, u32[]{:S(2)}) copy-start(bf16[128,128]{1,0:T(8,128)(2,1)S(1)} %collective-permute-done.refs_0_) | copy-start | bytes 98308
  29.4 24.6 %all-to-all-start.1 = ((bf16[8,384,128]{2,1,0:T(8,128)(2,1)}), bf16[8,384,128]{2,1,0:T(8,128)(2,1)S(1)}, u32[]{:S(2)}, u32[]{:S(2)}) async-start(bf16[8,384,128]{2,1,0:T(8,128)(2,1)} %broadcast_in_dim.19), calls=%async_computation.1 | async-start | bytes 1572864 | tf_op jit(solution)/shard_map/all_to_all | solution.py:158
  33.0 24.8 %collective-permute-start.3 = (bf16[128,128]{1,0:T(8,128)(2,1)S(1)}, bf16[128,128]{1,0:T(8,128)(2,1)S(1)}, u32[]{:S(2)}, u32[]{:S(2)}) collective-permute-start(bf16[128,128]{1,0:T(8,128)(2,1)S(1)} %collective-permute-done.refs_0_), channel_id=1, source_target_pairs={{1,0},{0,1},{3,2},{2,3},{5,4},{4,5},{7,6},{6,7},{9,8},{8,9},{11,10... | collective-permute-start | bytes 98312 | tf_op jit(solution)/shard_map/ppermute | solution.py:165
  35.8 22.1 %collective-permute-start.4 = (bf16[128,128]{1,0:T(8,128)(2,1)S(1)}, bf16[128,128]{1,0:T(8,128)(2,1)S(1)}, u32[]{:S(2)}, u32[]{:S(2)}) collective-permute-start(bf16[128,128]{1,0:T(8,128)(2,1)S(1)} %dynamic-slice_bitcast_fusion.7.refs_1_), channel_id=1, source_target_pairs={{1,0},{0,1},{3,2},{2,3},{5,4},{4,5},{7,6},{6,7},{9,8},{8,9},{11,10... | collective-permute-start | bytes 98312 | tf_op jit(solution)/shard_map/ppermute | solution.py:165
  36.4 21.5 %collective-permute-start.7 = (bf16[4,32,128]{2,1,0:T(8,128)(2,1)S(1)}, bf16[4,32,128]{2,1,0:T(8,128)(2,1)S(1)}, u32[]{:S(2)}, u32[]{:S(2)}) collective-permute-start(bf16[4,32,128]{2,1,0:T(8,128)(2,1)S(1)} %pad_maximum_fusion.2), channel_id=1, source_target_pairs={{1,0},{0,1},{3,2},{2,3},{5,4},{4,5},{7,6},{6,7},{9,8},{8,9},{11,10... | collective-permute-start | bytes 98312 | tf_op jit(solution)/shard_map/ppermute | solution.py:165
  54.1 3.8 %copy-start.2 = (bf16[128,128]{1,0:T(8,128)(2,1)}, bf16[128,128]{1,0:T(8,128)(2,1)S(1)}, u32[]{:S(2)}) copy-start(bf16[128,128]{1,0:T(8,128)(2,1)S(1)} %get-tuple-element.36.refs_3_) | copy-start | bytes 98308
  54.1 3.8 %copy-start.3 = (bf16[128,128]{1,0:T(8,128)(2,1)}, bf16[128,128]{1,0:T(8,128)(2,1)S(1)}, u32[]{:S(2)}) copy-start(bf16[128,128]{1,0:T(8,128)(2,1)S(1)} %get-tuple-element.37.refs_2_) | copy-start | bytes 98308
  54.1 3.9 %collective-permute-start.5 = (bf16[128,128]{1,0:T(8,128)(2,1)S(1)}, bf16[128,128]{1,0:T(8,128)(2,1)S(1)}, u32[]{:S(2)}, u32[]{:S(2)}) collective-permute-start(bf16[128,128]{1,0:T(8,128)(2,1)S(1)} %get-tuple-element.37.refs_2_), channel_id=1, source_target_pairs={{1,0},{0,1},{3,2},{2,3},{5,4},{4,5},{7,6},{6,7},{9,8},{8,9},{11,10... | collective-permute-start | bytes 98312 | tf_op jit(solution)/shard_map/ppermute | solution.py:165
  57.1 1.2 collective-permute-start.6
  57.9 0.6 copy-start.13
  57.9 0.6 copy-start.14
  57.9 0.6 copy-start.6
  58.0 0.6 copy-start.17
  64.5 15.4 %all-to-all-start.2 = ((bf16[16,160,128]{2,1,0:T(8,128)(2,1)}), bf16[16,160,128]{2,1,0:T(8,128)(2,1)S(1)}, u32[]{:S(2)}, u32[]{:S(2)}) async-start(bf16[16,160,128]{2,1,0:T(8,128)(2,1)} %get-tuple-element.16), calls=%async_computation.2 | async-start | bytes 1310720 | tf_op jit(solution)/shard_map/all_to_all | solution.py:158
  68.6 0.7 copy-start.31
  69.3 10.6 %collective-permute-start.8 = (bf16[32,128]{1,0:T(8,128)(2,1)S(1)}, bf16[32,128]{1,0:T(8,128)(2,1)S(1)}, u32[]{:S(2)}, u32[]{:S(2)}) collective-permute-start(bf16[32,128]{1,0:T(8,128)(2,1)S(1)} %copy-done.31), channel_id=1, source_target_pairs={{2,0},{4,2},{6,4},{8,6},{10,8},{12,10},{14,12},{16,14},{18,16},{20... | collective-permute-start | bytes 24584 | tf_op jit(solution)/shard_map/ppermute | solution.py:165
  79.9 6.8 %copy-start.8 = (bf16[32,128]{1,0:T(8,128)(2,1)}, bf16[32,128]{1,0:T(8,128)(2,1)S(1)}, u32[]{:S(2)}) copy-start(bf16[32,128]{1,0:T(8,128)(2,1)S(1)} %get-tuple-element.40.refs_1_) | copy-start | bytes 24580
  79.9 4.1 %copy-start.23 = (bf16[32,128]{1,0:T(8,128)(2,1)}, bf16[32,128]{1,0:T(8,128)(2,1)S(1)}, u32[]{:S(2)}) copy-start(bf16[32,128]{1,0:T(8,128)(2,1)S(1)} %collective-permute-done.8.refs_0_) | copy-start | bytes 24580
  80.6 11.2 %all-to-all-start.3 = ((bf16[8,64,128]{2,1,0:T(8,128)(2,1)}), bf16[8,64,128]{2,1,0:T(8,128)(2,1)S(1)}, u32[]{:S(2)}, u32[]{:S(2)}) async-start(bf16[8,64,128]{2,1,0:T(8,128)(2,1)} %broadcast_in_dim.20), calls=%async_computation.3 | async-start | bytes 262144 | tf_op jit(solution)/shard_map/all_to_all | solution.py:158
  84.0 12.5 %collective-permute-start.9 = (bf16[32,128]{1,0:T(8,128)(2,1)S(1)}, bf16[32,128]{1,0:T(8,128)(2,1)S(1)}, u32[]{:S(2)}, u32[]{:S(2)}) collective-permute-start(bf16[32,128]{1,0:T(8,128)(2,1)S(1)} %collective-permute-done.8.refs_0_), channel_id=1, source_target_pairs={{1,0},{0,1},{3,2},{2,3},{5,4},{4,5},{7,6},{6,7},{9,8},{8,9},{11,10... | collective-permute-start | bytes 24584 | tf_op jit(solution)/shard_map/ppermute | solution.py:165
  86.7 9.8 %collective-permute-start.10 = (bf16[32,128]{1,0:T(8,128)(2,1)S(1)}, bf16[32,128]{1,0:T(8,128)(2,1)S(1)}, u32[]{:S(2)}, u32[]{:S(2)}) collective-permute-start(bf16[32,128]{1,0:T(8,128)(2,1)S(1)} %get-tuple-element.40.refs_1_), channel_id=1, source_target_pairs={{1,0},{0,1},{3,2},{2,3},{5,4},{4,5},{7,6},{6,7},{9,8},{8,9},{11,10... | collective-permute-start | bytes 24584 | tf_op jit(solution)/shard_map/ppermute | solution.py:165
  91.8 4.6 %copy-start.9 = (bf16[32,128]{1,0:T(8,128)(2,1)}, bf16[32,128]{1,0:T(8,128)(2,1)S(1)}, u32[]{:S(2)}) copy-start(bf16[32,128]{1,0:T(8,128)(2,1)S(1)} %get-tuple-element.48.refs_3_) | copy-start | bytes 24580
  91.8 4.6 %copy-start.10 = (bf16[32,128]{1,0:T(8,128)(2,1)}, bf16[32,128]{1,0:T(8,128)(2,1)S(1)}, u32[]{:S(2)}) copy-start(bf16[32,128]{1,0:T(8,128)(2,1)S(1)} %get-tuple-element.49.refs_2_) | copy-start | bytes 24580
  91.8 4.7 %collective-permute-start.11 = (bf16[32,128]{1,0:T(8,128)(2,1)S(1)}, bf16[32,128]{1,0:T(8,128)(2,1)S(1)}, u32[]{:S(2)}, u32[]{:S(2)}) collective-permute-start(bf16[32,128]{1,0:T(8,128)(2,1)S(1)} %get-tuple-element.49.refs_2_), channel_id=1, source_target_pairs={{1,0},{0,1},{3,2},{2,3},{5,4},{4,5},{7,6},{6,7},{9,8},{8,9},{11,10... | collective-permute-start | bytes 24584 | tf_op jit(solution)/shard_map/ppermute | solution.py:165
  95.6 1.2 collective-permute-start.12
  100.6 3.7 %copy-start.30 = (bf16[128,128]{1,0:T(8,128)(2,1)S(1)}, bf16[128,128]{1,0:T(8,128)(2,1)}, u32[]{:S(2)}) copy-start(bf16[128,128]{1,0:T(8,128)(2,1)} %get-tuple-element.13) | copy-start | bytes 98308
  100.6 14.3 %all-to-all-start.4 = ((bf16[16,128,128]{2,1,0:T(8,128)(2,1)}), bf16[16,128,128]{2,1,0:T(8,128)(2,1)S(1)}, u32[]{:S(2)}, u32[]{:S(2)}) async-start(bf16[16,128,128]{2,1,0:T(8,128)(2,1)} %get-tuple-element.22), calls=%async_computation.4 | async-start | bytes 1048576 | tf_op jit(solution)/shard_map/all_to_all | solution.py:158
  104.3 10.6 %collective-permute-start.13 = (bf16[128,128]{1,0:T(8,128)(2,1)S(1)}, bf16[128,128]{1,0:T(8,128)(2,1)S(1)}, u32[]{:S(2)}, u32[]{:S(2)}) collective-permute-start(bf16[128,128]{1,0:T(8,128)(2,1)S(1)} %copy-done.30), channel_id=1, source_target_pairs={{254,0},{0,2},{2,4},{4,6},{6,8},{8,10},{10,12},{12,14},{14,16},{16... | collective-permute-start | bytes 98312 | tf_op jit(solution)/shard_map/ppermute | solution.py:165
  114.9 6.4 %copy-start.1 = (bf16[128,128]{1,0:T(8,128)(2,1)}, bf16[128,128]{1,0:T(8,128)(2,1)S(1)}, u32[]{:S(2)}) copy-start(bf16[128,128]{1,0:T(8,128)(2,1)S(1)} %get-tuple-element.45.refs_1_) | copy-start | bytes 98308
  114.9 4.4 %copy-start.12 = (bf16[128,128]{1,0:T(8,128)(2,1)}, bf16[128,128]{1,0:T(8,128)(2,1)S(1)}, u32[]{:S(2)}) copy-start(bf16[128,128]{1,0:T(8,128)(2,1)S(1)} %collective-permute-done.13.refs_0_) | copy-start | bytes 98308
  115.8 19.4 %all-to-all-start.5 = ((bf16[8,256,128]{2,1,0:T(8,128)(2,1)}), bf16[8,256,128]{2,1,0:T(8,128)(2,1)S(1)}, u32[]{:S(2)}, u32[]{:S(2)}) async-start(bf16[8,256,128]{2,1,0:T(8,128)(2,1)} %broadcast_in_dim.21), calls=%async_computation.5 | async-start | bytes 1048576 | tf_op jit(solution)/shard_map/all_to_all | solution.py:158
  119.3 18.6 %collective-permute-start.14 = (bf16[128,128]{1,0:T(8,128)(2,1)S(1)}, bf16[128,128]{1,0:T(8,128)(2,1)S(1)}, u32[]{:S(2)}, u32[]{:S(2)}) collective-permute-start(bf16[128,128]{1,0:T(8,128)(2,1)S(1)} %collective-permute-done.13.refs_0_), channel_id=1, source_target_pairs={{1,0},{0,1},{3,2},{2,3},{5,4},{4,5},{7,6},{6,7},{9,8},{8,9},{11,10... | collective-permute-start | bytes 98312 | tf_op jit(solution)/shard_map/ppermute | solution.py:165
  121.3 16.6 %collective-permute-start.15 = (bf16[128,128]{1,0:T(8,128)(2,1)S(1)}, bf16[128,128]{1,0:T(8,128)(2,1)S(1)}, u32[]{:S(2)}, u32[]{:S(2)}) collective-permute-start(bf16[128,128]{1,0:T(8,128)(2,1)S(1)} %get-tuple-element.45.refs_1_), channel_id=1, source_target_pairs={{1,0},{0,1},{3,2},{2,3},{5,4},{4,5},{7,6},{6,7},{9,8},{8,9},{11,10... | collective-permute-start | bytes 98312 | tf_op jit(solution)/shard_map/ppermute | solution.py:165
  135.2 3.8 %copy-start.4 = (bf16[128,128]{1,0:T(8,128)(2,1)}, bf16[128,128]{1,0:T(8,128)(2,1)S(1)}, u32[]{:S(2)}) copy-start(bf16[128,128]{1,0:T(8,128)(2,1)S(1)} %get-tuple-element.43.refs_3_) | copy-start | bytes 98308
  135.2 3.8 %copy-start.5 = (bf16[128,128]{1,0:T(8,128)(2,1)}, bf16[128,128]{1,0:T(8,128)(2,1)S(1)}, u32[]{:S(2)}) copy-start(bf16[128,128]{1,0:T(8,128)(2,1)S(1)} %get-tuple-element.44.refs_2_) | copy-start | bytes 98308
  135.2 3.4 %collective-permute-start.16 = (bf16[128,128]{1,0:T(8,128)(2,1)S(1)}, bf16[128,128]{1,0:T(8,128)(2,1)S(1)}, u32[]{:S(2)}, u32[]{:S(2)}) collective-permute-start(bf16[128,128]{1,0:T(8,128)(2,1)S(1)} %get-tuple-element.44.refs_2_), channel_id=1, source_target_pairs={{1,0},{0,1},{3,2},{2,3},{5,4},{4,5},{7,6},{6,7},{9,8},{8,9},{11,10... | collective-permute-start | bytes 98312 | tf_op jit(solution)/shard_map/ppermute | solution.py:165
  137.8 1.2 collective-permute-start.17
  137.9 1.1 copy-start.15
  137.9 1.1 copy-start.16
  (8 other events, 4.8 us)

commit v5 on v4

--- a/solution.py
+++ b/solution.py
@@ -43,7 +43,7 @@
     own, other = refs[:tiles], refs[tiles : 2 * tiles]
     own_marks_ref, other_marks_ref, *rest, factor_t_ref, mask_ref, sums_ref = refs[2 * tiles :]
     copies_ref = rest.pop() if copies else None
-    *extra, out_ref = rest
+    (out_ref,) = rest
     rank = own[0].shape[1]
     rows = own_marks_ref.shape[1]
     parts = []
@@ -76,10 +76,7 @@
     answer = relax(right, ridge, bound, rated, factors)
     out_ref[...] = answer
     for c in range(copies):
-        copies_ref[c, :rows, :] = answer
-        for k, ref in enumerate(extra):
-            users = ref.shape[0]
-            copies_ref[c, rows + k * users : rows + (k + 1) * users, :] = ref[...]
+        copies_ref[c] = answer
 
 
 def items_kernel(*refs):
@@ -115,14 +112,14 @@
     return [pl.BlockSpec(memory_space=VMEM)] * count
 
 
-def solve_users(own, other, own_marks, other_marks, copies=0, extra=()):
+def solve_users(own, other, own_marks, other_marks, copies=0):
     tiles, rows, half = own_marks.shape
     rank = own[0].shape[1]
     width = tiles * 2 * half
-    args = [*own, *other, own_marks, other_marks, *extra]
+    args = [*own, *other, own_marks, other_marks]
     shapes = [(rows, rank)]
     if copies:
-        shapes.append((copies, rows + sum(e.shape[0] for e in extra), rank))
+        shapes.append((copies, rows, rank))
     return pl.pallas_call(
         functools.partial(users_kernel, tiles=tiles, copies=copies),
         out_shape=tuple(jax.ShapeDtypeStruct(shape, jnp.bfloat16) for shape in shapes),
@@ -177,6 +174,25 @@
     return (place_on(("x", "y")) + (shift >> z_bits) + carry) & (plane - 1), (z + z_shift) & (ring - 1)
 
 
+def steps_to(place):
+    ny, nx = lax.axis_size("y"), lax.axis_size("x")
+    y, x = place & (ny - 1), place >> (ny.bit_length() - 1)
+    return (y - place_on("y")) & (ny - 1), (x - place_on("x")) & (nx - 1)
+
+
+def stepped(parts, axis, steps):
+    held = jnp.concatenate(parts, axis=0)
+    arrived = [held] + [fetched_from(held, axis, step) for step in range(1, lax.axis_size(axis))]
+    chosen, start = [], 0
+    for part, own_step in zip(parts, steps):
+        value = part
+        for step in range(1, len(arrived)):
+            value = jnp.where(own_step == step, arrived[step][start : start + part.shape[0]], value)
+        chosen.append(value)
+        start += part.shape[0]
+    return chosen
+
+
 def taken(source, index, start, size):
     zero = jnp.uint32(0)
     return lax.dynamic_slice(source, (index, zero + start, zero), (1, size, source.shape[2]))[0]
@@ -214,9 +230,8 @@
         return value
 
     shifts = (jnp.uint32(near), jnp.uint32(across), offset_at(third), offset_at(fourth))
-    forward = [shift_digits(shift, False) for shift in shifts]
+    forward = [shift_digits(shift, True) for shift in shifts]
     backward = [shift_digits(blocks - shift, False) for shift in shifts]
-    marks_at = [shift_digits(blocks - shift, True) for shift in shifts[2:]]
 
     bit_count = 32 // lax.axis_size("grp")
     item_bits = own_half * bit_count + lax.broadcasted_iota(jnp.int32, (1, 1, items), 2) // (items // bit_count)
@@ -230,29 +245,39 @@
     own_marks = jnp.stack(own_marks)
     other_marks = partner(jnp.stack(away_marks))
 
-    def gather(shard, copies, digits, near_shift, extra=(), direct=()):
+    def fetch_items(shard, copies, extra=(), extra_at=()):
         size = shard.shape[0]
-        neighbour = fetched_from(shard, AXES, near_shift)
+        fixed = [fetched_from(shard, AXES, shift) for shift in (near, across)]
+        held = swapped_with_all(copies, "z")
+        free = [taken(held, z_at, 0, size) for _, z_at in forward[2:]]
+        *free, fixed[0], fixed[1] = lax.optimization_barrier((*free, *fixed))
+        y_steps, x_steps = zip(*[steps_to(at) for at, _ in [*forward[2:], *extra_at]])
+        parts = stepped(stepped([*free, *extra], "y", y_steps), "x", x_steps)
+        own = [*fixed, *parts[:2]]
+        return own, [partner(value) for value in own], parts[2:]
+
+    def fetch_users(shard, copies, marks, fixed_marks):
+        size = shard.shape[0]
+        direct = [fetched_from(shard, AXES, -near)]
+        direct += [fetched_from(m, AXES, -shift) for m, shift in zip(fixed_marks, (near, across))]
         held = swapped_with_all(copies, ("x", "y"))
-        pieces = [neighbour] + [taken(held, at, 0, size) for at, _ in digits[1:]]
-        moving = jnp.concatenate([*pieces[2:], *extra], axis=0)
-        moving, pieces[0], *direct = lax.optimization_barrier((moving, neighbour, *direct))
-        ring_held = swapped_with_all(jnp.broadcast_to(moving, (ring, *moving.shape)), "z")
-        for k in (2, 3):
-            pieces[k] = taken(ring_held, digits[k][1], (k - 2) * size, size)
-        return held, ring_held, pieces, [partner(piece) for piece in pieces], direct
-
-    copies = jnp.broadcast_to(item_start, (plane, *item_start.shape))
-    sent = [fetched_from(m, AXES, -shift) for m, shift in zip(marks, (near, across))]
-    _, held, own, other, direct_marks = gather(item_start, copies, forward, near, marks[2:], sent)
-    moved = [taken(held, z_at, 2 * items + k * users, users) for k, (_, z_at) in enumerate(marks_at)]
-    first_users, copies = solve_users(own, other, own_marks, other_marks, plane, moved)
-
-    held, _, own, other, _ = gather(first_users, copies, backward, -near)
-    moved = [taken(held, at, rows + k * users, users) for k, (at, _) in enumerate(marks_at)]
-    item_factors, copies = solve_items(own, other, [*direct_marks, *moved], plane)
-
-    _, _, own, other, _ = gather(item_factors, copies, forward, near)
+        pieces = [taken(held, at, 0, size) for at, _ in backward[1:]]
+        moving = jnp.concatenate([*pieces[1:], *marks], axis=0)
+        moving, *direct = lax.optimization_barrier((moving, *direct))
+        held = swapped_with_all(jnp.broadcast_to(moving, (ring, *moving.shape)), "z")
+        free = [taken(held, z_at, k * size, size) for k, (_, z_at) in enumerate(backward[2:])]
+        moved = [taken(held, z_at, 2 * size + k * users, users) for k, (_, z_at) in enumerate(backward[2:])]
+        own = [direct[0], pieces[0], *free]
+        return own, [partner(value) for value in own], [*direct[1:], *moved]
+
+    copies = jnp.broadcast_to(item_start, (ring, *item_start.shape))
+    own, other, moved = fetch_items(item_start, copies, marks[2:], backward[2:])
+    first_users, copies = solve_users(own, other, own_marks, other_marks, plane)
+
+    own, other, moved = fetch_users(first_users, copies, moved, marks[:2])
+    item_factors, copies = solve_items(own, other, moved, ring)
+
+    own, other, _ = fetch_items(item_factors, copies)
     (user_factors,) = solve_users(own, other, own_marks, other_marks)
     return (user_factors, item_factors)
 

time: 146 us -> 134 us (0.918)
  waiting for transfers between devices: 58.2 us -> 36.8 us
  starting transfers between devices: 57.5 us -> 68.9 us
  local copies, waits for them, and re-layouts: 10.9 us -> 8.52 us
    all_to_all x6 -> x4, waiting for transfers between devices: 53.7 us -> 25.6 us  [swapped_with_all(): return lax.all_to_all(copies, axes, split_axis=0, concat_axis=0, tiled=True)]
    ppermute x18 -> x32, starting transfers between devices: 32.4 us -> 50.9 us  [fetched_from(): lax.ppermute(value, axis, [((target + steps) % count, target) for target...]
    all_to_all x6 -> x4, starting transfers between devices: 25.1 us -> 18 us  [swapped_with_all(): return lax.all_to_all(copies, axes, split_axis=0, concat_axis=0, tiled=True)]
    ppermute x18 -> x32, waiting for transfers between devices: 4.45 us -> 11.3 us  [fetched_from(): lax.ppermute(value, axis, [((target + steps) % count, target) for target...]
    broadcast_in_dim x4 -> x2, local copies, waits for them, and re-layouts: 4.28 us -> 2.33 us  [the longest x1 1.53 us: body(): copies = jnp.broadcast_to(item_start, (ring, *item_start.shape))]
    unnamed x69 -> x70, local copies, waits for them, and re-layouts: 4.68 us -> 4.88 us
  transfers between devices with their start and end apart: 24 -> 36, of which waited for: 11 -> 17; matrix products, arithmetic and copies ran while one was open for 3% -> 3% of each run, Pallas kernels for 0% -> 4%
where the time goes in v5:
time: 134 us; the launch traced here: 133 us
  starting transfers between devices  68.9 us (51%)
  waiting for transfers between devices  36.8 us (27%)
  Pallas kernels  13.6 us (10%)
  local copies, waits for them, and re-layouts  8.52 us (6%)
  between operations  3.84 us (3%)
    ppermute x32, starting transfers between devices, fetched_from(): lax.ppermute(value, axis, [((target + steps) % count, target) for target...  50.9 us
    all_to_all x4, waiting for transfers between devices, swapped_with_all(): return lax.all_to_all(copies, axes, split_axis=0, concat_axis=0, tiled=True)  25.6 us
    all_to_all x4, starting transfers between devices, swapped_with_all(): return lax.all_to_all(copies, axes, split_axis=0, concat_axis=0, tiled=True)  18 us
    ppermute x32, waiting for transfers between devices, fetched_from(): lax.ppermute(value, axis, [((target + steps) % count, target) for target...  11.3 us
    pallas_call x2, Pallas kernels, solve_users(): pl.pallas_call(functools.partial(users_kernel, tiles=tiles, copies=copies...  10.5 us
    unnamed x70, local copies, waits for them, and re-layouts  4.88 us
    pallas_call x1, Pallas kernels, solve_items(): pl.pallas_call(items_kernel, out_shape=(jax.ShapeDtypeStruct((items, rank...  3.13 us
  transfers between devices with their start and end apart: 36, of which 17 were waited for; matrix products, arithmetic and copies ran while one was open for 3% of the time, Pallas kernels for 4%

profile of v5, /device:TPU:1, one launch (start us, length us, event | category | flops | bytes accessed | tf_op | source)
XLA Modules:
  0.0 132.6 jit_solution(16276391870863022950)
XLA Ops:
  0.6 2.5 %collective-permute-start = (bf16[128,128]{1,0:T(8,128)(2,1)}, bf16[128,128]{1,0:T(8,128)(2,1)S(1)}, u32[]{:S(2)}, u32[]{:S(2)}) collective-permute-start(bf16[128,128]{1,0:T(8,128)(2,1)} %param.4), channel_id=1, source_target_pairs={{254,0},{0,2},{2,4},{4,6},{6,8},{8,10},{10,12},{12,14},{14,16},{16... | collective-permute-start | bytes 98312 | tf_op jit(solution)/shard_map/ppermute | solution.py:162
  3.2 2.7 %collective-permute-start.1 = (bf16[128,128]{1,0:T(8,128)(2,1)}, bf16[128,128]{1,0:T(8,128)(2,1)S(1)}, u32[]{:S(2)}, u32[]{:S(2)}) collective-permute-start(bf16[128,128]{1,0:T(8,128)(2,1)} %param.4), channel_id=1, source_target_pairs={{128,0},{130,2},{132,4},{134,6},{136,8},{138,10},{140,12},{142,14}... | collective-permute-start | bytes 98312 | tf_op jit(solution)/shard_map/ppermute | solution.py:162
  5.9 1.5 %broadcast_in_dim.11 = bf16[8,128,128]{2,1,0:T(8,128)(2,1)} broadcast(bf16[128,128]{1,0:T(8,128)(2,1)} %param.4), dimensions={1,2} | broadcast | bytes 294912 | tf_op jit(solution)/shard_map/broadcast_in_dim | solution.py:273
  7.4 7.3 %all-to-all-start = ((bf16[8,128,128]{2,1,0:T(8,128)(2,1)}), bf16[8,128,128]{2,1,0:T(8,128)(2,1)S(1)}, u32[]{:S(2)}, u32[]{:S(2)}) async-start(bf16[8,128,128]{2,1,0:T(8,128)(2,1)} %broadcast_in_dim.11), calls=%async_computation | async-start | bytes 524288 | tf_op jit(solution)/shard_map/all_to_all | solution.py:155
  14.7 0.6 copy-done.28
  15.4 0.6 fusion.26
  18.8 0.7 copy-done.5
  19.7 5.2 %all-to-all-done = bf16[8,128,128]{2,1,0:T(8,128)(2,1)S(1)} async-done(((bf16[8,128,128]{2,1,0:T(8,128)(2,1)}), bf16[8,128,128]{2,1,0:T(8,128)(2,1)S(1)}, u32[]{:S(2)}, u32[]{:S(2)}) %all-to-all-start) | async-done | bytes 262176 | tf_op jit(solution)/shard_map/all_to_all | solution.py:155
  25.1 2.8 %collective-permute-start.4 = (bf16[384,128]{1,0:T(8,128)(2,1)S(1)}, bf16[384,128]{1,0:T(8,128)(2,1)S(1)}, u32[]{:S(2)}, u32[]{:S(2)}) collective-permute-start(bf16[384,128]{1,0:T(8,128)(2,1)S(1)} %get-tuple-element.34), channel_id=1, source_target_pairs={{16,0},{32,16},{48,32},{0,48},{17,1},{33,17},{49,33},{1,49},{18,2}... | collective-permute-start | bytes 294920 | tf_op jit(solution)/shard_map/ppermute | solution.py:162
  28.2 0.7 collective-permute-start.2
  28.9 3.5 %collective-permute-start.8 = (bf16[128,128]{1,0:T(8,128)(2,1)S(1)}, bf16[128,128]{1,0:T(8,128)(2,1)S(1)}, u32[]{:S(2)}, u32[]{:S(2)}) collective-permute-start(bf16[128,128]{1,0:T(8,128)(2,1)S(1)} %collective-permute-done.refs_0_), channel_id=1, source_target_pairs={{1,0},{0,1},{3,2},{2,3},{5,4},{4,5},{7,6},{6,7},{9,8},{8,9},{11,10... | collective-permute-start | bytes 98312 | tf_op jit(solution)/shard_map/ppermute | solution.py:162
  33.0 1.0 collective-permute-done.2
  34.0 0.9 collective-permute-start.7
  34.9 1.2 collective-permute-start.6
  36.2 1.4 %collective-permute-done.7 = bf16[384,128]{1,0:T(8,128)(2,1)S(1)} collective-permute-done((bf16[384,128]{1,0:T(8,128)(2,1)S(1)}, bf16[384,128]{1,0:T(8,128)(2,1)S(1)}, u32[]{:S(2)}, u32[]{:S(2)}) %collective-permute-start.7) | collective-permute-done | bytes 98336 | tf_op jit(solution)/shard_map/ppermute | solution.py:162
  37.6 5.2 %collective-permute-start.12 = (bf16[4,32,128]{2,1,0:T(8,128)(2,1)S(1)}, bf16[4,32,128]{2,1,0:T(8,128)(2,1)S(1)}, u32[]{:S(2)}, u32[]{:S(2)}) collective-permute-start(bf16[4,32,128]{2,1,0:T(8,128)(2,1)S(1)} %pad_maximum_fusion.4), channel_id=1, source_target_pairs={{1,0},{0,1},{3,2},{2,3},{5,4},{4,5},{7,6},{6,7},{9,8},{8,9},{11,10... | collective-permute-start | bytes 98312 | tf_op jit(solution)/shard_map/ppermute | solution.py:162
  42.8 3.9 %collective-permute-start.10 = (bf16[128,128]{1,0:T(8,128)(2,1)S(1)}, bf16[128,128]{1,0:T(8,128)(2,1)S(1)}, u32[]{:S(2)}, u32[]{:S(2)}) collective-permute-start(bf16[128,128]{1,0:T(8,128)(2,1)S(1)} %get-tuple-element.47.refs_2_), channel_id=1, source_target_pairs={{1,0},{0,1},{3,2},{2,3},{5,4},{4,5},{7,6},{6,7},{9,8},{8,9},{11,10... | collective-permute-start | bytes 98312 | tf_op jit(solution)/shard_map/ppermute | solution.py:162
  46.9 0.6 pad_maximum_fusion.3.refs_8_
  47.6 1.2 collective-permute-start.15
  50.0 5.3 %users.2 = (bf16[32,128]{1,0:T(8,128)(2,1)}, bf16[16,32,128]{2,1,0:T(8,128)(2,1)}) custom-call(bf16[128,128]{1,0:T(8,128)(2,1)} %copy-done.6, bf16[128,128]{1,0:T(8,128)(2,1)} %copy-done.7, bf16[128,128]{1,0:T(8,128)(2,1)} %copy-done.1, bf16[128,128]{1,0:T(8,128)(2,1)} %copy-done, bf16[128,128]{1,0:T(8,128)(2,1)} %copy-done.8, bf16[128,128]{1,0:T(8,128)(2,1)} %copy-done.9, ...), custom_call_target="tpu_custom_call" | custom-call | tf_op jit(solution)/shard_map/users/pallas_call | solution.py:123
  55.3 3.7 %all-to-all-start.1 = ((bf16[16,32,128]{2,1,0:T(8,128)(2,1)}), bf16[16,32,128]{2,1,0:T(8,128)(2,1)S(1)}, u32[]{:S(2)}, u32[]{:S(2)}) async-start(bf16[16,32,128]{2,1,0:T(8,128)(2,1)} %get-tuple-element.22), calls=%async_computation.1 | async-start | bytes 262144 | tf_op jit(solution)/shard_map/all_to_all | solution.py:155
  59.1 0.7 copy-done.31
  59.7 4.7 %collective-permute-start.13 = (bf16[32,128]{1,0:T(8,128)(2,1)S(1)}, bf16[32,128]{1,0:T(8,128)(2,1)S(1)}, u32[]{:S(2)}, u32[]{:S(2)}) collective-permute-start(bf16[32,128]{1,0:T(8,128)(2,1)S(1)} %copy-done.31), channel_id=1, source_target_pairs={{2,0},{4,2},{6,4},{8,6},{10,8},{12,10},{14,12},{16,14},{18,16},{20... | collective-permute-start | bytes 24584 | tf_op jit(solution)/shard_map/ppermute | solution.py:162
  64.4 1.4 %all-to-all-done.1 = bf16[16,32,128]{2,1,0:T(8,128)(2,1)S(1)} async-done(((bf16[16,32,128]{2,1,0:T(8,128)(2,1)}), bf16[16,32,128]{2,1,0:T(8,128)(2,1)S(1)}, u32[]{:S(2)}, u32[]{:S(2)}) %all-to-all-start.1) | async-done | bytes 131104 | tf_op jit(solution)/shard_map/all_to_all | solution.py:155
  66.0 0.8 broadcast_in_dim.13
  66.8 3.5 %all-to-all-start.2 = ((bf16[8,192,128]{2,1,0:T(8,128)(2,1)}), bf16[8,192,128]{2,1,0:T(8,128)(2,1)S(1)}, u32[]{:S(2)}, u32[]{:S(2)}) async-start(bf16[8,192,128]{2,1,0:T(8,128)(2,1)} %broadcast_in_dim.13), calls=%async_computation.2 | async-start | bytes 786432 | tf_op jit(solution)/shard_map/all_to_all | solution.py:155
  70.2 2.6 %collective-permute-start.16 = (bf16[32,128]{1,0:T(8,128)(2,1)S(1)}, bf16[32,128]{1,0:T(8,128)(2,1)S(1)}, u32[]{:S(2)}, u32[]{:S(2)}) collective-permute-start(bf16[32,128]{1,0:T(8,128)(2,1)S(1)} %collective-permute-done.13.refs_0_), channel_id=1, source_target_pairs={{1,0},{0,1},{3,2},{2,3},{5,4},{4,5},{7,6},{6,7},{9,8},{8,9},{11,10... | collective-permute-start | bytes 24584 | tf_op jit(solution)/shard_map/ppermute | solution.py:162
  73.0 9.1 %all-to-all-done.2 = bf16[8,192,128]{2,1,0:T(8,128)(2,1)S(1)} async-done(((bf16[8,192,128]{2,1,0:T(8,128)(2,1)}), bf16[8,192,128]{2,1,0:T(8,128)(2,1)S(1)}, u32[]{:S(2)}, u32[]{:S(2)}) %all-to-all-start.2) | async-done | bytes 393248 | tf_op jit(solution)/shard_map/all_to_all | solution.py:155
  82.1 3.7 %collective-permute-start.18 = (bf16[32,128]{1,0:T(8,128)(2,1)S(1)}, bf16[32,128]{1,0:T(8,128)(2,1)S(1)}, u32[]{:S(2)}, u32[]{:S(2)}) collective-permute-start(bf16[32,128]{1,0:T(8,128)(2,1)S(1)} %get-tuple-element.45.refs_2_), channel_id=1, source_target_pairs={{1,0},{0,1},{3,2},{2,3},{5,4},{4,5},{7,6},{6,7},{9,8},{8,9},{11,10... | collective-permute-start | bytes 24584 | tf_op jit(solution)/shard_map/ppermute | solution.py:162
  85.9 0.6 dynamic-slice_bitcast_fusion.4
  87.6 3.1 %items.1 = (bf16[128,128]{1,0:T(8,128)(2,1)}, bf16[8,128,128]{2,1,0:T(8,128)(2,1)}) custom-call(bf16[32,128]{1,0:T(8,128)(2,1)} %copy-done.23, bf16[32,128]{1,0:T(8,128)(2,1)} %copy-done.12, bf16[32,128]{1,0:T(8,128)(2,1)} %copy-done.14, bf16[32,128]{1,0:T(8,128)(2,1)} %copy-done.13, bf16[32,128]{1,0:T(8,128)(2,1)} %copy-done.24, ...), custom_call_target="tpu_custom_call" | custom-call | tf_op jit(solution)/shard_map/items/pallas_call | solution.py:141
  90.7 3.5 %all-to-all-start.3 = ((bf16[8,128,128]{2,1,0:T(8,128)(2,1)}), bf16[8,128,128]{2,1,0:T(8,128)(2,1)S(1)}, u32[]{:S(2)}, u32[]{:S(2)}) async-start(bf16[8,128,128]{2,1,0:T(8,128)(2,1)} %get-tuple-element.28), calls=%async_computation.3 | async-start | bytes 524288 | tf_op jit(solution)/shard_map/all_to_all | solution.py:155
  94.2 1.4 %collective-permute-start.20 = (bf16[128,128]{1,0:T(8,128)(2,1)S(1)}, bf16[128,128]{1,0:T(8,128)(2,1)S(1)}, u32[]{:S(2)}, u32[]{:S(2)}) collective-permute-start(bf16[128,128]{1,0:T(8,128)(2,1)S(1)} %copy-done.30), channel_id=1, source_target_pairs={{254,0},{0,2},{2,4},{4,6},{6,8},{8,10},{10,12},{12,14},{14,16},{16... | collective-permute-start | bytes 98312 | tf_op jit(solution)/shard_map/ppermute | solution.py:162
  95.6 1.1 collective-permute-start.21
  96.7 9.8 %all-to-all-done.3 = bf16[8,128,128]{2,1,0:T(8,128)(2,1)S(1)} async-done(((bf16[8,128,128]{2,1,0:T(8,128)(2,1)}), bf16[8,128,128]{2,1,0:T(8,128)(2,1)S(1)}, u32[]{:S(2)}, u32[]{:S(2)}) %all-to-all-start.3) | async-done | bytes 262176 | tf_op jit(solution)/shard_map/all_to_all | solution.py:155
  106.6 1.3 collective-permute-start.24
  107.8 0.8 collective-permute-start.23
  108.7 1.1 collective-permute-done.24
  109.8 2.7 %collective-permute-done.23 = bf16[256,128]{1,0:T(8,128)(2,1)S(1)} collective-permute-done((bf16[256,128]{1,0:T(8,128)(2,1)S(1)}, bf16[256,128]{1,0:T(8,128)(2,1)S(1)}, u32[]{:S(2)}, u32[]{:S(2)}) %collective-permute-start.23) | collective-permute-done | bytes 65568 | tf_op jit(solution)/shard_map/ppermute | solution.py:162
  112.5 1.1 collective-permute-done.22
  113.6 3.5 %collective-permute-start.27 = (bf16[256,128]{1,0:T(8,128)(2,1)S(1)}, bf16[256,128]{1,0:T(8,128)(2,1)S(1)}, u32[]{:S(2)}, u32[]{:S(2)}) collective-permute-start(bf16[256,128]{1,0:T(8,128)(2,1)S(1)} %pad_maximum_fusion.1), channel_id=1, source_target_pairs={{64,0},{128,64},{192,128},{0,192},{65,1},{129,65},{193,129},{1,193... | collective-permute-start | bytes 196616 | tf_op jit(solution)/shard_map/ppermute | solution.py:162
  117.0 0.7 collective-permute-start.25
  117.7 2.3 %collective-permute-start.28 = (bf16[128,128]{1,0:T(8,128)(2,1)S(1)}, bf16[128,128]{1,0:T(8,128)(2,1)S(1)}, u32[]{:S(2)}, u32[]{:S(2)}) collective-permute-start(bf16[128,128]{1,0:T(8,128)(2,1)S(1)} %collective-permute-done.20.refs_0_), channel_id=1, source_target_pairs={{1,0},{0,1},{3,2},{2,3},{5,4},{4,5},{7,6},{6,7},{9,8},{8,9},{11,10... | collective-permute-start | bytes 98312 | tf_op jit(solution)/shard_map/ppermute | solution.py:162
  120.1 1.7 %collective-permute-done.26 = bf16[256,128]{1,0:T(8,128)(2,1)S(1)} collective-permute-done((bf16[256,128]{1,0:T(8,128)(2,1)S(1)}, bf16[256,128]{1,0:T(8,128)(2,1)S(1)}, u32[]{:S(2)}, u32[]{:S(2)}) %collective-permute-start.26) | collective-permute-done | bytes 65568 | tf_op jit(solution)/shard_map/ppermute | solution.py:162
  122.1 3.2 %collective-permute-start.30 = (bf16[128,128]{1,0:T(8,128)(2,1)S(1)}, bf16[128,128]{1,0:T(8,128)(2,1)S(1)}, u32[]{:S(2)}, u32[]{:S(2)}) collective-permute-start(bf16[128,128]{1,0:T(8,128)(2,1)S(1)} %get-tuple-element.59.refs_2_), channel_id=1, source_target_pairs={{1,0},{0,1},{3,2},{2,3},{5,4},{4,5},{7,6},{6,7},{9,8},{8,9},{11,10... | collective-permute-start | bytes 98312 | tf_op jit(solution)/shard_map/ppermute | solution.py:162
  125.4 0.7 collective-permute-done.30.refs_6_
  126.8 0.6 copy-done.20
  127.4 5.2 %users.3 = bf16[32,128]{1,0:T(8,128)(2,1)} custom-call(bf16[128,128]{1,0:T(8,128)(2,1)} %copy-done.15, bf16[128,128]{1,0:T(8,128)(2,1)} %copy-done.16, bf16[128,128]{1,0:T(8,128)(2,1)} %copy-done.4, bf16[128,128]{1,0:T(8,128)(2,1)} %copy-done.3, bf16[128,128]{1,0:T(8,128)(2,1)} %copy-done.17, bf16[128,128]{1,0:T(8,128)(2,1)} %copy-done.18, ...), custom_call_target="tpu_custom_call" | custom-call | tf_op jit(solution)/shard_map/users/pallas_call | solution.py:123
  (123 shorter events, 5.2 us)
Async XLA Ops:
  0.6 24.3 %collective-permute-start = (bf16[128,128]{1,0:T(8,128)(2,1)}, bf16[128,128]{1,0:T(8,128)(2,1)S(1)}, u32[]{:S(2)}, u32[]{:S(2)}) collective-permute-start(bf16[128,128]{1,0:T(8,128)(2,1)} %param.4), channel_id=1, source_target_pairs={{254,0},{0,2},{2,4},{4,6},{6,8},{8,10},{10,12},{12,14},{14,16},{16... | collective-permute-start | bytes 98312 | tf_op jit(solution)/shard_map/ppermute | solution.py:162
  3.2 21.8 %collective-permute-start.1 = (bf16[128,128]{1,0:T(8,128)(2,1)}, bf16[128,128]{1,0:T(8,128)(2,1)S(1)}, u32[]{:S(2)}, u32[]{:S(2)}) collective-permute-start(bf16[128,128]{1,0:T(8,128)(2,1)} %param.4), channel_id=1, source_target_pairs={{128,0},{130,2},{132,4},{134,6},{136,8},{138,10},{140,12},{142,14}... | collective-permute-start | bytes 98312 | tf_op jit(solution)/shard_map/ppermute | solution.py:162
  7.4 17.5 %all-to-all-start = ((bf16[8,128,128]{2,1,0:T(8,128)(2,1)}), bf16[8,128,128]{2,1,0:T(8,128)(2,1)S(1)}, u32[]{:S(2)}, u32[]{:S(2)}) async-start(bf16[8,128,128]{2,1,0:T(8,128)(2,1)} %broadcast_in_dim.11), calls=%async_computation | async-start | bytes 524288 | tf_op jit(solution)/shard_map/all_to_all | solution.py:155
  24.9 4.0 %copy-start.6 = (bf16[128,128]{1,0:T(8,128)(2,1)}, bf16[128,128]{1,0:T(8,128)(2,1)S(1)}, u32[]{:S(2)}) copy-start(bf16[128,128]{1,0:T(8,128)(2,1)S(1)} %collective-permute-done.refs_0_) | copy-start | bytes 98308
  24.9 7.5 %copy-start.7 = (bf16[128,128]{1,0:T(8,128)(2,1)}, bf16[128,128]{1,0:T(8,128)(2,1)S(1)}, u32[]{:S(2)}) copy-start(bf16[128,128]{1,0:T(8,128)(2,1)S(1)} %collective-permute-done.1.refs_1_) | copy-start | bytes 98308
  25.1 7.5 %collective-permute-start.4 = (bf16[384,128]{1,0:T(8,128)(2,1)S(1)}, bf16[384,128]{1,0:T(8,128)(2,1)S(1)}, u32[]{:S(2)}, u32[]{:S(2)}) collective-permute-start(bf16[384,128]{1,0:T(8,128)(2,1)S(1)} %get-tuple-element.34), channel_id=1, source_target_pairs={{16,0},{32,16},{48,32},{0,48},{17,1},{33,17},{49,33},{1,49},{18,2}... | collective-permute-start | bytes 294920 | tf_op jit(solution)/shard_map/ppermute | solution.py:162
  27.9 5.1 %collective-permute-start.3 = (bf16[384,128]{1,0:T(8,128)(2,1)S(1)}, bf16[384,128]{1,0:T(8,128)(2,1)S(1)}, u32[]{:S(2)}, u32[]{:S(2)}) collective-permute-start(bf16[384,128]{1,0:T(8,128)(2,1)S(1)} %get-tuple-element.34), channel_id=1, source_target_pairs={{32,0},{48,16},{0,32},{16,48},{33,1},{49,17},{1,33},{17,49},{34,2}... | collective-permute-start | bytes 294920 | tf_op jit(solution)/shard_map/ppermute | solution.py:162
  28.2 5.7 %collective-permute-start.2 = (bf16[384,128]{1,0:T(8,128)(2,1)S(1)}, bf16[384,128]{1,0:T(8,128)(2,1)S(1)}, u32[]{:S(2)}, u32[]{:S(2)}) collective-permute-start(bf16[384,128]{1,0:T(8,128)(2,1)S(1)} %get-tuple-element.34), channel_id=1, source_target_pairs={{48,0},{0,16},{16,32},{32,48},{49,1},{1,17},{17,33},{33,49},{50,2}... | collective-permute-start | bytes 294920 | tf_op jit(solution)/shard_map/ppermute | solution.py:162
  28.9 18.5 %collective-permute-start.8 = (bf16[128,128]{1,0:T(8,128)(2,1)S(1)}, bf16[128,128]{1,0:T(8,128)(2,1)S(1)}, u32[]{:S(2)}, u32[]{:S(2)}) collective-permute-start(bf16[128,128]{1,0:T(8,128)(2,1)S(1)} %collective-permute-done.refs_0_), channel_id=1, source_target_pairs={{1,0},{0,1},{3,2},{2,3},{5,4},{4,5},{7,6},{6,7},{9,8},{8,9},{11,10... | collective-permute-start | bytes 98312 | tf_op jit(solution)/shard_map/ppermute | solution.py:162
  32.4 15.2 %collective-permute-start.9 = (bf16[128,128]{1,0:T(8,128)(2,1)S(1)}, bf16[128,128]{1,0:T(8,128)(2,1)S(1)}, u32[]{:S(2)}, u32[]{:S(2)}) collective-permute-start(bf16[128,128]{1,0:T(8,128)(2,1)S(1)} %collective-permute-done.1.refs_1_), channel_id=1, source_target_pairs={{1,0},{0,1},{3,2},{2,3},{5,4},{4,5},{7,6},{6,7},{9,8},{8,9},{11,10... | collective-permute-start | bytes 98312 | tf_op jit(solution)/shard_map/ppermute | solution.py:162
  34.0 3.6 %collective-permute-start.7 = (bf16[384,128]{1,0:T(8,128)(2,1)S(1)}, bf16[384,128]{1,0:T(8,128)(2,1)S(1)}, u32[]{:S(2)}, u32[]{:S(2)}) collective-permute-start(bf16[384,128]{1,0:T(8,128)(2,1)S(1)} %pad_maximum_fusion), channel_id=1, source_target_pairs={{64,0},{128,64},{192,128},{0,192},{65,1},{129,65},{193,129},{1,193... | collective-permute-start | bytes 294920 | tf_op jit(solution)/shard_map/ppermute | solution.py:162
  34.9 7.8 %collective-permute-start.6 = (bf16[384,128]{1,0:T(8,128)(2,1)S(1)}, bf16[384,128]{1,0:T(8,128)(2,1)S(1)}, u32[]{:S(2)}, u32[]{:S(2)}) collective-permute-start(bf16[384,128]{1,0:T(8,128)(2,1)S(1)} %pad_maximum_fusion), channel_id=1, source_target_pairs={{128,0},{192,64},{0,128},{64,192},{129,1},{193,65},{1,129},{65,193... | collective-permute-start | bytes 294920 | tf_op jit(solution)/shard_map/ppermute | solution.py:162
  36.2 6.6 %collective-permute-start.5 = (bf16[384,128]{1,0:T(8,128)(2,1)S(1)}, bf16[384,128]{1,0:T(8,128)(2,1)S(1)}, u32[]{:S(2)}, u32[]{:S(2)}) collective-permute-start(bf16[384,128]{1,0:T(8,128)(2,1)S(1)} %pad_maximum_fusion), channel_id=1, source_target_pairs={{192,0},{0,64},{64,128},{128,192},{193,1},{1,65},{65,129},{129,193... | collective-permute-start | bytes 294920 | tf_op jit(solution)/shard_map/ppermute | solution.py:162
  37.6 11.2 %collective-permute-start.12 = (bf16[4,32,128]{2,1,0:T(8,128)(2,1)S(1)}, bf16[4,32,128]{2,1,0:T(8,128)(2,1)S(1)}, u32[]{:S(2)}, u32[]{:S(2)}) collective-permute-start(bf16[4,32,128]{2,1,0:T(8,128)(2,1)S(1)} %pad_maximum_fusion.4), channel_id=1, source_target_pairs={{1,0},{0,1},{3,2},{2,3},{5,4},{4,5},{7,6},{6,7},{9,8},{8,9},{11,10... | collective-permute-start | bytes 98312 | tf_op jit(solution)/shard_map/ppermute | solution.py:162
  42.8 4.7 %copy-start = (bf16[128,128]{1,0:T(8,128)(2,1)}, bf16[128,128]{1,0:T(8,128)(2,1)S(1)}, u32[]{:S(2)}) copy-start(bf16[128,128]{1,0:T(8,128)(2,1)S(1)} %get-tuple-element.46.refs_3_) | copy-start | bytes 98308
  42.8 4.7 %copy-start.1 = (bf16[128,128]{1,0:T(8,128)(2,1)}, bf16[128,128]{1,0:T(8,128)(2,1)S(1)}, u32[]{:S(2)}) copy-start(bf16[128,128]{1,0:T(8,128)(2,1)S(1)} %get-tuple-element.47.refs_2_) | copy-start | bytes 98308
  42.8 6.0 %collective-permute-start.10 = (bf16[128,128]{1,0:T(8,128)(2,1)S(1)}, bf16[128,128]{1,0:T(8,128)(2,1)S(1)}, u32[]{:S(2)}, u32[]{:S(2)}) collective-permute-start(bf16[128,128]{1,0:T(8,128)(2,1)S(1)} %get-tuple-element.47.refs_2_), channel_id=1, source_target_pairs={{1,0},{0,1},{3,2},{2,3},{5,4},{4,5},{7,6},{6,7},{9,8},{8,9},{11,10... | collective-permute-start | bytes 98312 | tf_op jit(solution)/shard_map/ppermute | solution.py:162
  46.8 2.0 %collective-permute-start.11 = (bf16[128,128]{1,0:T(8,128)(2,1)S(1)}, bf16[128,128]{1,0:T(8,128)(2,1)S(1)}, u32[]{:S(2)}, u32[]{:S(2)}) collective-permute-start(bf16[128,128]{1,0:T(8,128)(2,1)S(1)} %get-tuple-element.46.refs_3_), channel_id=1, source_target_pairs={{1,0},{0,1},{3,2},{2,3},{5,4},{4,5},{7,6},{6,7},{9,8},{8,9},{11,10... | collective-permute-start | bytes 98312 | tf_op jit(solution)/shard_map/ppermute | solution.py:162
  47.5 18.4 %collective-permute-start.14 = (bf16[64,128]{1,0:T(8,128)(2,1)S(1)}, bf16[64,128]{1,0:T(8,128)(2,1)S(1)}, u32[]{:S(2)}, u32[]{:S(2)}) collective-permute-start(bf16[64,128]{1,0:T(8,128)(2,1)S(1)} %pad_maximum_fusion.5), channel_id=1, source_target_pairs={{2,0},{4,2},{6,4},{8,6},{10,8},{12,10},{14,12},{16,14},{18,16},{20... | collective-permute-start | bytes 49160 | tf_op jit(solution)/shard_map/ppermute | solution.py:162
  47.6 18.3 %collective-permute-start.15 = (bf16[64,128]{1,0:T(8,128)(2,1)S(1)}, bf16[64,128]{1,0:T(8,128)(2,1)S(1)}, u32[]{:S(2)}, u32[]{:S(2)}) collective-permute-start(bf16[64,128]{1,0:T(8,128)(2,1)S(1)} %pad_maximum_fusion.6), channel_id=1, source_target_pairs={{128,0},{130,2},{132,4},{134,6},{136,8},{138,10},{140,12},{142,14}... | collective-permute-start | bytes 49160 | tf_op jit(solution)/shard_map/ppermute | solution.py:162
  55.3 10.6 %all-to-all-start.1 = ((bf16[16,32,128]{2,1,0:T(8,128)(2,1)}), bf16[16,32,128]{2,1,0:T(8,128)(2,1)S(1)}, u32[]{:S(2)}, u32[]{:S(2)}) async-start(bf16[16,32,128]{2,1,0:T(8,128)(2,1)} %get-tuple-element.22), calls=%async_computation.1 | async-start | bytes 262144 | tf_op jit(solution)/shard_map/all_to_all | solution.py:155
  59.7 6.2 %collective-permute-start.13 = (bf16[32,128]{1,0:T(8,128)(2,1)S(1)}, bf16[32,128]{1,0:T(8,128)(2,1)S(1)}, u32[]{:S(2)}, u32[]{:S(2)}) collective-permute-start(bf16[32,128]{1,0:T(8,128)(2,1)S(1)} %copy-done.31), channel_id=1, source_target_pairs={{2,0},{4,2},{6,4},{8,6},{10,8},{12,10},{14,12},{16,14},{18,16},{20... | collective-permute-start | bytes 24584 | tf_op jit(solution)/shard_map/ppermute | solution.py:162
  65.9 7.0 %copy-start.12 = (bf16[32,128]{1,0:T(8,128)(2,1)}, bf16[32,128]{1,0:T(8,128)(2,1)S(1)}, u32[]{:S(2)}) copy-start(bf16[32,128]{1,0:T(8,128)(2,1)S(1)} %get-tuple-element.62.refs_1_) | copy-start | bytes 24580
  65.9 4.3 %copy-start.23 = (bf16[32,128]{1,0:T(8,128)(2,1)}, bf16[32,128]{1,0:T(8,128)(2,1)S(1)}, u32[]{:S(2)}) copy-start(bf16[32,128]{1,0:T(8,128)(2,1)S(1)} %collective-permute-done.13.refs_0_) | copy-start | bytes 24580
  66.8 15.3 %all-to-all-start.2 = ((bf16[8,192,128]{2,1,0:T(8,128)(2,1)}), bf16[8,192,128]{2,1,0:T(8,128)(2,1)S(1)}, u32[]{:S(2)}, u32[]{:S(2)}) async-start(bf16[8,192,128]{2,1,0:T(8,128)(2,1)} %broadcast_in_dim.13), calls=%async_computation.2 | async-start | bytes 786432 | tf_op jit(solution)/shard_map/all_to_all | solution.py:155
  70.2 16.3 %collective-permute-start.16 = (bf16[32,128]{1,0:T(8,128)(2,1)S(1)}, bf16[32,128]{1,0:T(8,128)(2,1)S(1)}, u32[]{:S(2)}, u32[]{:S(2)}) collective-permute-start(bf16[32,128]{1,0:T(8,128)(2,1)S(1)} %collective-permute-done.13.refs_0_), channel_id=1, source_target_pairs={{1,0},{0,1},{3,2},{2,3},{5,4},{4,5},{7,6},{6,7},{9,8},{8,9},{11,10... | collective-permute-start | bytes 24584 | tf_op jit(solution)/shard_map/ppermute | solution.py:162
  72.9 13.7 %collective-permute-start.17 = (bf16[32,128]{1,0:T(8,128)(2,1)S(1)}, bf16[32,128]{1,0:T(8,128)(2,1)S(1)}, u32[]{:S(2)}, u32[]{:S(2)}) collective-permute-start(bf16[32,128]{1,0:T(8,128)(2,1)S(1)} %get-tuple-element.62.refs_1_), channel_id=1, source_target_pairs={{1,0},{0,1},{3,2},{2,3},{5,4},{4,5},{7,6},{6,7},{9,8},{8,9},{11,10... | collective-permute-start | bytes 24584 | tf_op jit(solution)/shard_map/ppermute | solution.py:162
  82.1 4.4 %copy-start.13 = (bf16[32,128]{1,0:T(8,128)(2,1)}, bf16[32,128]{1,0:T(8,128)(2,1)S(1)}, u32[]{:S(2)}) copy-start(bf16[32,128]{1,0:T(8,128)(2,1)S(1)} %get-tuple-element.44.refs_3_) | copy-start | bytes 24580
  82.1 4.4 %copy-start.14 = (bf16[32,128]{1,0:T(8,128)(2,1)}, bf16[32,128]{1,0:T(8,128)(2,1)S(1)}, u32[]{:S(2)}) copy-start(bf16[32,128]{1,0:T(8,128)(2,1)S(1)} %get-tuple-element.45.refs_2_) | copy-start | bytes 24580
  82.1 4.5 %collective-permute-start.18 = (bf16[32,128]{1,0:T(8,128)(2,1)S(1)}, bf16[32,128]{1,0:T(8,128)(2,1)S(1)}, u32[]{:S(2)}, u32[]{:S(2)}) collective-permute-start(bf16[32,128]{1,0:T(8,128)(2,1)S(1)} %get-tuple-element.45.refs_2_), channel_id=1, source_target_pairs={{1,0},{0,1},{3,2},{2,3},{5,4},{4,5},{7,6},{6,7},{9,8},{8,9},{11,10... | collective-permute-start | bytes 24584 | tf_op jit(solution)/shard_map/ppermute | solution.py:162
  85.8 1.2 collective-permute-start.19
  90.7 15.8 %all-to-all-start.3 = ((bf16[8,128,128]{2,1,0:T(8,128)(2,1)}), bf16[8,128,128]{2,1,0:T(8,128)(2,1)S(1)}, u32[]{:S(2)}, u32[]{:S(2)}) async-start(bf16[8,128,128]{2,1,0:T(8,128)(2,1)} %get-tuple-element.28), calls=%async_computation.3 | async-start | bytes 524288 | tf_op jit(solution)/shard_map/all_to_all | solution.py:155
  94.2 12.3 %collective-permute-start.20 = (bf16[128,128]{1,0:T(8,128)(2,1)S(1)}, bf16[128,128]{1,0:T(8,128)(2,1)S(1)}, u32[]{:S(2)}, u32[]{:S(2)}) collective-permute-start(bf16[128,128]{1,0:T(8,128)(2,1)S(1)} %copy-done.30), channel_id=1, source_target_pairs={{254,0},{0,2},{2,4},{4,6},{6,8},{8,10},{10,12},{12,14},{14,16},{16... | collective-permute-start | bytes 98312 | tf_op jit(solution)/shard_map/ppermute | solution.py:162
  95.6 10.9 %collective-permute-start.21 = (bf16[128,128]{1,0:T(8,128)(2,1)S(1)}, bf16[128,128]{1,0:T(8,128)(2,1)S(1)}, u32[]{:S(2)}, u32[]{:S(2)}) collective-permute-start(bf16[128,128]{1,0:T(8,128)(2,1)S(1)} %copy-done.30), channel_id=1, source_target_pairs={{128,0},{130,2},{132,4},{134,6},{136,8},{138,10},{140,12},{142,14}... | collective-permute-start | bytes 98312 | tf_op jit(solution)/shard_map/ppermute | solution.py:162
  106.5 11.2 %copy-start.15 = (bf16[128,128]{1,0:T(8,128)(2,1)}, bf16[128,128]{1,0:T(8,128)(2,1)S(1)}, u32[]{:S(2)}) copy-start(bf16[128,128]{1,0:T(8,128)(2,1)S(1)} %collective-permute-done.20.refs_0_) | copy-start | bytes 98308
  106.5 13.4 %copy-start.16 = (bf16[128,128]{1,0:T(8,128)(2,1)}, bf16[128,128]{1,0:T(8,128)(2,1)S(1)}, u32[]{:S(2)}) copy-start(bf16[128,128]{1,0:T(8,128)(2,1)S(1)} %collective-permute-done.21.refs_1_) | copy-start | bytes 98308
  106.6 3.2 %collective-permute-start.24 = (bf16[256,128]{1,0:T(8,128)(2,1)S(1)}, bf16[256,128]{1,0:T(8,128)(2,1)S(1)}, u32[]{:S(2)}, u32[]{:S(2)}) collective-permute-start(bf16[256,128]{1,0:T(8,128)(2,1)S(1)} %constant_dynamic-update-slice_fusion.6), channel_id=1, source_target_pairs={{16,0},{32,16},{48,32},{0,48},{17,1},{33,17},{49,33},{1,49},{18,2}... | collective-permute-start | bytes 196616 | tf_op jit(solution)/shard_map/ppermute | solution.py:162
  107.8 4.6 %collective-permute-start.23 = (bf16[256,128]{1,0:T(8,128)(2,1)S(1)}, bf16[256,128]{1,0:T(8,128)(2,1)S(1)}, u32[]{:S(2)}, u32[]{:S(2)}) collective-permute-start(bf16[256,128]{1,0:T(8,128)(2,1)S(1)} %constant_dynamic-update-slice_fusion.6), channel_id=1, source_target_pairs={{32,0},{48,16},{0,32},{16,48},{33,1},{49,17},{1,33},{17,49},{34,2}... | collective-permute-start | bytes 196616 | tf_op jit(solution)/shard_map/ppermute | solution.py:162
  108.6 4.9 %collective-permute-start.22 = (bf16[256,128]{1,0:T(8,128)(2,1)S(1)}, bf16[256,128]{1,0:T(8,128)(2,1)S(1)}, u32[]{:S(2)}, u32[]{:S(2)}) collective-permute-start(bf16[256,128]{1,0:T(8,128)(2,1)S(1)} %constant_dynamic-update-slice_fusion.6), channel_id=1, source_target_pairs={{48,0},{0,16},{16,32},{32,48},{49,1},{1,17},{17,33},{33,49},{50,2}... | collective-permute-start | bytes 196616 | tf_op jit(solution)/shard_map/ppermute | solution.py:162
  113.6 6.5 %collective-permute-start.27 = (bf16[256,128]{1,0:T(8,128)(2,1)S(1)}, bf16[256,128]{1,0:T(8,128)(2,1)S(1)}, u32[]{:S(2)}, u32[]{:S(2)}) collective-permute-start(bf16[256,128]{1,0:T(8,128)(2,1)S(1)} %pad_maximum_fusion.1), channel_id=1, source_target_pairs={{64,0},{128,64},{192,128},{0,192},{65,1},{129,65},{193,129},{1,193... | collective-permute-start | bytes 196616 | tf_op jit(solution)/shard_map/ppermute | solution.py:162
  117.0 4.7 %collective-permute-start.26 = (bf16[256,128]{1,0:T(8,128)(2,1)S(1)}, bf16[256,128]{1,0:T(8,128)(2,1)S(1)}, u32[]{:S(2)}, u32[]{:S(2)}) collective-permute-start(bf16[256,128]{1,0:T(8,128)(2,1)S(1)} %pad_maximum_fusion.1), channel_id=1, source_target_pairs={{128,0},{192,64},{0,128},{64,192},{129,1},{193,65},{1,129},{65,193... | collective-permute-start | bytes 196616 | tf_op jit(solution)/shard_map/ppermute | solution.py:162
  117.0 5.0 %collective-permute-start.25 = (bf16[256,128]{1,0:T(8,128)(2,1)S(1)}, bf16[256,128]{1,0:T(8,128)(2,1)S(1)}, u32[]{:S(2)}, u32[]{:S(2)}) collective-permute-start(bf16[256,128]{1,0:T(8,128)(2,1)S(1)} %pad_maximum_fusion.1), channel_id=1, source_target_pairs={{192,0},{0,64},{64,128},{128,192},{193,1},{1,65},{65,129},{129,193... | collective-permute-start | bytes 196616 | tf_op jit(solution)/shard_map/ppermute | solution.py:162
  117.7 7.7 %collective-permute-start.28 = (bf16[128,128]{1,0:T(8,128)(2,1)S(1)}, bf16[128,128]{1,0:T(8,128)(2,1)S(1)}, u32[]{:S(2)}, u32[]{:S(2)}) collective-permute-start(bf16[128,128]{1,0:T(8,128)(2,1)S(1)} %collective-permute-done.20.refs_0_), channel_id=1, source_target_pairs={{1,0},{0,1},{3,2},{2,3},{5,4},{4,5},{7,6},{6,7},{9,8},{8,9},{11,10... | collective-permute-start | bytes 98312 | tf_op jit(solution)/shard_map/ppermute | solution.py:162
  120.0 5.5 %collective-permute-start.29 = (bf16[128,128]{1,0:T(8,128)(2,1)S(1)}, bf16[128,128]{1,0:T(8,128)(2,1)S(1)}, u32[]{:S(2)}, u32[]{:S(2)}) collective-permute-start(bf16[128,128]{1,0:T(8,128)(2,1)S(1)} %collective-permute-done.21.refs_1_), channel_id=1, source_target_pairs={{1,0},{0,1},{3,2},{2,3},{5,4},{4,5},{7,6},{6,7},{9,8},{8,9},{11,10... | collective-permute-start | bytes 98312 | tf_op jit(solution)/shard_map/ppermute | solution.py:162
  122.1 4.4 %copy-start.3 = (bf16[128,128]{1,0:T(8,128)(2,1)}, bf16[128,128]{1,0:T(8,128)(2,1)S(1)}, u32[]{:S(2)}) copy-start(bf16[128,128]{1,0:T(8,128)(2,1)S(1)} %get-tuple-element.58.refs_3_) | copy-start | bytes 98308
  122.1 4.4 %copy-start.4 = (bf16[128,128]{1,0:T(8,128)(2,1)}, bf16[128,128]{1,0:T(8,128)(2,1)S(1)}, u32[]{:S(2)}) copy-start(bf16[128,128]{1,0:T(8,128)(2,1)S(1)} %get-tuple-element.59.refs_2_) | copy-start | bytes 98308
  122.1 4.1 %collective-permute-start.30 = (bf16[128,128]{1,0:T(8,128)(2,1)S(1)}, bf16[128,128]{1,0:T(8,128)(2,1)S(1)}, u32[]{:S(2)}, u32[]{:S(2)}) collective-permute-start(bf16[128,128]{1,0:T(8,128)(2,1)S(1)} %get-tuple-element.59.refs_2_), channel_id=1, source_target_pairs={{1,0},{0,1},{3,2},{2,3},{5,4},{4,5},{7,6},{6,7},{9,8},{8,9},{11,10... | collective-permute-start | bytes 98312 | tf_op jit(solution)/shard_map/ppermute | solution.py:162
  125.3 1.2 collective-permute-start.31
  (20 other events, 18.4 us)

commit v6 on v5

--- a/solution.py
+++ b/solution.py
@@ -39,16 +39,18 @@
     return answer.astype(jnp.bfloat16)
 
 
-def users_kernel(*refs, tiles, copies):
-    own, other = refs[:tiles], refs[tiles : 2 * tiles]
-    own_marks_ref, other_marks_ref, *rest, factor_t_ref, mask_ref, sums_ref = refs[2 * tiles :]
+def users_kernel(*refs, pieces, copies):
+    own, other = refs[:pieces], refs[pieces : 2 * pieces]
+    own_marks_ref, other_marks_ref, *rest, factor_t_ref, mask_ref, sums_ref = refs[2 * pieces :]
     copies_ref = rest.pop() if copies else None
     (out_ref,) = rest
     rank = own[0].shape[1]
     rows = own_marks_ref.shape[1]
     parts = []
-    for k in range(tiles):
-        parts += [own[k][...], other[k][...]]
+    half = own_marks_ref.shape[2]
+    for k in range(pieces):
+        for start in range(0, own[k].shape[0], half):
+            parts += [own[k][start : start + half, :], other[k][start : start + half, :]]
     marks = []
     for k in range(own_marks_ref.shape[0]):
         marks += [own_marks_ref[k], other_marks_ref[k]]
@@ -121,7 +123,7 @@
     if copies:
         shapes.append((copies, rows, rank))
     return pl.pallas_call(
-        functools.partial(users_kernel, tiles=tiles, copies=copies),
+        functools.partial(users_kernel, pieces=len(own), copies=copies),
         out_shape=tuple(jax.ShapeDtypeStruct(shape, jnp.bfloat16) for shape in shapes),
         in_specs=vmem_specs(len(args)),
         out_specs=tuple(vmem_specs(len(shapes))),
@@ -174,15 +176,38 @@
     return (place_on(("x", "y")) + (shift >> z_bits) + carry) & (plane - 1), (z + z_shift) & (ring - 1)
 
 
-def steps_to(place):
-    ny, nx = lax.axis_size("y"), lax.axis_size("x")
-    y, x = place & (ny - 1), place >> (ny.bit_length() - 1)
-    return (y - place_on("y")) & (ny - 1), (x - place_on("x")) & (nx - 1)
-
-
-def stepped(parts, axis, steps):
+def plane_steps(shift, z_first):
+    ring, ny, nx = lax.axis_size("z"), lax.axis_size("y"), lax.axis_size("x")
+    z_bits, y_bits = ring.bit_length() - 1, ny.bit_length() - 1
+    z, y, z_shift = place_on("z"), place_on("y"), shift & (ring - 1)
+    carry = (z + z_shift) >> z_bits if z_first else (z < z_shift).astype(jnp.uint32)
+    y_sum = ((shift >> z_bits) & (ny - 1)) + carry
+    x_shift = shift >> (z_bits + y_bits)
+    y_step = y_sum & (ny - 1)
+    y_then_x = (x_shift + ((y + y_sum) >> y_bits)) & (nx - 1)
+    x_then_y = (x_shift + (y < y_sum).astype(jnp.uint32)) & (nx - 1)
+    core = place_on("grp")
+    return jnp.where(core == 0, y_step, x_then_y), jnp.where(core == 0, y_then_x, y_step)
+
+
+def crossed_from(value, step, turn):
+    names = (*AXES, "grp")
+    nx, ny, nz, cores = (lax.axis_size(name) for name in names)
+    pairs = []
+    for x in range(nx):
+        for y in range(ny):
+            for z in range(nz):
+                for core in range(cores):
+                    along_y = (core == 0) == (turn == 0)
+                    x_from, y_from = (x, (y + step) % ny) if along_y else ((x + step) % nx, y)
+                    index = lambda i, j: ((i * ny + j) * nz + z) * cores + core
+                    pairs.append((index(x_from, y_from), index(x, y)))
+    return lax.ppermute(value, names, pairs)
+
+
+def stepped(parts, turn, steps):
     held = jnp.concatenate(parts, axis=0)
-    arrived = [held] + [fetched_from(held, axis, step) for step in range(1, lax.axis_size(axis))]
+    arrived = [held] + [crossed_from(held, step, turn) for step in range(1, lax.axis_size("y"))]
     chosen, start = [], 0
     for part, own_step in zip(parts, steps):
         value = part
@@ -245,15 +270,18 @@
     own_marks = jnp.stack(own_marks)
     other_marks = partner(jnp.stack(away_marks))
 
-    def fetch_items(shard, copies, extra=(), extra_at=()):
+    def fetch_items(shard, copies, extra=()):
         size = shard.shape[0]
         fixed = [fetched_from(shard, AXES, shift) for shift in (near, across)]
         held = swapped_with_all(copies, "z")
         free = [taken(held, z_at, 0, size) for _, z_at in forward[2:]]
         *free, fixed[0], fixed[1] = lax.optimization_barrier((*free, *fixed))
-        y_steps, x_steps = zip(*[steps_to(at) for at, _ in [*forward[2:], *extra_at]])
-        parts = stepped(stepped([*free, *extra], "y", y_steps), "x", x_steps)
-        own = [*fixed, *parts[:2]]
+        steps = [plane_steps(shift, True) for shift in shifts[2:]]
+        steps += [plane_steps(blocks - shift, False) for shift in shifts[2 : 2 + len(extra)]]
+        parts = [*free, *extra]
+        for turn in (0, 1):
+            parts = stepped(parts, turn, [step[turn] for step in steps])
+        own = [*fixed, jnp.concatenate(parts[:2], axis=0)]
         return own, [partner(value) for value in own], parts[2:]
 
     def fetch_users(shard, copies, marks, fixed_marks):
@@ -271,7 +299,7 @@
         return own, [partner(value) for value in own], [*direct[1:], *moved]
 
     copies = jnp.broadcast_to(item_start, (ring, *item_start.shape))
-    own, other, moved = fetch_items(item_start, copies, marks[2:], backward[2:])
+    own, other, moved = fetch_items(item_start, copies, marks[2:])
     first_users, copies = solve_users(own, other, own_marks, other_marks, plane)
 
     own, other, moved = fetch_users(first_users, copies, moved, marks[:2])

time: 134 us -> 133 us (level)
  waiting for transfers between devices: 36.8 us -> 34.6 us
  starting transfers between devices: 68.9 us -> 70.4 us
    ppermute x0 -> x12, starting transfers between devices: none -> 11.2 us  [crossed_from(): return lax.ppermute(value, names, pairs)]
    ppermute x0 -> x12, waiting for transfers between devices: none -> 11.1 us  [crossed_from(): return lax.ppermute(value, names, pairs)]
    ppermute x32 -> x18, waiting for transfers between devices: 11.3 us -> 1.31 us  [fetched_from(): lax.ppermute(value, axis, [((target + steps) % count, target) for target...]
    ppermute x32 -> x18, starting transfers between devices: 50.9 us -> 41.1 us  [fetched_from(): lax.ppermute(value, axis, [((target + steps) % count, target) for target...]
    all_to_all x4, waiting for transfers between devices: 25.6 us -> 22.1 us  [swapped_with_all(): return lax.all_to_all(copies, axes, split_axis=0, concat_axis=0, tiled=True)]
    unnamed x70 -> x62, local copies, waits for them, and re-layouts: 4.88 us -> 5.13 us
  transfers between devices with their start and end apart: 36 -> 34, of which waited for: 17 -> 15; matrix products, arithmetic and copies ran while one was open for 3% -> 3% of each run, Pallas kernels for 4% -> 4%
where the time goes in v6:
time: 133 us; the launch traced here: 132 us
  starting transfers between devices  70.4 us (53%)
  waiting for transfers between devices  34.6 us (26%)
  Pallas kernels  13.8 us (10%)
  local copies, waits for them, and re-layouts  8.82 us (7%)
  between operations  3.84 us (3%)
    ppermute x18, starting transfers between devices, fetched_from(): lax.ppermute(value, axis, [((target + steps) % count, target) for target...  41.1 us
    all_to_all x4, waiting for transfers between devices, swapped_with_all(): return lax.all_to_all(copies, axes, split_axis=0, concat_axis=0, tiled=True)  22.1 us
    all_to_all x4, starting transfers between devices, swapped_with_all(): return lax.all_to_all(copies, axes, split_axis=0, concat_axis=0, tiled=True)  18.1 us
    ppermute x12, starting transfers between devices, crossed_from(): return lax.ppermute(value, names, pairs)  11.2 us
    ppermute x12, waiting for transfers between devices, crossed_from(): return lax.ppermute(value, names, pairs)  11.1 us
    pallas_call x2, Pallas kernels, solve_users(): pl.pallas_call(functools.partial(users_kernel, pieces=len(own), copies=co...  10.6 us
    unnamed x62, local copies, waits for them, and re-layouts  5.13 us
    pallas_call x1, Pallas kernels, solve_items(): pl.pallas_call(items_kernel, out_shape=(jax.ShapeDtypeStruct((items, rank...  3.14 us
  transfers between devices with their start and end apart: 34, of which 15 were waited for; matrix products, arithmetic and copies ran while one was open for 3% of the time, Pallas kernels for 4%

profile of v6, /device:TPU:1, one launch (start us, length us, event | category | flops | bytes accessed | tf_op | source)
XLA Modules:
  0.0 132.2 jit_solution(3869936796880696775)
XLA Ops:
  0.6 2.5 %collective-permute-start = (bf16[128,128]{1,0:T(8,128)(2,1)}, bf16[128,128]{1,0:T(8,128)(2,1)S(1)}, u32[]{:S(2)}, u32[]{:S(2)}) collective-permute-start(bf16[128,128]{1,0:T(8,128)(2,1)} %param.4), channel_id=1, source_target_pairs={{254,0},{0,2},{2,4},{4,6},{6,8},{8,10},{10,12},{12,14},{14,16},{16... | collective-permute-start | bytes 98312 | tf_op jit(solution)/shard_map/ppermute | solution.py:164
  3.2 2.7 %collective-permute-start.1 = (bf16[128,128]{1,0:T(8,128)(2,1)}, bf16[128,128]{1,0:T(8,128)(2,1)S(1)}, u32[]{:S(2)}, u32[]{:S(2)}) collective-permute-start(bf16[128,128]{1,0:T(8,128)(2,1)} %param.4), channel_id=1, source_target_pairs={{128,0},{130,2},{132,4},{134,6},{136,8},{138,10},{140,12},{142,14}... | collective-permute-start | bytes 98312 | tf_op jit(solution)/shard_map/ppermute | solution.py:164
  5.9 1.5 %broadcast_in_dim.11 = bf16[8,128,128]{2,1,0:T(8,128)(2,1)} broadcast(bf16[128,128]{1,0:T(8,128)(2,1)} %param.4), dimensions={1,2} | broadcast | bytes 294912 | tf_op jit(solution)/shard_map/broadcast_in_dim | solution.py:301
  7.5 7.4 %all-to-all-start = ((bf16[8,128,128]{2,1,0:T(8,128)(2,1)}), bf16[8,128,128]{2,1,0:T(8,128)(2,1)S(1)}, u32[]{:S(2)}, u32[]{:S(2)}) async-start(bf16[8,128,128]{2,1,0:T(8,128)(2,1)} %broadcast_in_dim.11), calls=%async_computation | async-start | bytes 524288 | tf_op jit(solution)/shard_map/all_to_all | solution.py:157
  14.9 0.6 copy-done.24
  15.5 0.7 fusion.26
  18.2 0.7 copy-done.25
  19.0 5.8 %collective-permute-start.13 = (bf16[64,128]{1,0:T(8,128)(2,1)S(1)}, bf16[64,128]{1,0:T(8,128)(2,1)S(1)}, u32[]{:S(2)}, u32[]{:S(2)}) collective-permute-start(bf16[64,128]{1,0:T(8,128)(2,1)S(1)} %pad_maximum_fusion.7), channel_id=1, source_target_pairs={{2,0},{4,2},{6,4},{8,6},{10,8},{12,10},{14,12},{16,14},{18,16},{20... | collective-permute-start | bytes 49160 | tf_op jit(solution)/shard_map/ppermute | solution.py:164
  26.1 2.0 %collective-permute-start.3 = (bf16[384,128]{1,0:T(8,128)(2,1)S(1)}, bf16[384,128]{1,0:T(8,128)(2,1)S(1)}, u32[]{:S(2)}, u32[]{:S(2)}) collective-permute-start(bf16[384,128]{1,0:T(8,128)(2,1)S(1)} %get-tuple-element.34), channel_id=1, source_target_pairs={{32,0},{129,1},{34,2},{131,3},{36,4},{133,5},{38,6},{135,7},{40,8}... | collective-permute-start | bytes 294920 | tf_op jit(solution)/shard_map/ppermute | solution.py:205
  28.2 4.4 %collective-permute-start.8 = (bf16[128,128]{1,0:T(8,128)(2,1)S(1)}, bf16[128,128]{1,0:T(8,128)(2,1)S(1)}, u32[]{:S(2)}, u32[]{:S(2)}) collective-permute-start(bf16[128,128]{1,0:T(8,128)(2,1)S(1)} %collective-permute-done.refs_0_), channel_id=1, source_target_pairs={{1,0},{0,1},{3,2},{2,3},{5,4},{4,5},{7,6},{6,7},{9,8},{8,9},{11,10... | collective-permute-start | bytes 98312 | tf_op jit(solution)/shard_map/ppermute | solution.py:164
  32.9 2.4 %collective-permute-start.7 = (bf16[384,128]{1,0:T(8,128)(2,1)S(1)}, bf16[384,128]{1,0:T(8,128)(2,1)S(1)}, u32[]{:S(2)}, u32[]{:S(2)}) collective-permute-start(bf16[384,128]{1,0:T(8,128)(2,1)S(1)} %pad_maximum_fusion), channel_id=1, source_target_pairs={{64,0},{17,1},{66,2},{19,3},{68,4},{21,5},{70,6},{23,7},{72,8},{25... | collective-permute-start | bytes 294920 | tf_op jit(solution)/shard_map/ppermute | solution.py:205
  35.4 0.8 collective-permute-start.6
  36.1 1.8 %collective-permute-done.7 = bf16[384,128]{1,0:T(8,128)(2,1)S(1)} collective-permute-done((bf16[384,128]{1,0:T(8,128)(2,1)S(1)}, bf16[384,128]{1,0:T(8,128)(2,1)S(1)}, u32[]{:S(2)}, u32[]{:S(2)}) %collective-permute-start.7) | collective-permute-done | bytes 98336 | tf_op jit(solution)/shard_map/ppermute | solution.py:205
  38.0 4.9 %collective-permute-start.9 = (bf16[128,128]{1,0:T(8,128)(2,1)S(1)}, bf16[128,128]{1,0:T(8,128)(2,1)S(1)}, u32[]{:S(2)}, u32[]{:S(2)}) collective-permute-start(bf16[128,128]{1,0:T(8,128)(2,1)S(1)} %collective-permute-done.1.refs_1_), channel_id=1, source_target_pairs={{1,0},{0,1},{3,2},{2,3},{5,4},{4,5},{7,6},{6,7},{9,8},{8,9},{11,10... | collective-permute-start | bytes 98312 | tf_op jit(solution)/shard_map/ppermute | solution.py:164
  42.9 2.6 %collective-permute-start.11 = (bf16[4,32,128]{2,1,0:T(8,128)(2,1)S(1)}, bf16[4,32,128]{2,1,0:T(8,128)(2,1)S(1)}, u32[]{:S(2)}, u32[]{:S(2)}) collective-permute-start(bf16[4,32,128]{2,1,0:T(8,128)(2,1)S(1)} %pad_maximum_fusion.6), channel_id=1, source_target_pairs={{1,0},{0,1},{3,2},{2,3},{5,4},{4,5},{7,6},{6,7},{9,8},{8,9},{11,10... | collective-permute-start | bytes 98312 | tf_op jit(solution)/shard_map/ppermute | solution.py:164
  45.6 1.3 collective-permute-start.10
  46.9 0.6 pad_maximum_fusion.5.refs_6_
  47.5 1.1 collective-permute-start.14
  49.2 0.6 copy-done.3
  49.8 5.4 %users.2 = (bf16[32,128]{1,0:T(8,128)(2,1)}, bf16[16,32,128]{2,1,0:T(8,128)(2,1)}) custom-call(bf16[128,128]{1,0:T(8,128)(2,1)} %copy-done.6, bf16[128,128]{1,0:T(8,128)(2,1)} %copy-done.7, bf16[256,128]{1,0:T(8,128)(2,1)} %copy-done, bf16[128,128]{1,0:T(8,128)(2,1)} %copy-done.8, bf16[128,128]{1,0:T(8,128)(2,1)} %copy-done.9, bf16[256,128]{1,0:T(8,128)(2,1)} %copy-done.3, ...), custom_call_target="tpu_custom_call" | custom-call | tf_op jit(solution)/shard_map/users/pallas_call | solution.py:125
  55.2 3.7 %all-to-all-start.1 = ((bf16[16,32,128]{2,1,0:T(8,128)(2,1)}), bf16[16,32,128]{2,1,0:T(8,128)(2,1)S(1)}, u32[]{:S(2)}, u32[]{:S(2)}) async-start(bf16[16,32,128]{2,1,0:T(8,128)(2,1)} %get-tuple-element.22), calls=%async_computation.1 | async-start | bytes 262144 | tf_op jit(solution)/shard_map/all_to_all | solution.py:157
  58.9 0.7 copy-done.27
  59.6 3.9 %collective-permute-start.12 = (bf16[32,128]{1,0:T(8,128)(2,1)S(1)}, bf16[32,128]{1,0:T(8,128)(2,1)S(1)}, u32[]{:S(2)}, u32[]{:S(2)}) collective-permute-start(bf16[32,128]{1,0:T(8,128)(2,1)S(1)} %copy-done.27), channel_id=1, source_target_pairs={{2,0},{4,2},{6,4},{8,6},{10,8},{12,10},{14,12},{16,14},{18,16},{20... | collective-permute-start | bytes 24584 | tf_op jit(solution)/shard_map/ppermute | solution.py:164
  63.5 2.1 %all-to-all-done.1 = bf16[16,32,128]{2,1,0:T(8,128)(2,1)S(1)} async-done(((bf16[16,32,128]{2,1,0:T(8,128)(2,1)}), bf16[16,32,128]{2,1,0:T(8,128)(2,1)S(1)}, u32[]{:S(2)}, u32[]{:S(2)}) %all-to-all-start.1) | async-done | bytes 131104 | tf_op jit(solution)/shard_map/all_to_all | solution.py:157
  65.7 0.8 broadcast_in_dim.13
  66.5 3.5 %all-to-all-start.2 = ((bf16[8,192,128]{2,1,0:T(8,128)(2,1)}), bf16[8,192,128]{2,1,0:T(8,128)(2,1)S(1)}, u32[]{:S(2)}, u32[]{:S(2)}) async-start(bf16[8,192,128]{2,1,0:T(8,128)(2,1)} %broadcast_in_dim.13), calls=%async_computation.2 | async-start | bytes 786432 | tf_op jit(solution)/shard_map/all_to_all | solution.py:157
  70.0 1.8 %collective-permute-start.15 = (bf16[32,128]{1,0:T(8,128)(2,1)S(1)}, bf16[32,128]{1,0:T(8,128)(2,1)S(1)}, u32[]{:S(2)}, u32[]{:S(2)}) collective-permute-start(bf16[32,128]{1,0:T(8,128)(2,1)S(1)} %collective-permute-done.12.refs_0_), channel_id=1, source_target_pairs={{1,0},{0,1},{3,2},{2,3},{5,4},{4,5},{7,6},{6,7},{9,8},{8,9},{11,10... | collective-permute-start | bytes 24584 | tf_op jit(solution)/shard_map/ppermute | solution.py:164
  71.9 10.4 %all-to-all-done.2 = bf16[8,192,128]{2,1,0:T(8,128)(2,1)S(1)} async-done(((bf16[8,192,128]{2,1,0:T(8,128)(2,1)}), bf16[8,192,128]{2,1,0:T(8,128)(2,1)S(1)}, u32[]{:S(2)}, u32[]{:S(2)}) %all-to-all-start.2) | async-done | bytes 393248 | tf_op jit(solution)/shard_map/all_to_all | solution.py:157
  82.4 3.2 %collective-permute-start.17 = (bf16[32,128]{1,0:T(8,128)(2,1)S(1)}, bf16[32,128]{1,0:T(8,128)(2,1)S(1)}, u32[]{:S(2)}, u32[]{:S(2)}) collective-permute-start(bf16[32,128]{1,0:T(8,128)(2,1)S(1)} %get-tuple-element.45.refs_2_), channel_id=1, source_target_pairs={{1,0},{0,1},{3,2},{2,3},{5,4},{4,5},{7,6},{6,7},{9,8},{8,9},{11,10... | collective-permute-start | bytes 24584 | tf_op jit(solution)/shard_map/ppermute | solution.py:164
  85.6 0.6 dynamic-slice_bitcast_fusion.4
  87.3 3.1 %items.1 = (bf16[128,128]{1,0:T(8,128)(2,1)}, bf16[8,128,128]{2,1,0:T(8,128)(2,1)}) custom-call(bf16[32,128]{1,0:T(8,128)(2,1)} %copy-done.19, bf16[32,128]{1,0:T(8,128)(2,1)} %copy-done.10, bf16[32,128]{1,0:T(8,128)(2,1)} %copy-done.12, bf16[32,128]{1,0:T(8,128)(2,1)} %copy-done.11, bf16[32,128]{1,0:T(8,128)(2,1)} %copy-done.20, ...), custom_call_target="tpu_custom_call" | custom-call | tf_op jit(solution)/shard_map/items/pallas_call | solution.py:143
  90.4 3.5 %all-to-all-start.3 = ((bf16[8,128,128]{2,1,0:T(8,128)(2,1)}), bf16[8,128,128]{2,1,0:T(8,128)(2,1)S(1)}, u32[]{:S(2)}, u32[]{:S(2)}) async-start(bf16[8,128,128]{2,1,0:T(8,128)(2,1)} %get-tuple-element.28), calls=%async_computation.3 | async-start | bytes 524288 | tf_op jit(solution)/shard_map/all_to_all | solution.py:157
  94.0 1.4 %collective-permute-start.19 = (bf16[128,128]{1,0:T(8,128)(2,1)S(1)}, bf16[128,128]{1,0:T(8,128)(2,1)S(1)}, u32[]{:S(2)}, u32[]{:S(2)}) collective-permute-start(bf16[128,128]{1,0:T(8,128)(2,1)S(1)} %copy-done.26), channel_id=1, source_target_pairs={{254,0},{0,2},{2,4},{4,6},{6,8},{8,10},{10,12},{12,14},{14,16},{16... | collective-permute-start | bytes 98312 | tf_op jit(solution)/shard_map/ppermute | solution.py:164
  95.4 1.2 collective-permute-start.20
  96.6 9.6 %all-to-all-done.3 = bf16[8,128,128]{2,1,0:T(8,128)(2,1)S(1)} async-done(((bf16[8,128,128]{2,1,0:T(8,128)(2,1)}), bf16[8,128,128]{2,1,0:T(8,128)(2,1)S(1)}, u32[]{:S(2)}, u32[]{:S(2)}) %all-to-all-start.3) | async-done | bytes 262176 | tf_op jit(solution)/shard_map/all_to_all | solution.py:157
  106.3 1.1 collective-permute-start.23
  107.4 1.2 collective-permute-start.22
  108.6 0.9 collective-permute-done.23
  109.5 2.5 %collective-permute-done.22 = bf16[256,128]{1,0:T(8,128)(2,1)S(1)} collective-permute-done((bf16[256,128]{1,0:T(8,128)(2,1)S(1)}, bf16[256,128]{1,0:T(8,128)(2,1)S(1)}, u32[]{:S(2)}, u32[]{:S(2)}) %collective-permute-start.22) | collective-permute-done | bytes 65568 | tf_op jit(solution)/shard_map/ppermute | solution.py:205
  112.0 1.2 collective-permute-done.21
  113.3 2.5 %collective-permute-start.26 = (bf16[256,128]{1,0:T(8,128)(2,1)S(1)}, bf16[256,128]{1,0:T(8,128)(2,1)S(1)}, u32[]{:S(2)}, u32[]{:S(2)}) collective-permute-start(bf16[256,128]{1,0:T(8,128)(2,1)S(1)} %pad_maximum_fusion.2), channel_id=1, source_target_pairs={{64,0},{17,1},{66,2},{19,3},{68,4},{21,5},{70,6},{23,7},{72,8},{25... | collective-permute-start | bytes 196616 | tf_op jit(solution)/shard_map/ppermute | solution.py:205
  115.8 0.7 collective-permute-start.24
  116.5 0.7 collective-permute-done.26
  117.1 3.4 %collective-permute-done.25 = bf16[256,128]{1,0:T(8,128)(2,1)S(1)} collective-permute-done((bf16[256,128]{1,0:T(8,128)(2,1)S(1)}, bf16[256,128]{1,0:T(8,128)(2,1)S(1)}, u32[]{:S(2)}, u32[]{:S(2)}) %collective-permute-start.25) | collective-permute-done | bytes 65568 | tf_op jit(solution)/shard_map/ppermute | solution.py:205
  120.9 3.5 %collective-permute-start.29 = (bf16[256,128]{1,0:T(8,128)(2,1)S(1)}, bf16[256,128]{1,0:T(8,128)(2,1)S(1)}, u32[]{:S(2)}, u32[]{:S(2)}) collective-permute-start(bf16[256,128]{1,0:T(8,128)(2,1)S(1)} %pad_maximum_fusion.3.refs_2_), channel_id=1, source_target_pairs={{1,0},{0,1},{3,2},{2,3},{5,4},{4,5},{7,6},{6,7},{9,8},{8,9},{11,10... | collective-permute-start | bytes 196616 | tf_op jit(solution)/shard_map/ppermute | solution.py:164
  124.9 0.7 collective-permute-done.27.refs_3_
  126.4 0.6 copy-done.5
  127.0 5.3 %users.3 = bf16[32,128]{1,0:T(8,128)(2,1)} custom-call(bf16[128,128]{1,0:T(8,128)(2,1)} %copy-done.13, bf16[128,128]{1,0:T(8,128)(2,1)} %copy-done.14, bf16[256,128]{1,0:T(8,128)(2,1)} %copy-done.1, bf16[128,128]{1,0:T(8,128)(2,1)} %copy-done.15, bf16[128,128]{1,0:T(8,128)(2,1)} %copy-done.16, bf16[256,128]{1,0:T(8,128)(2,1)} %copy-done.5, ...), custom_call_target="tpu_custom_call" | custom-call | tf_op jit(solution)/shard_map/users/pallas_call | solution.py:125
  (113 shorter events, 4.7 us)
Async XLA Ops:
  0.6 24.9 %collective-permute-start = (bf16[128,128]{1,0:T(8,128)(2,1)}, bf16[128,128]{1,0:T(8,128)(2,1)S(1)}, u32[]{:S(2)}, u32[]{:S(2)}) collective-permute-start(bf16[128,128]{1,0:T(8,128)(2,1)} %param.4), channel_id=1, source_target_pairs={{254,0},{0,2},{2,4},{4,6},{6,8},{8,10},{10,12},{12,14},{14,16},{16... | collective-permute-start | bytes 98312 | tf_op jit(solution)/shard_map/ppermute | solution.py:164
  3.2 22.4 %collective-permute-start.1 = (bf16[128,128]{1,0:T(8,128)(2,1)}, bf16[128,128]{1,0:T(8,128)(2,1)S(1)}, u32[]{:S(2)}, u32[]{:S(2)}) collective-permute-start(bf16[128,128]{1,0:T(8,128)(2,1)} %param.4), channel_id=1, source_target_pairs={{128,0},{130,2},{132,4},{134,6},{136,8},{138,10},{140,12},{142,14}... | collective-permute-start | bytes 98312 | tf_op jit(solution)/shard_map/ppermute | solution.py:164
  7.4 10.7 %copy-start.4 = (bf16[4,64,128]{2,1,0:T(8,128)(2,1)S(1)}, bf16[4,64,128]{2,1,0:T(8,128)(2,1)}, u32[]{:S(2)}) copy-start(bf16[4,64,128]{2,1,0:T(8,128)(2,1)} %param.5) | copy-start | bytes 196612
  7.5 18.1 %all-to-all-start = ((bf16[8,128,128]{2,1,0:T(8,128)(2,1)}), bf16[8,128,128]{2,1,0:T(8,128)(2,1)S(1)}, u32[]{:S(2)}, u32[]{:S(2)}) async-start(bf16[8,128,128]{2,1,0:T(8,128)(2,1)} %broadcast_in_dim.11), calls=%async_computation | async-start | bytes 524288 | tf_op jit(solution)/shard_map/all_to_all | solution.py:157
  19.0 46.7 %collective-permute-start.13 = (bf16[64,128]{1,0:T(8,128)(2,1)S(1)}, bf16[64,128]{1,0:T(8,128)(2,1)S(1)}, u32[]{:S(2)}, u32[]{:S(2)}) collective-permute-start(bf16[64,128]{1,0:T(8,128)(2,1)S(1)} %pad_maximum_fusion.7), channel_id=1, source_target_pairs={{2,0},{4,2},{6,4},{8,6},{10,8},{12,10},{14,12},{16,14},{18,16},{20... | collective-permute-start | bytes 49160 | tf_op jit(solution)/shard_map/ppermute | solution.py:164
  25.6 2.6 %copy-start.6 = (bf16[128,128]{1,0:T(8,128)(2,1)}, bf16[128,128]{1,0:T(8,128)(2,1)S(1)}, u32[]{:S(2)}) copy-start(bf16[128,128]{1,0:T(8,128)(2,1)S(1)} %collective-permute-done.refs_0_) | copy-start | bytes 98308
  25.6 12.4 %copy-start.7 = (bf16[128,128]{1,0:T(8,128)(2,1)}, bf16[128,128]{1,0:T(8,128)(2,1)S(1)}, u32[]{:S(2)}) copy-start(bf16[128,128]{1,0:T(8,128)(2,1)S(1)} %collective-permute-done.1.refs_1_) | copy-start | bytes 98308
  25.7 6.9 %collective-permute-start.4 = (bf16[384,128]{1,0:T(8,128)(2,1)S(1)}, bf16[384,128]{1,0:T(8,128)(2,1)S(1)}, u32[]{:S(2)}, u32[]{:S(2)}) collective-permute-start(bf16[384,128]{1,0:T(8,128)(2,1)S(1)} %get-tuple-element.34), channel_id=1, source_target_pairs={{16,0},{65,1},{18,2},{67,3},{20,4},{69,5},{22,6},{71,7},{24,8},{73... | collective-permute-start | bytes 294920 | tf_op jit(solution)/shard_map/ppermute | solution.py:205
  26.1 6.4 %collective-permute-start.3 = (bf16[384,128]{1,0:T(8,128)(2,1)S(1)}, bf16[384,128]{1,0:T(8,128)(2,1)S(1)}, u32[]{:S(2)}, u32[]{:S(2)}) collective-permute-start(bf16[384,128]{1,0:T(8,128)(2,1)S(1)} %get-tuple-element.34), channel_id=1, source_target_pairs={{32,0},{129,1},{34,2},{131,3},{36,4},{133,5},{38,6},{135,7},{40,8}... | collective-permute-start | bytes 294920 | tf_op jit(solution)/shard_map/ppermute | solution.py:205
  28.2 4.7 %collective-permute-start.2 = (bf16[384,128]{1,0:T(8,128)(2,1)S(1)}, bf16[384,128]{1,0:T(8,128)(2,1)S(1)}, u32[]{:S(2)}, u32[]{:S(2)}) collective-permute-start(bf16[384,128]{1,0:T(8,128)(2,1)S(1)} %get-tuple-element.34), channel_id=1, source_target_pairs={{48,0},{193,1},{50,2},{195,3},{52,4},{197,5},{54,6},{199,7},{56,8}... | collective-permute-start | bytes 294920 | tf_op jit(solution)/shard_map/ppermute | solution.py:205
  28.2 19.3 %collective-permute-start.8 = (bf16[128,128]{1,0:T(8,128)(2,1)S(1)}, bf16[128,128]{1,0:T(8,128)(2,1)S(1)}, u32[]{:S(2)}, u32[]{:S(2)}) collective-permute-start(bf16[128,128]{1,0:T(8,128)(2,1)S(1)} %collective-permute-done.refs_0_), channel_id=1, source_target_pairs={{1,0},{0,1},{3,2},{2,3},{5,4},{4,5},{7,6},{6,7},{9,8},{8,9},{11,10... | collective-permute-start | bytes 98312 | tf_op jit(solution)/shard_map/ppermute | solution.py:164
  32.9 5.0 %collective-permute-start.7 = (bf16[384,128]{1,0:T(8,128)(2,1)S(1)}, bf16[384,128]{1,0:T(8,128)(2,1)S(1)}, u32[]{:S(2)}, u32[]{:S(2)}) collective-permute-start(bf16[384,128]{1,0:T(8,128)(2,1)S(1)} %pad_maximum_fusion), channel_id=1, source_target_pairs={{64,0},{17,1},{66,2},{19,3},{68,4},{21,5},{70,6},{23,7},{72,8},{25... | collective-permute-start | bytes 294920 | tf_op jit(solution)/shard_map/ppermute | solution.py:205
  35.4 7.5 %collective-permute-start.6 = (bf16[384,128]{1,0:T(8,128)(2,1)S(1)}, bf16[384,128]{1,0:T(8,128)(2,1)S(1)}, u32[]{:S(2)}, u32[]{:S(2)}) collective-permute-start(bf16[384,128]{1,0:T(8,128)(2,1)S(1)} %pad_maximum_fusion), channel_id=1, source_target_pairs={{128,0},{33,1},{130,2},{35,3},{132,4},{37,5},{134,6},{39,7},{136,8... | collective-permute-start | bytes 294920 | tf_op jit(solution)/shard_map/ppermute | solution.py:205
  36.1 9.4 %collective-permute-start.5 = (bf16[384,128]{1,0:T(8,128)(2,1)S(1)}, bf16[384,128]{1,0:T(8,128)(2,1)S(1)}, u32[]{:S(2)}, u32[]{:S(2)}) collective-permute-start(bf16[384,128]{1,0:T(8,128)(2,1)S(1)} %pad_maximum_fusion), channel_id=1, source_target_pairs={{192,0},{49,1},{194,2},{51,3},{196,4},{53,5},{198,6},{55,7},{200,8... | collective-permute-start | bytes 294920 | tf_op jit(solution)/shard_map/ppermute | solution.py:205
  38.0 10.6 %collective-permute-start.9 = (bf16[128,128]{1,0:T(8,128)(2,1)S(1)}, bf16[128,128]{1,0:T(8,128)(2,1)S(1)}, u32[]{:S(2)}, u32[]{:S(2)}) collective-permute-start(bf16[128,128]{1,0:T(8,128)(2,1)S(1)} %collective-permute-done.1.refs_1_), channel_id=1, source_target_pairs={{1,0},{0,1},{3,2},{2,3},{5,4},{4,5},{7,6},{6,7},{9,8},{8,9},{11,10... | collective-permute-start | bytes 98312 | tf_op jit(solution)/shard_map/ppermute | solution.py:164
  42.9 5.7 %collective-permute-start.11 = (bf16[4,32,128]{2,1,0:T(8,128)(2,1)S(1)}, bf16[4,32,128]{2,1,0:T(8,128)(2,1)S(1)}, u32[]{:S(2)}, u32[]{:S(2)}) collective-permute-start(bf16[4,32,128]{2,1,0:T(8,128)(2,1)S(1)} %pad_maximum_fusion.6), channel_id=1, source_target_pairs={{1,0},{0,1},{3,2},{2,3},{5,4},{4,5},{7,6},{6,7},{9,8},{8,9},{11,10... | collective-permute-start | bytes 98312 | tf_op jit(solution)/shard_map/ppermute | solution.py:164
  45.6 3.0 %copy-start = (bf16[256,128]{1,0:T(8,128)(2,1)}, bf16[256,128]{1,0:T(8,128)(2,1)S(1)}, u32[]{:S(2)}) copy-start(bf16[256,128]{1,0:T(8,128)(2,1)S(1)} %pad_maximum_fusion.1.refs_2_) | copy-start | bytes 196612
  45.6 3.0 %collective-permute-start.10 = (bf16[256,128]{1,0:T(8,128)(2,1)S(1)}, bf16[256,128]{1,0:T(8,128)(2,1)S(1)}, u32[]{:S(2)}, u32[]{:S(2)}) collective-permute-start(bf16[256,128]{1,0:T(8,128)(2,1)S(1)} %pad_maximum_fusion.1.refs_2_), channel_id=1, source_target_pairs={{1,0},{0,1},{3,2},{2,3},{5,4},{4,5},{7,6},{6,7},{9,8},{8,9},{11,10... | collective-permute-start | bytes 196616 | tf_op jit(solution)/shard_map/ppermute | solution.py:164
  47.5 1.1 copy-start.8
  47.5 18.1 %collective-permute-start.14 = (bf16[64,128]{1,0:T(8,128)(2,1)S(1)}, bf16[64,128]{1,0:T(8,128)(2,1)S(1)}, u32[]{:S(2)}, u32[]{:S(2)}) collective-permute-start(bf16[64,128]{1,0:T(8,128)(2,1)S(1)} %pad_maximum_fusion.8), channel_id=1, source_target_pairs={{128,0},{130,2},{132,4},{134,6},{136,8},{138,10},{140,12},{142,14}... | collective-permute-start | bytes 49160 | tf_op jit(solution)/shard_map/ppermute | solution.py:164
  55.2 10.4 %all-to-all-start.1 = ((bf16[16,32,128]{2,1,0:T(8,128)(2,1)}), bf16[16,32,128]{2,1,0:T(8,128)(2,1)S(1)}, u32[]{:S(2)}, u32[]{:S(2)}) async-start(bf16[16,32,128]{2,1,0:T(8,128)(2,1)} %get-tuple-element.22), calls=%async_computation.1 | async-start | bytes 262144 | tf_op jit(solution)/shard_map/all_to_all | solution.py:157
  59.6 6.0 %collective-permute-start.12 = (bf16[32,128]{1,0:T(8,128)(2,1)S(1)}, bf16[32,128]{1,0:T(8,128)(2,1)S(1)}, u32[]{:S(2)}, u32[]{:S(2)}) collective-permute-start(bf16[32,128]{1,0:T(8,128)(2,1)S(1)} %copy-done.27), channel_id=1, source_target_pairs={{2,0},{4,2},{6,4},{8,6},{10,8},{12,10},{14,12},{16,14},{18,16},{20... | collective-permute-start | bytes 24584 | tf_op jit(solution)/shard_map/ppermute | solution.py:164
  65.6 6.2 %copy-start.10 = (bf16[32,128]{1,0:T(8,128)(2,1)}, bf16[32,128]{1,0:T(8,128)(2,1)S(1)}, u32[]{:S(2)}) copy-start(bf16[32,128]{1,0:T(8,128)(2,1)S(1)} %get-tuple-element.62.refs_1_) | copy-start | bytes 24580
  65.6 0.9 copy-start.17
  65.7 4.3 %copy-start.19 = (bf16[32,128]{1,0:T(8,128)(2,1)}, bf16[32,128]{1,0:T(8,128)(2,1)S(1)}, u32[]{:S(2)}) copy-start(bf16[32,128]{1,0:T(8,128)(2,1)S(1)} %collective-permute-done.12.refs_0_) | copy-start | bytes 24580
  66.5 15.8 %all-to-all-start.2 = ((bf16[8,192,128]{2,1,0:T(8,128)(2,1)}), bf16[8,192,128]{2,1,0:T(8,128)(2,1)S(1)}, u32[]{:S(2)}, u32[]{:S(2)}) async-start(bf16[8,192,128]{2,1,0:T(8,128)(2,1)} %broadcast_in_dim.13), calls=%async_computation.2 | async-start | bytes 786432 | tf_op jit(solution)/shard_map/all_to_all | solution.py:157
  70.0 16.3 %collective-permute-start.15 = (bf16[32,128]{1,0:T(8,128)(2,1)S(1)}, bf16[32,128]{1,0:T(8,128)(2,1)S(1)}, u32[]{:S(2)}, u32[]{:S(2)}) collective-permute-start(bf16[32,128]{1,0:T(8,128)(2,1)S(1)} %collective-permute-done.12.refs_0_), channel_id=1, source_target_pairs={{1,0},{0,1},{3,2},{2,3},{5,4},{4,5},{7,6},{6,7},{9,8},{8,9},{11,10... | collective-permute-start | bytes 24584 | tf_op jit(solution)/shard_map/ppermute | solution.py:164
  71.8 14.5 %collective-permute-start.16 = (bf16[32,128]{1,0:T(8,128)(2,1)S(1)}, bf16[32,128]{1,0:T(8,128)(2,1)S(1)}, u32[]{:S(2)}, u32[]{:S(2)}) collective-permute-start(bf16[32,128]{1,0:T(8,128)(2,1)S(1)} %get-tuple-element.62.refs_1_), channel_id=1, source_target_pairs={{1,0},{0,1},{3,2},{2,3},{5,4},{4,5},{7,6},{6,7},{9,8},{8,9},{11,10... | collective-permute-start | bytes 24584 | tf_op jit(solution)/shard_map/ppermute | solution.py:164
  82.4 3.9 %copy-start.11 = (bf16[32,128]{1,0:T(8,128)(2,1)}, bf16[32,128]{1,0:T(8,128)(2,1)S(1)}, u32[]{:S(2)}) copy-start(bf16[32,128]{1,0:T(8,128)(2,1)S(1)} %get-tuple-element.44.refs_3_) | copy-start | bytes 24580
  82.4 3.9 %copy-start.12 = (bf16[32,128]{1,0:T(8,128)(2,1)}, bf16[32,128]{1,0:T(8,128)(2,1)S(1)}, u32[]{:S(2)}) copy-start(bf16[32,128]{1,0:T(8,128)(2,1)S(1)} %get-tuple-element.45.refs_2_) | copy-start | bytes 24580
  82.4 4.0 %collective-permute-start.17 = (bf16[32,128]{1,0:T(8,128)(2,1)S(1)}, bf16[32,128]{1,0:T(8,128)(2,1)S(1)}, u32[]{:S(2)}, u32[]{:S(2)}) collective-permute-start(bf16[32,128]{1,0:T(8,128)(2,1)S(1)} %get-tuple-element.45.refs_2_), channel_id=1, source_target_pairs={{1,0},{0,1},{3,2},{2,3},{5,4},{4,5},{7,6},{6,7},{9,8},{8,9},{11,10... | collective-permute-start | bytes 24584 | tf_op jit(solution)/shard_map/ppermute | solution.py:164
  85.5 1.2 collective-permute-start.18
  90.4 3.6 %copy-start.26 = (bf16[128,128]{1,0:T(8,128)(2,1)S(1)}, bf16[128,128]{1,0:T(8,128)(2,1)}, u32[]{:S(2)}) copy-start(bf16[128,128]{1,0:T(8,128)(2,1)} %get-tuple-element.17) | copy-start | bytes 98308
  90.4 15.8 %all-to-all-start.3 = ((bf16[8,128,128]{2,1,0:T(8,128)(2,1)}), bf16[8,128,128]{2,1,0:T(8,128)(2,1)S(1)}, u32[]{:S(2)}, u32[]{:S(2)}) async-start(bf16[8,128,128]{2,1,0:T(8,128)(2,1)} %get-tuple-element.28), calls=%async_computation.3 | async-start | bytes 524288 | tf_op jit(solution)/shard_map/all_to_all | solution.py:157
  94.0 12.2 %collective-permute-start.19 = (bf16[128,128]{1,0:T(8,128)(2,1)S(1)}, bf16[128,128]{1,0:T(8,128)(2,1)S(1)}, u32[]{:S(2)}, u32[]{:S(2)}) collective-permute-start(bf16[128,128]{1,0:T(8,128)(2,1)S(1)} %copy-done.26), channel_id=1, source_target_pairs={{254,0},{0,2},{2,4},{4,6},{6,8},{8,10},{10,12},{12,14},{14,16},{16... | collective-permute-start | bytes 98312 | tf_op jit(solution)/shard_map/ppermute | solution.py:164
  95.4 10.9 %collective-permute-start.20 = (bf16[128,128]{1,0:T(8,128)(2,1)S(1)}, bf16[128,128]{1,0:T(8,128)(2,1)S(1)}, u32[]{:S(2)}, u32[]{:S(2)}) collective-permute-start(bf16[128,128]{1,0:T(8,128)(2,1)S(1)} %copy-done.26), channel_id=1, source_target_pairs={{128,0},{130,2},{132,4},{134,6},{136,8},{138,10},{140,12},{142,14}... | collective-permute-start | bytes 98312 | tf_op jit(solution)/shard_map/ppermute | solution.py:164
  106.2 18.1 %copy-start.13 = (bf16[128,128]{1,0:T(8,128)(2,1)}, bf16[128,128]{1,0:T(8,128)(2,1)S(1)}, u32[]{:S(2)}) copy-start(bf16[128,128]{1,0:T(8,128)(2,1)S(1)} %collective-permute-done.19.refs_0_) | copy-start | bytes 98308
  106.3 18.2 %copy-start.14 = (bf16[128,128]{1,0:T(8,128)(2,1)}, bf16[128,128]{1,0:T(8,128)(2,1)S(1)}, u32[]{:S(2)}) copy-start(bf16[128,128]{1,0:T(8,128)(2,1)S(1)} %collective-permute-done.20.refs_1_) | copy-start | bytes 98308
  106.3 3.2 %collective-permute-start.23 = (bf16[256,128]{1,0:T(8,128)(2,1)S(1)}, bf16[256,128]{1,0:T(8,128)(2,1)S(1)}, u32[]{:S(2)}, u32[]{:S(2)}) collective-permute-start(bf16[256,128]{1,0:T(8,128)(2,1)S(1)} %constant_dynamic-update-slice_fusion.6), channel_id=1, source_target_pairs={{16,0},{65,1},{18,2},{67,3},{20,4},{69,5},{22,6},{71,7},{24,8},{73... | collective-permute-start | bytes 196616 | tf_op jit(solution)/shard_map/ppermute | solution.py:205
  107.4 4.6 %collective-permute-start.22 = (bf16[256,128]{1,0:T(8,128)(2,1)S(1)}, bf16[256,128]{1,0:T(8,128)(2,1)S(1)}, u32[]{:S(2)}, u32[]{:S(2)}) collective-permute-start(bf16[256,128]{1,0:T(8,128)(2,1)S(1)} %constant_dynamic-update-slice_fusion.6), channel_id=1, source_target_pairs={{32,0},{129,1},{34,2},{131,3},{36,4},{133,5},{38,6},{135,7},{40,8}... | collective-permute-start | bytes 196616 | tf_op jit(solution)/shard_map/ppermute | solution.py:205
  108.6 4.6 %collective-permute-start.21 = (bf16[256,128]{1,0:T(8,128)(2,1)S(1)}, bf16[256,128]{1,0:T(8,128)(2,1)S(1)}, u32[]{:S(2)}, u32[]{:S(2)}) collective-permute-start(bf16[256,128]{1,0:T(8,128)(2,1)S(1)} %constant_dynamic-update-slice_fusion.6), channel_id=1, source_target_pairs={{48,0},{193,1},{50,2},{195,3},{52,4},{197,5},{54,6},{199,7},{56,8}... | collective-permute-start | bytes 196616 | tf_op jit(solution)/shard_map/ppermute | solution.py:205
  113.3 3.8 %collective-permute-start.26 = (bf16[256,128]{1,0:T(8,128)(2,1)S(1)}, bf16[256,128]{1,0:T(8,128)(2,1)S(1)}, u32[]{:S(2)}, u32[]{:S(2)}) collective-permute-start(bf16[256,128]{1,0:T(8,128)(2,1)S(1)} %pad_maximum_fusion.2), channel_id=1, source_target_pairs={{64,0},{17,1},{66,2},{19,3},{68,4},{21,5},{70,6},{23,7},{72,8},{25... | collective-permute-start | bytes 196616 | tf_op jit(solution)/shard_map/ppermute | solution.py:205
  115.8 4.7 %collective-permute-start.25 = (bf16[256,128]{1,0:T(8,128)(2,1)S(1)}, bf16[256,128]{1,0:T(8,128)(2,1)S(1)}, u32[]{:S(2)}, u32[]{:S(2)}) collective-permute-start(bf16[256,128]{1,0:T(8,128)(2,1)S(1)} %pad_maximum_fusion.2), channel_id=1, source_target_pairs={{128,0},{33,1},{130,2},{35,3},{132,4},{37,5},{134,6},{39,7},{136,8... | collective-permute-start | bytes 196616 | tf_op jit(solution)/shard_map/ppermute | solution.py:205
  115.8 5.0 %collective-permute-start.24 = (bf16[256,128]{1,0:T(8,128)(2,1)S(1)}, bf16[256,128]{1,0:T(8,128)(2,1)S(1)}, u32[]{:S(2)}, u32[]{:S(2)}) collective-permute-start(bf16[256,128]{1,0:T(8,128)(2,1)S(1)} %pad_maximum_fusion.2), channel_id=1, source_target_pairs={{192,0},{49,1},{194,2},{51,3},{196,4},{53,5},{198,6},{55,7},{200,8... | collective-permute-start | bytes 196616 | tf_op jit(solution)/shard_map/ppermute | solution.py:205
  120.9 4.9 %copy-start.1 = (bf16[256,128]{1,0:T(8,128)(2,1)}, bf16[256,128]{1,0:T(8,128)(2,1)S(1)}, u32[]{:S(2)}) copy-start(bf16[256,128]{1,0:T(8,128)(2,1)S(1)} %pad_maximum_fusion.3.refs_2_) | copy-start | bytes 196612
  120.9 4.9 %collective-permute-start.29 = (bf16[256,128]{1,0:T(8,128)(2,1)S(1)}, bf16[256,128]{1,0:T(8,128)(2,1)S(1)}, u32[]{:S(2)}, u32[]{:S(2)}) collective-permute-start(bf16[256,128]{1,0:T(8,128)(2,1)S(1)} %pad_maximum_fusion.3.refs_2_), channel_id=1, source_target_pairs={{1,0},{0,1},{3,2},{2,3},{5,4},{4,5},{7,6},{6,7},{9,8},{8,9},{11,10... | collective-permute-start | bytes 196616 | tf_op jit(solution)/shard_map/ppermute | solution.py:164
  124.4 1.2 collective-permute-start.27
  124.5 1.3 collective-permute-start.28
  (14 other events, 9.0 us)

commit v7 on v6

--- a/solution.py
+++ b/solution.py
@@ -7,13 +7,13 @@
 from jax.experimental.pallas import tpu as pltpu
 from jax.sharding import Mesh, PartitionSpec as P
 
+
 SWEEPS = 4
 RIDGE = 0.005
 UNRATED = 64.0
 RATED_BELOW = 32.0
 AXES = ("x", "y", "z")
 VMEM = pltpu.MemorySpace.VMEM
-SMEM = pltpu.MemorySpace.SMEM
 
 
 def split_parts(value):
@@ -207,7 +207,10 @@
 
 def stepped(parts, turn, steps):
     held = jnp.concatenate(parts, axis=0)
-    arrived = [held] + [crossed_from(held, step, turn) for step in range(1, lax.axis_size("y"))]
+    count = lax.axis_size("y")
+    near_first = sorted(range(1, count), key=lambda step: min(step, count - step))
+    arrivals = {step: crossed_from(held, step, turn) for step in near_first}
+    arrived = [held] + [arrivals[step] for step in range(1, count)]
     chosen, start = [], 0
     for part, own_step in zip(parts, steps):
         value = part

time: 133 us -> 133 us (level)
  no operation moved by 1% of the time
where the time goes in v7:
time: 133 us; the launch traced here: 132 us
  starting transfers between devices  70.4 us (53%)
  waiting for transfers between devices  34.6 us (26%)
  Pallas kernels  13.8 us (10%)
  local copies, waits for them, and re-layouts  8.82 us (7%)
  between operations  3.84 us (3%)
    ppermute x18, starting transfers between devices, fetched_from(): lax.ppermute(value, axis, [((target + steps) % count, target) for target...  41.1 us
    all_to_all x4, waiting for transfers between devices, swapped_with_all(): return lax.all_to_all(copies, axes, split_axis=0, concat_axis=0, tiled=True)  22.1 us
    all_to_all x4, starting transfers between devices, swapped_with_all(): return lax.all_to_all(copies, axes, split_axis=0, concat_axis=0, tiled=True)  18.1 us
    ppermute x12, starting transfers between devices, crossed_from(): return lax.ppermute(value, names, pairs)  11.2 us
    ppermute x12, waiting for transfers between devices, crossed_from(): return lax.ppermute(value, names, pairs)  11.1 us
    pallas_call x2, Pallas kernels, solve_users(): pl.pallas_call(functools.partial(users_kernel, pieces=len(own), copies=co...  10.6 us
    unnamed x62, local copies, waits for them, and re-layouts  5.13 us
    pallas_call x1, Pallas kernels, solve_items(): pl.pallas_call(items_kernel, out_shape=(jax.ShapeDtypeStruct((items, rank...  3.14 us
  transfers between devices with their start and end apart: 34, of which 15 were waited for; matrix products, arithmetic and copies ran while one was open for 3% of the time, Pallas kernels for 4%

profile of v7, /device:TPU:1, one launch (start us, length us, event | category | flops | bytes accessed | tf_op | source)
XLA Modules:
  0.0 132.2 jit_solution(3869936796880696775)
XLA Ops:
  0.6 2.5 %collective-permute-start = (bf16[128,128]{1,0:T(8,128)(2,1)}, bf16[128,128]{1,0:T(8,128)(2,1)S(1)}, u32[]{:S(2)}, u32[]{:S(2)}) collective-permute-start(bf16[128,128]{1,0:T(8,128)(2,1)} %param.4), channel_id=1, source_target_pairs={{254,0},{0,2},{2,4},{4,6},{6,8},{8,10},{10,12},{12,14},{14,16},{16... | collective-permute-start | bytes 98312 | tf_op jit(solution)/shard_map/ppermute | solution.py:164
  3.2 2.7 %collective-permute-start.1 = (bf16[128,128]{1,0:T(8,128)(2,1)}, bf16[128,128]{1,0:T(8,128)(2,1)S(1)}, u32[]{:S(2)}, u32[]{:S(2)}) collective-permute-start(bf16[128,128]{1,0:T(8,128)(2,1)} %param.4), channel_id=1, source_target_pairs={{128,0},{130,2},{132,4},{134,6},{136,8},{138,10},{140,12},{142,14}... | collective-permute-start | bytes 98312 | tf_op jit(solution)/shard_map/ppermute | solution.py:164
  5.9 1.5 %broadcast_in_dim.11 = bf16[8,128,128]{2,1,0:T(8,128)(2,1)} broadcast(bf16[128,128]{1,0:T(8,128)(2,1)} %param.4), dimensions={1,2} | broadcast | bytes 294912 | tf_op jit(solution)/shard_map/broadcast_in_dim | solution.py:304
  7.5 7.4 %all-to-all-start = ((bf16[8,128,128]{2,1,0:T(8,128)(2,1)}), bf16[8,128,128]{2,1,0:T(8,128)(2,1)S(1)}, u32[]{:S(2)}, u32[]{:S(2)}) async-start(bf16[8,128,128]{2,1,0:T(8,128)(2,1)} %broadcast_in_dim.11), calls=%async_computation | async-start | bytes 524288 | tf_op jit(solution)/shard_map/all_to_all | solution.py:157
  14.9 0.6 copy-done.24
  15.5 0.7 fusion.26
  18.2 0.7 copy-done.25
  19.0 5.8 %collective-permute-start.13 = (bf16[64,128]{1,0:T(8,128)(2,1)S(1)}, bf16[64,128]{1,0:T(8,128)(2,1)S(1)}, u32[]{:S(2)}, u32[]{:S(2)}) collective-permute-start(bf16[64,128]{1,0:T(8,128)(2,1)S(1)} %pad_maximum_fusion.7), channel_id=1, source_target_pairs={{2,0},{4,2},{6,4},{8,6},{10,8},{12,10},{14,12},{16,14},{18,16},{20... | collective-permute-start | bytes 49160 | tf_op jit(solution)/shard_map/ppermute | solution.py:164
  26.1 2.0 %collective-permute-start.3 = (bf16[384,128]{1,0:T(8,128)(2,1)S(1)}, bf16[384,128]{1,0:T(8,128)(2,1)S(1)}, u32[]{:S(2)}, u32[]{:S(2)}) collective-permute-start(bf16[384,128]{1,0:T(8,128)(2,1)S(1)} %get-tuple-element.34), channel_id=1, source_target_pairs={{32,0},{129,1},{34,2},{131,3},{36,4},{133,5},{38,6},{135,7},{40,8}... | collective-permute-start | bytes 294920 | tf_op jit(solution)/shard_map/ppermute | solution.py:205
  28.2 4.4 %collective-permute-start.8 = (bf16[128,128]{1,0:T(8,128)(2,1)S(1)}, bf16[128,128]{1,0:T(8,128)(2,1)S(1)}, u32[]{:S(2)}, u32[]{:S(2)}) collective-permute-start(bf16[128,128]{1,0:T(8,128)(2,1)S(1)} %collective-permute-done.refs_0_), channel_id=1, source_target_pairs={{1,0},{0,1},{3,2},{2,3},{5,4},{4,5},{7,6},{6,7},{9,8},{8,9},{11,10... | collective-permute-start | bytes 98312 | tf_op jit(solution)/shard_map/ppermute | solution.py:164
  32.9 2.4 %collective-permute-start.7 = (bf16[384,128]{1,0:T(8,128)(2,1)S(1)}, bf16[384,128]{1,0:T(8,128)(2,1)S(1)}, u32[]{:S(2)}, u32[]{:S(2)}) collective-permute-start(bf16[384,128]{1,0:T(8,128)(2,1)S(1)} %pad_maximum_fusion), channel_id=1, source_target_pairs={{64,0},{17,1},{66,2},{19,3},{68,4},{21,5},{70,6},{23,7},{72,8},{25... | collective-permute-start | bytes 294920 | tf_op jit(solution)/shard_map/ppermute | solution.py:205
  35.4 0.8 collective-permute-start.6
  36.1 1.8 %collective-permute-done.7 = bf16[384,128]{1,0:T(8,128)(2,1)S(1)} collective-permute-done((bf16[384,128]{1,0:T(8,128)(2,1)S(1)}, bf16[384,128]{1,0:T(8,128)(2,1)S(1)}, u32[]{:S(2)}, u32[]{:S(2)}) %collective-permute-start.7) | collective-permute-done | bytes 98336 | tf_op jit(solution)/shard_map/ppermute | solution.py:205
  38.0 4.9 %collective-permute-start.9 = (bf16[128,128]{1,0:T(8,128)(2,1)S(1)}, bf16[128,128]{1,0:T(8,128)(2,1)S(1)}, u32[]{:S(2)}, u32[]{:S(2)}) collective-permute-start(bf16[128,128]{1,0:T(8,128)(2,1)S(1)} %collective-permute-done.1.refs_1_), channel_id=1, source_target_pairs={{1,0},{0,1},{3,2},{2,3},{5,4},{4,5},{7,6},{6,7},{9,8},{8,9},{11,10... | collective-permute-start | bytes 98312 | tf_op jit(solution)/shard_map/ppermute | solution.py:164
  42.9 2.6 %collective-permute-start.11 = (bf16[4,32,128]{2,1,0:T(8,128)(2,1)S(1)}, bf16[4,32,128]{2,1,0:T(8,128)(2,1)S(1)}, u32[]{:S(2)}, u32[]{:S(2)}) collective-permute-start(bf16[4,32,128]{2,1,0:T(8,128)(2,1)S(1)} %pad_maximum_fusion.6), channel_id=1, source_target_pairs={{1,0},{0,1},{3,2},{2,3},{5,4},{4,5},{7,6},{6,7},{9,8},{8,9},{11,10... | collective-permute-start | bytes 98312 | tf_op jit(solution)/shard_map/ppermute | solution.py:164
  45.6 1.3 collective-permute-start.10
  46.9 0.6 pad_maximum_fusion.5.refs_6_
  47.5 1.1 collective-permute-start.14
  49.2 0.6 copy-done.3
  49.8 5.4 %users.2 = (bf16[32,128]{1,0:T(8,128)(2,1)}, bf16[16,32,128]{2,1,0:T(8,128)(2,1)}) custom-call(bf16[128,128]{1,0:T(8,128)(2,1)} %copy-done.6, bf16[128,128]{1,0:T(8,128)(2,1)} %copy-done.7, bf16[256,128]{1,0:T(8,128)(2,1)} %copy-done, bf16[128,128]{1,0:T(8,128)(2,1)} %copy-done.8, bf16[128,128]{1,0:T(8,128)(2,1)} %copy-done.9, bf16[256,128]{1,0:T(8,128)(2,1)} %copy-done.3, ...), custom_call_target="tpu_custom_call" | custom-call | tf_op jit(solution)/shard_map/users/pallas_call | solution.py:125
  55.2 3.7 %all-to-all-start.1 = ((bf16[16,32,128]{2,1,0:T(8,128)(2,1)}), bf16[16,32,128]{2,1,0:T(8,128)(2,1)S(1)}, u32[]{:S(2)}, u32[]{:S(2)}) async-start(bf16[16,32,128]{2,1,0:T(8,128)(2,1)} %get-tuple-element.22), calls=%async_computation.1 | async-start | bytes 262144 | tf_op jit(solution)/shard_map/all_to_all | solution.py:157
  58.9 0.7 copy-done.27
  59.6 3.9 %collective-permute-start.12 = (bf16[32,128]{1,0:T(8,128)(2,1)S(1)}, bf16[32,128]{1,0:T(8,128)(2,1)S(1)}, u32[]{:S(2)}, u32[]{:S(2)}) collective-permute-start(bf16[32,128]{1,0:T(8,128)(2,1)S(1)} %copy-done.27), channel_id=1, source_target_pairs={{2,0},{4,2},{6,4},{8,6},{10,8},{12,10},{14,12},{16,14},{18,16},{20... | collective-permute-start | bytes 24584 | tf_op jit(solution)/shard_map/ppermute | solution.py:164
  63.5 2.1 %all-to-all-done.1 = bf16[16,32,128]{2,1,0:T(8,128)(2,1)S(1)} async-done(((bf16[16,32,128]{2,1,0:T(8,128)(2,1)}), bf16[16,32,128]{2,1,0:T(8,128)(2,1)S(1)}, u32[]{:S(2)}, u32[]{:S(2)}) %all-to-all-start.1) | async-done | bytes 131104 | tf_op jit(solution)/shard_map/all_to_all | solution.py:157
  65.7 0.8 broadcast_in_dim.13
  66.5 3.5 %all-to-all-start.2 = ((bf16[8,192,128]{2,1,0:T(8,128)(2,1)}), bf16[8,192,128]{2,1,0:T(8,128)(2,1)S(1)}, u32[]{:S(2)}, u32[]{:S(2)}) async-start(bf16[8,192,128]{2,1,0:T(8,128)(2,1)} %broadcast_in_dim.13), calls=%async_computation.2 | async-start | bytes 786432 | tf_op jit(solution)/shard_map/all_to_all | solution.py:157
  70.0 1.8 %collective-permute-start.15 = (bf16[32,128]{1,0:T(8,128)(2,1)S(1)}, bf16[32,128]{1,0:T(8,128)(2,1)S(1)}, u32[]{:S(2)}, u32[]{:S(2)}) collective-permute-start(bf16[32,128]{1,0:T(8,128)(2,1)S(1)} %collective-permute-done.12.refs_0_), channel_id=1, source_target_pairs={{1,0},{0,1},{3,2},{2,3},{5,4},{4,5},{7,6},{6,7},{9,8},{8,9},{11,10... | collective-permute-start | bytes 24584 | tf_op jit(solution)/shard_map/ppermute | solution.py:164
  71.9 10.4 %all-to-all-done.2 = bf16[8,192,128]{2,1,0:T(8,128)(2,1)S(1)} async-done(((bf16[8,192,128]{2,1,0:T(8,128)(2,1)}), bf16[8,192,128]{2,1,0:T(8,128)(2,1)S(1)}, u32[]{:S(2)}, u32[]{:S(2)}) %all-to-all-start.2) | async-done | bytes 393248 | tf_op jit(solution)/shard_map/all_to_all | solution.py:157
  82.4 3.2 %collective-permute-start.17 = (bf16[32,128]{1,0:T(8,128)(2,1)S(1)}, bf16[32,128]{1,0:T(8,128)(2,1)S(1)}, u32[]{:S(2)}, u32[]{:S(2)}) collective-permute-start(bf16[32,128]{1,0:T(8,128)(2,1)S(1)} %get-tuple-element.45.refs_2_), channel_id=1, source_target_pairs={{1,0},{0,1},{3,2},{2,3},{5,4},{4,5},{7,6},{6,7},{9,8},{8,9},{11,10... | collective-permute-start | bytes 24584 | tf_op jit(solution)/shard_map/ppermute | solution.py:164
  85.6 0.6 dynamic-slice_bitcast_fusion.4
  87.3 3.1 %items.1 = (bf16[128,128]{1,0:T(8,128)(2,1)}, bf16[8,128,128]{2,1,0:T(8,128)(2,1)}) custom-call(bf16[32,128]{1,0:T(8,128)(2,1)} %copy-done.19, bf16[32,128]{1,0:T(8,128)(2,1)} %copy-done.10, bf16[32,128]{1,0:T(8,128)(2,1)} %copy-done.12, bf16[32,128]{1,0:T(8,128)(2,1)} %copy-done.11, bf16[32,128]{1,0:T(8,128)(2,1)} %copy-done.20, ...), custom_call_target="tpu_custom_call" | custom-call | tf_op jit(solution)/shard_map/items/pallas_call | solution.py:143
  90.4 3.5 %all-to-all-start.3 = ((bf16[8,128,128]{2,1,0:T(8,128)(2,1)}), bf16[8,128,128]{2,1,0:T(8,128)(2,1)S(1)}, u32[]{:S(2)}, u32[]{:S(2)}) async-start(bf16[8,128,128]{2,1,0:T(8,128)(2,1)} %get-tuple-element.28), calls=%async_computation.3 | async-start | bytes 524288 | tf_op jit(solution)/shard_map/all_to_all | solution.py:157
  94.0 1.4 %collective-permute-start.19 = (bf16[128,128]{1,0:T(8,128)(2,1)S(1)}, bf16[128,128]{1,0:T(8,128)(2,1)S(1)}, u32[]{:S(2)}, u32[]{:S(2)}) collective-permute-start(bf16[128,128]{1,0:T(8,128)(2,1)S(1)} %copy-done.26), channel_id=1, source_target_pairs={{254,0},{0,2},{2,4},{4,6},{6,8},{8,10},{10,12},{12,14},{14,16},{16... | collective-permute-start | bytes 98312 | tf_op jit(solution)/shard_map/ppermute | solution.py:164
  95.4 1.2 collective-permute-start.20
  96.6 9.6 %all-to-all-done.3 = bf16[8,128,128]{2,1,0:T(8,128)(2,1)S(1)} async-done(((bf16[8,128,128]{2,1,0:T(8,128)(2,1)}), bf16[8,128,128]{2,1,0:T(8,128)(2,1)S(1)}, u32[]{:S(2)}, u32[]{:S(2)}) %all-to-all-start.3) | async-done | bytes 262176 | tf_op jit(solution)/shard_map/all_to_all | solution.py:157
  106.3 1.1 collective-permute-start.23
  107.4 1.2 collective-permute-start.22
  108.6 0.9 collective-permute-done.23
  109.5 2.5 %collective-permute-done.22 = bf16[256,128]{1,0:T(8,128)(2,1)S(1)} collective-permute-done((bf16[256,128]{1,0:T(8,128)(2,1)S(1)}, bf16[256,128]{1,0:T(8,128)(2,1)S(1)}, u32[]{:S(2)}, u32[]{:S(2)}) %collective-permute-start.22) | collective-permute-done | bytes 65568 | tf_op jit(solution)/shard_map/ppermute | solution.py:205
  112.0 1.2 collective-permute-done.21
  113.3 2.5 %collective-permute-start.26 = (bf16[256,128]{1,0:T(8,128)(2,1)S(1)}, bf16[256,128]{1,0:T(8,128)(2,1)S(1)}, u32[]{:S(2)}, u32[]{:S(2)}) collective-permute-start(bf16[256,128]{1,0:T(8,128)(2,1)S(1)} %pad_maximum_fusion.2), channel_id=1, source_target_pairs={{64,0},{17,1},{66,2},{19,3},{68,4},{21,5},{70,6},{23,7},{72,8},{25... | collective-permute-start | bytes 196616 | tf_op jit(solution)/shard_map/ppermute | solution.py:205
  115.8 0.7 collective-permute-start.24
  116.5 0.7 collective-permute-done.26
  117.1 3.4 %collective-permute-done.25 = bf16[256,128]{1,0:T(8,128)(2,1)S(1)} collective-permute-done((bf16[256,128]{1,0:T(8,128)(2,1)S(1)}, bf16[256,128]{1,0:T(8,128)(2,1)S(1)}, u32[]{:S(2)}, u32[]{:S(2)}) %collective-permute-start.25) | collective-permute-done | bytes 65568 | tf_op jit(solution)/shard_map/ppermute | solution.py:205
  120.9 3.5 %collective-permute-start.29 = (bf16[256,128]{1,0:T(8,128)(2,1)S(1)}, bf16[256,128]{1,0:T(8,128)(2,1)S(1)}, u32[]{:S(2)}, u32[]{:S(2)}) collective-permute-start(bf16[256,128]{1,0:T(8,128)(2,1)S(1)} %pad_maximum_fusion.3.refs_2_), channel_id=1, source_target_pairs={{1,0},{0,1},{3,2},{2,3},{5,4},{4,5},{7,6},{6,7},{9,8},{8,9},{11,10... | collective-permute-start | bytes 196616 | tf_op jit(solution)/shard_map/ppermute | solution.py:164
  124.9 0.7 collective-permute-done.27.refs_3_
  126.4 0.6 copy-done.5
  127.0 5.3 %users.3 = bf16[32,128]{1,0:T(8,128)(2,1)} custom-call(bf16[128,128]{1,0:T(8,128)(2,1)} %copy-done.13, bf16[128,128]{1,0:T(8,128)(2,1)} %copy-done.14, bf16[256,128]{1,0:T(8,128)(2,1)} %copy-done.1, bf16[128,128]{1,0:T(8,128)(2,1)} %copy-done.15, bf16[128,128]{1,0:T(8,128)(2,1)} %copy-done.16, bf16[256,128]{1,0:T(8,128)(2,1)} %copy-done.5, ...), custom_call_target="tpu_custom_call" | custom-call | tf_op jit(solution)/shard_map/users/pallas_call | solution.py:125
  (113 shorter events, 4.7 us)
Async XLA Ops:
  0.6 24.9 %collective-permute-start = (bf16[128,128]{1,0:T(8,128)(2,1)}, bf16[128,128]{1,0:T(8,128)(2,1)S(1)}, u32[]{:S(2)}, u32[]{:S(2)}) collective-permute-start(bf16[128,128]{1,0:T(8,128)(2,1)} %param.4), channel_id=1, source_target_pairs={{254,0},{0,2},{2,4},{4,6},{6,8},{8,10},{10,12},{12,14},{14,16},{16... | collective-permute-start | bytes 98312 | tf_op jit(solution)/shard_map/ppermute | solution.py:164
  3.2 22.4 %collective-permute-start.1 = (bf16[128,128]{1,0:T(8,128)(2,1)}, bf16[128,128]{1,0:T(8,128)(2,1)S(1)}, u32[]{:S(2)}, u32[]{:S(2)}) collective-permute-start(bf16[128,128]{1,0:T(8,128)(2,1)} %param.4), channel_id=1, source_target_pairs={{128,0},{130,2},{132,4},{134,6},{136,8},{138,10},{140,12},{142,14}... | collective-permute-start | bytes 98312 | tf_op jit(solution)/shard_map/ppermute | solution.py:164
  7.4 10.7 %copy-start.4 = (bf16[4,64,128]{2,1,0:T(8,128)(2,1)S(1)}, bf16[4,64,128]{2,1,0:T(8,128)(2,1)}, u32[]{:S(2)}) copy-start(bf16[4,64,128]{2,1,0:T(8,128)(2,1)} %param.5) | copy-start | bytes 196612
  7.5 18.1 %all-to-all-start = ((bf16[8,128,128]{2,1,0:T(8,128)(2,1)}), bf16[8,128,128]{2,1,0:T(8,128)(2,1)S(1)}, u32[]{:S(2)}, u32[]{:S(2)}) async-start(bf16[8,128,128]{2,1,0:T(8,128)(2,1)} %broadcast_in_dim.11), calls=%async_computation | async-start | bytes 524288 | tf_op jit(solution)/shard_map/all_to_all | solution.py:157
  19.0 46.7 %collective-permute-start.13 = (bf16[64,128]{1,0:T(8,128)(2,1)S(1)}, bf16[64,128]{1,0:T(8,128)(2,1)S(1)}, u32[]{:S(2)}, u32[]{:S(2)}) collective-permute-start(bf16[64,128]{1,0:T(8,128)(2,1)S(1)} %pad_maximum_fusion.7), channel_id=1, source_target_pairs={{2,0},{4,2},{6,4},{8,6},{10,8},{12,10},{14,12},{16,14},{18,16},{20... | collective-permute-start | bytes 49160 | tf_op jit(solution)/shard_map/ppermute | solution.py:164
  25.6 2.6 %copy-start.6 = (bf16[128,128]{1,0:T(8,128)(2,1)}, bf16[128,128]{1,0:T(8,128)(2,1)S(1)}, u32[]{:S(2)}) copy-start(bf16[128,128]{1,0:T(8,128)(2,1)S(1)} %collective-permute-done.refs_0_) | copy-start | bytes 98308
  25.6 12.4 %copy-start.7 = (bf16[128,128]{1,0:T(8,128)(2,1)}, bf16[128,128]{1,0:T(8,128)(2,1)S(1)}, u32[]{:S(2)}) copy-start(bf16[128,128]{1,0:T(8,128)(2,1)S(1)} %collective-permute-done.1.refs_1_) | copy-start | bytes 98308
  25.7 6.9 %collective-permute-start.4 = (bf16[384,128]{1,0:T(8,128)(2,1)S(1)}, bf16[384,128]{1,0:T(8,128)(2,1)S(1)}, u32[]{:S(2)}, u32[]{:S(2)}) collective-permute-start(bf16[384,128]{1,0:T(8,128)(2,1)S(1)} %get-tuple-element.34), channel_id=1, source_target_pairs={{16,0},{65,1},{18,2},{67,3},{20,4},{69,5},{22,6},{71,7},{24,8},{73... | collective-permute-start | bytes 294920 | tf_op jit(solution)/shard_map/ppermute | solution.py:205
  26.1 6.4 %collective-permute-start.3 = (bf16[384,128]{1,0:T(8,128)(2,1)S(1)}, bf16[384,128]{1,0:T(8,128)(2,1)S(1)}, u32[]{:S(2)}, u32[]{:S(2)}) collective-permute-start(bf16[384,128]{1,0:T(8,128)(2,1)S(1)} %get-tuple-element.34), channel_id=1, source_target_pairs={{32,0},{129,1},{34,2},{131,3},{36,4},{133,5},{38,6},{135,7},{40,8}... | collective-permute-start | bytes 294920 | tf_op jit(solution)/shard_map/ppermute | solution.py:205
  28.2 4.7 %collective-permute-start.2 = (bf16[384,128]{1,0:T(8,128)(2,1)S(1)}, bf16[384,128]{1,0:T(8,128)(2,1)S(1)}, u32[]{:S(2)}, u32[]{:S(2)}) collective-permute-start(bf16[384,128]{1,0:T(8,128)(2,1)S(1)} %get-tuple-element.34), channel_id=1, source_target_pairs={{48,0},{193,1},{50,2},{195,3},{52,4},{197,5},{54,6},{199,7},{56,8}... | collective-permute-start | bytes 294920 | tf_op jit(solution)/shard_map/ppermute | solution.py:205
  28.2 19.3 %collective-permute-start.8 = (bf16[128,128]{1,0:T(8,128)(2,1)S(1)}, bf16[128,128]{1,0:T(8,128)(2,1)S(1)}, u32[]{:S(2)}, u32[]{:S(2)}) collective-permute-start(bf16[128,128]{1,0:T(8,128)(2,1)S(1)} %collective-permute-done.refs_0_), channel_id=1, source_target_pairs={{1,0},{0,1},{3,2},{2,3},{5,4},{4,5},{7,6},{6,7},{9,8},{8,9},{11,10... | collective-permute-start | bytes 98312 | tf_op jit(solution)/shard_map/ppermute | solution.py:164
  32.9 5.0 %collective-permute-start.7 = (bf16[384,128]{1,0:T(8,128)(2,1)S(1)}, bf16[384,128]{1,0:T(8,128)(2,1)S(1)}, u32[]{:S(2)}, u32[]{:S(2)}) collective-permute-start(bf16[384,128]{1,0:T(8,128)(2,1)S(1)} %pad_maximum_fusion), channel_id=1, source_target_pairs={{64,0},{17,1},{66,2},{19,3},{68,4},{21,5},{70,6},{23,7},{72,8},{25... | collective-permute-start | bytes 294920 | tf_op jit(solution)/shard_map/ppermute | solution.py:205
  35.4 7.5 %collective-permute-start.6 = (bf16[384,128]{1,0:T(8,128)(2,1)S(1)}, bf16[384,128]{1,0:T(8,128)(2,1)S(1)}, u32[]{:S(2)}, u32[]{:S(2)}) collective-permute-start(bf16[384,128]{1,0:T(8,128)(2,1)S(1)} %pad_maximum_fusion), channel_id=1, source_target_pairs={{128,0},{33,1},{130,2},{35,3},{132,4},{37,5},{134,6},{39,7},{136,8... | collective-permute-start | bytes 294920 | tf_op jit(solution)/shard_map/ppermute | solution.py:205
  36.1 9.4 %collective-permute-start.5 = (bf16[384,128]{1,0:T(8,128)(2,1)S(1)}, bf16[384,128]{1,0:T(8,128)(2,1)S(1)}, u32[]{:S(2)}, u32[]{:S(2)}) collective-permute-start(bf16[384,128]{1,0:T(8,128)(2,1)S(1)} %pad_maximum_fusion), channel_id=1, source_target_pairs={{192,0},{49,1},{194,2},{51,3},{196,4},{53,5},{198,6},{55,7},{200,8... | collective-permute-start | bytes 294920 | tf_op jit(solution)/shard_map/ppermute | solution.py:205
  38.0 10.6 %collective-permute-start.9 = (bf16[128,128]{1,0:T(8,128)(2,1)S(1)}, bf16[128,128]{1,0:T(8,128)(2,1)S(1)}, u32[]{:S(2)}, u32[]{:S(2)}) collective-permute-start(bf16[128,128]{1,0:T(8,128)(2,1)S(1)} %collective-permute-done.1.refs_1_), channel_id=1, source_target_pairs={{1,0},{0,1},{3,2},{2,3},{5,4},{4,5},{7,6},{6,7},{9,8},{8,9},{11,10... | collective-permute-start | bytes 98312 | tf_op jit(solution)/shard_map/ppermute | solution.py:164
  42.9 5.7 %collective-permute-start.11 = (bf16[4,32,128]{2,1,0:T(8,128)(2,1)S(1)}, bf16[4,32,128]{2,1,0:T(8,128)(2,1)S(1)}, u32[]{:S(2)}, u32[]{:S(2)}) collective-permute-start(bf16[4,32,128]{2,1,0:T(8,128)(2,1)S(1)} %pad_maximum_fusion.6), channel_id=1, source_target_pairs={{1,0},{0,1},{3,2},{2,3},{5,4},{4,5},{7,6},{6,7},{9,8},{8,9},{11,10... | collective-permute-start | bytes 98312 | tf_op jit(solution)/shard_map/ppermute | solution.py:164
  45.6 3.0 %copy-start = (bf16[256,128]{1,0:T(8,128)(2,1)}, bf16[256,128]{1,0:T(8,128)(2,1)S(1)}, u32[]{:S(2)}) copy-start(bf16[256,128]{1,0:T(8,128)(2,1)S(1)} %pad_maximum_fusion.1.refs_2_) | copy-start | bytes 196612
  45.6 3.0 %collective-permute-start.10 = (bf16[256,128]{1,0:T(8,128)(2,1)S(1)}, bf16[256,128]{1,0:T(8,128)(2,1)S(1)}, u32[]{:S(2)}, u32[]{:S(2)}) collective-permute-start(bf16[256,128]{1,0:T(8,128)(2,1)S(1)} %pad_maximum_fusion.1.refs_2_), channel_id=1, source_target_pairs={{1,0},{0,1},{3,2},{2,3},{5,4},{4,5},{7,6},{6,7},{9,8},{8,9},{11,10... | collective-permute-start | bytes 196616 | tf_op jit(solution)/shard_map/ppermute | solution.py:164
  47.5 1.1 copy-start.8
  47.5 18.1 %collective-permute-start.14 = (bf16[64,128]{1,0:T(8,128)(2,1)S(1)}, bf16[64,128]{1,0:T(8,128)(2,1)S(1)}, u32[]{:S(2)}, u32[]{:S(2)}) collective-permute-start(bf16[64,128]{1,0:T(8,128)(2,1)S(1)} %pad_maximum_fusion.8), channel_id=1, source_target_pairs={{128,0},{130,2},{132,4},{134,6},{136,8},{138,10},{140,12},{142,14}... | collective-permute-start | bytes 49160 | tf_op jit(solution)/shard_map/ppermute | solution.py:164
  55.2 10.4 %all-to-all-start.1 = ((bf16[16,32,128]{2,1,0:T(8,128)(2,1)}), bf16[16,32,128]{2,1,0:T(8,128)(2,1)S(1)}, u32[]{:S(2)}, u32[]{:S(2)}) async-start(bf16[16,32,128]{2,1,0:T(8,128)(2,1)} %get-tuple-element.22), calls=%async_computation.1 | async-start | bytes 262144 | tf_op jit(solution)/shard_map/all_to_all | solution.py:157
  59.6 6.0 %collective-permute-start.12 = (bf16[32,128]{1,0:T(8,128)(2,1)S(1)}, bf16[32,128]{1,0:T(8,128)(2,1)S(1)}, u32[]{:S(2)}, u32[]{:S(2)}) collective-permute-start(bf16[32,128]{1,0:T(8,128)(2,1)S(1)} %copy-done.27), channel_id=1, source_target_pairs={{2,0},{4,2},{6,4},{8,6},{10,8},{12,10},{14,12},{16,14},{18,16},{20... | collective-permute-start | bytes 24584 | tf_op jit(solution)/shard_map/ppermute | solution.py:164
  65.6 6.2 %copy-start.10 = (bf16[32,128]{1,0:T(8,128)(2,1)}, bf16[32,128]{1,0:T(8,128)(2,1)S(1)}, u32[]{:S(2)}) copy-start(bf16[32,128]{1,0:T(8,128)(2,1)S(1)} %get-tuple-element.62.refs_1_) | copy-start | bytes 24580
  65.6 0.9 copy-start.17
  65.7 4.3 %copy-start.19 = (bf16[32,128]{1,0:T(8,128)(2,1)}, bf16[32,128]{1,0:T(8,128)(2,1)S(1)}, u32[]{:S(2)}) copy-start(bf16[32,128]{1,0:T(8,128)(2,1)S(1)} %collective-permute-done.12.refs_0_) | copy-start | bytes 24580
  66.5 15.8 %all-to-all-start.2 = ((bf16[8,192,128]{2,1,0:T(8,128)(2,1)}), bf16[8,192,128]{2,1,0:T(8,128)(2,1)S(1)}, u32[]{:S(2)}, u32[]{:S(2)}) async-start(bf16[8,192,128]{2,1,0:T(8,128)(2,1)} %broadcast_in_dim.13), calls=%async_computation.2 | async-start | bytes 786432 | tf_op jit(solution)/shard_map/all_to_all | solution.py:157
  70.0 16.3 %collective-permute-start.15 = (bf16[32,128]{1,0:T(8,128)(2,1)S(1)}, bf16[32,128]{1,0:T(8,128)(2,1)S(1)}, u32[]{:S(2)}, u32[]{:S(2)}) collective-permute-start(bf16[32,128]{1,0:T(8,128)(2,1)S(1)} %collective-permute-done.12.refs_0_), channel_id=1, source_target_pairs={{1,0},{0,1},{3,2},{2,3},{5,4},{4,5},{7,6},{6,7},{9,8},{8,9},{11,10... | collective-permute-start | bytes 24584 | tf_op jit(solution)/shard_map/ppermute | solution.py:164
  71.8 14.5 %collective-permute-start.16 = (bf16[32,128]{1,0:T(8,128)(2,1)S(1)}, bf16[32,128]{1,0:T(8,128)(2,1)S(1)}, u32[]{:S(2)}, u32[]{:S(2)}) collective-permute-start(bf16[32,128]{1,0:T(8,128)(2,1)S(1)} %get-tuple-element.62.refs_1_), channel_id=1, source_target_pairs={{1,0},{0,1},{3,2},{2,3},{5,4},{4,5},{7,6},{6,7},{9,8},{8,9},{11,10... | collective-permute-start | bytes 24584 | tf_op jit(solution)/shard_map/ppermute | solution.py:164
  82.4 3.9 %copy-start.11 = (bf16[32,128]{1,0:T(8,128)(2,1)}, bf16[32,128]{1,0:T(8,128)(2,1)S(1)}, u32[]{:S(2)}) copy-start(bf16[32,128]{1,0:T(8,128)(2,1)S(1)} %get-tuple-element.44.refs_3_) | copy-start | bytes 24580
  82.4 3.9 %copy-start.12 = (bf16[32,128]{1,0:T(8,128)(2,1)}, bf16[32,128]{1,0:T(8,128)(2,1)S(1)}, u32[]{:S(2)}) copy-start(bf16[32,128]{1,0:T(8,128)(2,1)S(1)} %get-tuple-element.45.refs_2_) | copy-start | bytes 24580
  82.4 4.0 %collective-permute-start.17 = (bf16[32,128]{1,0:T(8,128)(2,1)S(1)}, bf16[32,128]{1,0:T(8,128)(2,1)S(1)}, u32[]{:S(2)}, u32[]{:S(2)}) collective-permute-start(bf16[32,128]{1,0:T(8,128)(2,1)S(1)} %get-tuple-element.45.refs_2_), channel_id=1, source_target_pairs={{1,0},{0,1},{3,2},{2,3},{5,4},{4,5},{7,6},{6,7},{9,8},{8,9},{11,10... | collective-permute-start | bytes 24584 | tf_op jit(solution)/shard_map/ppermute | solution.py:164
  85.5 1.2 collective-permute-start.18
  90.4 3.6 %copy-start.26 = (bf16[128,128]{1,0:T(8,128)(2,1)S(1)}, bf16[128,128]{1,0:T(8,128)(2,1)}, u32[]{:S(2)}) copy-start(bf16[128,128]{1,0:T(8,128)(2,1)} %get-tuple-element.17) | copy-start | bytes 98308
  90.4 15.8 %all-to-all-start.3 = ((bf16[8,128,128]{2,1,0:T(8,128)(2,1)}), bf16[8,128,128]{2,1,0:T(8,128)(2,1)S(1)}, u32[]{:S(2)}, u32[]{:S(2)}) async-start(bf16[8,128,128]{2,1,0:T(8,128)(2,1)} %get-tuple-element.28), calls=%async_computation.3 | async-start | bytes 524288 | tf_op jit(solution)/shard_map/all_to_all | solution.py:157
  94.0 12.2 %collective-permute-start.19 = (bf16[128,128]{1,0:T(8,128)(2,1)S(1)}, bf16[128,128]{1,0:T(8,128)(2,1)S(1)}, u32[]{:S(2)}, u32[]{:S(2)}) collective-permute-start(bf16[128,128]{1,0:T(8,128)(2,1)S(1)} %copy-done.26), channel_id=1, source_target_pairs={{254,0},{0,2},{2,4},{4,6},{6,8},{8,10},{10,12},{12,14},{14,16},{16... | collective-permute-start | bytes 98312 | tf_op jit(solution)/shard_map/ppermute | solution.py:164
  95.4 10.9 %collective-permute-start.20 = (bf16[128,128]{1,0:T(8,128)(2,1)S(1)}, bf16[128,128]{1,0:T(8,128)(2,1)S(1)}, u32[]{:S(2)}, u32[]{:S(2)}) collective-permute-start(bf16[128,128]{1,0:T(8,128)(2,1)S(1)} %copy-done.26), channel_id=1, source_target_pairs={{128,0},{130,2},{132,4},{134,6},{136,8},{138,10},{140,12},{142,14}... | collective-permute-start | bytes 98312 | tf_op jit(solution)/shard_map/ppermute | solution.py:164
  106.2 18.1 %copy-start.13 = (bf16[128,128]{1,0:T(8,128)(2,1)}, bf16[128,128]{1,0:T(8,128)(2,1)S(1)}, u32[]{:S(2)}) copy-start(bf16[128,128]{1,0:T(8,128)(2,1)S(1)} %collective-permute-done.19.refs_0_) | copy-start | bytes 98308
  106.3 18.2 %copy-start.14 = (bf16[128,128]{1,0:T(8,128)(2,1)}, bf16[128,128]{1,0:T(8,128)(2,1)S(1)}, u32[]{:S(2)}) copy-start(bf16[128,128]{1,0:T(8,128)(2,1)S(1)} %collective-permute-done.20.refs_1_) | copy-start | bytes 98308
  106.3 3.2 %collective-permute-start.23 = (bf16[256,128]{1,0:T(8,128)(2,1)S(1)}, bf16[256,128]{1,0:T(8,128)(2,1)S(1)}, u32[]{:S(2)}, u32[]{:S(2)}) collective-permute-start(bf16[256,128]{1,0:T(8,128)(2,1)S(1)} %constant_dynamic-update-slice_fusion.6), channel_id=1, source_target_pairs={{16,0},{65,1},{18,2},{67,3},{20,4},{69,5},{22,6},{71,7},{24,8},{73... | collective-permute-start | bytes 196616 | tf_op jit(solution)/shard_map/ppermute | solution.py:205
  107.4 4.6 %collective-permute-start.22 = (bf16[256,128]{1,0:T(8,128)(2,1)S(1)}, bf16[256,128]{1,0:T(8,128)(2,1)S(1)}, u32[]{:S(2)}, u32[]{:S(2)}) collective-permute-start(bf16[256,128]{1,0:T(8,128)(2,1)S(1)} %constant_dynamic-update-slice_fusion.6), channel_id=1, source_target_pairs={{32,0},{129,1},{34,2},{131,3},{36,4},{133,5},{38,6},{135,7},{40,8}... | collective-permute-start | bytes 196616 | tf_op jit(solution)/shard_map/ppermute | solution.py:205
  108.6 4.6 %collective-permute-start.21 = (bf16[256,128]{1,0:T(8,128)(2,1)S(1)}, bf16[256,128]{1,0:T(8,128)(2,1)S(1)}, u32[]{:S(2)}, u32[]{:S(2)}) collective-permute-start(bf16[256,128]{1,0:T(8,128)(2,1)S(1)} %constant_dynamic-update-slice_fusion.6), channel_id=1, source_target_pairs={{48,0},{193,1},{50,2},{195,3},{52,4},{197,5},{54,6},{199,7},{56,8}... | collective-permute-start | bytes 196616 | tf_op jit(solution)/shard_map/ppermute | solution.py:205
  113.3 3.8 %collective-permute-start.26 = (bf16[256,128]{1,0:T(8,128)(2,1)S(1)}, bf16[256,128]{1,0:T(8,128)(2,1)S(1)}, u32[]{:S(2)}, u32[]{:S(2)}) collective-permute-start(bf16[256,128]{1,0:T(8,128)(2,1)S(1)} %pad_maximum_fusion.2), channel_id=1, source_target_pairs={{64,0},{17,1},{66,2},{19,3},{68,4},{21,5},{70,6},{23,7},{72,8},{25... | collective-permute-start | bytes 196616 | tf_op jit(solution)/shard_map/ppermute | solution.py:205
  115.8 4.7 %collective-permute-start.25 = (bf16[256,128]{1,0:T(8,128)(2,1)S(1)}, bf16[256,128]{1,0:T(8,128)(2,1)S(1)}, u32[]{:S(2)}, u32[]{:S(2)}) collective-permute-start(bf16[256,128]{1,0:T(8,128)(2,1)S(1)} %pad_maximum_fusion.2), channel_id=1, source_target_pairs={{128,0},{33,1},{130,2},{35,3},{132,4},{37,5},{134,6},{39,7},{136,8... | collective-permute-start | bytes 196616 | tf_op jit(solution)/shard_map/ppermute | solution.py:205
  115.8 5.0 %collective-permute-start.24 = (bf16[256,128]{1,0:T(8,128)(2,1)S(1)}, bf16[256,128]{1,0:T(8,128)(2,1)S(1)}, u32[]{:S(2)}, u32[]{:S(2)}) collective-permute-start(bf16[256,128]{1,0:T(8,128)(2,1)S(1)} %pad_maximum_fusion.2), channel_id=1, source_target_pairs={{192,0},{49,1},{194,2},{51,3},{196,4},{53,5},{198,6},{55,7},{200,8... | collective-permute-start | bytes 196616 | tf_op jit(solution)/shard_map/ppermute | solution.py:205
  120.9 4.9 %copy-start.1 = (bf16[256,128]{1,0:T(8,128)(2,1)}, bf16[256,128]{1,0:T(8,128)(2,1)S(1)}, u32[]{:S(2)}) copy-start(bf16[256,128]{1,0:T(8,128)(2,1)S(1)} %pad_maximum_fusion.3.refs_2_) | copy-start | bytes 196612
  120.9 4.9 %collective-permute-start.29 = (bf16[256,128]{1,0:T(8,128)(2,1)S(1)}, bf16[256,128]{1,0:T(8,128)(2,1)S(1)}, u32[]{:S(2)}, u32[]{:S(2)}) collective-permute-start(bf16[256,128]{1,0:T(8,128)(2,1)S(1)} %pad_maximum_fusion.3.refs_2_), channel_id=1, source_target_pairs={{1,0},{0,1},{3,2},{2,3},{5,4},{4,5},{7,6},{6,7},{9,8},{8,9},{11,10... | collective-permute-start | bytes 196616 | tf_op jit(solution)/shard_map/ppermute | solution.py:164
  124.4 1.2 collective-permute-start.27
  124.5 1.3 collective-permute-start.28
  (14 other events, 9.0 us)

commit v8 on v7

--- a/solution.py
+++ b/solution.py
@@ -289,8 +289,9 @@
 
     def fetch_users(shard, copies, marks, fixed_marks):
         size = shard.shape[0]
-        direct = [fetched_from(shard, AXES, -near)]
-        direct += [fetched_from(m, AXES, -shift) for m, shift in zip(fixed_marks, (near, across))]
+        near_marks, across_marks = lax.optimization_barrier((*fixed_marks, shard))[:2]
+        direct = [fetched_from(jnp.concatenate([shard, near_marks], axis=0), AXES, -near)]
+        direct += [fetched_from(across_marks, AXES, -across)]
         held = swapped_with_all(copies, ("x", "y"))
         pieces = [taken(held, at, 0, size) for at, _ in backward[1:]]
         moving = jnp.concatenate([*pieces[1:], *marks], axis=0)
@@ -298,8 +299,8 @@
         held = swapped_with_all(jnp.broadcast_to(moving, (ring, *moving.shape)), "z")
         free = [taken(held, z_at, k * size, size) for k, (_, z_at) in enumerate(backward[2:])]
         moved = [taken(held, z_at, 2 * size + k * users, users) for k, (_, z_at) in enumerate(backward[2:])]
-        own = [direct[0], pieces[0], *free]
-        return own, [partner(value) for value in own], [*direct[1:], *moved]
+        own = [direct[0][:size], pieces[0], *free]
+        return own, [partner(value) for value in own], [direct[0][size:], direct[1], *moved]
 
     copies = jnp.broadcast_to(item_start, (ring, *item_start.shape))
     own, other, moved = fetch_items(item_start, copies, marks[2:])

time: 133 us -> 132 us (level)
  starting transfers between devices: 70.4 us -> 63.9 us
  waiting for transfers between devices: 34.6 us -> 40.6 us
    ppermute x18 -> x17, starting transfers between devices: 41.1 us -> 30.2 us  [fetched_from(): lax.ppermute(value, axis, [((target + steps) % count, target) for target...]
    all_to_all x4, waiting for transfers between devices: 22.1 us -> 26.5 us  [swapped_with_all(): return lax.all_to_all(copies, axes, split_axis=0, concat_axis=0, tiled=True)]
    ppermute x18 -> x17, waiting for transfers between devices: 1.31 us -> 4.42 us  [fetched_from(): lax.ppermute(value, axis, [((target + steps) % count, target) for target...]
    ppermute x12, starting transfers between devices: 11.2 us -> 13.7 us  [crossed_from(): return lax.ppermute(value, names, pairs)]
    all_to_all x4, starting transfers between devices: 18.1 us -> 20 us  [swapped_with_all(): return lax.all_to_all(copies, axes, split_axis=0, concat_axis=0, tiled=True)]
    ppermute x12, waiting for transfers between devices: 11.1 us -> 9.7 us  [crossed_from(): return lax.ppermute(value, names, pairs)]
    unnamed x62 -> x60, local copies, waits for them, and re-layouts: 5.13 us -> 4.31 us
  transfers between devices with their start and end apart: 34 -> 33, of which waited for: 15 -> 16; matrix products, arithmetic and copies ran while one was open for 3% -> 3% of each run, Pallas kernels for 4% -> 0%
where the time goes in v8:
time: 132 us; the launch traced here: 131 us
  starting transfers between devices  63.9 us (48%)
  waiting for transfers between devices  40.6 us (31%)
  Pallas kernels  13.8 us (10%)
  local copies, waits for them, and re-layouts  8.55 us (6%)
  between operations  3.68 us (3%)
    ppermute x17, starting transfers between devices, fetched_from(): lax.ppermute(value, axis, [((target + steps) % count, target) for target...  30.2 us
    all_to_all x4, waiting for transfers between devices, swapped_with_all(): return lax.all_to_all(copies, axes, split_axis=0, concat_axis=0, tiled=True)  26.5 us
    all_to_all x4, starting transfers between devices, swapped_with_all(): return lax.all_to_all(copies, axes, split_axis=0, concat_axis=0, tiled=True)  20 us
    ppermute x12, starting transfers between devices, crossed_from(): return lax.ppermute(value, names, pairs)  13.7 us
    pallas_call x2, Pallas kernels, solve_users(): pl.pallas_call(functools.partial(users_kernel, pieces=len(own), copies=co...  10.7 us
    ppermute x12, waiting for transfers between devices, crossed_from(): return lax.ppermute(value, names, pairs)  9.7 us
    ppermute x17, waiting for transfers between devices, fetched_from(): lax.ppermute(value, axis, [((target + steps) % count, target) for target...  4.42 us
    unnamed x60, local copies, waits for them, and re-layouts  4.31 us
  transfers between devices with their start and end apart: 33, of which 16 were waited for; matrix products, arithmetic and copies ran while one was open for 3% of the time, Pallas kernels for 0%

profile of v8, /device:TPU:1, one launch (start us, length us, event | category | flops | bytes accessed | tf_op | source)
XLA Modules:
  0.0 131.4 jit_solution(560639083197610976)
XLA Ops:
  0.6 2.5 %collective-permute-start = (bf16[128,128]{1,0:T(8,128)(2,1)}, bf16[128,128]{1,0:T(8,128)(2,1)S(1)}, u32[]{:S(2)}, u32[]{:S(2)}) collective-permute-start(bf16[128,128]{1,0:T(8,128)(2,1)} %param.4), channel_id=1, source_target_pairs={{254,0},{0,2},{2,4},{4,6},{6,8},{8,10},{10,12},{12,14},{14,16},{16... | collective-permute-start | bytes 98312 | tf_op jit(solution)/shard_map/ppermute | solution.py:164
  3.2 2.7 %collective-permute-start.1 = (bf16[128,128]{1,0:T(8,128)(2,1)}, bf16[128,128]{1,0:T(8,128)(2,1)S(1)}, u32[]{:S(2)}, u32[]{:S(2)}) collective-permute-start(bf16[128,128]{1,0:T(8,128)(2,1)} %param.4), channel_id=1, source_target_pairs={{128,0},{130,2},{132,4},{134,6},{136,8},{138,10},{140,12},{142,14}... | collective-permute-start | bytes 98312 | tf_op jit(solution)/shard_map/ppermute | solution.py:164
  5.9 1.5 %broadcast_in_dim.11 = bf16[8,128,128]{2,1,0:T(8,128)(2,1)} broadcast(bf16[128,128]{1,0:T(8,128)(2,1)} %param.4), dimensions={1,2} | broadcast | bytes 294912 | tf_op jit(solution)/shard_map/broadcast_in_dim | solution.py:305
  7.5 7.4 %all-to-all-start = ((bf16[8,128,128]{2,1,0:T(8,128)(2,1)}), bf16[8,128,128]{2,1,0:T(8,128)(2,1)S(1)}, u32[]{:S(2)}, u32[]{:S(2)}) async-start(bf16[8,128,128]{2,1,0:T(8,128)(2,1)} %broadcast_in_dim.11), calls=%async_computation | async-start | bytes 524288 | tf_op jit(solution)/shard_map/all_to_all | solution.py:157
  14.9 0.6 fusion.26
  18.2 0.7 copy-done.4
  19.0 6.0 %all-to-all-done = bf16[8,128,128]{2,1,0:T(8,128)(2,1)S(1)} async-done(((bf16[8,128,128]{2,1,0:T(8,128)(2,1)}), bf16[8,128,128]{2,1,0:T(8,128)(2,1)S(1)}, u32[]{:S(2)}, u32[]{:S(2)}) %all-to-all-start) | async-done | bytes 262176 | tf_op jit(solution)/shard_map/all_to_all | solution.py:157
  25.6 1.7 %collective-permute-start.3 = (bf16[384,128]{1,0:T(8,128)(2,1)S(1)}, bf16[384,128]{1,0:T(8,128)(2,1)S(1)}, u32[]{:S(2)}, u32[]{:S(2)}) collective-permute-start(bf16[384,128]{1,0:T(8,128)(2,1)S(1)} %get-tuple-element.36), channel_id=1, source_target_pairs={{32,0},{129,1},{34,2},{131,3},{36,4},{133,5},{38,6},{135,7},{40,8}... | collective-permute-start | bytes 294920 | tf_op jit(solution)/shard_map/ppermute | solution.py:205
  27.3 0.8 collective-permute-start.4
  28.1 2.9 %collective-permute-done.2 = bf16[384,128]{1,0:T(8,128)(2,1)S(1)} collective-permute-done((bf16[384,128]{1,0:T(8,128)(2,1)S(1)}, bf16[384,128]{1,0:T(8,128)(2,1)S(1)}, u32[]{:S(2)}, u32[]{:S(2)}) %collective-permute-start.2) | collective-permute-done | bytes 98336 | tf_op jit(solution)/shard_map/ppermute | solution.py:205
  31.0 0.6 collective-permute-done.4
  31.7 1.7 %collective-permute-start.5 = (bf16[384,128]{1,0:T(8,128)(2,1)S(1)}, bf16[384,128]{1,0:T(8,128)(2,1)S(1)}, u32[]{:S(2)}, u32[]{:S(2)}) collective-permute-start(bf16[384,128]{1,0:T(8,128)(2,1)S(1)} %pad_maximum_fusion), channel_id=1, source_target_pairs={{192,0},{49,1},{194,2},{51,3},{196,4},{53,5},{198,6},{55,7},{200,8... | collective-permute-start | bytes 294920 | tf_op jit(solution)/shard_map/ppermute | solution.py:205
  33.4 2.6 %collective-permute-start.6 = (bf16[384,128]{1,0:T(8,128)(2,1)S(1)}, bf16[384,128]{1,0:T(8,128)(2,1)S(1)}, u32[]{:S(2)}, u32[]{:S(2)}) collective-permute-start(bf16[384,128]{1,0:T(8,128)(2,1)S(1)} %pad_maximum_fusion), channel_id=1, source_target_pairs={{128,0},{33,1},{130,2},{35,3},{132,4},{37,5},{134,6},{39,7},{136,8... | collective-permute-start | bytes 294920 | tf_op jit(solution)/shard_map/ppermute | solution.py:205
  36.0 1.1 collective-permute-start.7
  37.1 3.5 %collective-permute-start.11 = (bf16[4,32,128]{2,1,0:T(8,128)(2,1)S(1)}, bf16[4,32,128]{2,1,0:T(8,128)(2,1)S(1)}, u32[]{:S(2)}, u32[]{:S(2)}) collective-permute-start(bf16[4,32,128]{2,1,0:T(8,128)(2,1)S(1)} %pad_maximum_fusion.6), channel_id=1, source_target_pairs={{1,0},{0,1},{3,2},{2,3},{5,4},{4,5},{7,6},{6,7},{9,8},{8,9},{11,10... | collective-permute-start | bytes 98312 | tf_op jit(solution)/shard_map/ppermute | solution.py:164
  40.7 3.4 %collective-permute-start.9 = (bf16[128,128]{1,0:T(8,128)(2,1)S(1)}, bf16[128,128]{1,0:T(8,128)(2,1)S(1)}, u32[]{:S(2)}, u32[]{:S(2)}) collective-permute-start(bf16[128,128]{1,0:T(8,128)(2,1)S(1)} %collective-permute-done.1.refs_1_), channel_id=1, source_target_pairs={{1,0},{0,1},{3,2},{2,3},{5,4},{4,5},{7,6},{6,7},{9,8},{8,9},{11,10... | collective-permute-start | bytes 98312 | tf_op jit(solution)/shard_map/ppermute | solution.py:164
  44.1 1.0 collective-permute-start.10
  45.1 0.6 pad_maximum_fusion.5.refs_6_
  46.4 0.6 copy-done.3
  47.0 5.4 %users.2 = (bf16[32,128]{1,0:T(8,128)(2,1)}, bf16[16,32,128]{2,1,0:T(8,128)(2,1)}) custom-call(bf16[128,128]{1,0:T(8,128)(2,1)} %copy-done.6, bf16[128,128]{1,0:T(8,128)(2,1)} %copy-done.7, bf16[256,128]{1,0:T(8,128)(2,1)} %copy-done, bf16[128,128]{1,0:T(8,128)(2,1)} %copy-done.8, bf16[128,128]{1,0:T(8,128)(2,1)} %copy-done.9, bf16[256,128]{1,0:T(8,128)(2,1)} %copy-done.3, ...), custom_call_target="tpu_custom_call" | custom-call | tf_op jit(solution)/shard_map/users/pallas_call | solution.py:125
  52.3 5.6 %all-to-all-start.1 = ((bf16[16,32,128]{2,1,0:T(8,128)(2,1)}), bf16[16,32,128]{2,1,0:T(8,128)(2,1)S(1)}, u32[]{:S(2)}, u32[]{:S(2)}) async-start(bf16[16,32,128]{2,1,0:T(8,128)(2,1)} %get-tuple-element.23), calls=%async_computation.1 | async-start | bytes 262144 | tf_op jit(solution)/shard_map/all_to_all | solution.py:157
  57.9 0.7 copy-done.24
  58.6 4.8 %collective-permute-start.12 = (bf16[96,128]{1,0:T(8,128)(2,1)S(1)}, bf16[96,128]{1,0:T(8,128)(2,1)S(1)}, u32[]{:S(2)}, u32[]{:S(2)}) collective-permute-start(bf16[96,128]{1,0:T(8,128)(2,1)S(1)} %pad_maximum_fusion.7), channel_id=1, source_target_pairs={{2,0},{4,2},{6,4},{8,6},{10,8},{12,10},{14,12},{16,14},{18,16},{20... | collective-permute-start | bytes 73736 | tf_op jit(solution)/shard_map/ppermute | solution.py:164
  64.0 0.6 all-to-all-done.1
  64.7 2.9 %collective-permute-done.13.refs_9_ = bf16[64,128]{1,0:T(8,128)(2,1)S(1)} collective-permute-done((bf16[64,128]{1,0:T(8,128)(2,1)S(1)}, bf16[64,128]{1,0:T(8,128)(2,1)S(1)}, u32[]{:S(2)}, u32[]{:S(2)}) %collective-permute-start.13) | collective-permute-done | bytes 16416 | tf_op jit(solution)/shard_map/ppermute | solution.py:164
  67.5 0.8 broadcast_in_dim.13
  68.4 3.5 %all-to-all-start.2 = ((bf16[8,192,128]{2,1,0:T(8,128)(2,1)}), bf16[8,192,128]{2,1,0:T(8,128)(2,1)S(1)}, u32[]{:S(2)}, u32[]{:S(2)}) async-start(bf16[8,192,128]{2,1,0:T(8,128)(2,1)} %broadcast_in_dim.13), calls=%async_computation.2 | async-start | bytes 786432 | tf_op jit(solution)/shard_map/all_to_all | solution.py:157
  71.9 0.6 slice.155.refs_8_
  72.5 2.0 %collective-permute-start.14 = (bf16[32,128]{1,0:T(8,128)(2,1)S(1)}, bf16[32,128]{1,0:T(8,128)(2,1)S(1)}, u32[]{:S(2)}, u32[]{:S(2)}) collective-permute-start(bf16[32,128]{1,0:T(8,128)(2,1)S(1)} %slice.154.refs_0_), channel_id=1, source_target_pairs={{1,0},{0,1},{3,2},{2,3},{5,4},{4,5},{7,6},{6,7},{9,8},{8,9},{11,10... | collective-permute-start | bytes 24584 | tf_op jit(solution)/shard_map/ppermute | solution.py:164
  74.6 9.5 %all-to-all-done.2 = bf16[8,192,128]{2,1,0:T(8,128)(2,1)S(1)} async-done(((bf16[8,192,128]{2,1,0:T(8,128)(2,1)}), bf16[8,192,128]{2,1,0:T(8,128)(2,1)S(1)}, u32[]{:S(2)}, u32[]{:S(2)}) %all-to-all-start.2) | async-done | bytes 393248 | tf_op jit(solution)/shard_map/all_to_all | solution.py:157
  84.1 3.3 %collective-permute-start.16 = (bf16[32,128]{1,0:T(8,128)(2,1)S(1)}, bf16[32,128]{1,0:T(8,128)(2,1)S(1)}, u32[]{:S(2)}, u32[]{:S(2)}) collective-permute-start(bf16[32,128]{1,0:T(8,128)(2,1)S(1)} %get-tuple-element.47.refs_2_), channel_id=1, source_target_pairs={{1,0},{0,1},{3,2},{2,3},{5,4},{4,5},{7,6},{6,7},{9,8},{8,9},{11,10... | collective-permute-start | bytes 24584 | tf_op jit(solution)/shard_map/ppermute | solution.py:164
  87.5 0.6 dynamic-slice_bitcast_fusion.4
  89.2 3.1 %items.1 = (bf16[128,128]{1,0:T(8,128)(2,1)}, bf16[8,128,128]{2,1,0:T(8,128)(2,1)}) custom-call(bf16[32,128]{1,0:T(8,128)(2,1)} %copy-done.11, bf16[32,128]{1,0:T(8,128)(2,1)} %copy-done.10, bf16[32,128]{1,0:T(8,128)(2,1)} %copy-done.13, bf16[32,128]{1,0:T(8,128)(2,1)} %copy-done.12, bf16[32,128]{1,0:T(8,128)(2,1)} %copy-done.19, ...), custom_call_target="tpu_custom_call" | custom-call | tf_op jit(solution)/shard_map/items/pallas_call | solution.py:143
  92.3 3.5 %all-to-all-start.3 = ((bf16[8,128,128]{2,1,0:T(8,128)(2,1)}), bf16[8,128,128]{2,1,0:T(8,128)(2,1)S(1)}, u32[]{:S(2)}, u32[]{:S(2)}) async-start(bf16[8,128,128]{2,1,0:T(8,128)(2,1)} %get-tuple-element.30), calls=%async_computation.3 | async-start | bytes 524288 | tf_op jit(solution)/shard_map/all_to_all | solution.py:157
  95.9 1.4 %collective-permute-start.18 = (bf16[128,128]{1,0:T(8,128)(2,1)S(1)}, bf16[128,128]{1,0:T(8,128)(2,1)S(1)}, u32[]{:S(2)}, u32[]{:S(2)}) collective-permute-start(bf16[128,128]{1,0:T(8,128)(2,1)S(1)} %copy-done.26), channel_id=1, source_target_pairs={{254,0},{0,2},{2,4},{4,6},{6,8},{8,10},{10,12},{12,14},{14,16},{16... | collective-permute-start | bytes 98312 | tf_op jit(solution)/shard_map/ppermute | solution.py:164
  97.8 10.3 %all-to-all-done.3 = bf16[8,128,128]{2,1,0:T(8,128)(2,1)S(1)} async-done(((bf16[8,128,128]{2,1,0:T(8,128)(2,1)}), bf16[8,128,128]{2,1,0:T(8,128)(2,1)S(1)}, u32[]{:S(2)}, u32[]{:S(2)}) %all-to-all-start.3) | async-done | bytes 262176 | tf_op jit(solution)/shard_map/all_to_all | solution.py:157
  108.3 1.7 %collective-permute-start.21 = (bf16[256,128]{1,0:T(8,128)(2,1)S(1)}, bf16[256,128]{1,0:T(8,128)(2,1)S(1)}, u32[]{:S(2)}, u32[]{:S(2)}) collective-permute-start(bf16[256,128]{1,0:T(8,128)(2,1)S(1)} %constant_dynamic-update-slice_fusion.6), channel_id=1, source_target_pairs={{32,0},{129,1},{34,2},{131,3},{36,4},{133,5},{38,6},{135,7},{40,8}... | collective-permute-start | bytes 196616 | tf_op jit(solution)/shard_map/ppermute | solution.py:205
  110.0 0.9 collective-permute-start.22
  110.9 2.6 %collective-permute-done.20 = bf16[256,128]{1,0:T(8,128)(2,1)S(1)} collective-permute-done((bf16[256,128]{1,0:T(8,128)(2,1)S(1)}, bf16[256,128]{1,0:T(8,128)(2,1)S(1)}, u32[]{:S(2)}, u32[]{:S(2)}) %collective-permute-start.20) | collective-permute-done | bytes 65568 | tf_op jit(solution)/shard_map/ppermute | solution.py:205
  113.6 0.6 collective-permute-done.22
  114.3 2.0 %collective-permute-start.24 = (bf16[256,128]{1,0:T(8,128)(2,1)S(1)}, bf16[256,128]{1,0:T(8,128)(2,1)S(1)}, u32[]{:S(2)}, u32[]{:S(2)}) collective-permute-start(bf16[256,128]{1,0:T(8,128)(2,1)S(1)} %pad_maximum_fusion.2), channel_id=1, source_target_pairs={{128,0},{33,1},{130,2},{35,3},{132,4},{37,5},{134,6},{39,7},{136,8... | collective-permute-start | bytes 196616 | tf_op jit(solution)/shard_map/ppermute | solution.py:205
  116.3 0.6 collective-permute-start.25
  116.9 2.3 %collective-permute-done.23 = bf16[256,128]{1,0:T(8,128)(2,1)S(1)} collective-permute-done((bf16[256,128]{1,0:T(8,128)(2,1)S(1)}, bf16[256,128]{1,0:T(8,128)(2,1)S(1)}, u32[]{:S(2)}, u32[]{:S(2)}) %collective-permute-start.23) | collective-permute-done | bytes 65568 | tf_op jit(solution)/shard_map/ppermute | solution.py:205
  119.3 0.6 collective-permute-done.25
  119.9 3.6 %collective-permute-start.28 = (bf16[256,128]{1,0:T(8,128)(2,1)S(1)}, bf16[256,128]{1,0:T(8,128)(2,1)S(1)}, u32[]{:S(2)}, u32[]{:S(2)}) collective-permute-start(bf16[256,128]{1,0:T(8,128)(2,1)S(1)} %pad_maximum_fusion.3.refs_2_), channel_id=1, source_target_pairs={{1,0},{0,1},{3,2},{2,3},{5,4},{4,5},{7,6},{6,7},{9,8},{8,9},{11,10... | collective-permute-start | bytes 196616 | tf_op jit(solution)/shard_map/ppermute | solution.py:164
  124.1 0.7 collective-permute-done.26.refs_3_
  125.5 0.6 copy-done.5
  126.1 5.3 %users.3 = bf16[32,128]{1,0:T(8,128)(2,1)} custom-call(bf16[128,128]{1,0:T(8,128)(2,1)} %copy-done.14, bf16[128,128]{1,0:T(8,128)(2,1)} %copy-done.15, bf16[256,128]{1,0:T(8,128)(2,1)} %copy-done.1, bf16[128,128]{1,0:T(8,128)(2,1)} %copy-done.16, bf16[128,128]{1,0:T(8,128)(2,1)} %copy-done.17, bf16[256,128]{1,0:T(8,128)(2,1)} %copy-done.5, ...), custom_call_target="tpu_custom_call" | custom-call | tf_op jit(solution)/shard_map/users/pallas_call | solution.py:125
  (111 shorter events, 5.4 us)
Async XLA Ops:
  0.6 24.4 %collective-permute-start = (bf16[128,128]{1,0:T(8,128)(2,1)}, bf16[128,128]{1,0:T(8,128)(2,1)S(1)}, u32[]{:S(2)}, u32[]{:S(2)}) collective-permute-start(bf16[128,128]{1,0:T(8,128)(2,1)} %param.4), channel_id=1, source_target_pairs={{254,0},{0,2},{2,4},{4,6},{6,8},{8,10},{10,12},{12,14},{14,16},{16... | collective-permute-start | bytes 98312 | tf_op jit(solution)/shard_map/ppermute | solution.py:164
  3.2 21.9 %collective-permute-start.1 = (bf16[128,128]{1,0:T(8,128)(2,1)}, bf16[128,128]{1,0:T(8,128)(2,1)S(1)}, u32[]{:S(2)}, u32[]{:S(2)}) collective-permute-start(bf16[128,128]{1,0:T(8,128)(2,1)} %param.4), channel_id=1, source_target_pairs={{128,0},{130,2},{132,4},{134,6},{136,8},{138,10},{140,12},{142,14}... | collective-permute-start | bytes 98312 | tf_op jit(solution)/shard_map/ppermute | solution.py:164
  7.5 7.4 %copy-start.23 = (s32[4]{0:T(128)S(1)}, s32[4]{0:T(128)}, u32[]{:S(2)}) copy-start(s32[4]{0:T(128)} %param.7) | copy-start | bytes 52
  7.5 17.6 %all-to-all-start = ((bf16[8,128,128]{2,1,0:T(8,128)(2,1)}), bf16[8,128,128]{2,1,0:T(8,128)(2,1)S(1)}, u32[]{:S(2)}, u32[]{:S(2)}) async-start(bf16[8,128,128]{2,1,0:T(8,128)(2,1)} %broadcast_in_dim.11), calls=%async_computation | async-start | bytes 524288 | tf_op jit(solution)/shard_map/all_to_all | solution.py:157
  18.1 0.8 copy-start.4
  18.1 0.8 copy-start.25
  25.1 15.5 %copy-start.6 = (bf16[128,128]{1,0:T(8,128)(2,1)}, bf16[128,128]{1,0:T(8,128)(2,1)S(1)}, u32[]{:S(2)}) copy-start(bf16[128,128]{1,0:T(8,128)(2,1)S(1)} %collective-permute-done.refs_0_) | copy-start | bytes 98308
  25.1 15.6 %copy-start.7 = (bf16[128,128]{1,0:T(8,128)(2,1)}, bf16[128,128]{1,0:T(8,128)(2,1)S(1)}, u32[]{:S(2)}) copy-start(bf16[128,128]{1,0:T(8,128)(2,1)S(1)} %collective-permute-done.1.refs_1_) | copy-start | bytes 98308
  25.2 5.8 %collective-permute-start.2 = (bf16[384,128]{1,0:T(8,128)(2,1)S(1)}, bf16[384,128]{1,0:T(8,128)(2,1)S(1)}, u32[]{:S(2)}, u32[]{:S(2)}) collective-permute-start(bf16[384,128]{1,0:T(8,128)(2,1)S(1)} %get-tuple-element.36), channel_id=1, source_target_pairs={{48,0},{193,1},{50,2},{195,3},{52,4},{197,5},{54,6},{199,7},{56,8}... | collective-permute-start | bytes 294920 | tf_op jit(solution)/shard_map/ppermute | solution.py:205
  25.6 5.4 %collective-permute-start.3 = (bf16[384,128]{1,0:T(8,128)(2,1)S(1)}, bf16[384,128]{1,0:T(8,128)(2,1)S(1)}, u32[]{:S(2)}, u32[]{:S(2)}) collective-permute-start(bf16[384,128]{1,0:T(8,128)(2,1)S(1)} %get-tuple-element.36), channel_id=1, source_target_pairs={{32,0},{129,1},{34,2},{131,3},{36,4},{133,5},{38,6},{135,7},{40,8}... | collective-permute-start | bytes 294920 | tf_op jit(solution)/shard_map/ppermute | solution.py:205
  27.3 4.3 %collective-permute-start.4 = (bf16[384,128]{1,0:T(8,128)(2,1)S(1)}, bf16[384,128]{1,0:T(8,128)(2,1)S(1)}, u32[]{:S(2)}, u32[]{:S(2)}) collective-permute-start(bf16[384,128]{1,0:T(8,128)(2,1)S(1)} %get-tuple-element.36), channel_id=1, source_target_pairs={{16,0},{65,1},{18,2},{67,3},{20,4},{69,5},{22,6},{71,7},{24,8},{73... | collective-permute-start | bytes 294920 | tf_op jit(solution)/shard_map/ppermute | solution.py:205
  31.7 8.9 %collective-permute-start.5 = (bf16[384,128]{1,0:T(8,128)(2,1)S(1)}, bf16[384,128]{1,0:T(8,128)(2,1)S(1)}, u32[]{:S(2)}, u32[]{:S(2)}) collective-permute-start(bf16[384,128]{1,0:T(8,128)(2,1)S(1)} %pad_maximum_fusion), channel_id=1, source_target_pairs={{192,0},{49,1},{194,2},{51,3},{196,4},{53,5},{198,6},{55,7},{200,8... | collective-permute-start | bytes 294920 | tf_op jit(solution)/shard_map/ppermute | solution.py:205
  33.4 10.7 %collective-permute-start.6 = (bf16[384,128]{1,0:T(8,128)(2,1)S(1)}, bf16[384,128]{1,0:T(8,128)(2,1)S(1)}, u32[]{:S(2)}, u32[]{:S(2)}) collective-permute-start(bf16[384,128]{1,0:T(8,128)(2,1)S(1)} %pad_maximum_fusion), channel_id=1, source_target_pairs={{128,0},{33,1},{130,2},{35,3},{132,4},{37,5},{134,6},{39,7},{136,8... | collective-permute-start | bytes 294920 | tf_op jit(solution)/shard_map/ppermute | solution.py:205
  36.0 8.1 %collective-permute-start.7 = (bf16[384,128]{1,0:T(8,128)(2,1)S(1)}, bf16[384,128]{1,0:T(8,128)(2,1)S(1)}, u32[]{:S(2)}, u32[]{:S(2)}) collective-permute-start(bf16[384,128]{1,0:T(8,128)(2,1)S(1)} %pad_maximum_fusion), channel_id=1, source_target_pairs={{64,0},{17,1},{66,2},{19,3},{68,4},{21,5},{70,6},{23,7},{72,8},{25... | collective-permute-start | bytes 294920 | tf_op jit(solution)/shard_map/ppermute | solution.py:205
  37.1 8.6 %collective-permute-start.11 = (bf16[4,32,128]{2,1,0:T(8,128)(2,1)S(1)}, bf16[4,32,128]{2,1,0:T(8,128)(2,1)S(1)}, u32[]{:S(2)}, u32[]{:S(2)}) collective-permute-start(bf16[4,32,128]{2,1,0:T(8,128)(2,1)S(1)} %pad_maximum_fusion.6), channel_id=1, source_target_pairs={{1,0},{0,1},{3,2},{2,3},{5,4},{4,5},{7,6},{6,7},{9,8},{8,9},{11,10... | collective-permute-start | bytes 98312 | tf_op jit(solution)/shard_map/ppermute | solution.py:164
  40.6 5.2 %collective-permute-start.8 = (bf16[128,128]{1,0:T(8,128)(2,1)S(1)}, bf16[128,128]{1,0:T(8,128)(2,1)S(1)}, u32[]{:S(2)}, u32[]{:S(2)}) collective-permute-start(bf16[128,128]{1,0:T(8,128)(2,1)S(1)} %collective-permute-done.refs_0_), channel_id=1, source_target_pairs={{1,0},{0,1},{3,2},{2,3},{5,4},{4,5},{7,6},{6,7},{9,8},{8,9},{11,10... | collective-permute-start | bytes 98312 | tf_op jit(solution)/shard_map/ppermute | solution.py:164
  40.7 5.1 %collective-permute-start.9 = (bf16[128,128]{1,0:T(8,128)(2,1)S(1)}, bf16[128,128]{1,0:T(8,128)(2,1)S(1)}, u32[]{:S(2)}, u32[]{:S(2)}) collective-permute-start(bf16[128,128]{1,0:T(8,128)(2,1)S(1)} %collective-permute-done.1.refs_1_), channel_id=1, source_target_pairs={{1,0},{0,1},{3,2},{2,3},{5,4},{4,5},{7,6},{6,7},{9,8},{8,9},{11,10... | collective-permute-start | bytes 98312 | tf_op jit(solution)/shard_map/ppermute | solution.py:164
  44.1 1.9 %copy-start = (bf16[256,128]{1,0:T(8,128)(2,1)}, bf16[256,128]{1,0:T(8,128)(2,1)S(1)}, u32[]{:S(2)}) copy-start(bf16[256,128]{1,0:T(8,128)(2,1)S(1)} %pad_maximum_fusion.1.refs_2_) | copy-start | bytes 196612
  44.1 1.9 %collective-permute-start.10 = (bf16[256,128]{1,0:T(8,128)(2,1)S(1)}, bf16[256,128]{1,0:T(8,128)(2,1)S(1)}, u32[]{:S(2)}, u32[]{:S(2)}) collective-permute-start(bf16[256,128]{1,0:T(8,128)(2,1)S(1)} %pad_maximum_fusion.1.refs_2_), channel_id=1, source_target_pairs={{1,0},{0,1},{3,2},{2,3},{5,4},{4,5},{7,6},{6,7},{9,8},{8,9},{11,10... | collective-permute-start | bytes 196616 | tf_op jit(solution)/shard_map/ppermute | solution.py:164
  52.3 12.3 %all-to-all-start.1 = ((bf16[16,32,128]{2,1,0:T(8,128)(2,1)}), bf16[16,32,128]{2,1,0:T(8,128)(2,1)S(1)}, u32[]{:S(2)}, u32[]{:S(2)}) async-start(bf16[16,32,128]{2,1,0:T(8,128)(2,1)} %get-tuple-element.23), calls=%async_computation.1 | async-start | bytes 262144 | tf_op jit(solution)/shard_map/all_to_all | solution.py:157
  57.9 0.7 copy-start.24
  58.6 8.9 %collective-permute-start.12 = (bf16[96,128]{1,0:T(8,128)(2,1)S(1)}, bf16[96,128]{1,0:T(8,128)(2,1)S(1)}, u32[]{:S(2)}, u32[]{:S(2)}) collective-permute-start(bf16[96,128]{1,0:T(8,128)(2,1)S(1)} %pad_maximum_fusion.7), channel_id=1, source_target_pairs={{2,0},{4,2},{6,4},{8,6},{10,8},{12,10},{14,12},{16,14},{18,16},{20... | collective-permute-start | bytes 73736 | tf_op jit(solution)/shard_map/ppermute | solution.py:164
  63.4 4.1 %collective-permute-start.13 = (bf16[64,128]{1,0:T(8,128)(2,1)S(1)}, bf16[64,128]{1,0:T(8,128)(2,1)S(1)}, u32[]{:S(2)}, u32[]{:S(2)}) collective-permute-start(bf16[64,128]{1,0:T(8,128)(2,1)S(1)} %get-tuple-element.26), channel_id=1, source_target_pairs={{128,0},{130,2},{132,4},{134,6},{136,8},{138,10},{140,12},{142,14}... | collective-permute-start | bytes 49160 | tf_op jit(solution)/shard_map/ppermute | solution.py:164
  64.7 9.8 %copy-start.10 = (bf16[32,128]{1,0:T(8,128)(2,1)}, bf16[32,128]{1,0:T(8,128)(2,1)S(1)}, u32[]{:S(2)}) copy-start(bf16[32,128]{1,0:T(8,128)(2,1)S(1)} %get-tuple-element.64.refs_1_) | copy-start | bytes 24580
  67.5 0.8 copy-start.18
  68.4 15.7 %all-to-all-start.2 = ((bf16[8,192,128]{2,1,0:T(8,128)(2,1)}), bf16[8,192,128]{2,1,0:T(8,128)(2,1)S(1)}, u32[]{:S(2)}, u32[]{:S(2)}) async-start(bf16[8,192,128]{2,1,0:T(8,128)(2,1)} %broadcast_in_dim.13), calls=%async_computation.2 | async-start | bytes 786432 | tf_op jit(solution)/shard_map/all_to_all | solution.py:157
  72.5 15.6 %collective-permute-start.14 = (bf16[32,128]{1,0:T(8,128)(2,1)S(1)}, bf16[32,128]{1,0:T(8,128)(2,1)S(1)}, u32[]{:S(2)}, u32[]{:S(2)}) collective-permute-start(bf16[32,128]{1,0:T(8,128)(2,1)S(1)} %slice.154.refs_0_), channel_id=1, source_target_pairs={{1,0},{0,1},{3,2},{2,3},{5,4},{4,5},{7,6},{6,7},{9,8},{8,9},{11,10... | collective-permute-start | bytes 24584 | tf_op jit(solution)/shard_map/ppermute | solution.py:164
  74.5 13.6 %collective-permute-start.15 = (bf16[32,128]{1,0:T(8,128)(2,1)S(1)}, bf16[32,128]{1,0:T(8,128)(2,1)S(1)}, u32[]{:S(2)}, u32[]{:S(2)}) collective-permute-start(bf16[32,128]{1,0:T(8,128)(2,1)S(1)} %get-tuple-element.64.refs_1_), channel_id=1, source_target_pairs={{1,0},{0,1},{3,2},{2,3},{5,4},{4,5},{7,6},{6,7},{9,8},{8,9},{11,10... | collective-permute-start | bytes 24584 | tf_op jit(solution)/shard_map/ppermute | solution.py:164
  84.1 4.0 %copy-start.12 = (bf16[32,128]{1,0:T(8,128)(2,1)}, bf16[32,128]{1,0:T(8,128)(2,1)S(1)}, u32[]{:S(2)}) copy-start(bf16[32,128]{1,0:T(8,128)(2,1)S(1)} %get-tuple-element.46.refs_3_) | copy-start | bytes 24580
  84.1 4.0 %copy-start.13 = (bf16[32,128]{1,0:T(8,128)(2,1)}, bf16[32,128]{1,0:T(8,128)(2,1)S(1)}, u32[]{:S(2)}) copy-start(bf16[32,128]{1,0:T(8,128)(2,1)S(1)} %get-tuple-element.47.refs_2_) | copy-start | bytes 24580
  84.1 4.1 %collective-permute-start.16 = (bf16[32,128]{1,0:T(8,128)(2,1)S(1)}, bf16[32,128]{1,0:T(8,128)(2,1)S(1)}, u32[]{:S(2)}, u32[]{:S(2)}) collective-permute-start(bf16[32,128]{1,0:T(8,128)(2,1)S(1)} %get-tuple-element.47.refs_2_), channel_id=1, source_target_pairs={{1,0},{0,1},{3,2},{2,3},{5,4},{4,5},{7,6},{6,7},{9,8},{8,9},{11,10... | collective-permute-start | bytes 24584 | tf_op jit(solution)/shard_map/ppermute | solution.py:164
  87.4 1.2 collective-permute-start.17
  92.3 3.6 %copy-start.26 = (bf16[128,128]{1,0:T(8,128)(2,1)S(1)}, bf16[128,128]{1,0:T(8,128)(2,1)}, u32[]{:S(2)}) copy-start(bf16[128,128]{1,0:T(8,128)(2,1)} %get-tuple-element.18) | copy-start | bytes 98308
  92.3 15.8 %all-to-all-start.3 = ((bf16[8,128,128]{2,1,0:T(8,128)(2,1)}), bf16[8,128,128]{2,1,0:T(8,128)(2,1)S(1)}, u32[]{:S(2)}, u32[]{:S(2)}) async-start(bf16[8,128,128]{2,1,0:T(8,128)(2,1)} %get-tuple-element.30), calls=%async_computation.3 | async-start | bytes 524288 | tf_op jit(solution)/shard_map/all_to_all | solution.py:157
  95.9 12.2 %collective-permute-start.18 = (bf16[128,128]{1,0:T(8,128)(2,1)S(1)}, bf16[128,128]{1,0:T(8,128)(2,1)S(1)}, u32[]{:S(2)}, u32[]{:S(2)}) collective-permute-start(bf16[128,128]{1,0:T(8,128)(2,1)S(1)} %copy-done.26), channel_id=1, source_target_pairs={{254,0},{0,2},{2,4},{4,6},{6,8},{8,10},{10,12},{12,14},{14,16},{16... | collective-permute-start | bytes 98312 | tf_op jit(solution)/shard_map/ppermute | solution.py:164
  97.2 10.9 %collective-permute-start.19 = (bf16[128,128]{1,0:T(8,128)(2,1)S(1)}, bf16[128,128]{1,0:T(8,128)(2,1)S(1)}, u32[]{:S(2)}, u32[]{:S(2)}) collective-permute-start(bf16[128,128]{1,0:T(8,128)(2,1)S(1)} %copy-done.26), channel_id=1, source_target_pairs={{128,0},{130,2},{132,4},{134,6},{136,8},{138,10},{140,12},{142,14}... | collective-permute-start | bytes 98312 | tf_op jit(solution)/shard_map/ppermute | solution.py:164
  108.1 15.4 %copy-start.14 = (bf16[128,128]{1,0:T(8,128)(2,1)}, bf16[128,128]{1,0:T(8,128)(2,1)S(1)}, u32[]{:S(2)}) copy-start(bf16[128,128]{1,0:T(8,128)(2,1)S(1)} %collective-permute-done.18.refs_0_) | copy-start | bytes 98308
  108.1 15.5 %copy-start.15 = (bf16[128,128]{1,0:T(8,128)(2,1)}, bf16[128,128]{1,0:T(8,128)(2,1)S(1)}, u32[]{:S(2)}) copy-start(bf16[128,128]{1,0:T(8,128)(2,1)S(1)} %collective-permute-done.19.refs_1_) | copy-start | bytes 98308
  108.2 5.4 %collective-permute-start.20 = (bf16[256,128]{1,0:T(8,128)(2,1)S(1)}, bf16[256,128]{1,0:T(8,128)(2,1)S(1)}, u32[]{:S(2)}, u32[]{:S(2)}) collective-permute-start(bf16[256,128]{1,0:T(8,128)(2,1)S(1)} %constant_dynamic-update-slice_fusion.6), channel_id=1, source_target_pairs={{48,0},{193,1},{50,2},{195,3},{52,4},{197,5},{54,6},{199,7},{56,8}... | collective-permute-start | bytes 196616 | tf_op jit(solution)/shard_map/ppermute | solution.py:205
  108.3 5.3 %collective-permute-start.21 = (bf16[256,128]{1,0:T(8,128)(2,1)S(1)}, bf16[256,128]{1,0:T(8,128)(2,1)S(1)}, u32[]{:S(2)}, u32[]{:S(2)}) collective-permute-start(bf16[256,128]{1,0:T(8,128)(2,1)S(1)} %constant_dynamic-update-slice_fusion.6), channel_id=1, source_target_pairs={{32,0},{129,1},{34,2},{131,3},{36,4},{133,5},{38,6},{135,7},{40,8}... | collective-permute-start | bytes 196616 | tf_op jit(solution)/shard_map/ppermute | solution.py:205
  110.0 4.2 %collective-permute-start.22 = (bf16[256,128]{1,0:T(8,128)(2,1)S(1)}, bf16[256,128]{1,0:T(8,128)(2,1)S(1)}, u32[]{:S(2)}, u32[]{:S(2)}) collective-permute-start(bf16[256,128]{1,0:T(8,128)(2,1)S(1)} %constant_dynamic-update-slice_fusion.6), channel_id=1, source_target_pairs={{16,0},{65,1},{18,2},{67,3},{20,4},{69,5},{22,6},{71,7},{24,8},{73... | collective-permute-start | bytes 196616 | tf_op jit(solution)/shard_map/ppermute | solution.py:205
  114.2 5.1 %collective-permute-start.23 = (bf16[256,128]{1,0:T(8,128)(2,1)S(1)}, bf16[256,128]{1,0:T(8,128)(2,1)S(1)}, u32[]{:S(2)}, u32[]{:S(2)}) collective-permute-start(bf16[256,128]{1,0:T(8,128)(2,1)S(1)} %pad_maximum_fusion.2), channel_id=1, source_target_pairs={{192,0},{49,1},{194,2},{51,3},{196,4},{53,5},{198,6},{55,7},{200,8... | collective-permute-start | bytes 196616 | tf_op jit(solution)/shard_map/ppermute | solution.py:205
  114.3 5.0 %collective-permute-start.24 = (bf16[256,128]{1,0:T(8,128)(2,1)S(1)}, bf16[256,128]{1,0:T(8,128)(2,1)S(1)}, u32[]{:S(2)}, u32[]{:S(2)}) collective-permute-start(bf16[256,128]{1,0:T(8,128)(2,1)S(1)} %pad_maximum_fusion.2), channel_id=1, source_target_pairs={{128,0},{33,1},{130,2},{35,3},{132,4},{37,5},{134,6},{39,7},{136,8... | collective-permute-start | bytes 196616 | tf_op jit(solution)/shard_map/ppermute | solution.py:205
  116.3 3.5 %collective-permute-start.25 = (bf16[256,128]{1,0:T(8,128)(2,1)S(1)}, bf16[256,128]{1,0:T(8,128)(2,1)S(1)}, u32[]{:S(2)}, u32[]{:S(2)}) collective-permute-start(bf16[256,128]{1,0:T(8,128)(2,1)S(1)} %pad_maximum_fusion.2), channel_id=1, source_target_pairs={{64,0},{17,1},{66,2},{19,3},{68,4},{21,5},{70,6},{23,7},{72,8},{25... | collective-permute-start | bytes 196616 | tf_op jit(solution)/shard_map/ppermute | solution.py:205
  119.9 5.0 %copy-start.1 = (bf16[256,128]{1,0:T(8,128)(2,1)}, bf16[256,128]{1,0:T(8,128)(2,1)S(1)}, u32[]{:S(2)}) copy-start(bf16[256,128]{1,0:T(8,128)(2,1)S(1)} %pad_maximum_fusion.3.refs_2_) | copy-start | bytes 196612
  119.9 5.0 %collective-permute-start.28 = (bf16[256,128]{1,0:T(8,128)(2,1)S(1)}, bf16[256,128]{1,0:T(8,128)(2,1)S(1)}, u32[]{:S(2)}, u32[]{:S(2)}) collective-permute-start(bf16[256,128]{1,0:T(8,128)(2,1)S(1)} %pad_maximum_fusion.3.refs_2_), channel_id=1, source_target_pairs={{1,0},{0,1},{3,2},{2,3},{5,4},{4,5},{7,6},{6,7},{9,8},{8,9},{11,10... | collective-permute-start | bytes 196616 | tf_op jit(solution)/shard_map/ppermute | solution.py:164
  123.5 1.2 collective-permute-start.26
  123.7 1.3 collective-permute-start.27
  (12 other events, 7.2 us)
